TPU v7x, 512 devices: a whole 4x8x8 slice. The times are simulated.
512 devices in a mesh: dp: 16 (over z, core), fsdp: 32 (over x, y).
Axes of the slice: x: 4, y: 8, z: 8, core: 2. Of those that a mesh axis runs over, the one named last changes fastest.
Arguments:
- replica_grads: bfloat16 [16, 8192, 4096], P('dp', 'fsdp'), may hold values from -4 to 4
- slot_table: int32 [32], replicated, may hold values from 0 to 63, as said below
- left_gram_state: float32 [64, 4, 16, 16, 1024], P('fsdp', None, 'dp')
- right_gram_state: float32 [64, 4, 16, 16, 1024], P('fsdp', None, 'dp')
- left_inverse_root: bfloat16 [64, 4, 16, 16, 1024], P('fsdp', None, 'dp')
- right_inverse_root: bfloat16 [64, 4, 16, 16, 1024], P('fsdp', None, 'dp')
Outputs:
- direction: bfloat16 [32, 16, 16, 4096], P('fsdp', 'dp')
- left_new: float32 [64, 4, 16, 16, 1024], P('fsdp', None, 'dp')
- right_new: float32 [64, 4, 16, 16, 1024], P('fsdp', None, 'dp')
Inputs may be any that keep to these rules, and one draw needn't show every extreme that they name: `slot_table`: the entries are distinct; slot v belongs to owner v // 2 of the flat shards' devices; some owner holds 2 blocks.
All inputs are finite; a program needn't handle non-finite values.
Results may differ from a plain program's by a relative error of at most 0.02.
Values may be sent and summed in bfloat16 or wider, within the bound.
No kernel may reach another device: no remote copies, remote signals or barrier semaphores. Data moves between devices by JAX's collectives and lax.ppermute only.
A program may use at most 128 MiB of HBM per device.

v0:
```python
import jax
import jax.numpy as jnp
from jax import lax
from jax.sharding import PartitionSpec as P


def on_device(
    replica_grads,
    slot_table,
    left_gram_state,
    right_gram_state,
    left_inverse_root,
    right_inverse_root,
):
    slots_here = left_gram_state.shape[0]
    sub_blocks = left_gram_state.shape[1]
    strip_rows = left_gram_state.shape[3]
    block_size = left_gram_state.shape[4]
    band_rows = replica_grads.shape[1]
    model_width = replica_grads.shape[2]
    per_band = model_width // block_size
    shards = lax.axis_size("fsdp")
    groups = lax.axis_size("dp")
    total_slots = shards * slots_here
    block_count = slot_table.shape[0]
    band_index = lax.axis_index("fsdp")
    strip_index = lax.axis_index("dp")
    slot_indices = jnp.arange(total_slots, dtype=jnp.int32)
    right_entire = lax.all_gather(right_inverse_root, "dp", axis=2, tiled=True).reshape(
        slots_here, block_size, block_size
    )
    summed = lax.psum_scatter(
        replica_grads[0].astype(jnp.float32).astype(jnp.bfloat16),
        "dp",
        scatter_dimension=0,
        tiled=True,
    )
    row_block = band_index * band_rows // block_size
    targets = lax.dynamic_slice_in_dim(slot_table, row_block * per_band, per_band, 0)
    chooser = (targets[:, None] == slot_indices[None, :]).astype(jnp.bfloat16)
    own_slots = band_index * slots_here + jnp.arange(slots_here, dtype=jnp.int32)
    holder = slot_table[None, :] == own_slots[:, None]
    block_of = jnp.sum(
        jnp.where(holder, jnp.arange(block_count, dtype=jnp.int32)[None, :], 0), axis=1
    )
    first_band = block_of // per_band * sub_blocks
    outgoing = jnp.einsum(
        "cn,tcb->ntb",
        chooser,
        summed.reshape(strip_rows, per_band, block_size),
        preferred_element_type=jnp.float32,
    ).astype(jnp.bfloat16)
    outgoing = outgoing.reshape(shards, slots_here, strip_rows, block_size)
    arrived = lax.all_to_all(outgoing, "fsdp", split_axis=0, concat_axis=0, tiled=True)
    owned_rows = jax.vmap(
        lambda portion, offset: lax.dynamic_slice_in_dim(portion, offset, sub_blocks, 0),
        in_axes=(1, 0),
    )(arrived, first_band)
    owned_rows = owned_rows.reshape(slots_here, sub_blocks, 1, strip_rows, block_size)
    entire = lax.all_gather(owned_rows, "dp", axis=2, tiled=True).reshape(
        slots_here, block_size, block_size
    )
    my_rows = owned_rows.reshape(slots_here, sub_blocks * strip_rows, block_size)
    left_gram = jnp.einsum("mrc,mnc->mrn", my_rows, entire, preferred_element_type=jnp.float32)
    left_new = left_gram_state + (left_gram / block_size).reshape(left_gram_state.shape)
    my_columns = lax.dynamic_index_in_dim(
        entire.reshape(slots_here, block_size, sub_blocks, groups, strip_rows),
        strip_index,
        3,
        keepdims=False,
    )
    my_columns = my_columns.reshape(slots_here, block_size, sub_blocks * strip_rows)
    right_gram = jnp.einsum("mnr,mnc->mrc", my_columns, entire, preferred_element_type=jnp.float32)
    right_new = right_gram_state + (right_gram / block_size).reshape(right_gram_state.shape)
    left_rows = left_inverse_root.reshape(slots_here, sub_blocks * strip_rows, block_size)
    mixed_rows = jnp.einsum(
        "mrn,mnc->mrc", left_rows, entire, preferred_element_type=jnp.float32
    ).astype(jnp.bfloat16)
    result = jnp.einsum(
        "mrn,mnc->mrc", mixed_rows, right_entire, preferred_element_type=jnp.float32
    )
    outcome = result.astype(jnp.bfloat16).reshape(slots_here, sub_blocks, strip_rows, block_size)
    homeward = jax.vmap(
        lambda portion, offset: lax.dynamic_update_slice_in_dim(
            jnp.zeros((shards, strip_rows, block_size), jnp.bfloat16), portion, offset, 0
        ),
        out_axes=1,
    )(outcome, first_band)
    returned = lax.all_to_all(homeward, "fsdp", split_axis=0, concat_axis=0, tiled=True)
    picked = jnp.einsum(
        "cn,ntb->tcb",
        chooser,
        returned.reshape(total_slots, strip_rows, block_size),
        preferred_element_type=jnp.float32,
    ).astype(jnp.bfloat16)
    direction = picked.reshape(1, 1, strip_rows, model_width)
    return (direction, left_new, right_new)


def solution(mesh):
    placed = (
        P("dp", "fsdp", None),
        P(),
        P("fsdp", None, "dp", None, None),
        P("fsdp", None, "dp", None, None),
        P("fsdp", None, "dp", None, None),
        P("fsdp", None, "dp", None, None),
    )
    return jax.shard_map(
        on_device,
        mesh=mesh,
        in_specs=placed,
        out_specs=(
            P("fsdp", "dp", None, None),
            P("fsdp", None, "dp", None, None),
            P("fsdp", None, "dp", None, None),
        ),
        check_vma=False,
    )
```

profile of v0, /device:TPU:16, one launch (start us, length us, event | category | flops | bytes accessed | tf_op | source)
XLA Modules:
  0.0 276.2 jit_solution(1561728517146626942)
XLA Ops:
  7.2 0.0 copy-start
  7.2 0.0 reduce-scatter.2.cloned.1.call-start
  7.2 0.7 reduce-scatter.2.cloned.1.call-update
  7.9 0.0 all-gather.4.cloned.1.call-start
  8.0 0.7 all-gather.4.cloned.1.call-update
  8.7 0.7 dynamic_slice.7
  9.4 69.5 %reduce-scatter.2.cloned.1.call-done = bf16[16,4096]{1,0:T(8,128)(2,1)} async-done(((bf16[256,4096]{1,0:T(8,128)(2,1)}), bf16[16,4096]{1,0:T(8,128)(2,1)}) %reduce-scatter.2.cloned.1.call-update) | async-done | bytes 131088 | tf_op jit(solution)/shard_map/reduce_scatter | solution.py:32
  78.9 1.0 reshape.110
  79.9 0.8 convolution_convert_fusion
  80.7 0.0 copy-start.7
  80.7 0.0 copy-start.6
  80.7 2.5 copy.35
  83.2 9.8 %all-to-all-start = ((bf16[32,2,16,1024]{3,2,1,0:T(8,128)(2,1)}), bf16[32,2,16,1024]{3,2,1,0:T(8,128)(2,1)S(1)}, u32[]{:S(2)}, u32[]{:S(2)}) async-start(bf16[32,2,16,1024]{3,2,1,0:T(8,128)(2,1)} %bitcast.3), calls=%async_computation.1 | async-start | bytes 4194304 | tf_op jit(solution)/shard_map/all_to_all | solution.py:54
  93.1 0.0 all-gather.6.cloned.1.call-start
  93.1 0.0 copy-done.7
  93.1 0.2 fusion.11
  93.3 45.8 %all-to-all-done = bf16[32,2,16,1024]{3,2,1,0:T(8,128)(2,1)S(1)} async-done(((bf16[32,2,16,1024]{3,2,1,0:T(8,128)(2,1)}), bf16[32,2,16,1024]{3,2,1,0:T(8,128)(2,1)S(1)}, u32[]{:S(2)}, u32[]{:S(2)}) %all-to-all-start) | async-done | bytes 2097184 | tf_op jit(solution)/shard_map/all_to_all | solution.py:54
  139.1 1.3 gather_fusion
  140.4 0.0 all-gather.6.cloned.1.call-update
  140.4 0.0 copy-done.6
  140.4 0.1 pad_clamp_fusion
  140.5 0.1 copy.29
  140.6 42.7 %all-gather.6.cloned.1.call-done = bf16[2,4,256,1024]{3,2,1,0:T(8,128)(2,1)} async-done(((bf16[2,4,16,1024]{3,2,1,0:T(8,128)(2,1)}), bf16[2,4,256,1024]{3,2,1,0:T(8,128)(2,1)}) %all-gather.6.cloned.1.call-update) | async-done | bytes 4194320 | tf_op jit(solution)/shard_map/all_gather | solution.py:60
  183.4 5.1 %convolution_convert_fusion.2 = bf16[2,64,1024]{2,1,0:T(8,128)(2,1)S(1)} fusion(bf16[2,1024,1024]{2,1,0:T(8,128)(2,1)} %bitcast.80, bf16[2,64,1024]{2,1,0:T(8,128)(2,1)S(1)} %bitcast.75, bf16[2,1024,1024]{2,1,0:T(8,128)(2,1)} %bitcast.76), kind=kOutput, calls=%fused_computation.12 | convolution fusion | flops 537133056 | bytes 8912896 | tf_op jit(solution)/shard_map/mrn,mnc->mrc/dot_general | solution.py:79
  188.4 1.6 broadcast_in_dim.16.clone
  190.0 0.0 copy-done.5
  190.0 17.4 %while.1 = (s32[]{:T(128)}, bf16[2,32,16,1024]{3,2,0,1:T(8,128)(2,1)}, s32[2,4]{1,0:T(2,128)S(1)}, bf16[2,4,16,1024]{3,2,1,0:T(8,128)(2,1)S(1)}, s32[]{:T(128)}, /*index=5*/s32[4]{0:T(128)S(1)}) while((s32[]{:T(128)}, bf16[2,32,16,1024]{3,2,0,1:T(8,128)(2,1)}, s32[2,4]{1,0:T(2,128)S(1)}, bf16[2,4,16,1024]{3,2,1,0:T(8,128)(2,1)S(1)}, s32[]{:T(128)}, ...), condition=%wide.while_cond, body=%wide.while_body.sunk | while | flops 65565 | bytes 657586 | solution.py:84
  190.0 0.7 fusion.24
  190.7 3.3 %and_reduce_fusion.2 = pred[]{:T(512)} fusion(s32[4]{0:T(128)S(1)} %get-tuple-element.91, s32[1]{0:T(128)} %bitcast.71, s32[1]{0:T(128)} %bitcast.72, s32[1]{0:T(128)} %bitcast.73, s32[1]{0:T(128)} %bitcast.74), kind=kLoop, calls=%fused_computation.3.clone.1 | loop fusion | flops 27 | bytes 33 | tf_op jit(solution)/shard_map/vmap(vmap())/scatter
  194.0 2.2 constant_dynamic-slice_fusion.6
  196.2 2.6 bitcast_dynamic-update-slice_fusion.2
  198.7 0.7 fusion.24
  199.4 3.3 %and_reduce_fusion.2 = pred[]{:T(512)} fusion(s32[4]{0:T(128)S(1)} %get-tuple-element.91, s32[1]{0:T(128)} %bitcast.71, s32[1]{0:T(128)} %bitcast.72, s32[1]{0:T(128)} %bitcast.73, s32[1]{0:T(128)} %bitcast.74), kind=kLoop, calls=%fused_computation.3.clone.1 | loop fusion | flops 27 | bytes 33 | tf_op jit(solution)/shard_map/vmap(vmap())/scatter
  202.7 2.2 constant_dynamic-slice_fusion.6
  204.9 2.6 bitcast_dynamic-update-slice_fusion.2
  207.5 9.8 %all-to-all-start.1 = ((bf16[32,2,16,1024]{3,2,1,0:T(8,128)(2,1)}), bf16[32,2,16,1024]{3,2,1,0:T(8,128)(2,1)S(1)}, u32[]{:S(2)}, u32[]{:S(2)}) async-start(bf16[32,2,16,1024]{3,2,1,0:T(8,128)(2,1)} %bitcast.10), calls=%async_computation.2 | async-start | bytes 4194304 | tf_op jit(solution)/shard_map/all_to_all | solution.py:89
  217.3 7.5 %copy.33 = bf16[2,4,256,1024]{2,1,3,0:T(4,128)(2,1)} copy(bf16[2,4,256,1024]{3,2,1,0:T(8,128)(2,1)} %all-gather.6.cloned.1.call-done) | data formatting | bytes 8388608 | tf_op jit(solution)/shard_map/all_gather | solution.py:60
  224.8 7.7 %reshape_reshape.7 = bf16[2,1024,4,16,16]{1,4,3,2,0:T(8,128)(2,1)} reshape(bf16[2,4,256,1024]{2,1,3,0:T(4,128)(2,1)} %copy.33) | data formatting | bytes 8388608 | tf_op jit(solution)/shard_map/reshape;reshape | solution.py:67
  232.6 1.1 constant_dynamic-slice_fusion.2
  233.7 3.5 %convolution_multiply_fusion = f32[2,64,1024]{2,1,0:T(8,128)S(1)} fusion(bf16[2,1024,64]{1,2,0:T(8,128)(2,1)S(1)} %bitcast.84, bf16[2,1024,1024]{2,1,0:T(8,128)(2,1)} %bitcast.77), kind=kOutput, calls=%fused_computation.9 | convolution fusion | flops 268566528 | bytes 4980736 | tf_op jit(solution)/shard_map/mnr,mnc->mrc/dot_general | solution.py:73
  237.2 0.0 copy-start.4
  237.2 0.9 add.53
  238.1 0.0 copy-done.1
  238.1 1.4 convolution_multiply_fusion.1
  239.5 0.9 add.51
  240.3 27.4 %all-to-all-done.1 = bf16[32,2,16,1024]{3,2,1,0:T(8,128)(2,1)S(1)} async-done(((bf16[32,2,16,1024]{3,2,1,0:T(8,128)(2,1)}), bf16[32,2,16,1024]{3,2,1,0:T(8,128)(2,1)S(1)}, u32[]{:S(2)}, u32[]{:S(2)}) %all-to-all-start.1) | async-done | bytes 2097184 | tf_op jit(solution)/shard_map/all_to_all | solution.py:89
  267.7 1.2 fusion.5
  268.9 0.7 reshape.118
  (15 shorter events, 0.1 us)
Async XLA Ops:
  7.2 176.2 %copy-start = (bf16[2,4,1,16,1024]{4,3,2,1,0:T(8,128)(2,1)S(1)}, bf16[2,4,1,16,1024]{4,3,2,1,0:T(8,128)(2,1)}, u32[]{:S(2)}) copy-start(bf16[2,4,1,16,1024]{4,3,2,1,0:T(8,128)(2,1)} %param.10) | copy-start | bytes 786436
  7.2 71.7 %reduce-scatter.2.cloned.1.call-start = ((), (), s32[]{:S(2)}) async-start(), calls=%async_computation.3 | async-start | bytes 2228224 | tf_op jit(solution)/shard_map/reduce_scatter | solution.py:32
  7.9 132.7 %all-gather.4.cloned.1.call-start = ((), (), s32[]{:S(2)}) async-start(), calls=%async_computation.4 | async-start | bytes 4456448 | tf_op jit(solution)/shard_map/all_gather | solution.py:29
  80.7 12.4 %copy-start.7 = (s32[32]{0:T(128)S(1)}, s32[32]{0:T(128)}, u32[]{:S(2)}) copy-start(s32[32]{0:T(128)} %param.7) | copy-start | bytes 388
  80.7 59.7 %copy-start.6 = (s32[3]{0:T(128)S(1)}, s32[3]{0:T(128)}, u32[]{:S(2)}) copy-start(s32[3]{0:T(128)} %constant.55.clone.1) | copy-start | bytes 40
  83.2 55.9 %all-to-all-start = ((bf16[32,2,16,1024]{3,2,1,0:T(8,128)(2,1)}), bf16[32,2,16,1024]{3,2,1,0:T(8,128)(2,1)S(1)}, u32[]{:S(2)}, u32[]{:S(2)}) async-start(bf16[32,2,16,1024]{3,2,1,0:T(8,128)(2,1)} %bitcast.3), calls=%async_computation.1 | async-start | bytes 4194304 | tf_op jit(solution)/shard_map/all_to_all | solution.py:54
  93.1 90.3 %all-gather.6.cloned.1.call-start = ((), (), s32[]{:S(2)}) async-start(), calls=%async_computation.5 | async-start | bytes 4456448 | tf_op jit(solution)/shard_map/all_gather | solution.py:60
  183.4 6.7 %copy-start.5 = (s32[4]{0:T(128)S(1)}, s32[4]{0:T(128)}, u32[]{:S(2)}) copy-start(s32[4]{0:T(128)} %constant.139) | copy-start | bytes 52
  207.5 60.3 %all-to-all-start.1 = ((bf16[32,2,16,1024]{3,2,1,0:T(8,128)(2,1)}), bf16[32,2,16,1024]{3,2,1,0:T(8,128)(2,1)S(1)}, u32[]{:S(2)}, u32[]{:S(2)}) async-start(bf16[32,2,16,1024]{3,2,1,0:T(8,128)(2,1)} %bitcast.10), calls=%async_computation.2 | async-start | bytes 4194304 | tf_op jit(solution)/shard_map/all_to_all | solution.py:89
  232.6 4.6 %copy-start.3 = (f32[2,4,1,16,1024]{4,3,2,1,0:T(8,128)S(1)}, f32[2,4,1,16,1024]{4,3,2,1,0:T(8,128)}, u32[]{:S(2)}) copy-start(f32[2,4,1,16,1024]{4,3,2,1,0:T(8,128)} %param.9) | copy-start | bytes 1572868
  232.6 5.5 %copy-start.1 = (bf16[2,4,256,1024]{3,2,1,0:T(8,128)(2,1)S(1)}, bf16[2,4,256,1024]{3,2,1,0:T(8,128)(2,1)}, u32[]{:S(2)}) copy-start(bf16[2,4,256,1024]{3,2,1,0:T(8,128)(2,1)} %all-gather.6.cloned.1.call-done) | copy-start | bytes 12582916
  232.6 5.5 %copy-start.2 = (bf16[2,4,16,1024]{3,2,1,0:T(8,128)(2,1)S(1)}, bf16[2,4,16,1024]{3,2,1,0:T(8,128)(2,1)}, u32[]{:S(2)}) copy-start(bf16[2,4,16,1024]{3,2,1,0:T(8,128)(2,1)} %gather_fusion) | copy-start | bytes 786436
  237.2 2.3 copy-start.4
Sparse Core Ops, SparseCore 0:
  10.8 68.0 reduce-scatter.1
  81.0 42.9 all-gather.3
  140.6 42.7 all-gather.5
where the time goes:
time: 277 us; the launch traced here: 276 us
  waiting for transfers between devices  187 us (68%)
  local copies, waits for them, and re-layouts  30.1 us (11%)
  starting transfers between devices  19.8 us (7%)
  between operations  13.9 us (5%)
  other arithmetic  13.7 us (5%)
  matrix products  12 us (4%)
    reduce_scatter x1, waiting for transfers between devices, on_device(): lax.psum_scatter(replica_grads[0].astype(jnp.float32).astype(jnp.bfloat16...  69.5 us
    all_to_all x1, waiting for transfers between devices, on_device(): lax.all_to_all(outgoing, 'fsdp', split_axis=0, concat_axis=0, tiled=True)  45.8 us
    all_gather x1, waiting for transfers between devices, on_device(): lax.all_gather(owned_rows, 'dp', axis=2, tiled=True)  42.7 us
    all_to_all x1, waiting for transfers between devices, on_device(): lax.all_to_all(homeward, 'fsdp', split_axis=0, concat_axis=0, tiled=True)  27.4 us
    scatter x4, other arithmetic  11.7 us
    all_to_all x1, starting transfers between devices, on_device(): lax.all_to_all(outgoing, 'fsdp', split_axis=0, concat_axis=0, tiled=True)  9.83 us
    all_to_all x1, starting transfers between devices, on_device(): lax.all_to_all(homeward, 'fsdp', split_axis=0, concat_axis=0, tiled=True)  9.82 us
    another operation x1, local copies, waits for them, and re-layouts, on_device(): entire.reshape(slots_here, block_size, sub_blocks, groups, strip_rows)  7.75 us
  transfers between devices with their start and end apart: 5, of which 4 were waited for; matrix products, arithmetic and copies ran while one was open for 11% of the time, Pallas kernels for 0%

commit v1 on v0

v1 whole, which is shorter than its diff:
```python
import functools

import jax
import jax.numpy as jnp
from jax import lax
from jax.experimental import pallas as pl
from jax.experimental.pallas import tpu as pltpu
from jax.sharding import Mesh, PartitionSpec as P

BF = jnp.bfloat16
F32 = jnp.float32
BANDS = ("x", "yh", "yl")
ROWS = ("z", "c")
VM = pl.BlockSpec(memory_space=pltpu.VMEM)
SM = pl.BlockSpec(memory_space=pltpu.SMEM)


def call(kernel, out, inputs, scalars=0, scratch=(), flops=1000000):
    moved = sum(a.size * a.dtype.itemsize for a in inputs)
    return pl.pallas_call(
        kernel,
        out_shape=out,
        in_specs=[VM] * (len(inputs) - scalars) + [SM] * scalars,
        out_specs=jax.tree.map(lambda _: VM, out),
        scratch_shapes=scratch,
        compiler_params=pltpu.CompilerParams(vmem_limit_bytes=32 * 1024 * 1024),
        cost_estimate=pl.CostEstimate(flops=flops, bytes_accessed=moved, transcendentals=0),
    )(*inputs)


def shape(dims, dtype=BF):
    return jax.ShapeDtypeStruct(dims, dtype)


def spread_roots(left_ref, right_ref, out_ref):
    for slot in range(2):
        for sub in range(4):
            for part in range(8):
                columns = slice(part * 128, part * 128 + 128)
                out_ref[sub * 8 + part, slot, 0] = left_ref[slot, sub, 0, :, columns]
                out_ref[sub * 8 + part, slot, 1] = right_ref[slot, sub, 0, :, columns]


def pick_roots(in_ref, table_ref, out_ref):
    for block in range(32):
        out_ref[block] = in_ref[table_ref[block]]


def join_roots(in_ref, left_ref, right_ref):
    for sub in range(4):
        for part in range(8):
            columns = slice(part * 128, part * 128 + 128)
            left_ref[sub, :, columns] = in_ref[sub * 8 + part, 0]
            right_ref[sub, :, columns] = in_ref[sub * 8 + part, 1]


def add_replicas(in_ref, out_ref):
    for column in range(4):
        columns = slice(column * 1024, column * 1024 + 1024)
        total = in_ref[0, :, columns].astype(F32)
        for source in range(1, 8):
            total = total + in_ref[source, :, columns].astype(F32)
        out_ref[column] = total.astype(BF)


def place_rows(whole, mine_ref, other_ref, core):
    for z in range(8):
        for sub in range(4):
            base = sub * 256 + z * 32
            whole[pl.ds(pl.multiple_of(base + core * 16, 16), 16), :] = mine_ref[z, sub]
            whole[pl.ds(pl.multiple_of(base + 16 - core * 16, 16), 16), :] = other_ref[z, sub]


def products(mine_ref, other_ref, rows_ref, left_ref, where_ref, gram_ref, mixed_ref, whole, both):
    core = where_ref[1]
    strip = where_ref[0] * 2 + core
    place_rows(whole, mine_ref, other_ref, core)
    row = lax.broadcasted_iota(jnp.int32, (64, 1024), 0)
    column = lax.broadcasted_iota(jnp.int32, (64, 1024), 1)
    chosen = (row // 16) * 256 + strip * 16 + row % 16
    both[0:64] = rows_ref[...].reshape(64, 1024)
    both[64:128] = jnp.where(column == chosen, 1.0, 0.0).astype(BF)
    first = lax.dot_general(
        both[...], whole[...], (((1,), (1,)), ((), ())), preferred_element_type=F32
    )
    both[0:64] = first[64:128].astype(BF)
    both[64:128] = left_ref[...].reshape(64, 1024)
    second = jnp.dot(both[...], whole[...], preferred_element_type=F32)
    left_gram = (first[0:64] * (1.0 / 1024)).astype(BF)
    right_gram = (second[0:64] * (1.0 / 1024)).astype(BF)
    for sub in range(4):
        for part in range(8):
            columns = slice(part * 128, part * 128 + 128)
            gram_ref[sub * 8 + part, 0] = left_gram[sub * 16 : sub * 16 + 16, columns]
            gram_ref[sub * 8 + part, 1] = right_gram[sub * 16 : sub * 16 + 16, columns]
    mixed_ref[...] = second[64:128].astype(BF)


def to_slots(in_ref, holder_ref, out_ref):
    for slot in range(64):
        block = holder_ref[slot]
        piece = in_ref[jnp.maximum(block, 0)]
        out_ref[slot // 2, slot % 2] = jnp.where(block >= 0, piece, jnp.zeros_like(piece))


def finish_grams(in_ref, left_ref, right_ref, left_out, right_out):
    for slot in range(2):
        for sub in range(4):
            for part in range(8):
                columns = slice(part * 128, part * 128 + 128)
                piece = sub * 8 + part
                left_out[slot, sub, 0, :, columns] = left_ref[slot, sub, 0, :, columns] + in_ref[
                    piece, slot, 0
                ].astype(F32)
                right_out[slot, sub, 0, :, columns] = right_ref[slot, sub, 0, :, columns] + in_ref[
                    piece, slot, 1
                ].astype(F32)


def right_product(mine_ref, other_ref, mixed_ref, where_ref, out_ref, whole):
    place_rows(whole, mine_ref, other_ref, where_ref[1])
    out_ref[...] = (
        jnp.dot(mixed_ref[...], whole[...], preferred_element_type=F32)
        .astype(BF)
        .reshape(4, 16, 1024)
    )


def exchange(value, axes):
    return lax.all_to_all(value, axes, split_axis=0, concat_axis=0, tiled=True)


def swap(value):
    return lax.ppermute(value, "c", [(0, 1), (1, 0)])


def on_device(grads, table, left_state, right_state, left_root, right_root):
    z, core = lax.axis_index("z"), lax.axis_index("c")
    where = jnp.stack([z, core]).astype(jnp.int32)
    slots = jnp.arange(64, dtype=jnp.int32)
    blocks = jnp.arange(32, dtype=jnp.int32)
    holder = jnp.sum(jnp.where(table[None, :] == slots[:, None], blocks[None, :] + 1, 0), axis=1) - 1

    with jax.named_scope("reduce"):
        strips = grads.reshape(8, 2, 16, 4096)
        theirs = lax.dynamic_index_in_dim(strips, 1 - core, 1, keepdims=False)
        ours = lax.dynamic_index_in_dim(strips, core, 1, keepdims=False)
        pair = (ours.astype(F32) + swap(theirs).astype(F32)).astype(BF)
        arrived = exchange(pair, "z")
        strip = call(add_replicas, shape((4, 16, 1024)), [arrived])
        rows = exchange(strip, "yl")

    with jax.named_scope("roots"):
        pieces = call(spread_roots, shape((32, 2, 2, 16, 128)), [left_root, right_root])
        pieces = exchange(pieces, BANDS).reshape(64, 2, 16, 128)
        picked = call(pick_roots, shape((32, 2, 16, 128)), [pieces, table], scalars=1)
        picked = exchange(picked, BANDS)
        left_rows, right_rows = call(
            join_roots, (shape((4, 16, 1024)), shape((4, 16, 1024))), [picked]
        )

    with jax.named_scope("gather"):
        mine = exchange(jnp.broadcast_to(rows[None], (8, 4, 16, 1024)), "z")
        other = swap(mine)
        gram, mixed = call(
            products,
            (shape((32, 2, 16, 128)), shape((64, 1024))),
            [mine, other, rows, left_rows, where],
            scalars=1,
            scratch=[pltpu.VMEM((1024, 1024), BF), pltpu.VMEM((128, 1024), BF)],
            flops=2 * 256 * 1024 * 1024,
        )

    with jax.named_scope("grams"):
        gram = exchange(gram, BANDS)
        gram = call(to_slots, shape((32, 2, 2, 16, 128)), [gram, holder], scalars=1)
        gram = exchange(gram, BANDS)
        left_new, right_new = call(
            finish_grams,
            (shape(left_state.shape, F32), shape(right_state.shape, F32)),
            [gram, left_state, right_state],
        )

    with jax.named_scope("direction"):
        (right_rows, _) = lax.optimization_barrier((right_rows, mine))
        right_mine = exchange(jnp.broadcast_to(right_rows[None], (8, 4, 16, 1024)), "z")
        right_other = swap(right_mine)
        result = call(
            right_product,
            shape((4, 16, 1024)),
            [right_mine, right_other, mixed, where],
            scalars=1,
            scratch=[pltpu.VMEM((1024, 1024), BF)],
            flops=2 * 64 * 1024 * 1024,
        )
        home = exchange(result, "yl")
        direction = home.transpose(1, 0, 2).reshape(1, 1, 16, 4096)
    return direction, left_new, right_new


def solution(mesh):
    fine = Mesh(mesh.devices.reshape(8, 2, 4, 2, 4), ROWS + BANDS)
    state = P(BANDS, None, ROWS, None, None)
    return jax.shard_map(
        on_device,
        mesh=fine,
        in_specs=(P(ROWS, BANDS, None), P(), state, state, state, state),
        out_specs=(P(BANDS, ROWS, None, None), state, state),
        check_vma=False,
    )
```

time: 277 us -> 210 us (0.76)
  the two profiles are of different devices: /device:TPU:16 before, /device:TPU:8 now
where the time goes in v1:
time: 210 us; the launch traced here: 209 us
  waiting for transfers between devices  128 us (61%)
  starting transfers between devices  53 us (25%)
  Pallas kernels  9.3 us (4%)
  blocking collectives  8.54 us (4%)
  local copies, waits for them, and re-layouts  6.61 us (3%)
  other arithmetic  2.63 us (1%)
    all_to_all x8, waiting for transfers between devices, exchange(): return lax.all_to_all(value, axes, split_axis=0, concat_axis=0, tiled=True)  126 us
    all_to_all x8, starting transfers between devices, exchange(): return lax.all_to_all(value, axes, split_axis=0, concat_axis=0, tiled=True)  47.2 us
    pallas_call x8, Pallas kernels, call(): pl.pallas_call(kernel, out_shape=out, in_specs=[VM] * (len(inputs) - scal...  9.3 us
    all_to_all x1, blocking collectives, exchange(): return lax.all_to_all(value, axes, split_axis=0, concat_axis=0, tiled=True)  8.54 us
    ppermute x3, starting transfers between devices, swap(): return lax.ppermute(value, 'c', [(0, 1), (1, 0)])  5.75 us
  transfers between devices with their start and end apart: 11, of which 9 were waited for; matrix products, arithmetic and copies ran while one was open for 1% of the time, Pallas kernels for 4%

profile of v1, /device:TPU:8, one launch (start us, length us, event | category | flops | bytes accessed | tf_op | source)
XLA Modules:
  0.0 209.0 jit_solution(14636161305715690475)
XLA Ops:
  0.6 0.0 copy-start.2
  0.6 0.0 copy-start.3
  0.7 0.0 copy-start.5
  0.7 2.4 %dynamic-slice_bitcast_fusion = bf16[8,16,4096]{2,1,0:T(8,128)(2,1)} fusion(bf16[8,2,16,4096]{3,2,1,0:T(8,128)(2,1)} %bitcast.13, s32[]{:T(128)S(6)} %select_n.12), kind=kLoop, calls=%fused_computation.2 | loop fusion | bytes 2097156 | tf_op jit(solution)/shard_map/reduce/jit(dynamic_index_in_dim)/squeeze | solution.py:146
  3.1 1.9 collective-permute-start
  5.0 0.0 copy-done.2
  5.0 0.0 copy-done.3
  5.0 0.9 roots.3
  5.9 10.2 %all-to-all-start = ((bf16[32,2,2,16,128]{4,3,2,1,0:T(8,128)(2,1)}), bf16[32,2,2,16,128]{4,3,2,1,0:T(8,128)(2,1)S(1)}, u32[]{:S(2)}, u32[]{:S(2)}) async-start(bf16[32,2,2,16,128]{4,3,2,1,0:T(8,128)(2,1)} %roots.3), calls=%async_computation | async-start | bytes 1048576 | tf_op jit(solution)/shard_map/roots/all_to_all | solution.py:130
  16.1 0.0 copy-start.4
  16.1 0.0 collective-permute-done
  16.1 0.0 copy-done.5
  16.1 2.4 %fusion = bf16[8,16,4096]{2,1,0:T(8,128)(2,1)} fusion(bf16[8,16,4096]{2,1,0:T(8,128)(2,1)} %collective-permute-done, bf16[8,2,16,4096]{3,2,1,0:T(8,128)(2,1)S(1)} %bitcast.14, s32[]{:T(128)S(6)} %select_n.11), kind=kLoop, calls=%fused_computation.1 | loop fusion | flops 2097152 | bytes 3145732 | tf_op jit(solution)/shard_map/reduce/convert_element_type | solution.py:148
  18.6 15.8 %all-to-all-done = bf16[32,2,2,16,128]{4,3,2,1,0:T(8,128)(2,1)S(1)} async-done(((bf16[32,2,2,16,128]{4,3,2,1,0:T(8,128)(2,1)}), bf16[32,2,2,16,128]{4,3,2,1,0:T(8,128)(2,1)S(1)}, u32[]{:S(2)}, u32[]{:S(2)}) %all-to-all-start) | async-done | bytes 524320 | tf_op jit(solution)/shard_map/roots/all_to_all | solution.py:130
  34.4 10.3 %all-to-all-start.2 = ((bf16[8,16,4096]{2,1,0:T(8,128)(2,1)}), bf16[8,16,4096]{2,1,0:T(8,128)(2,1)S(1)}, u32[]{:S(2)}, u32[]{:S(2)}) async-start(bf16[8,16,4096]{2,1,0:T(8,128)(2,1)} %fusion), calls=%async_computation.2 | async-start | bytes 2097152 | tf_op jit(solution)/shard_map/reduce/all_to_all | solution.py:130
  44.7 0.0 copy-done.4
  44.7 1.3 roots.4
  46.0 26.4 %all-to-all-done.2.in_ref = bf16[8,16,4096]{2,1,0:T(8,128)(2,1)S(1)} async-done(((bf16[8,16,4096]{2,1,0:T(8,128)(2,1)}), bf16[8,16,4096]{2,1,0:T(8,128)(2,1)S(1)}, u32[]{:S(2)}, u32[]{:S(2)}) %all-to-all-start.2) | async-done | bytes 1048608 | tf_op jit(solution)/shard_map/reduce/all_to_all | solution.py:130
  72.4 5.8 %all-to-all-start.1 = ((bf16[32,2,16,128]{3,2,1,0:T(8,128)(2,1)}), bf16[32,2,16,128]{3,2,1,0:T(8,128)(2,1)S(1)}, u32[]{:S(2)}, u32[]{:S(2)}) async-start(bf16[32,2,16,128]{3,2,1,0:T(8,128)(2,1)} %roots.4), calls=%async_computation.1 | async-start | bytes 524288 | tf_op jit(solution)/shard_map/roots/all_to_all | solution.py:130
  78.2 0.1 reduce.1
  78.3 12.3 %all-to-all-done.1.in_ref = bf16[32,2,16,128]{3,2,1,0:T(8,128)(2,1)S(1)} async-done(((bf16[32,2,16,128]{3,2,1,0:T(8,128)(2,1)}), bf16[32,2,16,128]{3,2,1,0:T(8,128)(2,1)S(1)}, u32[]{:S(2)}, u32[]{:S(2)}) %all-to-all-start.1) | async-done | bytes 262176 | tf_op jit(solution)/shard_map/roots/all_to_all | solution.py:130
  90.6 8.5 %all_to_all.45.rows_ref = bf16[4,16,1024]{2,1,0:T(8,128)(2,1)S(1)} all-to-all(bf16[4,16,1024]{2,1,0:T(8,128)(2,1)S(1)} %reduce.1), channel_id=1, replica_groups=mesh['z'=8,'c'=2,'x'=4,'yh'=2,'yl'=4] {'yl'}, dimensions={0} | all-to-all | bytes 262144 | tf_op jit(solution)/shard_map/reduce/all_to_all | solution.py:130
  99.1 1.1 broadcast_in_dim.16
  100.3 3.6 %all-to-all-start.4 = ((bf16[8,4,16,1024]{3,2,1,0:T(8,128)(2,1)}), bf16[8,4,16,1024]{3,2,1,0:T(8,128)(2,1)S(1)}, u32[]{:S(2)}, u32[]{:S(2)}) async-start(bf16[8,4,16,1024]{3,2,1,0:T(8,128)(2,1)} %broadcast_in_dim.16), calls=%async_computation.4 | async-start | bytes 2097152 | tf_op jit(solution)/shard_map/gather/all_to_all | solution.py:130
  103.9 26.2 %all-to-all-done.4.mine_ref = bf16[8,4,16,1024]{3,2,1,0:T(8,128)(2,1)S(1)} async-done(((bf16[8,4,16,1024]{3,2,1,0:T(8,128)(2,1)}), bf16[8,4,16,1024]{3,2,1,0:T(8,128)(2,1)S(1)}, u32[]{:S(2)}, u32[]{:S(2)}) %all-to-all-start.4) | async-done | bytes 1048608 | tf_op jit(solution)/shard_map/gather/all_to_all | solution.py:130
  130.1 1.1 broadcast_in_dim.17
  131.2 3.6 %all-to-all-start.5 = ((bf16[8,4,16,1024]{3,2,1,0:T(8,128)(2,1)}), bf16[8,4,16,1024]{3,2,1,0:T(8,128)(2,1)S(1)}, u32[]{:S(2)}, u32[]{:S(2)}) async-start(bf16[8,4,16,1024]{3,2,1,0:T(8,128)(2,1)} %broadcast_in_dim.17), calls=%async_computation.5 | async-start | bytes 2097152 | tf_op jit(solution)/shard_map/direction/all_to_all | solution.py:130
  134.8 1.9 collective-permute-start.2
  136.7 0.1 pad_add_fusion.where_ref
  136.8 2.5 %collective-permute-done.2.other_ref = bf16[8,4,16,1024]{3,2,1,0:T(8,128)(2,1)S(1)} collective-permute-done((bf16[8,4,16,1024]{3,2,1,0:T(8,128)(2,1)S(1)}, bf16[8,4,16,1024]{3,2,1,0:T(8,128)(2,1)S(1)}, u32[]{:S(2)}, u32[]{:S(2)}) %collective-permute-start.2) | collective-permute-done | bytes 1048608 | tf_op jit(solution)/shard_map/gather/ppermute | solution.py:134
  139.3 2.5 %gather.1 = (bf16[32,2,16,128]{3,2,1,0:T(8,128)(2,1)}, bf16[64,1024]{1,0:T(8,128)(2,1)S(1)}) custom-call(bf16[8,4,16,1024]{3,2,1,0:T(8,128)(2,1)S(1)} %all-to-all-done.4.mine_ref, bf16[8,4,16,1024]{3,2,1,0:T(8,128)(2,1)S(1)} %collective-permute-done.2.other_ref, bf16[4,16,1024]{2,1,0:T(8,128)(2,1)S(1)} %all_to_all.45.rows_ref, ...), custom_call_target="tpu_custom_call" | custom-call | flops 536870912 | bytes 2359304 | tf_op jit(solution)/shard_map/gather/pallas_call | solution.py:20
  141.9 19.5 %all-to-all-done.5.mine_ref = bf16[8,4,16,1024]{3,2,1,0:T(8,128)(2,1)S(1)} async-done(((bf16[8,4,16,1024]{3,2,1,0:T(8,128)(2,1)}), bf16[8,4,16,1024]{3,2,1,0:T(8,128)(2,1)S(1)}, u32[]{:S(2)}, u32[]{:S(2)}) %all-to-all-start.5) | async-done | bytes 1048608 | tf_op jit(solution)/shard_map/direction/all_to_all | solution.py:130
  161.4 5.7 %all-to-all-start.7 = ((bf16[32,2,16,128]{3,2,1,0:T(8,128)(2,1)}), bf16[32,2,16,128]{3,2,1,0:T(8,128)(2,1)S(1)}, u32[]{:S(2)}, u32[]{:S(2)}) async-start(bf16[32,2,16,128]{3,2,1,0:T(8,128)(2,1)} %get-tuple-element.14), calls=%async_computation.7 | async-start | bytes 524288 | tf_op jit(solution)/shard_map/grams/all_to_all | solution.py:130
  167.1 0.1 select_reduce_fusion
  167.2 1.9 collective-permute-start.1
  169.1 0.0 copy-start
  169.1 9.1 %all-to-all-done.7.in_ref = bf16[32,2,16,128]{3,2,1,0:T(8,128)(2,1)S(1)} async-done(((bf16[32,2,16,128]{3,2,1,0:T(8,128)(2,1)}), bf16[32,2,16,128]{3,2,1,0:T(8,128)(2,1)S(1)}, u32[]{:S(2)}, u32[]{:S(2)}) %all-to-all-start.7) | async-done | bytes 262176 | tf_op jit(solution)/shard_map/grams/all_to_all | solution.py:130
  178.2 1.5 grams.2
  179.7 4.3 %all-to-all-start.8 = ((bf16[32,2,2,16,128]{4,3,2,1,0:T(8,128)(2,1)}), bf16[32,2,2,16,128]{4,3,2,1,0:T(8,128)(2,1)S(1)}, u32[]{:S(2)}, u32[]{:S(2)}) async-start(bf16[32,2,2,16,128]{4,3,2,1,0:T(8,128)(2,1)} %grams.2), calls=%async_computation.8 | async-start | bytes 1048576 | tf_op jit(solution)/shard_map/grams/all_to_all | solution.py:130
  184.1 0.0 collective-permute-done.1.other_ref
  184.1 1.8 direction.1
  185.9 13.3 %all-to-all-done.8.in_ref = bf16[32,2,2,16,128]{4,3,2,1,0:T(8,128)(2,1)S(1)} async-done(((bf16[32,2,2,16,128]{4,3,2,1,0:T(8,128)(2,1)}), bf16[32,2,2,16,128]{4,3,2,1,0:T(8,128)(2,1)S(1)}, u32[]{:S(2)}, u32[]{:S(2)}) %all-to-all-start.8) | async-done | bytes 524320 | tf_op jit(solution)/shard_map/grams/all_to_all | solution.py:130
  199.2 3.9 %all-to-all-start.6 = ((bf16[4,16,1024]{2,1,0:T(8,128)(2,1)}), bf16[4,16,1024]{2,1,0:T(8,128)(2,1)S(1)}, u32[]{:S(2)}, u32[]{:S(2)}) async-start(bf16[4,16,1024]{2,1,0:T(8,128)(2,1)} %direction.1), calls=%async_computation.6 | async-start | bytes 262144 | tf_op jit(solution)/shard_map/direction/all_to_all | solution.py:130
  203.0 1.0 copy-done.1
  204.1 1.1 grams.3
  205.2 3.1 %all-to-all-done.6 = bf16[4,16,1024]{2,1,0:T(8,128)(2,1)S(1)} async-done(((bf16[4,16,1024]{2,1,0:T(8,128)(2,1)}), bf16[4,16,1024]{2,1,0:T(8,128)(2,1)S(1)}, u32[]{:S(2)}, u32[]{:S(2)}) %all-to-all-start.6) | async-done | bytes 131104 | tf_op jit(solution)/shard_map/direction/all_to_all | solution.py:130
  208.2 0.1 copy.12
  208.3 0.7 reshape.27
  (5 shorter events, 0.1 us)
Async XLA Ops:
  0.6 4.4 %copy-start.2 = (bf16[2,4,1,16,1024]{4,3,2,1,0:T(8,128)(2,1)S(1)}, bf16[2,4,1,16,1024]{4,3,2,1,0:T(8,128)(2,1)}, u32[]{:S(2)}) copy-start(bf16[2,4,1,16,1024]{4,3,2,1,0:T(8,128)(2,1)} %left_ref.2) | copy-start | bytes 786436
  0.6 4.4 %copy-start.3 = (bf16[2,4,1,16,1024]{4,3,2,1,0:T(8,128)(2,1)S(1)}, bf16[2,4,1,16,1024]{4,3,2,1,0:T(8,128)(2,1)}, u32[]{:S(2)}) copy-start(bf16[2,4,1,16,1024]{4,3,2,1,0:T(8,128)(2,1)} %right_ref.2) | copy-start | bytes 786436
  0.7 15.5 %copy-start.5 = (bf16[1,256,4096]{2,1,0:T(8,128)(2,1)S(1)}, bf16[1,256,4096]{2,1,0:T(8,128)(2,1)}, u32[]{:S(2)}) copy-start(bf16[1,256,4096]{2,1,0:T(8,128)(2,1)} %param.6) | copy-start | bytes 6291460
  3.1 13.0 %collective-permute-start = (bf16[8,16,4096]{2,1,0:T(8,128)(2,1)}, bf16[8,16,4096]{2,1,0:T(8,128)(2,1)}, u32[]{:S(2)}, u32[]{:S(2)}) collective-permute-start(bf16[8,16,4096]{2,1,0:T(8,128)(2,1)} %dynamic-slice_bitcast_fusion), channel_id=1, source_target_pairs={{0,32},{32,0},{1,33},{33,1},{2,34},{34,2},{3,35},{35,3},{4,36},{36... | collective-permute-start | bytes 3145736 | tf_op jit(solution)/shard_map/reduce/ppermute | solution.py:134
  5.9 28.5 %all-to-all-start = ((bf16[32,2,2,16,128]{4,3,2,1,0:T(8,128)(2,1)}), bf16[32,2,2,16,128]{4,3,2,1,0:T(8,128)(2,1)S(1)}, u32[]{:S(2)}, u32[]{:S(2)}) async-start(bf16[32,2,2,16,128]{4,3,2,1,0:T(8,128)(2,1)} %roots.3), calls=%async_computation | async-start | bytes 1048576 | tf_op jit(solution)/shard_map/roots/all_to_all | solution.py:130
  16.1 28.6 %copy-start.4 = (s32[32]{0:T(128)S(1)}, s32[32]{0:T(128)}, u32[]{:S(2)}) copy-start(s32[32]{0:T(128)} %table_ref.1) | copy-start | bytes 388
  34.4 38.0 %all-to-all-start.2 = ((bf16[8,16,4096]{2,1,0:T(8,128)(2,1)}), bf16[8,16,4096]{2,1,0:T(8,128)(2,1)S(1)}, u32[]{:S(2)}, u32[]{:S(2)}) async-start(bf16[8,16,4096]{2,1,0:T(8,128)(2,1)} %fusion), calls=%async_computation.2 | async-start | bytes 2097152 | tf_op jit(solution)/shard_map/reduce/all_to_all | solution.py:130
  72.4 18.2 %all-to-all-start.1 = ((bf16[32,2,16,128]{3,2,1,0:T(8,128)(2,1)}), bf16[32,2,16,128]{3,2,1,0:T(8,128)(2,1)S(1)}, u32[]{:S(2)}, u32[]{:S(2)}) async-start(bf16[32,2,16,128]{3,2,1,0:T(8,128)(2,1)} %roots.4), calls=%async_computation.1 | async-start | bytes 524288 | tf_op jit(solution)/shard_map/roots/all_to_all | solution.py:130
  100.3 29.8 %all-to-all-start.4 = ((bf16[8,4,16,1024]{3,2,1,0:T(8,128)(2,1)}), bf16[8,4,16,1024]{3,2,1,0:T(8,128)(2,1)S(1)}, u32[]{:S(2)}, u32[]{:S(2)}) async-start(bf16[8,4,16,1024]{3,2,1,0:T(8,128)(2,1)} %broadcast_in_dim.16), calls=%async_computation.4 | async-start | bytes 2097152 | tf_op jit(solution)/shard_map/gather/all_to_all | solution.py:130
  131.2 30.2 %all-to-all-start.5 = ((bf16[8,4,16,1024]{3,2,1,0:T(8,128)(2,1)}), bf16[8,4,16,1024]{3,2,1,0:T(8,128)(2,1)S(1)}, u32[]{:S(2)}, u32[]{:S(2)}) async-start(bf16[8,4,16,1024]{3,2,1,0:T(8,128)(2,1)} %broadcast_in_dim.17), calls=%async_computation.5 | async-start | bytes 2097152 | tf_op jit(solution)/shard_map/direction/all_to_all | solution.py:130
  134.8 4.6 %collective-permute-start.2 = (bf16[8,4,16,1024]{3,2,1,0:T(8,128)(2,1)S(1)}, bf16[8,4,16,1024]{3,2,1,0:T(8,128)(2,1)S(1)}, u32[]{:S(2)}, u32[]{:S(2)}) collective-permute-start(bf16[8,4,16,1024]{3,2,1,0:T(8,128)(2,1)S(1)} %all-to-all-done.4.mine_ref), channel_id=1, source_target_pairs={{0,32},{32,0},{1,33},{33,1},{2,34},{34,2},{3,35},{35,3},{4,36},{36... | collective-permute-start | bytes 3145736 | tf_op jit(solution)/shard_map/gather/ppermute | solution.py:134
  161.4 16.8 %all-to-all-start.7 = ((bf16[32,2,16,128]{3,2,1,0:T(8,128)(2,1)}), bf16[32,2,16,128]{3,2,1,0:T(8,128)(2,1)S(1)}, u32[]{:S(2)}, u32[]{:S(2)}) async-start(bf16[32,2,16,128]{3,2,1,0:T(8,128)(2,1)} %get-tuple-element.14), calls=%async_computation.7 | async-start | bytes 524288 | tf_op jit(solution)/shard_map/grams/all_to_all | solution.py:130
  167.2 16.9 %collective-permute-start.1 = (bf16[8,4,16,1024]{3,2,1,0:T(8,128)(2,1)S(1)}, bf16[8,4,16,1024]{3,2,1,0:T(8,128)(2,1)S(1)}, u32[]{:S(2)}, u32[]{:S(2)}) collective-permute-start(bf16[8,4,16,1024]{3,2,1,0:T(8,128)(2,1)S(1)} %all-to-all-done.5.mine_ref), channel_id=1, source_target_pairs={{0,32},{32,0},{1,33},{33,1},{2,34},{34,2},{3,35},{35,3},{4,36},{36... | collective-permute-start | bytes 3145736 | tf_op jit(solution)/shard_map/direction/ppermute | solution.py:134
  169.1 33.9 %copy-start = (f32[2,4,1,16,1024]{4,3,2,1,0:T(8,128)S(1)}, f32[2,4,1,16,1024]{4,3,2,1,0:T(8,128)}, u32[]{:S(2)}) copy-start(f32[2,4,1,16,1024]{4,3,2,1,0:T(8,128)} %left_ref.3) | copy-start | bytes 1572868
  179.7 19.4 %all-to-all-start.8 = ((bf16[32,2,2,16,128]{4,3,2,1,0:T(8,128)(2,1)}), bf16[32,2,2,16,128]{4,3,2,1,0:T(8,128)(2,1)S(1)}, u32[]{:S(2)}, u32[]{:S(2)}) async-start(bf16[32,2,2,16,128]{4,3,2,1,0:T(8,128)(2,1)} %grams.2), calls=%async_computation.8 | async-start | bytes 1048576 | tf_op jit(solution)/shard_map/grams/all_to_all | solution.py:130
  199.2 9.0 %all-to-all-start.6 = ((bf16[4,16,1024]{2,1,0:T(8,128)(2,1)}), bf16[4,16,1024]{2,1,0:T(8,128)(2,1)S(1)}, u32[]{:S(2)}, u32[]{:S(2)}) async-start(bf16[4,16,1024]{2,1,0:T(8,128)(2,1)} %direction.1), calls=%async_computation.6 | async-start | bytes 262144 | tf_op jit(solution)/shard_map/direction/all_to_all | solution.py:130
  203.0 1.0 copy-start.1

commit v2 on v1

v2 whole, which is shorter than its diff:
```python
import jax
import jax.numpy as jnp
from jax import lax
from jax.experimental import pallas as pl
from jax.experimental.pallas import tpu as pltpu
from jax.sharding import Mesh, PartitionSpec as P


BF = jnp.bfloat16
F32 = jnp.float32
BANDS = ("x", "yh", "yl")
ROWS = ("z", "c")
DISTANCES = (4, 3, 5, 2, 6, 1, 7)
VM = pl.BlockSpec(memory_space=pltpu.VMEM)
SM = pl.BlockSpec(memory_space=pltpu.SMEM)


def call(kernel, out, inputs, scalars=0, scratch=(), flops=1000000):
    moved = sum(a.size * a.dtype.itemsize for a in inputs)
    return pl.pallas_call(
        kernel,
        out_shape=out,
        in_specs=[VM] * (len(inputs) - scalars) + [SM] * scalars,
        out_specs=jax.tree.map(lambda _: VM, out),
        scratch_shapes=scratch,
        compiler_params=pltpu.CompilerParams(vmem_limit_bytes=32 * 1024 * 1024),
        cost_estimate=pl.CostEstimate(flops=flops, bytes_accessed=moved, transcendentals=0),
    )(*inputs)


def shape(dims, dtype=BF):
    return jax.ShapeDtypeStruct(dims, dtype)


def spread_roots(left_ref, right_ref, out_ref):
    for slot in range(2):
        for sub in range(4):
            for part in range(8):
                columns = slice(part * 128, part * 128 + 128)
                out_ref[sub * 8 + part, slot, 0] = left_ref[slot, sub, 0, :, columns]
                out_ref[sub * 8 + part, slot, 1] = right_ref[slot, sub, 0, :, columns]


def pick_roots(in_ref, table_ref, out_ref):
    for block in range(32):
        out_ref[block] = in_ref[table_ref[block]]


def join_roots(in_ref, left_ref, right_ref):
    for sub in range(4):
        for part in range(8):
            columns = slice(part * 128, part * 128 + 128)
            left_ref[sub, :, columns] = in_ref[sub * 8 + part, 0]
            right_ref[sub, :, columns] = in_ref[sub * 8 + part, 1]


def pick_theirs(grads_ref, where_ref, out_ref, sems):
    copies = []
    for k in range(8):
        strip = lax.rem(where_ref[0] + k, 8) * 2 + 1 - where_ref[1]
        rows = pl.ds(pl.multiple_of(strip * 16, 16), 16)
        copies.append(pltpu.make_async_copy(grads_ref.at[0, rows, :], out_ref.at[k], sems.at[k]))
    for copy in copies:
        copy.start()
    for copy in copies:
        copy.wait()


def add_pair(grads_ref, theirs_ref, where_ref, *out_refs):
    for k in range(8):
        strip = lax.rem(where_ref[0] + k, 8) * 2 + where_ref[1]
        rows = pl.ds(pl.multiple_of(strip * 16, 16), 16)
        out_refs[k][...] = (
            grads_ref[0, rows, :].astype(F32) + theirs_ref[k].astype(F32)
        ).astype(BF)


def add_replicas(*refs):
    out_ref = refs[-1]
    for column in range(4):
        columns = slice(column * 1024, column * 1024 + 1024)
        total = refs[0][:, columns].astype(F32)
        for term in refs[1:-1]:
            total = total + term[:, columns].astype(F32)
        out_ref[column] = total.astype(BF)


def stack_rows(*refs):
    for k in range(8):
        refs[-1][k] = refs[k][...]


def place_rows(whole, mine_ref, other_ref, core, first):
    for k in range(8):
        z = lax.rem(first + 8 - k, 8)
        for sub in range(4):
            base = sub * 256 + z * 32
            whole[pl.ds(pl.multiple_of(base + core * 16, 16), 16), :] = mine_ref[k, sub]
            whole[pl.ds(pl.multiple_of(base + 16 - core * 16, 16), 16), :] = other_ref[k, sub]


def products(mine_ref, other_ref, rows_ref, left_ref, where_ref, gram_ref, mixed_ref, whole, both):
    core = where_ref[1]
    strip = where_ref[0] * 2 + core
    place_rows(whole, mine_ref, other_ref, core, where_ref[0])
    row = lax.broadcasted_iota(jnp.int32, (64, 1024), 0)
    column = lax.broadcasted_iota(jnp.int32, (64, 1024), 1)
    chosen = (row // 16) * 256 + strip * 16 + row % 16
    both[0:64] = rows_ref[...].reshape(64, 1024)
    both[64:128] = jnp.where(column == chosen, 1.0, 0.0).astype(BF)
    first = lax.dot_general(
        both[...], whole[...], (((1,), (1,)), ((), ())), preferred_element_type=F32
    )
    both[0:64] = first[64:128].astype(BF)
    both[64:128] = left_ref[...].reshape(64, 1024)
    second = jnp.dot(both[...], whole[...], preferred_element_type=F32)
    left_gram = (first[0:64] * (1.0 / 1024)).astype(BF)
    right_gram = (second[0:64] * (1.0 / 1024)).astype(BF)
    for sub in range(4):
        for part in range(8):
            columns = slice(part * 128, part * 128 + 128)
            gram_ref[sub * 8 + part, 0] = left_gram[sub * 16 : sub * 16 + 16, columns]
            gram_ref[sub * 8 + part, 1] = right_gram[sub * 16 : sub * 16 + 16, columns]
    mixed_ref[...] = second[64:128].astype(BF)


def to_slots(in_ref, holder_ref, out_ref):
    for slot in range(64):
        block = holder_ref[slot]
        piece = in_ref[jnp.maximum(block, 0)]
        out_ref[slot // 2, slot % 2] = jnp.where(block >= 0, piece, jnp.zeros_like(piece))


def finish_grams(in_ref, left_ref, right_ref, left_out, right_out):
    for slot in range(2):
        for sub in range(4):
            for part in range(8):
                columns = slice(part * 128, part * 128 + 128)
                piece = sub * 8 + part
                left_out[slot, sub, 0, :, columns] = left_ref[slot, sub, 0, :, columns] + in_ref[
                    piece, slot, 0
                ].astype(F32)
                right_out[slot, sub, 0, :, columns] = right_ref[slot, sub, 0, :, columns] + in_ref[
                    piece, slot, 1
                ].astype(F32)


def right_product(mine_ref, other_ref, mixed_ref, where_ref, *refs):
    whole, rows = refs[4:]
    place_rows(whole, mine_ref, other_ref, where_ref[1], where_ref[0])
    product = jnp.dot(mixed_ref[...], whole[...], preferred_element_type=F32)
    rows[...] = product.astype(BF).reshape(4, 16, 1024)
    for k in range(4):
        refs[k][...] = rows[lax.rem(where_ref[2] + k, 4)]


def join_columns(*refs):
    where_ref, out_ref = refs[4:]
    for k in range(4):
        column = lax.rem(where_ref[2] + 4 - k, 4) * 1024
        out_ref[0, 0, :, pl.ds(pl.multiple_of(column, 1024), 1024)] = refs[k][...]


def exchange(value, axes):
    return lax.all_to_all(value, axes, split_axis=0, concat_axis=0, tiled=True)


def swap(value):
    return lax.ppermute(value, "c", [(0, 1), (1, 0)])


def shift(value, axis, distance):
    size = lax.axis_size(axis)
    return lax.ppermute(value, axis, [(i, (i + distance) % size) for i in range(size)])


def gathered(rows):
    arrived = {k: shift(rows, "z", k) for k in DISTANCES}
    arrived[0] = rows
    return call(stack_rows, shape((8, 4, 16, 1024)), [arrived[k] for k in range(8)])


def step(grads, table, left_state, right_state, left_root, right_root):
    z, core = lax.axis_index("z"), lax.axis_index("c")
    where = jnp.stack([z, core, lax.axis_index("yl")]).astype(jnp.int32)
    slots = jnp.arange(64, dtype=jnp.int32)
    blocks = jnp.arange(32, dtype=jnp.int32)
    holder = jnp.sum(jnp.where(table[None, :] == slots[:, None], blocks[None, :] + 1, 0), axis=1) - 1

    theirs = pl.pallas_call(
        pick_theirs,
        out_shape=shape((8, 16, 4096)),
        in_specs=[pl.BlockSpec(memory_space=pltpu.HBM), SM],
        out_specs=VM,
        scratch_shapes=[pltpu.SemaphoreType.DMA((8,))],
        cost_estimate=pl.CostEstimate(flops=1000000, bytes_accessed=2097152, transcendentals=0),
    )(grads, where)
    pairs = call(
        add_pair, (shape((16, 4096)),) * 8, [grads, swap(theirs), where], scalars=1
    )
    terms = [pairs[0]] + [shift(pairs[k], "z", k) for k in DISTANCES]
    strip = call(add_replicas, shape((4, 16, 1024)), terms)
    rows = exchange(strip, "yl")

    pieces = call(spread_roots, shape((32, 2, 2, 16, 128)), [left_root, right_root])
    pieces = exchange(pieces, BANDS).reshape(64, 2, 16, 128)
    picked = call(pick_roots, shape((32, 2, 16, 128)), [pieces, table], scalars=1)
    picked, rows = lax.optimization_barrier((picked, rows))
    picked = exchange(picked, BANDS)
    left_rows, right_rows = call(join_roots, (shape((4, 16, 1024)), shape((4, 16, 1024))), [picked])

    mine = gathered(rows)
    other = swap(mine)
    gram, mixed = call(
        products,
        (shape((32, 2, 16, 128)), shape((64, 1024))),
        [mine, other, rows, left_rows, where],
        scalars=1,
        scratch=[pltpu.VMEM((1024, 1024), BF), pltpu.VMEM((128, 1024), BF)],
        flops=2 * 256 * 1024 * 1024,
    )

    gram = exchange(gram, BANDS)
    gram = call(to_slots, shape((32, 2, 2, 16, 128)), [gram, holder], scalars=1)
    gram = exchange(gram, BANDS)
    left_new, right_new = call(
        finish_grams,
        (shape(left_state.shape, F32), shape(right_state.shape, F32)),
        [gram, left_state, right_state],
    )

    right_rows, mixed = lax.optimization_barrier((right_rows, mixed))
    right_mine = gathered(right_rows)
    right_other = swap(right_mine)
    result = call(
        right_product,
        (shape((16, 1024)),) * 4,
        [right_mine, right_other, mixed, where],
        scalars=1,
        scratch=[pltpu.VMEM((1024, 1024), BF), pltpu.VMEM((4, 16, 1024), BF)],
        flops=2 * 64 * 1024 * 1024,
    )
    home = [result[0]] + [shift(result[k], "yl", k) for k in range(1, 4)]
    direction = call(join_columns, shape((1, 1, 16, 4096)), [*home, where], scalars=1)
    return direction, left_new, right_new


def solution(mesh):
    fine = Mesh(mesh.devices.reshape(8, 2, 4, 2, 4), ROWS + BANDS)
    state = P(BANDS, None, ROWS, None, None)
    return jax.shard_map(
        step,
        mesh=fine,
        in_specs=(P(ROWS, BANDS, None), P(), state, state, state, state),
        out_specs=(P(BANDS, ROWS, None, None), state, state),
        check_vma=False,
    )
```

time: 210 us -> 211 us (level)
  the two profiles are of different devices: /device:TPU:8 before, /device:TPU:64 now
where the time goes in v2:
time: 211 us; the launch traced here: 210 us
  starting transfers between devices  134 us (64%)
  waiting for transfers between devices  36.8 us (17%)
  blocking collectives  20.8 us (10%)
  Pallas kernels  14.7 us (7%)
    ppermute x24, starting transfers between devices, shift(): lax.ppermute(value, axis, [(i, (i + distance) % size) for i in range(size)])  99.6 us
    ppermute x24, waiting for transfers between devices, shift(): lax.ppermute(value, axis, [(i, (i + distance) % size) for i in range(size)])  30.6 us
    all_to_all x4, starting transfers between devices, exchange(): return lax.all_to_all(value, axes, split_axis=0, concat_axis=0, tiled=True)  29.1 us
    all_to_all x1, blocking collectives, exchange(): return lax.all_to_all(value, axes, split_axis=0, concat_axis=0, tiled=True)  20.8 us
    pallas_call x12, Pallas kernels, call(): pl.pallas_call(kernel, out_shape=out, in_specs=[VM] * (len(inputs) - scal...  11.5 us
    all_to_all x4, waiting for transfers between devices, exchange(): return lax.all_to_all(value, axes, split_axis=0, concat_axis=0, tiled=True)  6.17 us
    ppermute x3, starting transfers between devices, swap(): return lax.ppermute(value, 'c', [(0, 1), (1, 0)])  5.77 us
  transfers between devices with their start and end apart: 31, of which 13 were waited for; matrix products, arithmetic and copies ran while one was open for 0% of the time, Pallas kernels for 4%

profile of v2, /device:TPU:64, one launch (start us, length us, event | category | flops | bytes accessed | tf_op | source)
XLA Modules:
  0.0 209.5 jit_solution(4558430017332671333)
XLA Ops:
  1.2 3.1 %shard_map.87 = bf16[8,16,4096]{2,1,0:T(8,128)(2,1)} custom-call(bf16[1,256,4096]{2,1,0:T(8,128)(2,1)} %grads_ref.3, s32[3]{0:T(128)} %pad_add_fusion.where_ref.refs_4_), custom_call_target="tpu_custom_call" | custom-call | flops 1000000 | bytes 2097152 | tf_op jit(solution)/shard_map/pallas_call | solution.py:190
  4.4 1.9 collective-permute-start
  7.2 9.9 %all-to-all-start = ((bf16[32,2,2,16,128]{4,3,2,1,0:T(8,128)(2,1)}), bf16[32,2,2,16,128]{4,3,2,1,0:T(8,128)(2,1)S(1)}, u32[]{:S(2)}, u32[]{:S(2)}) async-start(bf16[32,2,2,16,128]{4,3,2,1,0:T(8,128)(2,1)} %shard_map.85), calls=%async_computation | async-start | bytes 1048576 | tf_op jit(solution)/shard_map/all_to_all | solution.py:165
  17.2 1.6 shard_map.88
  18.8 10.0 %collective-permute-start.1 = (bf16[16,4096]{1,0:T(8,128)(2,1)S(1)}, bf16[16,4096]{1,0:T(8,128)(2,1)S(1)}, u32[]{:S(2)}, u32[]{:S(2)}) collective-permute-start(bf16[16,4096]{1,0:T(8,128)(2,1)S(1)} %get-tuple-element.26), channel_id=1, source_target_pairs={{0,256},{64,320},{128,384},{192,448},{256,0},{320,64},{384,128},{4... | collective-permute-start | bytes 393224 | tf_op jit(solution)/shard_map/ppermute | solution.py:174
  28.8 1.9 collective-permute-start.2
  30.8 6.9 %collective-permute-start.3 = (bf16[16,4096]{1,0:T(8,128)(2,1)S(1)}, bf16[16,4096]{1,0:T(8,128)(2,1)S(1)}, u32[]{:S(2)}, u32[]{:S(2)}) collective-permute-start(bf16[16,4096]{1,0:T(8,128)(2,1)S(1)} %get-tuple-element.28), channel_id=1, source_target_pairs={{0,320},{64,384},{128,448},{192,0},{256,64},{320,128},{384,192},{4... | collective-permute-start | bytes 393224 | tf_op jit(solution)/shard_map/ppermute | solution.py:174
  37.7 3.1 %collective-permute-start.4 = (bf16[16,4096]{1,0:T(8,128)(2,1)S(1)}, bf16[16,4096]{1,0:T(8,128)(2,1)S(1)}, u32[]{:S(2)}, u32[]{:S(2)}) collective-permute-start(bf16[16,4096]{1,0:T(8,128)(2,1)S(1)} %get-tuple-element.29), channel_id=1, source_target_pairs={{0,128},{64,192},{128,256},{192,320},{256,384},{320,448},{384,0},{... | collective-permute-start | bytes 393224 | tf_op jit(solution)/shard_map/ppermute | solution.py:174
  40.8 4.9 %collective-permute-start.5 = (bf16[16,4096]{1,0:T(8,128)(2,1)S(1)}, bf16[16,4096]{1,0:T(8,128)(2,1)S(1)}, u32[]{:S(2)}, u32[]{:S(2)}) collective-permute-start(bf16[16,4096]{1,0:T(8,128)(2,1)S(1)} %get-tuple-element.30), channel_id=1, source_target_pairs={{0,384},{64,448},{128,0},{192,64},{256,128},{320,192},{384,256},{4... | collective-permute-start | bytes 393224 | tf_op jit(solution)/shard_map/ppermute | solution.py:174
  45.7 2.2 %collective-permute-start.6 = (bf16[16,4096]{1,0:T(8,128)(2,1)S(1)}, bf16[16,4096]{1,0:T(8,128)(2,1)S(1)}, u32[]{:S(2)}, u32[]{:S(2)}) collective-permute-start(bf16[16,4096]{1,0:T(8,128)(2,1)S(1)} %get-tuple-element.31), channel_id=1, source_target_pairs={{0,64},{64,128},{128,192},{192,256},{256,320},{320,384},{384,448},... | collective-permute-start | bytes 393224 | tf_op jit(solution)/shard_map/ppermute | solution.py:174
  47.9 3.7 %collective-permute-start.7 = (bf16[16,4096]{1,0:T(8,128)(2,1)S(1)}, bf16[16,4096]{1,0:T(8,128)(2,1)S(1)}, u32[]{:S(2)}, u32[]{:S(2)}) collective-permute-start(bf16[16,4096]{1,0:T(8,128)(2,1)S(1)} %get-tuple-element.32), channel_id=1, source_target_pairs={{0,448},{64,0},{128,64},{192,128},{256,192},{320,256},{384,320},{4... | collective-permute-start | bytes 393224 | tf_op jit(solution)/shard_map/ppermute | solution.py:174
  51.6 2.1 %collective-permute-done.6.refs_6_ = bf16[16,4096]{1,0:T(8,128)(2,1)S(1)} collective-permute-done((bf16[16,4096]{1,0:T(8,128)(2,1)S(1)}, bf16[16,4096]{1,0:T(8,128)(2,1)S(1)}, u32[]{:S(2)}, u32[]{:S(2)}) %collective-permute-start.6) | collective-permute-done | bytes 131104 | tf_op jit(solution)/shard_map/ppermute | solution.py:174
  53.7 1.6 collective-permute-done.7.refs_7_
  56.1 4.6 %all-to-all-start.1 = ((bf16[4,16,1024]{2,1,0:T(8,128)(2,1)}), bf16[4,16,1024]{2,1,0:T(8,128)(2,1)S(1)}, u32[]{:S(2)}, u32[]{:S(2)}) async-start(bf16[4,16,1024]{2,1,0:T(8,128)(2,1)} %shard_map.89), calls=%async_computation.1 | async-start | bytes 262144 | tf_op jit(solution)/shard_map/all_to_all | solution.py:165
  61.2 5.3 %all-to-all-done.1.refs_0_.rows_ref = bf16[4,16,1024]{2,1,0:T(8,128)(2,1)S(1)} async-done(((bf16[4,16,1024]{2,1,0:T(8,128)(2,1)}), bf16[4,16,1024]{2,1,0:T(8,128)(2,1)S(1)}, u32[]{:S(2)}, u32[]{:S(2)}) %all-to-all-start.1) | async-done | bytes 131104 | tf_op jit(solution)/shard_map/all_to_all | solution.py:165
  66.6 3.7 %collective-permute-start.8 = (bf16[4,16,1024]{2,1,0:T(8,128)(2,1)S(1)}, bf16[4,16,1024]{2,1,0:T(8,128)(2,1)S(1)}, u32[]{:S(2)}, u32[]{:S(2)}) collective-permute-start(bf16[4,16,1024]{2,1,0:T(8,128)(2,1)S(1)} %all-to-all-done.1.refs_0_.rows_ref), channel_id=1, source_target_pairs={{0,64},{64,128},{128,192},{192,256},{256,320},{320,384},{384,448},... | collective-permute-start | bytes 393224 | tf_op jit(solution)/shard_map/ppermute | solution.py:174
  70.3 2.7 %collective-permute-start.9 = (bf16[4,16,1024]{2,1,0:T(8,128)(2,1)S(1)}, bf16[4,16,1024]{2,1,0:T(8,128)(2,1)S(1)}, u32[]{:S(2)}, u32[]{:S(2)}) collective-permute-start(bf16[4,16,1024]{2,1,0:T(8,128)(2,1)S(1)} %all-to-all-done.1.refs_0_.rows_ref), channel_id=1, source_target_pairs={{0,128},{64,192},{128,256},{192,320},{256,384},{320,448},{384,0},{... | collective-permute-start | bytes 393224 | tf_op jit(solution)/shard_map/ppermute | solution.py:174
  72.9 6.2 %collective-permute-start.10 = (bf16[4,16,1024]{2,1,0:T(8,128)(2,1)S(1)}, bf16[4,16,1024]{2,1,0:T(8,128)(2,1)S(1)}, u32[]{:S(2)}, u32[]{:S(2)}) collective-permute-start(bf16[4,16,1024]{2,1,0:T(8,128)(2,1)S(1)} %all-to-all-done.1.refs_0_.rows_ref), channel_id=1, source_target_pairs={{0,192},{64,256},{128,320},{192,384},{256,448},{320,0},{384,64},{4... | collective-permute-start | bytes 393224 | tf_op jit(solution)/shard_map/ppermute | solution.py:174
  79.1 3.7 %collective-permute-start.11 = (bf16[4,16,1024]{2,1,0:T(8,128)(2,1)S(1)}, bf16[4,16,1024]{2,1,0:T(8,128)(2,1)S(1)}, u32[]{:S(2)}, u32[]{:S(2)}) collective-permute-start(bf16[4,16,1024]{2,1,0:T(8,128)(2,1)S(1)} %all-to-all-done.1.refs_0_.rows_ref), channel_id=1, source_target_pairs={{0,256},{64,320},{128,384},{192,448},{256,0},{320,64},{384,128},{4... | collective-permute-start | bytes 393224 | tf_op jit(solution)/shard_map/ppermute | solution.py:174
  82.9 4.8 %collective-permute-start.12 = (bf16[4,16,1024]{2,1,0:T(8,128)(2,1)S(1)}, bf16[4,16,1024]{2,1,0:T(8,128)(2,1)S(1)}, u32[]{:S(2)}, u32[]{:S(2)}) collective-permute-start(bf16[4,16,1024]{2,1,0:T(8,128)(2,1)S(1)} %all-to-all-done.1.refs_0_.rows_ref), channel_id=1, source_target_pairs={{0,320},{64,384},{128,448},{192,0},{256,64},{320,128},{384,192},{4... | collective-permute-start | bytes 393224 | tf_op jit(solution)/shard_map/ppermute | solution.py:174
  87.7 3.1 %collective-permute-start.13 = (bf16[4,16,1024]{2,1,0:T(8,128)(2,1)S(1)}, bf16[4,16,1024]{2,1,0:T(8,128)(2,1)S(1)}, u32[]{:S(2)}, u32[]{:S(2)}) collective-permute-start(bf16[4,16,1024]{2,1,0:T(8,128)(2,1)S(1)} %all-to-all-done.1.refs_0_.rows_ref), channel_id=1, source_target_pairs={{0,384},{64,448},{128,0},{192,64},{256,128},{320,192},{384,256},{4... | collective-permute-start | bytes 393224 | tf_op jit(solution)/shard_map/ppermute | solution.py:174
  90.9 3.2 %collective-permute-start.14 = (bf16[4,16,1024]{2,1,0:T(8,128)(2,1)S(1)}, bf16[4,16,1024]{2,1,0:T(8,128)(2,1)S(1)}, u32[]{:S(2)}, u32[]{:S(2)}) collective-permute-start(bf16[4,16,1024]{2,1,0:T(8,128)(2,1)S(1)} %all-to-all-done.1.refs_0_.rows_ref), channel_id=1, source_target_pairs={{0,448},{64,0},{128,64},{192,128},{256,192},{320,256},{384,320},{4... | collective-permute-start | bytes 393224 | tf_op jit(solution)/shard_map/ppermute | solution.py:174
  94.0 1.6 collective-permute-done.11.refs_4_
  95.6 4.6 %collective-permute-done.12.refs_5_ = bf16[4,16,1024]{2,1,0:T(8,128)(2,1)S(1)} collective-permute-done((bf16[4,16,1024]{2,1,0:T(8,128)(2,1)S(1)}, bf16[4,16,1024]{2,1,0:T(8,128)(2,1)S(1)}, u32[]{:S(2)}, u32[]{:S(2)}) %collective-permute-start.12) | collective-permute-done | bytes 131104 | tf_op jit(solution)/shard_map/ppermute | solution.py:174
  100.2 2.4 %collective-permute-done.13.refs_6_ = bf16[4,16,1024]{2,1,0:T(8,128)(2,1)S(1)} collective-permute-done((bf16[4,16,1024]{2,1,0:T(8,128)(2,1)S(1)}, bf16[4,16,1024]{2,1,0:T(8,128)(2,1)S(1)}, u32[]{:S(2)}, u32[]{:S(2)}) %collective-permute-start.13) | collective-permute-done | bytes 131104 | tf_op jit(solution)/shard_map/ppermute | solution.py:174
  102.6 1.9 collective-permute-done.14.refs_7_
  104.6 1.9 collective-permute-start.15
  106.5 20.8 %all_to_all.25.in_ref = bf16[32,2,16,128]{3,2,1,0:T(8,128)(2,1)S(1)} all-to-all(bf16[32,2,16,128]{3,2,1,0:T(8,128)(2,1)S(1)} %shard_map.86), channel_id=1, replica_groups=mesh['z'=8,'c'=2,'x'=4,'yh'=2,'yl'=4] {'x','yh','yl'}, dimensions={0} | all-to-all | bytes 524288 | tf_op jit(solution)/shard_map/all_to_all | solution.py:165
  127.3 2.5 %shard_map.92 = (bf16[32,2,16,128]{3,2,1,0:T(8,128)(2,1)}, bf16[64,1024]{1,0:T(8,128)(2,1)S(1)}) custom-call(bf16[8,4,16,1024]{3,2,1,0:T(8,128)(2,1)S(1)} %shard_map.91.mine_ref, bf16[8,4,16,1024]{3,2,1,0:T(8,128)(2,1)S(1)} %collective-permute-done.15.other_ref, bf16[4,16,1024]{2,1,0:T(8,128)(2,1)S(1)} %all-to-all-done.1.refs_0_.rows_ref, ...), custom_call_target="tpu_custom_call" | custom-call | flops 536870912 | bytes 2359308 | tf_op jit(solution)/shard_map/pallas_call | solution.py:20
  129.8 2.5 %collective-permute-start.16 = (bf16[4,16,1024]{2,1,0:T(8,128)(2,1)S(1)}, bf16[4,16,1024]{2,1,0:T(8,128)(2,1)S(1)}, u32[]{:S(2)}, u32[]{:S(2)}) collective-permute-start(bf16[4,16,1024]{2,1,0:T(8,128)(2,1)S(1)} %get-tuple-element.38.refs_0_), channel_id=1, source_target_pairs={{0,64},{64,128},{128,192},{192,256},{256,320},{320,384},{384,448},... | collective-permute-start | bytes 393224 | tf_op jit(solution)/shard_map/ppermute | solution.py:174
  132.4 5.2 %collective-permute-start.17 = (bf16[4,16,1024]{2,1,0:T(8,128)(2,1)S(1)}, bf16[4,16,1024]{2,1,0:T(8,128)(2,1)S(1)}, u32[]{:S(2)}, u32[]{:S(2)}) collective-permute-start(bf16[4,16,1024]{2,1,0:T(8,128)(2,1)S(1)} %get-tuple-element.38.refs_0_), channel_id=1, source_target_pairs={{0,128},{64,192},{128,256},{192,320},{256,384},{320,448},{384,0},{... | collective-permute-start | bytes 393224 | tf_op jit(solution)/shard_map/ppermute | solution.py:174
  137.5 5.0 %all-to-all-start.3 = ((bf16[32,2,16,128]{3,2,1,0:T(8,128)(2,1)}), bf16[32,2,16,128]{3,2,1,0:T(8,128)(2,1)S(1)}, u32[]{:S(2)}, u32[]{:S(2)}) async-start(bf16[32,2,16,128]{3,2,1,0:T(8,128)(2,1)} %get-tuple-element.44), calls=%async_computation.3 | async-start | bytes 524288 | tf_op jit(solution)/shard_map/all_to_all | solution.py:165
  142.6 4.2 %collective-permute-start.18 = (bf16[4,16,1024]{2,1,0:T(8,128)(2,1)S(1)}, bf16[4,16,1024]{2,1,0:T(8,128)(2,1)S(1)}, u32[]{:S(2)}, u32[]{:S(2)}) collective-permute-start(bf16[4,16,1024]{2,1,0:T(8,128)(2,1)S(1)} %get-tuple-element.38.refs_0_), channel_id=1, source_target_pairs={{0,192},{64,256},{128,320},{192,384},{256,448},{320,0},{384,64},{4... | collective-permute-start | bytes 393224 | tf_op jit(solution)/shard_map/ppermute | solution.py:174
  146.8 4.6 %collective-permute-start.19 = (bf16[4,16,1024]{2,1,0:T(8,128)(2,1)S(1)}, bf16[4,16,1024]{2,1,0:T(8,128)(2,1)S(1)}, u32[]{:S(2)}, u32[]{:S(2)}) collective-permute-start(bf16[4,16,1024]{2,1,0:T(8,128)(2,1)S(1)} %get-tuple-element.38.refs_0_), channel_id=1, source_target_pairs={{0,256},{64,320},{128,384},{192,448},{256,0},{320,64},{384,128},{4... | collective-permute-start | bytes 393224 | tf_op jit(solution)/shard_map/ppermute | solution.py:174
  151.5 4.3 %collective-permute-start.20 = (bf16[4,16,1024]{2,1,0:T(8,128)(2,1)S(1)}, bf16[4,16,1024]{2,1,0:T(8,128)(2,1)S(1)}, u32[]{:S(2)}, u32[]{:S(2)}) collective-permute-start(bf16[4,16,1024]{2,1,0:T(8,128)(2,1)S(1)} %get-tuple-element.38.refs_0_), channel_id=1, source_target_pairs={{0,320},{64,384},{128,448},{192,0},{256,64},{320,128},{384,192},{4... | collective-permute-start | bytes 393224 | tf_op jit(solution)/shard_map/ppermute | solution.py:174
  155.8 2.9 %collective-permute-start.21 = (bf16[4,16,1024]{2,1,0:T(8,128)(2,1)S(1)}, bf16[4,16,1024]{2,1,0:T(8,128)(2,1)S(1)}, u32[]{:S(2)}, u32[]{:S(2)}) collective-permute-start(bf16[4,16,1024]{2,1,0:T(8,128)(2,1)S(1)} %get-tuple-element.38.refs_0_), channel_id=1, source_target_pairs={{0,384},{64,448},{128,0},{192,64},{256,128},{320,192},{384,256},{4... | collective-permute-start | bytes 393224 | tf_op jit(solution)/shard_map/ppermute | solution.py:174
  158.7 4.5 %collective-permute-start.22 = (bf16[4,16,1024]{2,1,0:T(8,128)(2,1)S(1)}, bf16[4,16,1024]{2,1,0:T(8,128)(2,1)S(1)}, u32[]{:S(2)}, u32[]{:S(2)}) collective-permute-start(bf16[4,16,1024]{2,1,0:T(8,128)(2,1)S(1)} %get-tuple-element.38.refs_0_), channel_id=1, source_target_pairs={{0,448},{64,0},{128,64},{192,128},{256,192},{320,256},{384,320},{4... | collective-permute-start | bytes 393224 | tf_op jit(solution)/shard_map/ppermute | solution.py:174
  163.3 7.5 %collective-permute-done.20.refs_5_ = bf16[4,16,1024]{2,1,0:T(8,128)(2,1)S(1)} collective-permute-done((bf16[4,16,1024]{2,1,0:T(8,128)(2,1)S(1)}, bf16[4,16,1024]{2,1,0:T(8,128)(2,1)S(1)}, u32[]{:S(2)}, u32[]{:S(2)}) %collective-permute-start.20) | collective-permute-done | bytes 131104 | tf_op jit(solution)/shard_map/ppermute | solution.py:174
  170.8 2.0 collective-permute-done.21.refs_6_
  172.8 2.2 %collective-permute-done.22.refs_7_ = bf16[4,16,1024]{2,1,0:T(8,128)(2,1)S(1)} collective-permute-done((bf16[4,16,1024]{2,1,0:T(8,128)(2,1)S(1)}, bf16[4,16,1024]{2,1,0:T(8,128)(2,1)S(1)}, u32[]{:S(2)}, u32[]{:S(2)}) %collective-permute-start.22) | collective-permute-done | bytes 131104 | tf_op jit(solution)/shard_map/ppermute | solution.py:174
  175.0 1.9 collective-permute-start.23
  177.0 1.5 shard_map.96
  178.5 9.5 %all-to-all-start.4 = ((bf16[32,2,2,16,128]{4,3,2,1,0:T(8,128)(2,1)}), bf16[32,2,2,16,128]{4,3,2,1,0:T(8,128)(2,1)S(1)}, u32[]{:S(2)}, u32[]{:S(2)}) async-start(bf16[32,2,2,16,128]{4,3,2,1,0:T(8,128)(2,1)} %shard_map.96), calls=%async_computation.4 | async-start | bytes 1048576 | tf_op jit(solution)/shard_map/all_to_all | solution.py:165
  189.2 3.7 %collective-permute-start.24 = (bf16[16,1024]{1,0:T(8,128)(2,1)S(1)}, bf16[16,1024]{1,0:T(8,128)(2,1)S(1)}, u32[]{:S(2)}, u32[]{:S(2)}) collective-permute-start(bf16[16,1024]{1,0:T(8,128)(2,1)S(1)} %get-tuple-element.41), channel_id=1, source_target_pairs={{0,1},{1,2},{2,3},{3,0},{4,5},{5,6},{6,7},{7,4},{8,9},{9,10},{10,1... | collective-permute-start | bytes 98312 | tf_op jit(solution)/shard_map/ppermute | solution.py:174
  192.9 4.3 %collective-permute-start.25 = (bf16[16,1024]{1,0:T(8,128)(2,1)S(1)}, bf16[16,1024]{1,0:T(8,128)(2,1)S(1)}, u32[]{:S(2)}, u32[]{:S(2)}) collective-permute-start(bf16[16,1024]{1,0:T(8,128)(2,1)S(1)} %get-tuple-element.42), channel_id=1, source_target_pairs={{0,2},{1,3},{2,0},{3,1},{4,6},{5,7},{6,4},{7,5},{8,10},{9,11},{10,... | collective-permute-start | bytes 98312 | tf_op jit(solution)/shard_map/ppermute | solution.py:174
  197.2 3.4 %collective-permute-start.26 = (bf16[16,1024]{1,0:T(8,128)(2,1)S(1)}, bf16[16,1024]{1,0:T(8,128)(2,1)S(1)}, u32[]{:S(2)}, u32[]{:S(2)}) collective-permute-start(bf16[16,1024]{1,0:T(8,128)(2,1)S(1)} %get-tuple-element.43), channel_id=1, source_target_pairs={{0,3},{1,0},{2,1},{3,2},{4,7},{5,4},{6,5},{7,6},{8,11},{9,8},{10,9... | collective-permute-start | bytes 98312 | tf_op jit(solution)/shard_map/ppermute | solution.py:174
  200.6 3.9 %collective-permute-done.24.refs_1_ = bf16[16,1024]{1,0:T(8,128)(2,1)S(1)} collective-permute-done((bf16[16,1024]{1,0:T(8,128)(2,1)S(1)}, bf16[16,1024]{1,0:T(8,128)(2,1)S(1)}, u32[]{:S(2)}, u32[]{:S(2)}) %collective-permute-start.24) | collective-permute-done | bytes 32800 | tf_op jit(solution)/shard_map/ppermute | solution.py:174
  205.4 1.2 shard_map.95
  (46 shorter events, 8.2 us)
Async XLA Ops:
  0.6 5.7 %copy-start.3 = (bf16[2,4,1,16,1024]{4,3,2,1,0:T(8,128)(2,1)S(1)}, bf16[2,4,1,16,1024]{4,3,2,1,0:T(8,128)(2,1)}, u32[]{:S(2)}) copy-start(bf16[2,4,1,16,1024]{4,3,2,1,0:T(8,128)(2,1)} %left_ref.2) | copy-start | bytes 786436
  0.6 5.7 %copy-start.4 = (bf16[2,4,1,16,1024]{4,3,2,1,0:T(8,128)(2,1)S(1)}, bf16[2,4,1,16,1024]{4,3,2,1,0:T(8,128)(2,1)}, u32[]{:S(2)}) copy-start(bf16[2,4,1,16,1024]{4,3,2,1,0:T(8,128)(2,1)} %right_ref.2) | copy-start | bytes 786436
  1.2 16.0 %copy-start = (bf16[1,256,4096]{2,1,0:T(8,128)(2,1)S(1)}, bf16[1,256,4096]{2,1,0:T(8,128)(2,1)}, u32[]{:S(2)}) copy-start(bf16[1,256,4096]{2,1,0:T(8,128)(2,1)} %grads_ref.3) | copy-start | bytes 6291460
  1.2 16.0 %copy-start.5 = (s32[3]{0:T(128)S(1)}, s32[3]{0:T(128)}, u32[]{:S(2)}) copy-start(s32[3]{0:T(128)} %pad_add_fusion.where_ref.refs_4_) | copy-start | bytes 40
  4.4 12.8 %collective-permute-start = (bf16[8,16,4096]{2,1,0:T(8,128)(2,1)}, bf16[8,16,4096]{2,1,0:T(8,128)(2,1)}, u32[]{:S(2)}, u32[]{:S(2)}) collective-permute-start(bf16[8,16,4096]{2,1,0:T(8,128)(2,1)} %shard_map.87), channel_id=1, source_target_pairs={{0,32},{32,0},{1,33},{33,1},{2,34},{34,2},{3,35},{35,3},{4,36},{36... | collective-permute-start | bytes 3145736 | tf_op jit(solution)/shard_map/ppermute | solution.py:169
  7.2 48.8 %all-to-all-start = ((bf16[32,2,2,16,128]{4,3,2,1,0:T(8,128)(2,1)}), bf16[32,2,2,16,128]{4,3,2,1,0:T(8,128)(2,1)S(1)}, u32[]{:S(2)}, u32[]{:S(2)}) async-start(bf16[32,2,2,16,128]{4,3,2,1,0:T(8,128)(2,1)} %shard_map.85), calls=%async_computation | async-start | bytes 1048576 | tf_op jit(solution)/shard_map/all_to_all | solution.py:165
  17.2 43.5 %copy-start.6 = (s32[32]{0:T(128)S(1)}, s32[32]{0:T(128)}, u32[]{:S(2)}) copy-start(s32[32]{0:T(128)} %table_ref.1) | copy-start | bytes 388
  18.8 26.9 %collective-permute-start.1 = (bf16[16,4096]{1,0:T(8,128)(2,1)S(1)}, bf16[16,4096]{1,0:T(8,128)(2,1)S(1)}, u32[]{:S(2)}, u32[]{:S(2)}) collective-permute-start(bf16[16,4096]{1,0:T(8,128)(2,1)S(1)} %get-tuple-element.26), channel_id=1, source_target_pairs={{0,256},{64,320},{128,384},{192,448},{256,0},{320,64},{384,128},{4... | collective-permute-start | bytes 393224 | tf_op jit(solution)/shard_map/ppermute | solution.py:174
  28.8 19.0 %collective-permute-start.2 = (bf16[16,4096]{1,0:T(8,128)(2,1)S(1)}, bf16[16,4096]{1,0:T(8,128)(2,1)S(1)}, u32[]{:S(2)}, u32[]{:S(2)}) collective-permute-start(bf16[16,4096]{1,0:T(8,128)(2,1)S(1)} %get-tuple-element.27), channel_id=1, source_target_pairs={{0,192},{64,256},{128,320},{192,384},{256,448},{320,0},{384,64},{4... | collective-permute-start | bytes 393224 | tf_op jit(solution)/shard_map/ppermute | solution.py:174
  30.8 20.8 %collective-permute-start.3 = (bf16[16,4096]{1,0:T(8,128)(2,1)S(1)}, bf16[16,4096]{1,0:T(8,128)(2,1)S(1)}, u32[]{:S(2)}, u32[]{:S(2)}) collective-permute-start(bf16[16,4096]{1,0:T(8,128)(2,1)S(1)} %get-tuple-element.28), channel_id=1, source_target_pairs={{0,320},{64,384},{128,448},{192,0},{256,64},{320,128},{384,192},{4... | collective-permute-start | bytes 393224 | tf_op jit(solution)/shard_map/ppermute | solution.py:174
  37.7 13.9 %collective-permute-start.4 = (bf16[16,4096]{1,0:T(8,128)(2,1)S(1)}, bf16[16,4096]{1,0:T(8,128)(2,1)S(1)}, u32[]{:S(2)}, u32[]{:S(2)}) collective-permute-start(bf16[16,4096]{1,0:T(8,128)(2,1)S(1)} %get-tuple-element.29), channel_id=1, source_target_pairs={{0,128},{64,192},{128,256},{192,320},{256,384},{320,448},{384,0},{... | collective-permute-start | bytes 393224 | tf_op jit(solution)/shard_map/ppermute | solution.py:174
  40.8 10.8 %collective-permute-start.5 = (bf16[16,4096]{1,0:T(8,128)(2,1)S(1)}, bf16[16,4096]{1,0:T(8,128)(2,1)S(1)}, u32[]{:S(2)}, u32[]{:S(2)}) collective-permute-start(bf16[16,4096]{1,0:T(8,128)(2,1)S(1)} %get-tuple-element.30), channel_id=1, source_target_pairs={{0,384},{64,448},{128,0},{192,64},{256,128},{320,192},{384,256},{4... | collective-permute-start | bytes 393224 | tf_op jit(solution)/shard_map/ppermute | solution.py:174
  45.7 8.0 %collective-permute-start.6 = (bf16[16,4096]{1,0:T(8,128)(2,1)S(1)}, bf16[16,4096]{1,0:T(8,128)(2,1)S(1)}, u32[]{:S(2)}, u32[]{:S(2)}) collective-permute-start(bf16[16,4096]{1,0:T(8,128)(2,1)S(1)} %get-tuple-element.31), channel_id=1, source_target_pairs={{0,64},{64,128},{128,192},{192,256},{256,320},{320,384},{384,448},... | collective-permute-start | bytes 393224 | tf_op jit(solution)/shard_map/ppermute | solution.py:174
  47.9 7.4 %collective-permute-start.7 = (bf16[16,4096]{1,0:T(8,128)(2,1)S(1)}, bf16[16,4096]{1,0:T(8,128)(2,1)S(1)}, u32[]{:S(2)}, u32[]{:S(2)}) collective-permute-start(bf16[16,4096]{1,0:T(8,128)(2,1)S(1)} %get-tuple-element.32), channel_id=1, source_target_pairs={{0,448},{64,0},{128,64},{192,128},{256,192},{320,256},{384,320},{4... | collective-permute-start | bytes 393224 | tf_op jit(solution)/shard_map/ppermute | solution.py:174
  56.1 10.5 %all-to-all-start.1 = ((bf16[4,16,1024]{2,1,0:T(8,128)(2,1)}), bf16[4,16,1024]{2,1,0:T(8,128)(2,1)S(1)}, u32[]{:S(2)}, u32[]{:S(2)}) async-start(bf16[4,16,1024]{2,1,0:T(8,128)(2,1)} %shard_map.89), calls=%async_computation.1 | async-start | bytes 262144 | tf_op jit(solution)/shard_map/all_to_all | solution.py:165
  66.6 21.2 %collective-permute-start.8 = (bf16[4,16,1024]{2,1,0:T(8,128)(2,1)S(1)}, bf16[4,16,1024]{2,1,0:T(8,128)(2,1)S(1)}, u32[]{:S(2)}, u32[]{:S(2)}) collective-permute-start(bf16[4,16,1024]{2,1,0:T(8,128)(2,1)S(1)} %all-to-all-done.1.refs_0_.rows_ref), channel_id=1, source_target_pairs={{0,64},{64,128},{128,192},{192,256},{256,320},{320,384},{384,448},... | collective-permute-start | bytes 393224 | tf_op jit(solution)/shard_map/ppermute | solution.py:174
  70.3 20.6 %collective-permute-start.9 = (bf16[4,16,1024]{2,1,0:T(8,128)(2,1)S(1)}, bf16[4,16,1024]{2,1,0:T(8,128)(2,1)S(1)}, u32[]{:S(2)}, u32[]{:S(2)}) collective-permute-start(bf16[4,16,1024]{2,1,0:T(8,128)(2,1)S(1)} %all-to-all-done.1.refs_0_.rows_ref), channel_id=1, source_target_pairs={{0,128},{64,192},{128,256},{192,320},{256,384},{320,448},{384,0},{... | collective-permute-start | bytes 393224 | tf_op jit(solution)/shard_map/ppermute | solution.py:174
  72.9 21.1 %collective-permute-start.10 = (bf16[4,16,1024]{2,1,0:T(8,128)(2,1)S(1)}, bf16[4,16,1024]{2,1,0:T(8,128)(2,1)S(1)}, u32[]{:S(2)}, u32[]{:S(2)}) collective-permute-start(bf16[4,16,1024]{2,1,0:T(8,128)(2,1)S(1)} %all-to-all-done.1.refs_0_.rows_ref), channel_id=1, source_target_pairs={{0,192},{64,256},{128,320},{192,384},{256,448},{320,0},{384,64},{4... | collective-permute-start | bytes 393224 | tf_op jit(solution)/shard_map/ppermute | solution.py:174
  79.1 16.5 %collective-permute-start.11 = (bf16[4,16,1024]{2,1,0:T(8,128)(2,1)S(1)}, bf16[4,16,1024]{2,1,0:T(8,128)(2,1)S(1)}, u32[]{:S(2)}, u32[]{:S(2)}) collective-permute-start(bf16[4,16,1024]{2,1,0:T(8,128)(2,1)S(1)} %all-to-all-done.1.refs_0_.rows_ref), channel_id=1, source_target_pairs={{0,256},{64,320},{128,384},{192,448},{256,0},{320,64},{384,128},{4... | collective-permute-start | bytes 393224 | tf_op jit(solution)/shard_map/ppermute | solution.py:174
  82.9 17.4 %collective-permute-start.12 = (bf16[4,16,1024]{2,1,0:T(8,128)(2,1)S(1)}, bf16[4,16,1024]{2,1,0:T(8,128)(2,1)S(1)}, u32[]{:S(2)}, u32[]{:S(2)}) collective-permute-start(bf16[4,16,1024]{2,1,0:T(8,128)(2,1)S(1)} %all-to-all-done.1.refs_0_.rows_ref), channel_id=1, source_target_pairs={{0,320},{64,384},{128,448},{192,0},{256,64},{320,128},{384,192},{4... | collective-permute-start | bytes 393224 | tf_op jit(solution)/shard_map/ppermute | solution.py:174
  87.7 14.9 %collective-permute-start.13 = (bf16[4,16,1024]{2,1,0:T(8,128)(2,1)S(1)}, bf16[4,16,1024]{2,1,0:T(8,128)(2,1)S(1)}, u32[]{:S(2)}, u32[]{:S(2)}) collective-permute-start(bf16[4,16,1024]{2,1,0:T(8,128)(2,1)S(1)} %all-to-all-done.1.refs_0_.rows_ref), channel_id=1, source_target_pairs={{0,384},{64,448},{128,0},{192,64},{256,128},{320,192},{384,256},{4... | collective-permute-start | bytes 393224 | tf_op jit(solution)/shard_map/ppermute | solution.py:174
  90.9 13.6 %collective-permute-start.14 = (bf16[4,16,1024]{2,1,0:T(8,128)(2,1)S(1)}, bf16[4,16,1024]{2,1,0:T(8,128)(2,1)S(1)}, u32[]{:S(2)}, u32[]{:S(2)}) collective-permute-start(bf16[4,16,1024]{2,1,0:T(8,128)(2,1)S(1)} %all-to-all-done.1.refs_0_.rows_ref), channel_id=1, source_target_pairs={{0,448},{64,0},{128,64},{192,128},{256,192},{320,256},{384,320},{4... | collective-permute-start | bytes 393224 | tf_op jit(solution)/shard_map/ppermute | solution.py:174
  104.6 22.7 %collective-permute-start.15 = (bf16[8,4,16,1024]{3,2,1,0:T(8,128)(2,1)S(1)}, bf16[8,4,16,1024]{3,2,1,0:T(8,128)(2,1)S(1)}, u32[]{:S(2)}, u32[]{:S(2)}) collective-permute-start(bf16[8,4,16,1024]{3,2,1,0:T(8,128)(2,1)S(1)} %shard_map.91.mine_ref), channel_id=1, source_target_pairs={{0,32},{32,0},{1,33},{33,1},{2,34},{34,2},{3,35},{35,3},{4,36},{36... | collective-permute-start | bytes 3145736 | tf_op jit(solution)/shard_map/ppermute | solution.py:169
  129.8 26.0 %collective-permute-start.16 = (bf16[4,16,1024]{2,1,0:T(8,128)(2,1)S(1)}, bf16[4,16,1024]{2,1,0:T(8,128)(2,1)S(1)}, u32[]{:S(2)}, u32[]{:S(2)}) collective-permute-start(bf16[4,16,1024]{2,1,0:T(8,128)(2,1)S(1)} %get-tuple-element.38.refs_0_), channel_id=1, source_target_pairs={{0,64},{64,128},{128,192},{192,256},{256,320},{320,384},{384,448},... | collective-permute-start | bytes 393224 | tf_op jit(solution)/shard_map/ppermute | solution.py:174
  132.4 26.3 %collective-permute-start.17 = (bf16[4,16,1024]{2,1,0:T(8,128)(2,1)S(1)}, bf16[4,16,1024]{2,1,0:T(8,128)(2,1)S(1)}, u32[]{:S(2)}, u32[]{:S(2)}) collective-permute-start(bf16[4,16,1024]{2,1,0:T(8,128)(2,1)S(1)} %get-tuple-element.38.refs_0_), channel_id=1, source_target_pairs={{0,128},{64,192},{128,256},{192,320},{256,384},{320,448},{384,0},{... | collective-permute-start | bytes 393224 | tf_op jit(solution)/shard_map/ppermute | solution.py:174
  137.5 39.5 %all-to-all-start.3 = ((bf16[32,2,16,128]{3,2,1,0:T(8,128)(2,1)}), bf16[32,2,16,128]{3,2,1,0:T(8,128)(2,1)S(1)}, u32[]{:S(2)}, u32[]{:S(2)}) async-start(bf16[32,2,16,128]{3,2,1,0:T(8,128)(2,1)} %get-tuple-element.44), calls=%async_computation.3 | async-start | bytes 524288 | tf_op jit(solution)/shard_map/all_to_all | solution.py:165
  142.6 20.7 %collective-permute-start.18 = (bf16[4,16,1024]{2,1,0:T(8,128)(2,1)S(1)}, bf16[4,16,1024]{2,1,0:T(8,128)(2,1)S(1)}, u32[]{:S(2)}, u32[]{:S(2)}) collective-permute-start(bf16[4,16,1024]{2,1,0:T(8,128)(2,1)S(1)} %get-tuple-element.38.refs_0_), channel_id=1, source_target_pairs={{0,192},{64,256},{128,320},{192,384},{256,448},{320,0},{384,64},{4... | collective-permute-start | bytes 393224 | tf_op jit(solution)/shard_map/ppermute | solution.py:174
  146.8 16.5 %collective-permute-start.19 = (bf16[4,16,1024]{2,1,0:T(8,128)(2,1)S(1)}, bf16[4,16,1024]{2,1,0:T(8,128)(2,1)S(1)}, u32[]{:S(2)}, u32[]{:S(2)}) collective-permute-start(bf16[4,16,1024]{2,1,0:T(8,128)(2,1)S(1)} %get-tuple-element.38.refs_0_), channel_id=1, source_target_pairs={{0,256},{64,320},{128,384},{192,448},{256,0},{320,64},{384,128},{4... | collective-permute-start | bytes 393224 | tf_op jit(solution)/shard_map/ppermute | solution.py:174
  151.5 19.4 %collective-permute-start.20 = (bf16[4,16,1024]{2,1,0:T(8,128)(2,1)S(1)}, bf16[4,16,1024]{2,1,0:T(8,128)(2,1)S(1)}, u32[]{:S(2)}, u32[]{:S(2)}) collective-permute-start(bf16[4,16,1024]{2,1,0:T(8,128)(2,1)S(1)} %get-tuple-element.38.refs_0_), channel_id=1, source_target_pairs={{0,320},{64,384},{128,448},{192,0},{256,64},{320,128},{384,192},{4... | collective-permute-start | bytes 393224 | tf_op jit(solution)/shard_map/ppermute | solution.py:174
  155.8 17.0 %collective-permute-start.21 = (bf16[4,16,1024]{2,1,0:T(8,128)(2,1)S(1)}, bf16[4,16,1024]{2,1,0:T(8,128)(2,1)S(1)}, u32[]{:S(2)}, u32[]{:S(2)}) collective-permute-start(bf16[4,16,1024]{2,1,0:T(8,128)(2,1)S(1)} %get-tuple-element.38.refs_0_), channel_id=1, source_target_pairs={{0,384},{64,448},{128,0},{192,64},{256,128},{320,192},{384,256},{4... | collective-permute-start | bytes 393224 | tf_op jit(solution)/shard_map/ppermute | solution.py:174
  158.7 16.3 %collective-permute-start.22 = (bf16[4,16,1024]{2,1,0:T(8,128)(2,1)S(1)}, bf16[4,16,1024]{2,1,0:T(8,128)(2,1)S(1)}, u32[]{:S(2)}, u32[]{:S(2)}) collective-permute-start(bf16[4,16,1024]{2,1,0:T(8,128)(2,1)S(1)} %get-tuple-element.38.refs_0_), channel_id=1, source_target_pairs={{0,448},{64,0},{128,64},{192,128},{256,192},{320,256},{384,320},{4... | collective-permute-start | bytes 393224 | tf_op jit(solution)/shard_map/ppermute | solution.py:174
  175.0 13.0 %collective-permute-start.23 = (bf16[8,4,16,1024]{3,2,1,0:T(8,128)(2,1)S(1)}, bf16[8,4,16,1024]{3,2,1,0:T(8,128)(2,1)S(1)}, u32[]{:S(2)}, u32[]{:S(2)}) collective-permute-start(bf16[8,4,16,1024]{3,2,1,0:T(8,128)(2,1)S(1)} %shard_map.93.mine_ref), channel_id=1, source_target_pairs={{0,32},{32,0},{1,33},{33,1},{2,34},{34,2},{3,35},{35,3},{4,36},{36... | collective-permute-start | bytes 3145736 | tf_op jit(solution)/shard_map/ppermute | solution.py:169
  177.0 30.5 %copy-start.1 = (f32[2,4,1,16,1024]{4,3,2,1,0:T(8,128)S(1)}, f32[2,4,1,16,1024]{4,3,2,1,0:T(8,128)}, u32[]{:S(2)}) copy-start(f32[2,4,1,16,1024]{4,3,2,1,0:T(8,128)} %left_ref.3) | copy-start | bytes 1572868
  178.5 28.9 %all-to-all-start.4 = ((bf16[32,2,2,16,128]{4,3,2,1,0:T(8,128)(2,1)}), bf16[32,2,2,16,128]{4,3,2,1,0:T(8,128)(2,1)S(1)}, u32[]{:S(2)}, u32[]{:S(2)}) async-start(bf16[32,2,2,16,128]{4,3,2,1,0:T(8,128)(2,1)} %shard_map.96), calls=%async_computation.4 | async-start | bytes 1048576 | tf_op jit(solution)/shard_map/all_to_all | solution.py:165
  189.2 15.3 %collective-permute-start.24 = (bf16[16,1024]{1,0:T(8,128)(2,1)S(1)}, bf16[16,1024]{1,0:T(8,128)(2,1)S(1)}, u32[]{:S(2)}, u32[]{:S(2)}) collective-permute-start(bf16[16,1024]{1,0:T(8,128)(2,1)S(1)} %get-tuple-element.41), channel_id=1, source_target_pairs={{0,1},{1,2},{2,3},{3,0},{4,5},{5,6},{6,7},{7,4},{8,9},{9,10},{10,1... | collective-permute-start | bytes 98312 | tf_op jit(solution)/shard_map/ppermute | solution.py:174
  192.9 12.4 %collective-permute-start.25 = (bf16[16,1024]{1,0:T(8,128)(2,1)S(1)}, bf16[16,1024]{1,0:T(8,128)(2,1)S(1)}, u32[]{:S(2)}, u32[]{:S(2)}) collective-permute-start(bf16[16,1024]{1,0:T(8,128)(2,1)S(1)} %get-tuple-element.42), channel_id=1, source_target_pairs={{0,2},{1,3},{2,0},{3,1},{4,6},{5,7},{6,4},{7,5},{8,10},{9,11},{10,... | collective-permute-start | bytes 98312 | tf_op jit(solution)/shard_map/ppermute | solution.py:174
  197.2 8.2 %collective-permute-start.26 = (bf16[16,1024]{1,0:T(8,128)(2,1)S(1)}, bf16[16,1024]{1,0:T(8,128)(2,1)S(1)}, u32[]{:S(2)}, u32[]{:S(2)}) collective-permute-start(bf16[16,1024]{1,0:T(8,128)(2,1)S(1)} %get-tuple-element.43), channel_id=1, source_target_pairs={{0,3},{1,0},{2,1},{3,2},{4,7},{5,4},{6,5},{7,6},{8,11},{9,8},{10,9... | collective-permute-start | bytes 98312 | tf_op jit(solution)/shard_map/ppermute | solution.py:174
  207.4 1.0 copy-start.2

commit v3 on v2

--- a/solution.py
+++ b/solution.py
@@ -54,24 +54,12 @@
             right_ref[sub, :, columns] = in_ref[sub * 8 + part, 1]
 
 
-def pick_theirs(grads_ref, where_ref, out_ref, sems):
-    copies = []
-    for k in range(8):
-        strip = lax.rem(where_ref[0] + k, 8) * 2 + 1 - where_ref[1]
-        rows = pl.ds(pl.multiple_of(strip * 16, 16), 16)
-        copies.append(pltpu.make_async_copy(grads_ref.at[0, rows, :], out_ref.at[k], sems.at[k]))
-    for copy in copies:
-        copy.start()
-    for copy in copies:
-        copy.wait()
-
-
 def add_pair(grads_ref, theirs_ref, where_ref, *out_refs):
     for k in range(8):
         strip = lax.rem(where_ref[0] + k, 8) * 2 + where_ref[1]
         rows = pl.ds(pl.multiple_of(strip * 16, 16), 16)
         out_refs[k][...] = (
-            grads_ref[0, rows, :].astype(F32) + theirs_ref[k].astype(F32)
+            grads_ref[0, rows, :].astype(F32) + theirs_ref[0, rows, :].astype(F32)
         ).astype(BF)
 
 
@@ -82,31 +70,27 @@
         total = refs[0][:, columns].astype(F32)
         for term in refs[1:-1]:
             total = total + term[:, columns].astype(F32)
-        out_ref[column] = total.astype(BF)
-
-
-def stack_rows(*refs):
-    for k in range(8):
-        refs[-1][k] = refs[k][...]
-
-
-def place_rows(whole, mine_ref, other_ref, core, first):
-    for k in range(8):
-        z = lax.rem(first + 8 - k, 8)
-        for sub in range(4):
-            base = sub * 256 + z * 32
-            whole[pl.ds(pl.multiple_of(base + core * 16, 16), 16), :] = mine_ref[k, sub]
-            whole[pl.ds(pl.multiple_of(base + 16 - core * 16, 16), 16), :] = other_ref[k, sub]
-
-
-def products(mine_ref, other_ref, rows_ref, left_ref, where_ref, gram_ref, mixed_ref, whole, both):
+        total = total.astype(BF)
+        for z in range(8):
+            out_ref[z * 4 + column] = total
+
+
+def place(whole, rows, z, parity):
+    for sub in range(4):
+        base = sub * 256 + z * 32 + parity * 16
+        whole[pl.ds(pl.multiple_of(base, 16), 16), :] = rows[sub]
+
+
+def products(mine_ref, other_ref, left_ref, where_ref, gram_ref, mixed_ref, whole, both):
     core = where_ref[1]
     strip = where_ref[0] * 2 + core
-    place_rows(whole, mine_ref, other_ref, core, where_ref[0])
+    for z in range(8):
+        place(whole, mine_ref.at[z], z, core)
+        place(whole, other_ref.at[z], z, 1 - core)
     row = lax.broadcasted_iota(jnp.int32, (64, 1024), 0)
     column = lax.broadcasted_iota(jnp.int32, (64, 1024), 1)
     chosen = (row // 16) * 256 + strip * 16 + row % 16
-    both[0:64] = rows_ref[...].reshape(64, 1024)
+    both[0:64] = mine_ref[where_ref[0]].reshape(64, 1024)
     both[64:128] = jnp.where(column == chosen, 1.0, 0.0).astype(BF)
     first = lax.dot_general(
         both[...], whole[...], (((1,), (1,)), ((), ())), preferred_element_type=F32
@@ -145,9 +129,33 @@
                 ].astype(F32)
 
 
-def right_product(mine_ref, other_ref, mixed_ref, where_ref, *refs):
+def pair_up(mine_ref, other_ref, where_ref, out_ref):
+    out_ref[where_ref[1]] = mine_ref[...]
+    out_ref[1 - where_ref[1]] = other_ref[...]
+
+
+def take_parity(in_ref, where_ref, out_ref):
+    out_ref[...] = in_ref[where_ref[1]]
+
+
+def stack_rows(first_ref, second_ref, third_ref, last_ref, out_ref):
+    for hop, ref in enumerate((first_ref, second_ref, third_ref)):
+        out_ref[2 * hop] = ref[0]
+        out_ref[2 * hop + 1] = ref[1]
+    out_ref[6] = last_ref[...]
+
+
+def right_product(pair_ref, mine_ref, other_ref, mixed_ref, where_ref, *refs):
     whole, rows = refs[4:]
-    place_rows(whole, mine_ref, other_ref, where_ref[1], where_ref[0])
+    z, core = where_ref[0], where_ref[1]
+    for parity in range(2):
+        place(whole, pair_ref.at[parity], z, parity)
+        for hop in range(3):
+            ahead = (1 - 2 * core) * (hop + 1)
+            place(whole, mine_ref.at[2 * hop + parity], lax.rem(z + 8 + ahead, 8), parity)
+            place(whole, other_ref.at[2 * hop + parity], lax.rem(z + 8 - ahead, 8), parity)
+    place(whole, mine_ref.at[6], lax.rem(z + 4, 8), core)
+    place(whole, other_ref.at[6], lax.rem(z + 4, 8), 1 - core)
     product = jnp.dot(mixed_ref[...], whole[...], preferred_element_type=F32)
     rows[...] = product.astype(BF).reshape(4, 16, 1024)
     for k in range(4):
@@ -174,10 +182,9 @@
     return lax.ppermute(value, axis, [(i, (i + distance) % size) for i in range(size)])
 
 
-def gathered(rows):
-    arrived = {k: shift(rows, "z", k) for k in DISTANCES}
-    arrived[0] = rows
-    return call(stack_rows, shape((8, 4, 16, 1024)), [arrived[k] for k in range(8)])
+def around(value):
+    pairs = [(2 * z + c, 2 * ((z - 1 + 2 * c) % 8) + c) for z in range(8) for c in range(2)]
+    return lax.ppermute(value, ROWS, pairs)
 
 
 def step(grads, table, left_state, right_state, left_root, right_root):
@@ -187,34 +194,23 @@
     blocks = jnp.arange(32, dtype=jnp.int32)
     holder = jnp.sum(jnp.where(table[None, :] == slots[:, None], blocks[None, :] + 1, 0), axis=1) - 1
 
-    theirs = pl.pallas_call(
-        pick_theirs,
-        out_shape=shape((8, 16, 4096)),
-        in_specs=[pl.BlockSpec(memory_space=pltpu.HBM), SM],
-        out_specs=VM,
-        scratch_shapes=[pltpu.SemaphoreType.DMA((8,))],
-        cost_estimate=pl.CostEstimate(flops=1000000, bytes_accessed=2097152, transcendentals=0),
-    )(grads, where)
-    pairs = call(
-        add_pair, (shape((16, 4096)),) * 8, [grads, swap(theirs), where], scalars=1
-    )
+    theirs = swap(grads)
+    pairs = call(add_pair, (shape((16, 4096)),) * 8, [grads, theirs, where], scalars=1)
     terms = [pairs[0]] + [shift(pairs[k], "z", k) for k in DISTANCES]
-    strip = call(add_replicas, shape((4, 16, 1024)), terms)
-    rows = exchange(strip, "yl")
+    strip = call(add_replicas, shape((32, 16, 1024)), terms)
 
     pieces = call(spread_roots, shape((32, 2, 2, 16, 128)), [left_root, right_root])
     pieces = exchange(pieces, BANDS).reshape(64, 2, 16, 128)
     picked = call(pick_roots, shape((32, 2, 16, 128)), [pieces, table], scalars=1)
-    picked, rows = lax.optimization_barrier((picked, rows))
     picked = exchange(picked, BANDS)
     left_rows, right_rows = call(join_roots, (shape((4, 16, 1024)), shape((4, 16, 1024))), [picked])
 
-    mine = gathered(rows)
+    mine = exchange(strip, ("z", "yl")).reshape(8, 4, 16, 1024)
     other = swap(mine)
     gram, mixed = call(
         products,
         (shape((32, 2, 16, 128)), shape((64, 1024))),
-        [mine, other, rows, left_rows, where],
+        [mine, other, left_rows, where],
         scalars=1,
         scratch=[pltpu.VMEM((1024, 1024), BF), pltpu.VMEM((128, 1024), BF)],
         flops=2 * 256 * 1024 * 1024,
@@ -229,13 +225,21 @@
         [gram, left_state, right_state],
     )
 
-    right_rows, mixed = lax.optimization_barrier((right_rows, mixed))
-    right_mine = gathered(right_rows)
+    theirs = swap(right_rows)
+    pair = call(
+        pair_up, shape((2, 4, 16, 1024)), [right_rows, theirs, where], scalars=1
+    )
+    rings = [around(pair)]
+    rings.append(around(rings[0]))
+    rings.append(around(rings[1]))
+    half = call(take_parity, shape((4, 16, 1024)), [rings[2], where], scalars=1)
+    rings.append(around(half))
+    right_mine = call(stack_rows, shape((7, 4, 16, 1024)), rings)
     right_other = swap(right_mine)
     result = call(
         right_product,
         (shape((16, 1024)),) * 4,
-        [right_mine, right_other, mixed, where],
+        [pair, right_mine, right_other, mixed, where],
         scalars=1,
         scratch=[pltpu.VMEM((1024, 1024), BF), pltpu.VMEM((4, 16, 1024), BF)],
         flops=2 * 64 * 1024 * 1024,

time: 211 us -> 187 us (0.89)
  the two profiles are of different devices: /device:TPU:64 before, /device:TPU:56 now
where the time goes in v3:
time: 187 us; the launch traced here: 186 us
  starting transfers between devices  110 us (59%)
  waiting for transfers between devices  58.7 us (31%)
  Pallas kernels  13.8 us (7%)
  local copies, waits for them, and re-layouts  1.91 us (1%)
    ppermute x10, starting transfers between devices, shift(): lax.ppermute(value, axis, [(i, (i + distance) % size) for i in range(size)])  44.9 us
    all_to_all x5, starting transfers between devices, exchange(): return lax.all_to_all(value, axes, split_axis=0, concat_axis=0, tiled=True)  44 us
    all_to_all x5, waiting for transfers between devices, exchange(): return lax.all_to_all(value, axes, split_axis=0, concat_axis=0, tiled=True)  32.7 us
    pallas_call x13, Pallas kernels, call(): pl.pallas_call(kernel, out_shape=out, in_specs=[VM] * (len(inputs) - scal...  13.8 us
    ppermute x4, starting transfers between devices, around(): return lax.ppermute(value, ROWS, pairs)  13.3 us
    ppermute x10, waiting for transfers between devices, shift(): lax.ppermute(value, axis, [(i, (i + distance) % size) for i in range(size)])  11.3 us
    ppermute x4, waiting for transfers between devices, around(): return lax.ppermute(value, ROWS, pairs)  11 us
    ppermute x4, starting transfers between devices, swap(): return lax.ppermute(value, 'c', [(0, 1), (1, 0)])  7.95 us
  transfers between devices with their start and end apart: 23, of which 11 were waited for; matrix products, arithmetic and copies ran while one was open for 0% of the time, Pallas kernels for 7%

profile of v3, /device:TPU:56, one launch (start us, length us, event | category | flops | bytes accessed | tf_op | source)
XLA Modules:
  0.0 185.8 jit_solution(3835292320488346298)
XLA Ops:
  0.6 2.1 %collective-permute-start.6 = (bf16[1,256,4096]{2,1,0:T(8,128)(2,1)}, bf16[1,256,4096]{2,1,0:T(8,128)(2,1)}, u32[]{:S(2)}, u32[]{:S(2)}) collective-permute-start(bf16[1,256,4096]{2,1,0:T(8,128)(2,1)} %grads_ref.1), channel_id=1, source_target_pairs={{0,32},{32,0},{1,33},{33,1},{2,34},{34,2},{3,35},{35,3},{4,36},{36... | collective-permute-start | bytes 6291464 | tf_op jit(solution)/shard_map/ppermute | solution.py:177
  2.7 0.9 copy-done.3
  3.7 0.9 copy-done.4
  4.6 0.9 shard_map.85
  5.5 9.5 %all-to-all-start = ((bf16[32,2,2,16,128]{4,3,2,1,0:T(8,128)(2,1)}), bf16[32,2,2,16,128]{4,3,2,1,0:T(8,128)(2,1)S(1)}, u32[]{:S(2)}, u32[]{:S(2)}) async-start(bf16[32,2,2,16,128]{4,3,2,1,0:T(8,128)(2,1)} %shard_map.85), calls=%async_computation | async-start | bytes 1048576 | tf_op jit(solution)/shard_map/all_to_all | solution.py:173
  15.1 1.9 shard_map.91
  16.9 6.1 %collective-permute-start.10 = (bf16[16,4096]{1,0:T(8,128)(2,1)S(1)}, bf16[16,4096]{1,0:T(8,128)(2,1)S(1)}, u32[]{:S(2)}, u32[]{:S(2)}) collective-permute-start(bf16[16,4096]{1,0:T(8,128)(2,1)S(1)} %get-tuple-element.26), channel_id=1, source_target_pairs={{0,128},{64,192},{128,256},{192,320},{256,384},{320,448},{384,0},{... | collective-permute-start | bytes 393224 | tf_op jit(solution)/shard_map/ppermute | solution.py:182
  23.0 6.8 %collective-permute-start.11 = (bf16[16,4096]{1,0:T(8,128)(2,1)S(1)}, bf16[16,4096]{1,0:T(8,128)(2,1)S(1)}, u32[]{:S(2)}, u32[]{:S(2)}) collective-permute-start(bf16[16,4096]{1,0:T(8,128)(2,1)S(1)} %get-tuple-element.27), channel_id=1, source_target_pairs={{0,384},{64,448},{128,0},{192,64},{256,128},{320,192},{384,256},{4... | collective-permute-start | bytes 393224 | tf_op jit(solution)/shard_map/ppermute | solution.py:182
  29.8 3.4 %collective-permute-start.12 = (bf16[16,4096]{1,0:T(8,128)(2,1)S(1)}, bf16[16,4096]{1,0:T(8,128)(2,1)S(1)}, u32[]{:S(2)}, u32[]{:S(2)}) collective-permute-start(bf16[16,4096]{1,0:T(8,128)(2,1)S(1)} %get-tuple-element.28), channel_id=1, source_target_pairs={{0,64},{64,128},{128,192},{192,256},{256,320},{320,384},{384,448},... | collective-permute-start | bytes 393224 | tf_op jit(solution)/shard_map/ppermute | solution.py:182
  33.2 3.7 %collective-permute-start.13 = (bf16[16,4096]{1,0:T(8,128)(2,1)S(1)}, bf16[16,4096]{1,0:T(8,128)(2,1)S(1)}, u32[]{:S(2)}, u32[]{:S(2)}) collective-permute-start(bf16[16,4096]{1,0:T(8,128)(2,1)S(1)} %get-tuple-element.29), channel_id=1, source_target_pairs={{0,448},{64,0},{128,64},{192,128},{256,192},{320,256},{384,320},{4... | collective-permute-start | bytes 393224 | tf_op jit(solution)/shard_map/ppermute | solution.py:182
  36.9 6.0 %collective-permute-start.7 = (bf16[16,4096]{1,0:T(8,128)(2,1)S(1)}, bf16[16,4096]{1,0:T(8,128)(2,1)S(1)}, u32[]{:S(2)}, u32[]{:S(2)}) collective-permute-start(bf16[16,4096]{1,0:T(8,128)(2,1)S(1)} %get-tuple-element.23), channel_id=1, source_target_pairs={{0,256},{64,320},{128,384},{192,448},{256,0},{320,64},{384,128},{4... | collective-permute-start | bytes 393224 | tf_op jit(solution)/shard_map/ppermute | solution.py:182
  42.9 2.8 %collective-permute-start.8 = (bf16[16,4096]{1,0:T(8,128)(2,1)S(1)}, bf16[16,4096]{1,0:T(8,128)(2,1)S(1)}, u32[]{:S(2)}, u32[]{:S(2)}) collective-permute-start(bf16[16,4096]{1,0:T(8,128)(2,1)S(1)} %get-tuple-element.24), channel_id=1, source_target_pairs={{0,192},{64,256},{128,320},{192,384},{256,448},{320,0},{384,64},{4... | collective-permute-start | bytes 393224 | tf_op jit(solution)/shard_map/ppermute | solution.py:182
  45.7 6.1 %collective-permute-start.9 = (bf16[16,4096]{1,0:T(8,128)(2,1)S(1)}, bf16[16,4096]{1,0:T(8,128)(2,1)S(1)}, u32[]{:S(2)}, u32[]{:S(2)}) collective-permute-start(bf16[16,4096]{1,0:T(8,128)(2,1)S(1)} %get-tuple-element.25), channel_id=1, source_target_pairs={{0,320},{64,384},{128,448},{192,0},{256,64},{320,128},{384,192},{4... | collective-permute-start | bytes 393224 | tf_op jit(solution)/shard_map/ppermute | solution.py:182
  51.8 0.4 collective-permute-done.7.refs_1_
  52.2 5.4 %collective-permute-done.8.refs_2_ = bf16[16,4096]{1,0:T(8,128)(2,1)S(1)} collective-permute-done((bf16[16,4096]{1,0:T(8,128)(2,1)S(1)}, bf16[16,4096]{1,0:T(8,128)(2,1)S(1)}, u32[]{:S(2)}, u32[]{:S(2)}) %collective-permute-start.8) | collective-permute-done | bytes 131104 | tf_op jit(solution)/shard_map/ppermute | solution.py:182
  57.6 0.9 collective-permute-done.9.refs_3_
  58.5 1.1 shard_map.92
  59.6 10.2 %all-to-all-start.2 = ((bf16[32,16,1024]{2,1,0:T(8,128)(2,1)}), bf16[32,16,1024]{2,1,0:T(8,128)(2,1)S(1)}, u32[]{:S(2)}, u32[]{:S(2)}) async-start(bf16[32,16,1024]{2,1,0:T(8,128)(2,1)} %shard_map.92), calls=%async_computation.2 | async-start | bytes 2097152 | tf_op jit(solution)/shard_map/all_to_all | solution.py:173
  69.8 1.3 shard_map.86
  71.1 25.8 %all-to-all-done.2 = bf16[32,16,1024]{2,1,0:T(8,128)(2,1)S(1)} async-done(((bf16[32,16,1024]{2,1,0:T(8,128)(2,1)}), bf16[32,16,1024]{2,1,0:T(8,128)(2,1)S(1)}, u32[]{:S(2)}, u32[]{:S(2)}) %all-to-all-start.2) | async-done | bytes 1048608 | tf_op jit(solution)/shard_map/all_to_all | solution.py:173
  96.9 7.7 %all-to-all-start.1 = ((bf16[32,2,16,128]{3,2,1,0:T(8,128)(2,1)}), bf16[32,2,16,128]{3,2,1,0:T(8,128)(2,1)S(1)}, u32[]{:S(2)}, u32[]{:S(2)}) async-start(bf16[32,2,16,128]{3,2,1,0:T(8,128)(2,1)} %shard_map.86), calls=%async_computation.1 | async-start | bytes 524288 | tf_op jit(solution)/shard_map/all_to_all | solution.py:173
  104.6 1.9 %collective-permute-start.14 = (bf16[8,4,16,1024]{3,2,1,0:T(8,128)(2,1)S(1)}, bf16[8,4,16,1024]{3,2,1,0:T(8,128)(2,1)S(1)}, u32[]{:S(2)}, u32[]{:S(2)}) collective-permute-start(bf16[8,4,16,1024]{3,2,1,0:T(8,128)(2,1)S(1)} %bitcast.5), channel_id=1, source_target_pairs={{0,32},{32,0},{1,33},{33,1},{2,34},{34,2},{3,35},{35,3},{4,36},{36... | collective-permute-start | bytes 3145736 | tf_op jit(solution)/shard_map/ppermute | solution.py:177
  106.5 6.9 %all-to-all-done.1.in_ref = bf16[32,2,16,128]{3,2,1,0:T(8,128)(2,1)S(1)} async-done(((bf16[32,2,16,128]{3,2,1,0:T(8,128)(2,1)}), bf16[32,2,16,128]{3,2,1,0:T(8,128)(2,1)S(1)}, u32[]{:S(2)}, u32[]{:S(2)}) %all-to-all-start.1) | async-done | bytes 262176 | tf_op jit(solution)/shard_map/all_to_all | solution.py:173
  113.5 1.9 %collective-permute-start = (bf16[4,16,1024]{2,1,0:T(8,128)(2,1)S(1)}, bf16[4,16,1024]{2,1,0:T(8,128)(2,1)S(1)}, u32[]{:S(2)}, u32[]{:S(2)}) collective-permute-start(bf16[4,16,1024]{2,1,0:T(8,128)(2,1)S(1)} %get-tuple-element.21.mine_ref), channel_id=1, source_target_pairs={{0,32},{32,0},{1,33},{33,1},{2,34},{34,2},{3,35},{35,3},{4,36},{36... | collective-permute-start | bytes 393224 | tf_op jit(solution)/shard_map/ppermute | solution.py:177
  115.4 1.3 collective-permute-done.other_ref
  116.7 0.6 shard_map.88.pair_ref
  117.3 2.6 %collective-permute-start.1 = (bf16[2,4,16,1024]{3,2,1,0:T(8,128)(2,1)S(1)}, bf16[2,4,16,1024]{3,2,1,0:T(8,128)(2,1)S(1)}, u32[]{:S(2)}, u32[]{:S(2)}) collective-permute-start(bf16[2,4,16,1024]{3,2,1,0:T(8,128)(2,1)S(1)} %shard_map.88.pair_ref), channel_id=1, source_target_pairs={{0,448},{32,96},{64,0},{96,160},{128,64},{160,224},{192,128},{224,... | collective-permute-start | bytes 786440 | tf_op jit(solution)/shard_map/ppermute | solution.py:187
  119.8 5.7 %collective-permute-done.1.first_ref = bf16[2,4,16,1024]{3,2,1,0:T(8,128)(2,1)S(1)} collective-permute-done((bf16[2,4,16,1024]{3,2,1,0:T(8,128)(2,1)S(1)}, bf16[2,4,16,1024]{3,2,1,0:T(8,128)(2,1)S(1)}, u32[]{:S(2)}, u32[]{:S(2)}) %collective-permute-start.1) | collective-permute-done | bytes 262176 | tf_op jit(solution)/shard_map/ppermute | solution.py:187
  125.5 3.8 %collective-permute-start.2 = (bf16[2,4,16,1024]{3,2,1,0:T(8,128)(2,1)S(1)}, bf16[2,4,16,1024]{3,2,1,0:T(8,128)(2,1)S(1)}, u32[]{:S(2)}, u32[]{:S(2)}) collective-permute-start(bf16[2,4,16,1024]{3,2,1,0:T(8,128)(2,1)S(1)} %collective-permute-done.1.first_ref), channel_id=1, source_target_pairs={{0,448},{32,96},{64,0},{96,160},{128,64},{160,224},{192,128},{224,... | collective-permute-start | bytes 786440 | tf_op jit(solution)/shard_map/ppermute | solution.py:187
  129.3 2.5 %shard_map.93 = (bf16[32,2,16,128]{3,2,1,0:T(8,128)(2,1)}, bf16[64,1024]{1,0:T(8,128)(2,1)S(1)}) custom-call(bf16[8,4,16,1024]{3,2,1,0:T(8,128)(2,1)S(1)} %bitcast.6, bf16[8,4,16,1024]{3,2,1,0:T(8,128)(2,1)S(1)} %collective-permute-done.14.other_ref, bf16[4,16,1024]{2,1,0:T(8,128)(2,1)S(1)} %get-tuple-element.30.left_ref, s32[3]{0:T(128)S(1)} %pad_add_fusion.where_ref.refs_4_), custom_call_target="tpu_custom_call" | custom-call | flops 536870912 | bytes 2228236 | tf_op jit(solution)/shard_map/pallas_call | solution.py:20
  131.8 6.9 %all-to-all-start.3 = ((bf16[32,2,16,128]{3,2,1,0:T(8,128)(2,1)}), bf16[32,2,16,128]{3,2,1,0:T(8,128)(2,1)S(1)}, u32[]{:S(2)}, u32[]{:S(2)}) async-start(bf16[32,2,16,128]{3,2,1,0:T(8,128)(2,1)} %get-tuple-element.36), calls=%async_computation.3 | async-start | bytes 524288 | tf_op jit(solution)/shard_map/all_to_all | solution.py:173
  138.7 2.9 %collective-permute-start.3 = (bf16[2,4,16,1024]{3,2,1,0:T(8,128)(2,1)S(1)}, bf16[2,4,16,1024]{3,2,1,0:T(8,128)(2,1)S(1)}, u32[]{:S(2)}, u32[]{:S(2)}) collective-permute-start(bf16[2,4,16,1024]{3,2,1,0:T(8,128)(2,1)S(1)} %collective-permute-done.2.second_ref), channel_id=1, source_target_pairs={{0,448},{32,96},{64,0},{96,160},{128,64},{160,224},{192,128},{224,... | collective-permute-start | bytes 786440 | tf_op jit(solution)/shard_map/ppermute | solution.py:187
  141.7 0.1 select_reduce_fusion
  141.7 5.2 %collective-permute-done.3.in_ref.third_ref = bf16[2,4,16,1024]{3,2,1,0:T(8,128)(2,1)S(1)} collective-permute-done((bf16[2,4,16,1024]{3,2,1,0:T(8,128)(2,1)S(1)}, bf16[2,4,16,1024]{3,2,1,0:T(8,128)(2,1)S(1)}, u32[]{:S(2)}, u32[]{:S(2)}) %collective-permute-start.3) | collective-permute-done | bytes 262176 | tf_op jit(solution)/shard_map/ppermute | solution.py:187
  147.0 0.6 shard_map.89
  147.5 4.1 %collective-permute-start.4 = (bf16[4,16,1024]{2,1,0:T(8,128)(2,1)S(1)}, bf16[4,16,1024]{2,1,0:T(8,128)(2,1)S(1)}, u32[]{:S(2)}, u32[]{:S(2)}) collective-permute-start(bf16[4,16,1024]{2,1,0:T(8,128)(2,1)S(1)} %shard_map.89), channel_id=1, source_target_pairs={{0,448},{32,96},{64,0},{96,160},{128,64},{160,224},{192,128},{224,... | collective-permute-start | bytes 393224 | tf_op jit(solution)/shard_map/ppermute | solution.py:187
  151.7 1.5 shard_map.96
  153.2 9.8 %all-to-all-start.4 = ((bf16[32,2,2,16,128]{4,3,2,1,0:T(8,128)(2,1)}), bf16[32,2,2,16,128]{4,3,2,1,0:T(8,128)(2,1)S(1)}, u32[]{:S(2)}, u32[]{:S(2)}) async-start(bf16[32,2,2,16,128]{4,3,2,1,0:T(8,128)(2,1)} %shard_map.96), calls=%async_computation.4 | async-start | bytes 1048576 | tf_op jit(solution)/shard_map/all_to_all | solution.py:173
  163.1 2.1 %collective-permute-start.5 = (bf16[7,4,16,1024]{3,2,1,0:T(8,128)(2,1)S(1)}, bf16[7,4,16,1024]{3,2,1,0:T(8,128)(2,1)S(1)}, u32[]{:S(2)}, u32[]{:S(2)}) collective-permute-start(bf16[7,4,16,1024]{3,2,1,0:T(8,128)(2,1)S(1)} %shard_map.90.mine_ref), channel_id=1, source_target_pairs={{0,32},{32,0},{1,33},{33,1},{2,34},{34,2},{3,35},{35,3},{4,36},{36... | collective-permute-start | bytes 2752520 | tf_op jit(solution)/shard_map/ppermute | solution.py:177
  165.2 2.4 %collective-permute-done.5.other_ref = bf16[7,4,16,1024]{3,2,1,0:T(8,128)(2,1)S(1)} collective-permute-done((bf16[7,4,16,1024]{3,2,1,0:T(8,128)(2,1)S(1)}, bf16[7,4,16,1024]{3,2,1,0:T(8,128)(2,1)S(1)}, u32[]{:S(2)}, u32[]{:S(2)}) %collective-permute-start.5) | collective-permute-done | bytes 917536 | tf_op jit(solution)/shard_map/ppermute | solution.py:177
  167.6 1.2 shard_map.94
  168.8 5.2 %collective-permute-start.15 = (bf16[16,1024]{1,0:T(8,128)(2,1)S(1)}, bf16[16,1024]{1,0:T(8,128)(2,1)S(1)}, u32[]{:S(2)}, u32[]{:S(2)}) collective-permute-start(bf16[16,1024]{1,0:T(8,128)(2,1)S(1)} %get-tuple-element.33), channel_id=1, source_target_pairs={{0,1},{1,2},{2,3},{3,0},{4,5},{5,6},{6,7},{7,4},{8,9},{9,10},{10,1... | collective-permute-start | bytes 98312 | tf_op jit(solution)/shard_map/ppermute | solution.py:182
  174.0 1.9 %collective-permute-start.16 = (bf16[16,1024]{1,0:T(8,128)(2,1)S(1)}, bf16[16,1024]{1,0:T(8,128)(2,1)S(1)}, u32[]{:S(2)}, u32[]{:S(2)}) collective-permute-start(bf16[16,1024]{1,0:T(8,128)(2,1)S(1)} %get-tuple-element.34), channel_id=1, source_target_pairs={{0,2},{1,3},{2,0},{3,1},{4,6},{5,7},{6,4},{7,5},{8,10},{9,11},{10,... | collective-permute-start | bytes 98312 | tf_op jit(solution)/shard_map/ppermute | solution.py:182
  175.9 3.0 %collective-permute-start.17 = (bf16[16,1024]{1,0:T(8,128)(2,1)S(1)}, bf16[16,1024]{1,0:T(8,128)(2,1)S(1)}, u32[]{:S(2)}, u32[]{:S(2)}) collective-permute-start(bf16[16,1024]{1,0:T(8,128)(2,1)S(1)} %get-tuple-element.35), channel_id=1, source_target_pairs={{0,3},{1,0},{2,1},{3,2},{4,7},{5,4},{6,5},{7,6},{8,11},{9,8},{10,9... | collective-permute-start | bytes 98312 | tf_op jit(solution)/shard_map/ppermute | solution.py:182
  178.9 1.7 collective-permute-done.16.refs_2_
  180.7 2.8 %collective-permute-done.17.refs_3_ = bf16[16,1024]{1,0:T(8,128)(2,1)S(1)} collective-permute-done((bf16[16,1024]{1,0:T(8,128)(2,1)S(1)}, bf16[16,1024]{1,0:T(8,128)(2,1)S(1)}, u32[]{:S(2)}, u32[]{:S(2)}) %collective-permute-start.17) | collective-permute-done | bytes 32800 | tf_op jit(solution)/shard_map/ppermute | solution.py:182
  183.5 1.2 shard_map.95
  184.7 1.1 shard_map.97
  (27 shorter events, 0.2 us)
Async XLA Ops:
  0.6 14.4 %copy-start = (bf16[1,256,4096]{2,1,0:T(8,128)(2,1)S(1)}, bf16[1,256,4096]{2,1,0:T(8,128)(2,1)}, u32[]{:S(2)}) copy-start(bf16[1,256,4096]{2,1,0:T(8,128)(2,1)} %grads_ref.1) | copy-start | bytes 6291460
  0.6 14.4 %collective-permute-start.6 = (bf16[1,256,4096]{2,1,0:T(8,128)(2,1)}, bf16[1,256,4096]{2,1,0:T(8,128)(2,1)}, u32[]{:S(2)}, u32[]{:S(2)}) collective-permute-start(bf16[1,256,4096]{2,1,0:T(8,128)(2,1)} %grads_ref.1), channel_id=1, source_target_pairs={{0,32},{32,0},{1,33},{33,1},{2,34},{34,2},{3,35},{35,3},{4,36},{36... | collective-permute-start | bytes 6291464 | tf_op jit(solution)/shard_map/ppermute | solution.py:177
  2.7 1.0 copy-start.3
  3.7 0.9 copy-start.4
  5.5 54.1 %all-to-all-start = ((bf16[32,2,2,16,128]{4,3,2,1,0:T(8,128)(2,1)}), bf16[32,2,2,16,128]{4,3,2,1,0:T(8,128)(2,1)S(1)}, u32[]{:S(2)}, u32[]{:S(2)}) async-start(bf16[32,2,2,16,128]{4,3,2,1,0:T(8,128)(2,1)} %shard_map.85), calls=%async_computation | async-start | bytes 1048576 | tf_op jit(solution)/shard_map/all_to_all | solution.py:173
  16.9 26.0 %collective-permute-start.10 = (bf16[16,4096]{1,0:T(8,128)(2,1)S(1)}, bf16[16,4096]{1,0:T(8,128)(2,1)S(1)}, u32[]{:S(2)}, u32[]{:S(2)}) collective-permute-start(bf16[16,4096]{1,0:T(8,128)(2,1)S(1)} %get-tuple-element.26), channel_id=1, source_target_pairs={{0,128},{64,192},{128,256},{192,320},{256,384},{320,448},{384,0},{... | collective-permute-start | bytes 393224 | tf_op jit(solution)/shard_map/ppermute | solution.py:182
  23.0 22.7 %collective-permute-start.11 = (bf16[16,4096]{1,0:T(8,128)(2,1)S(1)}, bf16[16,4096]{1,0:T(8,128)(2,1)S(1)}, u32[]{:S(2)}, u32[]{:S(2)}) collective-permute-start(bf16[16,4096]{1,0:T(8,128)(2,1)S(1)} %get-tuple-element.27), channel_id=1, source_target_pairs={{0,384},{64,448},{128,0},{192,64},{256,128},{320,192},{384,256},{4... | collective-permute-start | bytes 393224 | tf_op jit(solution)/shard_map/ppermute | solution.py:182
  29.8 22.0 %collective-permute-start.12 = (bf16[16,4096]{1,0:T(8,128)(2,1)S(1)}, bf16[16,4096]{1,0:T(8,128)(2,1)S(1)}, u32[]{:S(2)}, u32[]{:S(2)}) collective-permute-start(bf16[16,4096]{1,0:T(8,128)(2,1)S(1)} %get-tuple-element.28), channel_id=1, source_target_pairs={{0,64},{64,128},{128,192},{192,256},{256,320},{320,384},{384,448},... | collective-permute-start | bytes 393224 | tf_op jit(solution)/shard_map/ppermute | solution.py:182
  33.2 18.6 %collective-permute-start.13 = (bf16[16,4096]{1,0:T(8,128)(2,1)S(1)}, bf16[16,4096]{1,0:T(8,128)(2,1)S(1)}, u32[]{:S(2)}, u32[]{:S(2)}) collective-permute-start(bf16[16,4096]{1,0:T(8,128)(2,1)S(1)} %get-tuple-element.29), channel_id=1, source_target_pairs={{0,448},{64,0},{128,64},{192,128},{256,192},{320,256},{384,320},{4... | collective-permute-start | bytes 393224 | tf_op jit(solution)/shard_map/ppermute | solution.py:182
  36.9 15.3 %collective-permute-start.7 = (bf16[16,4096]{1,0:T(8,128)(2,1)S(1)}, bf16[16,4096]{1,0:T(8,128)(2,1)S(1)}, u32[]{:S(2)}, u32[]{:S(2)}) collective-permute-start(bf16[16,4096]{1,0:T(8,128)(2,1)S(1)} %get-tuple-element.23), channel_id=1, source_target_pairs={{0,256},{64,320},{128,384},{192,448},{256,0},{320,64},{384,128},{4... | collective-permute-start | bytes 393224 | tf_op jit(solution)/shard_map/ppermute | solution.py:182
  42.9 14.7 %collective-permute-start.8 = (bf16[16,4096]{1,0:T(8,128)(2,1)S(1)}, bf16[16,4096]{1,0:T(8,128)(2,1)S(1)}, u32[]{:S(2)}, u32[]{:S(2)}) collective-permute-start(bf16[16,4096]{1,0:T(8,128)(2,1)S(1)} %get-tuple-element.24), channel_id=1, source_target_pairs={{0,192},{64,256},{128,320},{192,384},{256,448},{320,0},{384,64},{4... | collective-permute-start | bytes 393224 | tf_op jit(solution)/shard_map/ppermute | solution.py:182
  45.7 12.8 %collective-permute-start.9 = (bf16[16,4096]{1,0:T(8,128)(2,1)S(1)}, bf16[16,4096]{1,0:T(8,128)(2,1)S(1)}, u32[]{:S(2)}, u32[]{:S(2)}) collective-permute-start(bf16[16,4096]{1,0:T(8,128)(2,1)S(1)} %get-tuple-element.25), channel_id=1, source_target_pairs={{0,320},{64,384},{128,448},{192,0},{256,64},{320,128},{384,192},{4... | collective-permute-start | bytes 393224 | tf_op jit(solution)/shard_map/ppermute | solution.py:182
  58.5 11.3 %copy-start.5 = (s32[32]{0:T(128)S(1)}, s32[32]{0:T(128)}, u32[]{:S(2)}) copy-start(s32[32]{0:T(128)} %table_ref.1) | copy-start | bytes 388
  59.6 37.3 %all-to-all-start.2 = ((bf16[32,16,1024]{2,1,0:T(8,128)(2,1)}), bf16[32,16,1024]{2,1,0:T(8,128)(2,1)S(1)}, u32[]{:S(2)}, u32[]{:S(2)}) async-start(bf16[32,16,1024]{2,1,0:T(8,128)(2,1)} %shard_map.92), calls=%async_computation.2 | async-start | bytes 2097152 | tf_op jit(solution)/shard_map/all_to_all | solution.py:173
  96.9 16.5 %all-to-all-start.1 = ((bf16[32,2,16,128]{3,2,1,0:T(8,128)(2,1)}), bf16[32,2,16,128]{3,2,1,0:T(8,128)(2,1)S(1)}, u32[]{:S(2)}, u32[]{:S(2)}) async-start(bf16[32,2,16,128]{3,2,1,0:T(8,128)(2,1)} %shard_map.86), calls=%async_computation.1 | async-start | bytes 524288 | tf_op jit(solution)/shard_map/all_to_all | solution.py:173
  104.6 24.7 %collective-permute-start.14 = (bf16[8,4,16,1024]{3,2,1,0:T(8,128)(2,1)S(1)}, bf16[8,4,16,1024]{3,2,1,0:T(8,128)(2,1)S(1)}, u32[]{:S(2)}, u32[]{:S(2)}) collective-permute-start(bf16[8,4,16,1024]{3,2,1,0:T(8,128)(2,1)S(1)} %bitcast.5), channel_id=1, source_target_pairs={{0,32},{32,0},{1,33},{33,1},{2,34},{34,2},{3,35},{35,3},{4,36},{36... | collective-permute-start | bytes 3145736 | tf_op jit(solution)/shard_map/ppermute | solution.py:177
  113.5 3.2 %collective-permute-start = (bf16[4,16,1024]{2,1,0:T(8,128)(2,1)S(1)}, bf16[4,16,1024]{2,1,0:T(8,128)(2,1)S(1)}, u32[]{:S(2)}, u32[]{:S(2)}) collective-permute-start(bf16[4,16,1024]{2,1,0:T(8,128)(2,1)S(1)} %get-tuple-element.21.mine_ref), channel_id=1, source_target_pairs={{0,32},{32,0},{1,33},{33,1},{2,34},{34,2},{3,35},{35,3},{4,36},{36... | collective-permute-start | bytes 393224 | tf_op jit(solution)/shard_map/ppermute | solution.py:177
  117.3 8.3 %collective-permute-start.1 = (bf16[2,4,16,1024]{3,2,1,0:T(8,128)(2,1)S(1)}, bf16[2,4,16,1024]{3,2,1,0:T(8,128)(2,1)S(1)}, u32[]{:S(2)}, u32[]{:S(2)}) collective-permute-start(bf16[2,4,16,1024]{3,2,1,0:T(8,128)(2,1)S(1)} %shard_map.88.pair_ref), channel_id=1, source_target_pairs={{0,448},{32,96},{64,0},{96,160},{128,64},{160,224},{192,128},{224,... | collective-permute-start | bytes 786440 | tf_op jit(solution)/shard_map/ppermute | solution.py:187
  125.5 13.2 %collective-permute-start.2 = (bf16[2,4,16,1024]{3,2,1,0:T(8,128)(2,1)S(1)}, bf16[2,4,16,1024]{3,2,1,0:T(8,128)(2,1)S(1)}, u32[]{:S(2)}, u32[]{:S(2)}) collective-permute-start(bf16[2,4,16,1024]{3,2,1,0:T(8,128)(2,1)S(1)} %collective-permute-done.1.first_ref), channel_id=1, source_target_pairs={{0,448},{32,96},{64,0},{96,160},{128,64},{160,224},{192,128},{224,... | collective-permute-start | bytes 786440 | tf_op jit(solution)/shard_map/ppermute | solution.py:187
  131.8 19.9 %all-to-all-start.3 = ((bf16[32,2,16,128]{3,2,1,0:T(8,128)(2,1)}), bf16[32,2,16,128]{3,2,1,0:T(8,128)(2,1)S(1)}, u32[]{:S(2)}, u32[]{:S(2)}) async-start(bf16[32,2,16,128]{3,2,1,0:T(8,128)(2,1)} %get-tuple-element.36), calls=%async_computation.3 | async-start | bytes 524288 | tf_op jit(solution)/shard_map/all_to_all | solution.py:173
  138.7 8.3 %collective-permute-start.3 = (bf16[2,4,16,1024]{3,2,1,0:T(8,128)(2,1)S(1)}, bf16[2,4,16,1024]{3,2,1,0:T(8,128)(2,1)S(1)}, u32[]{:S(2)}, u32[]{:S(2)}) collective-permute-start(bf16[2,4,16,1024]{3,2,1,0:T(8,128)(2,1)S(1)} %collective-permute-done.2.second_ref), channel_id=1, source_target_pairs={{0,448},{32,96},{64,0},{96,160},{128,64},{160,224},{192,128},{224,... | collective-permute-start | bytes 786440 | tf_op jit(solution)/shard_map/ppermute | solution.py:187
  147.5 15.5 %collective-permute-start.4 = (bf16[4,16,1024]{2,1,0:T(8,128)(2,1)S(1)}, bf16[4,16,1024]{2,1,0:T(8,128)(2,1)S(1)}, u32[]{:S(2)}, u32[]{:S(2)}) collective-permute-start(bf16[4,16,1024]{2,1,0:T(8,128)(2,1)S(1)} %shard_map.89), channel_id=1, source_target_pairs={{0,448},{32,96},{64,0},{96,160},{128,64},{160,224},{192,128},{224,... | collective-permute-start | bytes 393224 | tf_op jit(solution)/shard_map/ppermute | solution.py:187
  153.2 31.5 %all-to-all-start.4 = ((bf16[32,2,2,16,128]{4,3,2,1,0:T(8,128)(2,1)}), bf16[32,2,2,16,128]{4,3,2,1,0:T(8,128)(2,1)S(1)}, u32[]{:S(2)}, u32[]{:S(2)}) async-start(bf16[32,2,2,16,128]{4,3,2,1,0:T(8,128)(2,1)} %shard_map.96), calls=%async_computation.4 | async-start | bytes 1048576 | tf_op jit(solution)/shard_map/all_to_all | solution.py:173
  163.0 21.7 %copy-start.1 = (f32[2,4,1,16,1024]{4,3,2,1,0:T(8,128)S(1)}, f32[2,4,1,16,1024]{4,3,2,1,0:T(8,128)}, u32[]{:S(2)}) copy-start(f32[2,4,1,16,1024]{4,3,2,1,0:T(8,128)} %left_ref.3) | copy-start | bytes 1572868
  163.0 21.7 %copy-start.2 = (f32[2,4,1,16,1024]{4,3,2,1,0:T(8,128)S(1)}, f32[2,4,1,16,1024]{4,3,2,1,0:T(8,128)}, u32[]{:S(2)}) copy-start(f32[2,4,1,16,1024]{4,3,2,1,0:T(8,128)} %right_ref.3) | copy-start | bytes 1572868
  163.1 4.5 %collective-permute-start.5 = (bf16[7,4,16,1024]{3,2,1,0:T(8,128)(2,1)S(1)}, bf16[7,4,16,1024]{3,2,1,0:T(8,128)(2,1)S(1)}, u32[]{:S(2)}, u32[]{:S(2)}) collective-permute-start(bf16[7,4,16,1024]{3,2,1,0:T(8,128)(2,1)S(1)} %shard_map.90.mine_ref), channel_id=1, source_target_pairs={{0,32},{32,0},{1,33},{33,1},{2,34},{34,2},{3,35},{35,3},{4,36},{36... | collective-permute-start | bytes 2752520 | tf_op jit(solution)/shard_map/ppermute | solution.py:177
  168.8 10.1 %collective-permute-start.15 = (bf16[16,1024]{1,0:T(8,128)(2,1)S(1)}, bf16[16,1024]{1,0:T(8,128)(2,1)S(1)}, u32[]{:S(2)}, u32[]{:S(2)}) collective-permute-start(bf16[16,1024]{1,0:T(8,128)(2,1)S(1)} %get-tuple-element.33), channel_id=1, source_target_pairs={{0,1},{1,2},{2,3},{3,0},{4,5},{5,6},{6,7},{7,4},{8,9},{9,10},{10,1... | collective-permute-start | bytes 98312 | tf_op jit(solution)/shard_map/ppermute | solution.py:182
  174.0 6.7 %collective-permute-start.16 = (bf16[16,1024]{1,0:T(8,128)(2,1)S(1)}, bf16[16,1024]{1,0:T(8,128)(2,1)S(1)}, u32[]{:S(2)}, u32[]{:S(2)}) collective-permute-start(bf16[16,1024]{1,0:T(8,128)(2,1)S(1)} %get-tuple-element.34), channel_id=1, source_target_pairs={{0,2},{1,3},{2,0},{3,1},{4,6},{5,7},{6,4},{7,5},{8,10},{9,11},{10,... | collective-permute-start | bytes 98312 | tf_op jit(solution)/shard_map/ppermute | solution.py:182
  175.9 7.6 %collective-permute-start.17 = (bf16[16,1024]{1,0:T(8,128)(2,1)S(1)}, bf16[16,1024]{1,0:T(8,128)(2,1)S(1)}, u32[]{:S(2)}, u32[]{:S(2)}) collective-permute-start(bf16[16,1024]{1,0:T(8,128)(2,1)S(1)} %get-tuple-element.35), channel_id=1, source_target_pairs={{0,3},{1,0},{2,1},{3,2},{4,7},{5,4},{6,5},{7,6},{8,11},{9,8},{10,9... | collective-permute-start | bytes 98312 | tf_op jit(solution)/shard_map/ppermute | solution.py:182

commit v4 on v3

--- a/solution.py
+++ b/solution.py
@@ -10,7 +10,6 @@
 F32 = jnp.float32
 BANDS = ("x", "yh", "yl")
 ROWS = ("z", "c")
-DISTANCES = (4, 3, 5, 2, 6, 1, 7)
 VM = pl.BlockSpec(memory_space=pltpu.VMEM)
 SM = pl.BlockSpec(memory_space=pltpu.SMEM)
 
@@ -54,23 +53,40 @@
             right_ref[sub, :, columns] = in_ref[sub * 8 + part, 1]
 
 
-def add_pair(grads_ref, theirs_ref, where_ref, *out_refs):
-    for k in range(8):
-        strip = lax.rem(where_ref[0] + k, 8) * 2 + where_ref[1]
+def add_pair(grads_ref, theirs_ref, where_ref, own_ref, one_ref, two_ref, three_ref, four_ref):
+    z, core = where_ref[0], where_ref[1]
+    ahead = 1 - 2 * core
+
+    def pair(k, parity):
+        strip = lax.rem(z + 8 + k * ahead, 8) * 2 + parity
         rows = pl.ds(pl.multiple_of(strip * 16, 16), 16)
-        out_refs[k][...] = (
-            grads_ref[0, rows, :].astype(F32) + theirs_ref[0, rows, :].astype(F32)
-        ).astype(BF)
-
-
-def add_replicas(*refs):
-    out_ref = refs[-1]
+        return (grads_ref[0, rows, :].astype(F32) + theirs_ref[0, rows, :].astype(F32)).astype(BF)
+
+    four_ref[...] = pair(4, core)
+    for k, ref in ((3, three_ref), (2, two_ref), (1, one_ref)):
+        for parity in range(2):
+            ref[parity] = pair(k, parity)
+    own_ref[...] = pair(0, core)
+
+
+def add_half(both_ref, half_ref, where_ref, out_ref):
+    core = where_ref[1]
+    out_ref[1 - core] = both_ref[1 - core]
+    out_ref[core] = (both_ref[core].astype(F32) + half_ref[...].astype(F32)).astype(BF)
+
+
+def add_both(left_ref, right_ref, out_ref):
+    out_ref[...] = (left_ref[...].astype(F32) + right_ref[...].astype(F32)).astype(BF)
+
+
+def add_replicas(own_ref, mine_ref, theirs_ref, where_ref, out_ref):
     for column in range(4):
         columns = slice(column * 1024, column * 1024 + 1024)
-        total = refs[0][:, columns].astype(F32)
-        for term in refs[1:-1]:
-            total = total + term[:, columns].astype(F32)
-        total = total.astype(BF)
+        total = (
+            own_ref[:, columns].astype(F32)
+            + mine_ref[where_ref[1], :, columns].astype(F32)
+            + theirs_ref[:, columns].astype(F32)
+        ).astype(BF)
         for z in range(8):
             out_ref[z * 4 + column] = total
 
@@ -182,8 +198,8 @@
     return lax.ppermute(value, axis, [(i, (i + distance) % size) for i in range(size)])
 
 
-def around(value):
-    pairs = [(2 * z + c, 2 * ((z - 1 + 2 * c) % 8) + c) for z in range(8) for c in range(2)]
+def around(value, way):
+    pairs = [(2 * z + c, 2 * ((z + way - 2 * way * c) % 8) + c) for z in range(8) for c in range(2)]
     return lax.ppermute(value, ROWS, pairs)
 
 
@@ -195,9 +211,25 @@
     holder = jnp.sum(jnp.where(table[None, :] == slots[:, None], blocks[None, :] + 1, 0), axis=1) - 1
 
     theirs = swap(grads)
-    pairs = call(add_pair, (shape((16, 4096)),) * 8, [grads, theirs, where], scalars=1)
-    terms = [pairs[0]] + [shift(pairs[k], "z", k) for k in DISTANCES]
-    strip = call(add_replicas, shape((32, 16, 1024)), terms)
+    both = shape((2, 16, 4096))
+    own, one, two, three, four = call(
+        add_pair,
+        (shape((16, 4096)), both, both, both, shape((16, 4096))),
+        [grads, theirs, where],
+        scalars=1,
+    )
+    partial = around(four, 1)
+    partial = call(add_half, both, [three, partial, where], scalars=1)
+    partial = around(partial, 1)
+    partial = call(add_both, both, [two, partial])
+    partial = around(partial, 1)
+    partial = call(add_both, both, [one, partial])
+    partial = around(partial, 1)
+    other = call(take_parity, shape((16, 4096)), [partial, 1 - where], scalars=1)
+    other = swap(other)
+    strip = call(
+        add_replicas, shape((32, 16, 1024)), [own, partial, other, where], scalars=1
+    )
 
     pieces = call(spread_roots, shape((32, 2, 2, 16, 128)), [left_root, right_root])
     pieces = exchange(pieces, BANDS).reshape(64, 2, 16, 128)
@@ -229,11 +261,11 @@
     pair = call(
         pair_up, shape((2, 4, 16, 1024)), [right_rows, theirs, where], scalars=1
     )
-    rings = [around(pair)]
-    rings.append(around(rings[0]))
-    rings.append(around(rings[1]))
+    rings = [around(pair, -1)]
+    rings.append(around(rings[0], -1))
+    rings.append(around(rings[1], -1))
     half = call(take_parity, shape((4, 16, 1024)), [rings[2], where], scalars=1)
-    rings.append(around(half))
+    rings.append(around(half, -1))
     right_mine = call(stack_rows, shape((7, 4, 16, 1024)), rings)
     right_other = swap(right_mine)
     result = call(

time: 187 us -> 189 us (1.011)
  waiting for transfers between devices: 58.7 us -> 81.8 us
  starting transfers between devices: 110 us -> 89 us
    ppermute x10 -> x3, starting transfers between devices: 44.9 us -> 10.1 us  [shift(): lax.ppermute(value, axis, [(i, (i + distance) % size) for i in range(size)])]
    ppermute x4 -> x8, waiting for transfers between devices: 11 us -> 34.5 us  [around(): return lax.ppermute(value, ROWS, pairs)]
    ppermute x4 -> x8, starting transfers between devices: 13.3 us -> 26.1 us  [around(): return lax.ppermute(value, ROWS, pairs)]
    ppermute x10 -> x3, waiting for transfers between devices: 11.3 us -> 4.57 us  [shift(): lax.ppermute(value, axis, [(i, (i + distance) % size) for i in range(size)])]
    ppermute x4 -> x5, waiting for transfers between devices: 3.76 us -> 9.32 us  [swap(): return lax.ppermute(value, 'c', [(0, 1), (1, 0)])]
    ppermute x4 -> x5, starting transfers between devices: 7.95 us -> 9.74 us  [swap(): return lax.ppermute(value, 'c', [(0, 1), (1, 0)])]
    pallas_call x13 -> x17, Pallas kernels: 13.8 us -> 14.5 us  [call(): pl.pallas_call(kernel, out_shape=out, in_specs=[VM] * (len(inputs) - scal...]
  transfers between devices with their start and end apart: 23 -> 21, of which waited for: 11 -> 13; matrix products, arithmetic and copies ran while one was open for 0% -> 0% of each run, Pallas kernels for 7% -> 7%
where the time goes in v4:
time: 189 us; the launch traced here: 188 us
  starting transfers between devices  89 us (47%)
  waiting for transfers between devices  81.8 us (43%)
  Pallas kernels  14.5 us (8%)
    all_to_all x5, starting transfers between devices, exchange(): return lax.all_to_all(value, axes, split_axis=0, concat_axis=0, tiled=True)  43 us
    ppermute x8, waiting for transfers between devices, around(): return lax.ppermute(value, ROWS, pairs)  34.5 us
    all_to_all x5, waiting for transfers between devices, exchange(): return lax.all_to_all(value, axes, split_axis=0, concat_axis=0, tiled=True)  33.4 us
    ppermute x8, starting transfers between devices, around(): return lax.ppermute(value, ROWS, pairs)  26.1 us
    pallas_call x17, Pallas kernels, call(): pl.pallas_call(kernel, out_shape=out, in_specs=[VM] * (len(inputs) - scal...  14.5 us
    ppermute x3, starting transfers between devices, shift(): lax.ppermute(value, axis, [(i, (i + distance) % size) for i in range(size)])  10.1 us
    ppermute x5, starting transfers between devices, swap(): return lax.ppermute(value, 'c', [(0, 1), (1, 0)])  9.74 us
    ppermute x5, waiting for transfers between devices, swap(): return lax.ppermute(value, 'c', [(0, 1), (1, 0)])  9.32 us
  transfers between devices with their start and end apart: 21, of which 13 were waited for; matrix products, arithmetic and copies ran while one was open for 0% of the time, Pallas kernels for 7%

profile of v4, /device:TPU:56, one launch (start us, length us, event | category | flops | bytes accessed | tf_op | source)
XLA Modules:
  0.0 188.1 jit_solution(8330029554640369228)
XLA Ops:
  0.6 1.9 %collective-permute-start.6 = (bf16[1,256,4096]{2,1,0:T(8,128)(2,1)}, bf16[1,256,4096]{2,1,0:T(8,128)(2,1)S(1)}, u32[]{:S(2)}, u32[]{:S(2)}) collective-permute-start(bf16[1,256,4096]{2,1,0:T(8,128)(2,1)} %grads_ref.1), channel_id=1, source_target_pairs={{0,32},{32,0},{1,33},{33,1},{2,34},{34,2},{3,35},{35,3},{4,36},{36... | collective-permute-start | bytes 6291464 | tf_op jit(solution)/shard_map/ppermute | solution.py:193
  2.6 4.3 %collective-permute-done.6.theirs_ref = bf16[1,256,4096]{2,1,0:T(8,128)(2,1)S(1)} collective-permute-done((bf16[1,256,4096]{2,1,0:T(8,128)(2,1)}, bf16[1,256,4096]{2,1,0:T(8,128)(2,1)S(1)}, u32[]{:S(2)}, u32[]{:S(2)}) %collective-permute-start.6) | collective-permute-done | bytes 2097184 | tf_op jit(solution)/shard_map/ppermute | solution.py:193
  6.9 1.6 copy-done
  8.5 0.8 shard_map.91
  9.3 4.3 %collective-permute-start.7 = (bf16[16,4096]{1,0:T(8,128)(2,1)S(1)}, bf16[16,4096]{1,0:T(8,128)(2,1)S(1)}, u32[]{:S(2)}, u32[]{:S(2)}) collective-permute-start(bf16[16,4096]{1,0:T(8,128)(2,1)S(1)} %get-tuple-element.23), channel_id=1, source_target_pairs={{0,64},{32,480},{64,128},{96,32},{128,192},{160,96},{192,256},{224... | collective-permute-start | bytes 393224 | tf_op jit(solution)/shard_map/ppermute | solution.py:203
  13.6 0.9 shard_map.85
  14.5 9.5 %all-to-all-start = ((bf16[32,2,2,16,128]{4,3,2,1,0:T(8,128)(2,1)}), bf16[32,2,2,16,128]{4,3,2,1,0:T(8,128)(2,1)S(1)}, u32[]{:S(2)}, u32[]{:S(2)}) async-start(bf16[32,2,2,16,128]{4,3,2,1,0:T(8,128)(2,1)} %shard_map.85), calls=%async_computation | async-start | bytes 1048576 | tf_op jit(solution)/shard_map/all_to_all | solution.py:189
  24.0 0.6 shard_map.92
  24.6 4.3 %collective-permute-start.8 = (bf16[2,16,4096]{2,1,0:T(8,128)(2,1)S(1)}, bf16[2,16,4096]{2,1,0:T(8,128)(2,1)S(1)}, u32[]{:S(2)}, u32[]{:S(2)}) collective-permute-start(bf16[2,16,4096]{2,1,0:T(8,128)(2,1)S(1)} %shard_map.92), channel_id=1, source_target_pairs={{0,64},{32,480},{64,128},{96,32},{128,192},{160,96},{192,256},{224... | collective-permute-start | bytes 786440 | tf_op jit(solution)/shard_map/ppermute | solution.py:203
  28.9 8.6 %collective-permute-done.8.right_ref = bf16[2,16,4096]{2,1,0:T(8,128)(2,1)S(1)} collective-permute-done((bf16[2,16,4096]{2,1,0:T(8,128)(2,1)S(1)}, bf16[2,16,4096]{2,1,0:T(8,128)(2,1)S(1)}, u32[]{:S(2)}, u32[]{:S(2)}) %collective-permute-start.8) | collective-permute-done | bytes 262176 | tf_op jit(solution)/shard_map/ppermute | solution.py:203
  37.6 1.9 %collective-permute-start.9 = (bf16[2,16,4096]{2,1,0:T(8,128)(2,1)S(1)}, bf16[2,16,4096]{2,1,0:T(8,128)(2,1)S(1)}, u32[]{:S(2)}, u32[]{:S(2)}) collective-permute-start(bf16[2,16,4096]{2,1,0:T(8,128)(2,1)S(1)} %shard_map.93), channel_id=1, source_target_pairs={{0,64},{32,480},{64,128},{96,32},{128,192},{160,96},{192,256},{224... | collective-permute-start | bytes 786440 | tf_op jit(solution)/shard_map/ppermute | solution.py:203
  39.5 7.5 %collective-permute-done.9.right_ref = bf16[2,16,4096]{2,1,0:T(8,128)(2,1)S(1)} collective-permute-done((bf16[2,16,4096]{2,1,0:T(8,128)(2,1)S(1)}, bf16[2,16,4096]{2,1,0:T(8,128)(2,1)S(1)}, u32[]{:S(2)}, u32[]{:S(2)}) %collective-permute-start.9) | collective-permute-done | bytes 262176 | tf_op jit(solution)/shard_map/ppermute | solution.py:203
  47.1 1.9 %collective-permute-start.10 = (bf16[2,16,4096]{2,1,0:T(8,128)(2,1)S(1)}, bf16[2,16,4096]{2,1,0:T(8,128)(2,1)S(1)}, u32[]{:S(2)}, u32[]{:S(2)}) collective-permute-start(bf16[2,16,4096]{2,1,0:T(8,128)(2,1)S(1)} %shard_map.94), channel_id=1, source_target_pairs={{0,64},{32,480},{64,128},{96,32},{128,192},{160,96},{192,256},{224... | collective-permute-start | bytes 786440 | tf_op jit(solution)/shard_map/ppermute | solution.py:203
  49.1 7.5 %collective-permute-done.10.in_ref.mine_ref = bf16[2,16,4096]{2,1,0:T(8,128)(2,1)S(1)} collective-permute-done((bf16[2,16,4096]{2,1,0:T(8,128)(2,1)S(1)}, bf16[2,16,4096]{2,1,0:T(8,128)(2,1)S(1)}, u32[]{:S(2)}, u32[]{:S(2)}) %collective-permute-start.10) | collective-permute-done | bytes 262176 | tf_op jit(solution)/shard_map/ppermute | solution.py:203
  56.6 0.6 shard_map.95
  57.2 1.9 %collective-permute-start.11 = (bf16[16,4096]{1,0:T(8,128)(2,1)S(1)}, bf16[16,4096]{1,0:T(8,128)(2,1)S(1)}, u32[]{:S(2)}, u32[]{:S(2)}) collective-permute-start(bf16[16,4096]{1,0:T(8,128)(2,1)S(1)} %shard_map.95), channel_id=1, source_target_pairs={{0,32},{32,0},{1,33},{33,1},{2,34},{34,2},{3,35},{35,3},{4,36},{36... | collective-permute-start | bytes 393224 | tf_op jit(solution)/shard_map/ppermute | solution.py:193
  59.1 1.3 collective-permute-done.11.theirs_ref
  60.4 1.6 shard_map.96
  62.0 9.3 %all-to-all-start.2 = ((bf16[32,16,1024]{2,1,0:T(8,128)(2,1)}), bf16[32,16,1024]{2,1,0:T(8,128)(2,1)S(1)}, u32[]{:S(2)}, u32[]{:S(2)}) async-start(bf16[32,16,1024]{2,1,0:T(8,128)(2,1)} %shard_map.96), calls=%async_computation.2 | async-start | bytes 2097152 | tf_op jit(solution)/shard_map/all_to_all | solution.py:189
  71.4 1.3 shard_map.86
  72.6 26.4 %all-to-all-done.2 = bf16[32,16,1024]{2,1,0:T(8,128)(2,1)S(1)} async-done(((bf16[32,16,1024]{2,1,0:T(8,128)(2,1)}), bf16[32,16,1024]{2,1,0:T(8,128)(2,1)S(1)}, u32[]{:S(2)}, u32[]{:S(2)}) %all-to-all-start.2) | async-done | bytes 1048608 | tf_op jit(solution)/shard_map/all_to_all | solution.py:189
  99.0 7.8 %all-to-all-start.1 = ((bf16[32,2,16,128]{3,2,1,0:T(8,128)(2,1)}), bf16[32,2,16,128]{3,2,1,0:T(8,128)(2,1)S(1)}, u32[]{:S(2)}, u32[]{:S(2)}) async-start(bf16[32,2,16,128]{3,2,1,0:T(8,128)(2,1)} %shard_map.86), calls=%async_computation.1 | async-start | bytes 524288 | tf_op jit(solution)/shard_map/all_to_all | solution.py:189
  106.9 1.9 %collective-permute-start.12 = (bf16[8,4,16,1024]{3,2,1,0:T(8,128)(2,1)S(1)}, bf16[8,4,16,1024]{3,2,1,0:T(8,128)(2,1)S(1)}, u32[]{:S(2)}, u32[]{:S(2)}) collective-permute-start(bf16[8,4,16,1024]{3,2,1,0:T(8,128)(2,1)S(1)} %bitcast.5), channel_id=1, source_target_pairs={{0,32},{32,0},{1,33},{33,1},{2,34},{34,2},{3,35},{35,3},{4,36},{36... | collective-permute-start | bytes 3145736 | tf_op jit(solution)/shard_map/ppermute | solution.py:193
  108.8 7.0 %all-to-all-done.1.in_ref = bf16[32,2,16,128]{3,2,1,0:T(8,128)(2,1)S(1)} async-done(((bf16[32,2,16,128]{3,2,1,0:T(8,128)(2,1)}), bf16[32,2,16,128]{3,2,1,0:T(8,128)(2,1)S(1)}, u32[]{:S(2)}, u32[]{:S(2)}) %all-to-all-start.1) | async-done | bytes 262176 | tf_op jit(solution)/shard_map/all_to_all | solution.py:189
  115.9 1.9 %collective-permute-start = (bf16[4,16,1024]{2,1,0:T(8,128)(2,1)S(1)}, bf16[4,16,1024]{2,1,0:T(8,128)(2,1)S(1)}, u32[]{:S(2)}, u32[]{:S(2)}) collective-permute-start(bf16[4,16,1024]{2,1,0:T(8,128)(2,1)S(1)} %get-tuple-element.18.mine_ref), channel_id=1, source_target_pairs={{0,32},{32,0},{1,33},{33,1},{2,34},{34,2},{3,35},{35,3},{4,36},{36... | collective-permute-start | bytes 393224 | tf_op jit(solution)/shard_map/ppermute | solution.py:193
  117.8 1.3 collective-permute-done.other_ref
  119.1 0.6 shard_map.88.pair_ref
  119.7 2.7 %collective-permute-start.1 = (bf16[2,4,16,1024]{3,2,1,0:T(8,128)(2,1)S(1)}, bf16[2,4,16,1024]{3,2,1,0:T(8,128)(2,1)S(1)}, u32[]{:S(2)}, u32[]{:S(2)}) collective-permute-start(bf16[2,4,16,1024]{3,2,1,0:T(8,128)(2,1)S(1)} %shard_map.88.pair_ref), channel_id=1, source_target_pairs={{0,448},{32,96},{64,0},{96,160},{128,64},{160,224},{192,128},{224,... | collective-permute-start | bytes 786440 | tf_op jit(solution)/shard_map/ppermute | solution.py:203
  122.4 5.6 %collective-permute-done.1.first_ref = bf16[2,4,16,1024]{3,2,1,0:T(8,128)(2,1)S(1)} collective-permute-done((bf16[2,4,16,1024]{3,2,1,0:T(8,128)(2,1)S(1)}, bf16[2,4,16,1024]{3,2,1,0:T(8,128)(2,1)S(1)}, u32[]{:S(2)}, u32[]{:S(2)}) %collective-permute-start.1) | collective-permute-done | bytes 262176 | tf_op jit(solution)/shard_map/ppermute | solution.py:203
  128.0 3.9 %collective-permute-start.2 = (bf16[2,4,16,1024]{3,2,1,0:T(8,128)(2,1)S(1)}, bf16[2,4,16,1024]{3,2,1,0:T(8,128)(2,1)S(1)}, u32[]{:S(2)}, u32[]{:S(2)}) collective-permute-start(bf16[2,4,16,1024]{3,2,1,0:T(8,128)(2,1)S(1)} %collective-permute-done.1.first_ref), channel_id=1, source_target_pairs={{0,448},{32,96},{64,0},{96,160},{128,64},{160,224},{192,128},{224,... | collective-permute-start | bytes 786440 | tf_op jit(solution)/shard_map/ppermute | solution.py:203
  131.9 2.5 %shard_map.97 = (bf16[32,2,16,128]{3,2,1,0:T(8,128)(2,1)}, bf16[64,1024]{1,0:T(8,128)(2,1)S(1)}) custom-call(bf16[8,4,16,1024]{3,2,1,0:T(8,128)(2,1)S(1)} %bitcast.6, bf16[8,4,16,1024]{3,2,1,0:T(8,128)(2,1)S(1)} %collective-permute-done.12.other_ref, bf16[4,16,1024]{2,1,0:T(8,128)(2,1)S(1)} %get-tuple-element.24.left_ref, ...), custom_call_target="tpu_custom_call" | custom-call | flops 536870912 | bytes 2228236 | tf_op jit(solution)/shard_map/pallas_call | solution.py:19
  134.4 6.6 %all-to-all-start.3 = ((bf16[32,2,16,128]{3,2,1,0:T(8,128)(2,1)}), bf16[32,2,16,128]{3,2,1,0:T(8,128)(2,1)S(1)}, u32[]{:S(2)}, u32[]{:S(2)}) async-start(bf16[32,2,16,128]{3,2,1,0:T(8,128)(2,1)} %get-tuple-element.30), calls=%async_computation.3 | async-start | bytes 524288 | tf_op jit(solution)/shard_map/all_to_all | solution.py:189
  141.0 3.0 %collective-permute-start.3 = (bf16[2,4,16,1024]{3,2,1,0:T(8,128)(2,1)S(1)}, bf16[2,4,16,1024]{3,2,1,0:T(8,128)(2,1)S(1)}, u32[]{:S(2)}, u32[]{:S(2)}) collective-permute-start(bf16[2,4,16,1024]{3,2,1,0:T(8,128)(2,1)S(1)} %collective-permute-done.2.second_ref), channel_id=1, source_target_pairs={{0,448},{32,96},{64,0},{96,160},{128,64},{160,224},{192,128},{224,... | collective-permute-start | bytes 786440 | tf_op jit(solution)/shard_map/ppermute | solution.py:203
  144.1 5.2 %collective-permute-done.3.in_ref.third_ref = bf16[2,4,16,1024]{3,2,1,0:T(8,128)(2,1)S(1)} collective-permute-done((bf16[2,4,16,1024]{3,2,1,0:T(8,128)(2,1)S(1)}, bf16[2,4,16,1024]{3,2,1,0:T(8,128)(2,1)S(1)}, u32[]{:S(2)}, u32[]{:S(2)}) %collective-permute-start.3) | collective-permute-done | bytes 262176 | tf_op jit(solution)/shard_map/ppermute | solution.py:203
  149.2 0.6 shard_map.89
  149.8 4.2 %collective-permute-start.4 = (bf16[4,16,1024]{2,1,0:T(8,128)(2,1)S(1)}, bf16[4,16,1024]{2,1,0:T(8,128)(2,1)S(1)}, u32[]{:S(2)}, u32[]{:S(2)}) collective-permute-start(bf16[4,16,1024]{2,1,0:T(8,128)(2,1)S(1)} %shard_map.89), channel_id=1, source_target_pairs={{0,448},{32,96},{64,0},{96,160},{128,64},{160,224},{192,128},{224,... | collective-permute-start | bytes 393224 | tf_op jit(solution)/shard_map/ppermute | solution.py:203
  154.0 1.5 shard_map.100
  155.5 9.8 %all-to-all-start.4 = ((bf16[32,2,2,16,128]{4,3,2,1,0:T(8,128)(2,1)}), bf16[32,2,2,16,128]{4,3,2,1,0:T(8,128)(2,1)S(1)}, u32[]{:S(2)}, u32[]{:S(2)}) async-start(bf16[32,2,2,16,128]{4,3,2,1,0:T(8,128)(2,1)} %shard_map.100), calls=%async_computation.4 | async-start | bytes 1048576 | tf_op jit(solution)/shard_map/all_to_all | solution.py:189
  165.4 2.1 %collective-permute-start.5 = (bf16[7,4,16,1024]{3,2,1,0:T(8,128)(2,1)S(1)}, bf16[7,4,16,1024]{3,2,1,0:T(8,128)(2,1)S(1)}, u32[]{:S(2)}, u32[]{:S(2)}) collective-permute-start(bf16[7,4,16,1024]{3,2,1,0:T(8,128)(2,1)S(1)} %shard_map.90.mine_ref), channel_id=1, source_target_pairs={{0,32},{32,0},{1,33},{33,1},{2,34},{34,2},{3,35},{35,3},{4,36},{36... | collective-permute-start | bytes 2752520 | tf_op jit(solution)/shard_map/ppermute | solution.py:193
  167.5 2.4 %collective-permute-done.5.other_ref = bf16[7,4,16,1024]{3,2,1,0:T(8,128)(2,1)S(1)} collective-permute-done((bf16[7,4,16,1024]{3,2,1,0:T(8,128)(2,1)S(1)}, bf16[7,4,16,1024]{3,2,1,0:T(8,128)(2,1)S(1)}, u32[]{:S(2)}, u32[]{:S(2)}) %collective-permute-start.5) | collective-permute-done | bytes 917536 | tf_op jit(solution)/shard_map/ppermute | solution.py:193
  169.9 1.2 shard_map.98
  171.1 5.2 %collective-permute-start.13 = (bf16[16,1024]{1,0:T(8,128)(2,1)S(1)}, bf16[16,1024]{1,0:T(8,128)(2,1)S(1)}, u32[]{:S(2)}, u32[]{:S(2)}) collective-permute-start(bf16[16,1024]{1,0:T(8,128)(2,1)S(1)} %get-tuple-element.27), channel_id=1, source_target_pairs={{0,1},{1,2},{2,3},{3,0},{4,5},{5,6},{6,7},{7,4},{8,9},{9,10},{10,1... | collective-permute-start | bytes 98312 | tf_op jit(solution)/shard_map/ppermute | solution.py:198
  176.3 1.9 %collective-permute-start.14 = (bf16[16,1024]{1,0:T(8,128)(2,1)S(1)}, bf16[16,1024]{1,0:T(8,128)(2,1)S(1)}, u32[]{:S(2)}, u32[]{:S(2)}) collective-permute-start(bf16[16,1024]{1,0:T(8,128)(2,1)S(1)} %get-tuple-element.28), channel_id=1, source_target_pairs={{0,2},{1,3},{2,0},{3,1},{4,6},{5,7},{6,4},{7,5},{8,10},{9,11},{10,... | collective-permute-start | bytes 98312 | tf_op jit(solution)/shard_map/ppermute | solution.py:198
  178.2 3.0 %collective-permute-start.15 = (bf16[16,1024]{1,0:T(8,128)(2,1)S(1)}, bf16[16,1024]{1,0:T(8,128)(2,1)S(1)}, u32[]{:S(2)}, u32[]{:S(2)}) collective-permute-start(bf16[16,1024]{1,0:T(8,128)(2,1)S(1)} %get-tuple-element.29), channel_id=1, source_target_pairs={{0,3},{1,0},{2,1},{3,2},{4,7},{5,4},{6,5},{7,6},{8,11},{9,8},{10,9... | collective-permute-start | bytes 98312 | tf_op jit(solution)/shard_map/ppermute | solution.py:198
  181.3 1.7 collective-permute-done.14.refs_2_
  183.0 2.8 %collective-permute-done.15.refs_3_ = bf16[16,1024]{1,0:T(8,128)(2,1)S(1)} collective-permute-done((bf16[16,1024]{1,0:T(8,128)(2,1)S(1)}, bf16[16,1024]{1,0:T(8,128)(2,1)S(1)}, u32[]{:S(2)}, u32[]{:S(2)}) %collective-permute-start.15) | collective-permute-done | bytes 32800 | tf_op jit(solution)/shard_map/ppermute | solution.py:198
  185.8 1.2 shard_map.99
  187.0 1.1 shard_map.101
  (27 shorter events, 0.5 us)
Async XLA Ops:
  0.6 6.3 %collective-permute-start.6 = (bf16[1,256,4096]{2,1,0:T(8,128)(2,1)}, bf16[1,256,4096]{2,1,0:T(8,128)(2,1)S(1)}, u32[]{:S(2)}, u32[]{:S(2)}) collective-permute-start(bf16[1,256,4096]{2,1,0:T(8,128)(2,1)} %grads_ref.1), channel_id=1, source_target_pairs={{0,32},{32,0},{1,33},{33,1},{2,34},{34,2},{3,35},{35,3},{4,36},{36... | collective-permute-start | bytes 6291464 | tf_op jit(solution)/shard_map/ppermute | solution.py:193
  6.9 1.6 copy-start
  8.5 5.1 %copy-start.3 = (bf16[2,4,1,16,1024]{4,3,2,1,0:T(8,128)(2,1)S(1)}, bf16[2,4,1,16,1024]{4,3,2,1,0:T(8,128)(2,1)}, u32[]{:S(2)}) copy-start(bf16[2,4,1,16,1024]{4,3,2,1,0:T(8,128)(2,1)} %left_ref.2) | copy-start | bytes 786436
  8.5 5.1 %copy-start.4 = (bf16[2,4,1,16,1024]{4,3,2,1,0:T(8,128)(2,1)S(1)}, bf16[2,4,1,16,1024]{4,3,2,1,0:T(8,128)(2,1)}, u32[]{:S(2)}) copy-start(bf16[2,4,1,16,1024]{4,3,2,1,0:T(8,128)(2,1)} %right_ref.2) | copy-start | bytes 786436
  9.3 14.7 %collective-permute-start.7 = (bf16[16,4096]{1,0:T(8,128)(2,1)S(1)}, bf16[16,4096]{1,0:T(8,128)(2,1)S(1)}, u32[]{:S(2)}, u32[]{:S(2)}) collective-permute-start(bf16[16,4096]{1,0:T(8,128)(2,1)S(1)} %get-tuple-element.23), channel_id=1, source_target_pairs={{0,64},{32,480},{64,128},{96,32},{128,192},{160,96},{192,256},{224... | collective-permute-start | bytes 393224 | tf_op jit(solution)/shard_map/ppermute | solution.py:203
  14.5 47.5 %all-to-all-start = ((bf16[32,2,2,16,128]{4,3,2,1,0:T(8,128)(2,1)}), bf16[32,2,2,16,128]{4,3,2,1,0:T(8,128)(2,1)S(1)}, u32[]{:S(2)}, u32[]{:S(2)}) async-start(bf16[32,2,2,16,128]{4,3,2,1,0:T(8,128)(2,1)} %shard_map.85), calls=%async_computation | async-start | bytes 1048576 | tf_op jit(solution)/shard_map/all_to_all | solution.py:189
  24.6 12.9 %collective-permute-start.8 = (bf16[2,16,4096]{2,1,0:T(8,128)(2,1)S(1)}, bf16[2,16,4096]{2,1,0:T(8,128)(2,1)S(1)}, u32[]{:S(2)}, u32[]{:S(2)}) collective-permute-start(bf16[2,16,4096]{2,1,0:T(8,128)(2,1)S(1)} %shard_map.92), channel_id=1, source_target_pairs={{0,64},{32,480},{64,128},{96,32},{128,192},{160,96},{192,256},{224... | collective-permute-start | bytes 786440 | tf_op jit(solution)/shard_map/ppermute | solution.py:203
  37.6 9.5 %collective-permute-start.9 = (bf16[2,16,4096]{2,1,0:T(8,128)(2,1)S(1)}, bf16[2,16,4096]{2,1,0:T(8,128)(2,1)S(1)}, u32[]{:S(2)}, u32[]{:S(2)}) collective-permute-start(bf16[2,16,4096]{2,1,0:T(8,128)(2,1)S(1)} %shard_map.93), channel_id=1, source_target_pairs={{0,64},{32,480},{64,128},{96,32},{128,192},{160,96},{192,256},{224... | collective-permute-start | bytes 786440 | tf_op jit(solution)/shard_map/ppermute | solution.py:203
  47.1 24.3 %copy-start.5 = (s32[32]{0:T(128)S(1)}, s32[32]{0:T(128)}, u32[]{:S(2)}) copy-start(s32[32]{0:T(128)} %table_ref.1) | copy-start | bytes 388
  47.1 9.5 %collective-permute-start.10 = (bf16[2,16,4096]{2,1,0:T(8,128)(2,1)S(1)}, bf16[2,16,4096]{2,1,0:T(8,128)(2,1)S(1)}, u32[]{:S(2)}, u32[]{:S(2)}) collective-permute-start(bf16[2,16,4096]{2,1,0:T(8,128)(2,1)S(1)} %shard_map.94), channel_id=1, source_target_pairs={{0,64},{32,480},{64,128},{96,32},{128,192},{160,96},{192,256},{224... | collective-permute-start | bytes 786440 | tf_op jit(solution)/shard_map/ppermute | solution.py:203
  57.2 3.2 %collective-permute-start.11 = (bf16[16,4096]{1,0:T(8,128)(2,1)S(1)}, bf16[16,4096]{1,0:T(8,128)(2,1)S(1)}, u32[]{:S(2)}, u32[]{:S(2)}) collective-permute-start(bf16[16,4096]{1,0:T(8,128)(2,1)S(1)} %shard_map.95), channel_id=1, source_target_pairs={{0,32},{32,0},{1,33},{33,1},{2,34},{34,2},{3,35},{35,3},{4,36},{36... | collective-permute-start | bytes 393224 | tf_op jit(solution)/shard_map/ppermute | solution.py:193
  62.0 37.0 %all-to-all-start.2 = ((bf16[32,16,1024]{2,1,0:T(8,128)(2,1)}), bf16[32,16,1024]{2,1,0:T(8,128)(2,1)S(1)}, u32[]{:S(2)}, u32[]{:S(2)}) async-start(bf16[32,16,1024]{2,1,0:T(8,128)(2,1)} %shard_map.96), calls=%async_computation.2 | async-start | bytes 2097152 | tf_op jit(solution)/shard_map/all_to_all | solution.py:189
  99.0 16.8 %all-to-all-start.1 = ((bf16[32,2,16,128]{3,2,1,0:T(8,128)(2,1)}), bf16[32,2,16,128]{3,2,1,0:T(8,128)(2,1)S(1)}, u32[]{:S(2)}, u32[]{:S(2)}) async-start(bf16[32,2,16,128]{3,2,1,0:T(8,128)(2,1)} %shard_map.86), calls=%async_computation.1 | async-start | bytes 524288 | tf_op jit(solution)/shard_map/all_to_all | solution.py:189
  106.9 25.0 %collective-permute-start.12 = (bf16[8,4,16,1024]{3,2,1,0:T(8,128)(2,1)S(1)}, bf16[8,4,16,1024]{3,2,1,0:T(8,128)(2,1)S(1)}, u32[]{:S(2)}, u32[]{:S(2)}) collective-permute-start(bf16[8,4,16,1024]{3,2,1,0:T(8,128)(2,1)S(1)} %bitcast.5), channel_id=1, source_target_pairs={{0,32},{32,0},{1,33},{33,1},{2,34},{34,2},{3,35},{35,3},{4,36},{36... | collective-permute-start | bytes 3145736 | tf_op jit(solution)/shard_map/ppermute | solution.py:193
  115.9 3.2 %collective-permute-start = (bf16[4,16,1024]{2,1,0:T(8,128)(2,1)S(1)}, bf16[4,16,1024]{2,1,0:T(8,128)(2,1)S(1)}, u32[]{:S(2)}, u32[]{:S(2)}) collective-permute-start(bf16[4,16,1024]{2,1,0:T(8,128)(2,1)S(1)} %get-tuple-element.18.mine_ref), channel_id=1, source_target_pairs={{0,32},{32,0},{1,33},{33,1},{2,34},{34,2},{3,35},{35,3},{4,36},{36... | collective-permute-start | bytes 393224 | tf_op jit(solution)/shard_map/ppermute | solution.py:193
  119.7 8.3 %collective-permute-start.1 = (bf16[2,4,16,1024]{3,2,1,0:T(8,128)(2,1)S(1)}, bf16[2,4,16,1024]{3,2,1,0:T(8,128)(2,1)S(1)}, u32[]{:S(2)}, u32[]{:S(2)}) collective-permute-start(bf16[2,4,16,1024]{3,2,1,0:T(8,128)(2,1)S(1)} %shard_map.88.pair_ref), channel_id=1, source_target_pairs={{0,448},{32,96},{64,0},{96,160},{128,64},{160,224},{192,128},{224,... | collective-permute-start | bytes 786440 | tf_op jit(solution)/shard_map/ppermute | solution.py:203
  128.0 13.0 %collective-permute-start.2 = (bf16[2,4,16,1024]{3,2,1,0:T(8,128)(2,1)S(1)}, bf16[2,4,16,1024]{3,2,1,0:T(8,128)(2,1)S(1)}, u32[]{:S(2)}, u32[]{:S(2)}) collective-permute-start(bf16[2,4,16,1024]{3,2,1,0:T(8,128)(2,1)S(1)} %collective-permute-done.1.first_ref), channel_id=1, source_target_pairs={{0,448},{32,96},{64,0},{96,160},{128,64},{160,224},{192,128},{224,... | collective-permute-start | bytes 786440 | tf_op jit(solution)/shard_map/ppermute | solution.py:203
  134.4 19.6 %all-to-all-start.3 = ((bf16[32,2,16,128]{3,2,1,0:T(8,128)(2,1)}), bf16[32,2,16,128]{3,2,1,0:T(8,128)(2,1)S(1)}, u32[]{:S(2)}, u32[]{:S(2)}) async-start(bf16[32,2,16,128]{3,2,1,0:T(8,128)(2,1)} %get-tuple-element.30), calls=%async_computation.3 | async-start | bytes 524288 | tf_op jit(solution)/shard_map/all_to_all | solution.py:189
  141.0 8.3 %collective-permute-start.3 = (bf16[2,4,16,1024]{3,2,1,0:T(8,128)(2,1)S(1)}, bf16[2,4,16,1024]{3,2,1,0:T(8,128)(2,1)S(1)}, u32[]{:S(2)}, u32[]{:S(2)}) collective-permute-start(bf16[2,4,16,1024]{3,2,1,0:T(8,128)(2,1)S(1)} %collective-permute-done.2.second_ref), channel_id=1, source_target_pairs={{0,448},{32,96},{64,0},{96,160},{128,64},{160,224},{192,128},{224,... | collective-permute-start | bytes 786440 | tf_op jit(solution)/shard_map/ppermute | solution.py:203
  149.8 15.6 %collective-permute-start.4 = (bf16[4,16,1024]{2,1,0:T(8,128)(2,1)S(1)}, bf16[4,16,1024]{2,1,0:T(8,128)(2,1)S(1)}, u32[]{:S(2)}, u32[]{:S(2)}) collective-permute-start(bf16[4,16,1024]{2,1,0:T(8,128)(2,1)S(1)} %shard_map.89), channel_id=1, source_target_pairs={{0,448},{32,96},{64,0},{96,160},{128,64},{160,224},{192,128},{224,... | collective-permute-start | bytes 393224 | tf_op jit(solution)/shard_map/ppermute | solution.py:203
  155.5 31.5 %all-to-all-start.4 = ((bf16[32,2,2,16,128]{4,3,2,1,0:T(8,128)(2,1)}), bf16[32,2,2,16,128]{4,3,2,1,0:T(8,128)(2,1)S(1)}, u32[]{:S(2)}, u32[]{:S(2)}) async-start(bf16[32,2,2,16,128]{4,3,2,1,0:T(8,128)(2,1)} %shard_map.100), calls=%async_computation.4 | async-start | bytes 1048576 | tf_op jit(solution)/shard_map/all_to_all | solution.py:189
  165.3 21.7 %copy-start.1 = (f32[2,4,1,16,1024]{4,3,2,1,0:T(8,128)S(1)}, f32[2,4,1,16,1024]{4,3,2,1,0:T(8,128)}, u32[]{:S(2)}) copy-start(f32[2,4,1,16,1024]{4,3,2,1,0:T(8,128)} %left_ref.3) | copy-start | bytes 1572868
  165.3 21.7 %copy-start.2 = (f32[2,4,1,16,1024]{4,3,2,1,0:T(8,128)S(1)}, f32[2,4,1,16,1024]{4,3,2,1,0:T(8,128)}, u32[]{:S(2)}) copy-start(f32[2,4,1,16,1024]{4,3,2,1,0:T(8,128)} %right_ref.3) | copy-start | bytes 1572868
  165.4 4.5 %collective-permute-start.5 = (bf16[7,4,16,1024]{3,2,1,0:T(8,128)(2,1)S(1)}, bf16[7,4,16,1024]{3,2,1,0:T(8,128)(2,1)S(1)}, u32[]{:S(2)}, u32[]{:S(2)}) collective-permute-start(bf16[7,4,16,1024]{3,2,1,0:T(8,128)(2,1)S(1)} %shard_map.90.mine_ref), channel_id=1, source_target_pairs={{0,32},{32,0},{1,33},{33,1},{2,34},{34,2},{3,35},{35,3},{4,36},{36... | collective-permute-start | bytes 2752520 | tf_op jit(solution)/shard_map/ppermute | solution.py:193
  171.1 10.1 %collective-permute-start.13 = (bf16[16,1024]{1,0:T(8,128)(2,1)S(1)}, bf16[16,1024]{1,0:T(8,128)(2,1)S(1)}, u32[]{:S(2)}, u32[]{:S(2)}) collective-permute-start(bf16[16,1024]{1,0:T(8,128)(2,1)S(1)} %get-tuple-element.27), channel_id=1, source_target_pairs={{0,1},{1,2},{2,3},{3,0},{4,5},{5,6},{6,7},{7,4},{8,9},{9,10},{10,1... | collective-permute-start | bytes 98312 | tf_op jit(solution)/shard_map/ppermute | solution.py:198
  176.3 6.7 %collective-permute-start.14 = (bf16[16,1024]{1,0:T(8,128)(2,1)S(1)}, bf16[16,1024]{1,0:T(8,128)(2,1)S(1)}, u32[]{:S(2)}, u32[]{:S(2)}) collective-permute-start(bf16[16,1024]{1,0:T(8,128)(2,1)S(1)} %get-tuple-element.28), channel_id=1, source_target_pairs={{0,2},{1,3},{2,0},{3,1},{4,6},{5,7},{6,4},{7,5},{8,10},{9,11},{10,... | collective-permute-start | bytes 98312 | tf_op jit(solution)/shard_map/ppermute | solution.py:198
  178.2 7.6 %collective-permute-start.15 = (bf16[16,1024]{1,0:T(8,128)(2,1)S(1)}, bf16[16,1024]{1,0:T(8,128)(2,1)S(1)}, u32[]{:S(2)}, u32[]{:S(2)}) collective-permute-start(bf16[16,1024]{1,0:T(8,128)(2,1)S(1)} %get-tuple-element.29), channel_id=1, source_target_pairs={{0,3},{1,0},{2,1},{3,2},{4,7},{5,4},{6,5},{7,6},{8,11},{9,8},{10,9... | collective-permute-start | bytes 98312 | tf_op jit(solution)/shard_map/ppermute | solution.py:198

commit v5 on v4

--- a/solution.py
+++ b/solution.py
@@ -69,22 +69,27 @@
     own_ref[...] = pair(0, core)
 
 
-def add_half(both_ref, half_ref, where_ref, out_ref):
+def add_passed(two_ref, three_ref, four_ref, where_ref, out_ref):
     core = where_ref[1]
-    out_ref[1 - core] = both_ref[1 - core]
-    out_ref[core] = (both_ref[core].astype(F32) + half_ref[...].astype(F32)).astype(BF)
-
-
-def add_both(left_ref, right_ref, out_ref):
-    out_ref[...] = (left_ref[...].astype(F32) + right_ref[...].astype(F32)).astype(BF)
-
-
-def add_replicas(own_ref, mine_ref, theirs_ref, where_ref, out_ref):
+    for parity in range(2):
+        out_ref[parity] = (two_ref[parity].astype(F32) + three_ref[parity].astype(F32)).astype(BF)
+    out_ref[core] = (
+        two_ref[core].astype(F32) + three_ref[core].astype(F32) + four_ref[...].astype(F32)
+    ).astype(BF)
+
+
+def add_other(one_ref, two_ref, where_ref, out_ref):
+    parity = 1 - where_ref[1]
+    out_ref[...] = (one_ref[parity].astype(F32) + two_ref[parity].astype(F32)).astype(BF)
+
+
+def add_replicas(own_ref, one_ref, two_ref, theirs_ref, where_ref, out_ref):
     for column in range(4):
         columns = slice(column * 1024, column * 1024 + 1024)
         total = (
             own_ref[:, columns].astype(F32)
-            + mine_ref[where_ref[1], :, columns].astype(F32)
+            + one_ref[where_ref[1], :, columns].astype(F32)
+            + two_ref[where_ref[1], :, columns].astype(F32)
             + theirs_ref[:, columns].astype(F32)
         ).astype(BF)
         for z in range(8):
@@ -161,8 +166,7 @@
     out_ref[6] = last_ref[...]
 
 
-def right_product(pair_ref, mine_ref, other_ref, mixed_ref, where_ref, *refs):
-    whole, rows = refs[4:]
+def right_product(pair_ref, mine_ref, other_ref, mixed_ref, where_ref, out_ref, whole):
     z, core = where_ref[0], where_ref[1]
     for parity in range(2):
         place(whole, pair_ref.at[parity], z, parity)
@@ -173,16 +177,12 @@
     place(whole, mine_ref.at[6], lax.rem(z + 4, 8), core)
     place(whole, other_ref.at[6], lax.rem(z + 4, 8), 1 - core)
     product = jnp.dot(mixed_ref[...], whole[...], preferred_element_type=F32)
-    rows[...] = product.astype(BF).reshape(4, 16, 1024)
-    for k in range(4):
-        refs[k][...] = rows[lax.rem(where_ref[2] + k, 4)]
-
-
-def join_columns(*refs):
-    where_ref, out_ref = refs[4:]
-    for k in range(4):
-        column = lax.rem(where_ref[2] + 4 - k, 4) * 1024
-        out_ref[0, 0, :, pl.ds(pl.multiple_of(column, 1024), 1024)] = refs[k][...]
+    out_ref[...] = product.astype(BF).reshape(4, 16, 1024)
+
+
+def join_columns(in_ref, out_ref):
+    for column in range(4):
+        out_ref[0, 0, :, column * 1024 : column * 1024 + 1024] = in_ref[column]
 
 
 def exchange(value, axes):
@@ -191,11 +191,6 @@
 
 def swap(value):
     return lax.ppermute(value, "c", [(0, 1), (1, 0)])
-
-
-def shift(value, axis, distance):
-    size = lax.axis_size(axis)
-    return lax.ppermute(value, axis, [(i, (i + distance) % size) for i in range(size)])
 
 
 def around(value, way):
@@ -205,7 +200,7 @@
 
 def step(grads, table, left_state, right_state, left_root, right_root):
     z, core = lax.axis_index("z"), lax.axis_index("c")
-    where = jnp.stack([z, core, lax.axis_index("yl")]).astype(jnp.int32)
+    where = jnp.stack([z, core]).astype(jnp.int32)
     slots = jnp.arange(64, dtype=jnp.int32)
     blocks = jnp.arange(32, dtype=jnp.int32)
     holder = jnp.sum(jnp.where(table[None, :] == slots[:, None], blocks[None, :] + 1, 0), axis=1) - 1
@@ -218,17 +213,15 @@
         [grads, theirs, where],
         scalars=1,
     )
-    partial = around(four, 1)
-    partial = call(add_half, both, [three, partial, where], scalars=1)
-    partial = around(partial, 1)
-    partial = call(add_both, both, [two, partial])
-    partial = around(partial, 1)
-    partial = call(add_both, both, [one, partial])
-    partial = around(partial, 1)
-    other = call(take_parity, shape((16, 4096)), [partial, 1 - where], scalars=1)
+    four = around(four, 2)
+    three = around(three, 1)
+    one = around(one, 1)
+    two = call(add_passed, both, [two, three, four, where], scalars=1)
+    two = around(two, 2)
+    other = call(add_other, shape((16, 4096)), [one, two, where], scalars=1)
     other = swap(other)
     strip = call(
-        add_replicas, shape((32, 16, 1024)), [own, partial, other, where], scalars=1
+        add_replicas, shape((32, 16, 1024)), [own, one, two, other, where], scalars=1
     )
 
     pieces = call(spread_roots, shape((32, 2, 2, 16, 128)), [left_root, right_root])
@@ -261,23 +254,22 @@
     pair = call(
         pair_up, shape((2, 4, 16, 1024)), [right_rows, theirs, where], scalars=1
     )
-    rings = [around(pair, -1)]
-    rings.append(around(rings[0], -1))
-    rings.append(around(rings[1], -1))
-    half = call(take_parity, shape((4, 16, 1024)), [rings[2], where], scalars=1)
-    rings.append(around(half, -1))
-    right_mine = call(stack_rows, shape((7, 4, 16, 1024)), rings)
+    second = around(pair, -2)
+    first = around(pair, -1)
+    half = call(take_parity, shape((4, 16, 1024)), [second, where], scalars=1)
+    third = around(second, -1)
+    last = around(half, -2)
+    right_mine = call(stack_rows, shape((7, 4, 16, 1024)), [first, second, third, last])
     right_other = swap(right_mine)
     result = call(
         right_product,
-        (shape((16, 1024)),) * 4,
+        shape((4, 16, 1024)),
         [pair, right_mine, right_other, mixed, where],
         scalars=1,
-        scratch=[pltpu.VMEM((1024, 1024), BF), pltpu.VMEM((4, 16, 1024), BF)],
+        scratch=[pltpu.VMEM((1024, 1024), BF)],
         flops=2 * 64 * 1024 * 1024,
     )
-    home = [result[0]] + [shift(result[k], "yl", k) for k in range(1, 4)]
-    direction = call(join_columns, shape((1, 1, 16, 4096)), [*home, where], scalars=1)
+    direction = call(join_columns, shape((1, 1, 16, 4096)), [exchange(result, "yl")])
     return direction, left_new, right_new
 
 

time: 189 us -> 192 us (1.016)
  the two profiles are of different devices: /device:TPU:56 before, /device:TPU:8 now
where the time goes in v5:
time: 192 us; the launch traced here: 191 us
  waiting for transfers between devices  89 us (46%)
  starting transfers between devices  82.1 us (43%)
  Pallas kernels  16.4 us (9%)
  local copies, waits for them, and re-layouts  1.92 us (1%)
    all_to_all x6, waiting for transfers between devices, exchange(): return lax.all_to_all(value, axes, split_axis=0, concat_axis=0, tiled=True)  64.2 us
    all_to_all x6, starting transfers between devices, exchange(): return lax.all_to_all(value, axes, split_axis=0, concat_axis=0, tiled=True)  40.2 us
    ppermute x8, starting transfers between devices, around(): return lax.ppermute(value, ROWS, pairs)  30 us
    ppermute x8, waiting for transfers between devices, around(): return lax.ppermute(value, ROWS, pairs)  22.2 us
    pallas_call x15, Pallas kernels, call(): pl.pallas_call(kernel, out_shape=out, in_specs=[VM] * (len(inputs) - scal...  16.4 us
    ppermute x5, starting transfers between devices, swap(): return lax.ppermute(value, 'c', [(0, 1), (1, 0)])  11.9 us
  transfers between devices with their start and end apart: 19, of which 11 were waited for; matrix products, arithmetic and copies ran while one was open for 0% of the time, Pallas kernels for 8%

profile of v5, /device:TPU:8, one launch (start us, length us, event | category | flops | bytes accessed | tf_op | source)
XLA Modules:
  0.0 190.6 jit_solution(14071580158536996921)
XLA Ops:
  0.6 2.1 %collective-permute-start.6 = (bf16[1,256,4096]{2,1,0:T(8,128)(2,1)}, bf16[1,256,4096]{2,1,0:T(8,128)(2,1)}, u32[]{:S(2)}, u32[]{:S(2)}) collective-permute-start(bf16[1,256,4096]{2,1,0:T(8,128)(2,1)} %grads_ref.1), channel_id=1, source_target_pairs={{0,32},{32,0},{1,33},{33,1},{2,34},{34,2},{3,35},{35,3},{4,36},{36... | collective-permute-start | bytes 6291464 | tf_op jit(solution)/shard_map/ppermute | solution.py:193
  2.7 0.9 copy-done.3
  3.7 0.9 copy-done.4
  4.6 0.9 shard_map.85
  5.5 10.2 %all-to-all-start = ((bf16[32,2,2,16,128]{4,3,2,1,0:T(8,128)(2,1)}), bf16[32,2,2,16,128]{4,3,2,1,0:T(8,128)(2,1)S(1)}, u32[]{:S(2)}, u32[]{:S(2)}) async-start(bf16[32,2,2,16,128]{4,3,2,1,0:T(8,128)(2,1)} %shard_map.85), calls=%async_computation | async-start | bytes 1048576 | tf_op jit(solution)/shard_map/all_to_all | solution.py:189
  15.7 0.1 pad_add_fusion.where_ref
  15.7 1.9 shard_map.91
  17.6 4.3 %collective-permute-start.8 = (bf16[2,16,4096]{2,1,0:T(8,128)(2,1)S(1)}, bf16[2,16,4096]{2,1,0:T(8,128)(2,1)S(1)}, u32[]{:S(2)}, u32[]{:S(2)}) collective-permute-start(bf16[2,16,4096]{2,1,0:T(8,128)(2,1)S(1)} %get-tuple-element.18), channel_id=1, source_target_pairs={{0,64},{32,480},{64,128},{96,32},{128,192},{160,96},{192,256},{224... | collective-permute-start | bytes 786440 | tf_op jit(solution)/shard_map/ppermute | solution.py:198
  21.9 6.1 %collective-permute-start.9 = (bf16[16,4096]{1,0:T(8,128)(2,1)S(1)}, bf16[16,4096]{1,0:T(8,128)(2,1)S(1)}, u32[]{:S(2)}, u32[]{:S(2)}) collective-permute-start(bf16[16,4096]{1,0:T(8,128)(2,1)S(1)} %get-tuple-element.19), channel_id=1, source_target_pairs={{0,128},{32,416},{64,192},{96,480},{128,256},{160,32},{192,320},{2... | collective-permute-start | bytes 393224 | tf_op jit(solution)/shard_map/ppermute | solution.py:198
  28.0 5.5 %collective-permute-start.7 = (bf16[2,16,4096]{2,1,0:T(8,128)(2,1)S(1)}, bf16[2,16,4096]{2,1,0:T(8,128)(2,1)S(1)}, u32[]{:S(2)}, u32[]{:S(2)}) collective-permute-start(bf16[2,16,4096]{2,1,0:T(8,128)(2,1)S(1)} %get-tuple-element.16), channel_id=1, source_target_pairs={{0,64},{32,480},{64,128},{96,32},{128,192},{160,96},{192,256},{224... | collective-permute-start | bytes 786440 | tf_op jit(solution)/shard_map/ppermute | solution.py:198
  33.5 3.8 %collective-permute-done.9.four_ref = bf16[16,4096]{1,0:T(8,128)(2,1)S(1)} collective-permute-done((bf16[16,4096]{1,0:T(8,128)(2,1)S(1)}, bf16[16,4096]{1,0:T(8,128)(2,1)S(1)}, u32[]{:S(2)}, u32[]{:S(2)}) %collective-permute-start.9) | collective-permute-done | bytes 131104 | tf_op jit(solution)/shard_map/ppermute | solution.py:198
  37.3 0.7 shard_map.92
  37.9 1.9 %collective-permute-start.10 = (bf16[2,16,4096]{2,1,0:T(8,128)(2,1)S(1)}, bf16[2,16,4096]{2,1,0:T(8,128)(2,1)S(1)}, u32[]{:S(2)}, u32[]{:S(2)}) collective-permute-start(bf16[2,16,4096]{2,1,0:T(8,128)(2,1)S(1)} %shard_map.92), channel_id=1, source_target_pairs={{0,128},{32,416},{64,192},{96,480},{128,256},{160,32},{192,320},{2... | collective-permute-start | bytes 786440 | tf_op jit(solution)/shard_map/ppermute | solution.py:198
  39.9 9.0 %collective-permute-done.10.two_ref = bf16[2,16,4096]{2,1,0:T(8,128)(2,1)S(1)} collective-permute-done((bf16[2,16,4096]{2,1,0:T(8,128)(2,1)S(1)}, bf16[2,16,4096]{2,1,0:T(8,128)(2,1)S(1)}, u32[]{:S(2)}, u32[]{:S(2)}) %collective-permute-start.10) | collective-permute-done | bytes 262176 | tf_op jit(solution)/shard_map/ppermute | solution.py:198
  48.8 0.6 shard_map.93
  49.4 1.9 %collective-permute-start.11 = (bf16[16,4096]{1,0:T(8,128)(2,1)S(1)}, bf16[16,4096]{1,0:T(8,128)(2,1)S(1)}, u32[]{:S(2)}, u32[]{:S(2)}) collective-permute-start(bf16[16,4096]{1,0:T(8,128)(2,1)S(1)} %shard_map.93), channel_id=1, source_target_pairs={{0,32},{32,0},{1,33},{33,1},{2,34},{34,2},{3,35},{35,3},{4,36},{36... | collective-permute-start | bytes 393224 | tf_op jit(solution)/shard_map/ppermute | solution.py:193
  51.3 1.3 collective-permute-done.11.theirs_ref
  52.7 1.6 shard_map.94
  54.3 8.8 %all-to-all-start.2 = ((bf16[32,16,1024]{2,1,0:T(8,128)(2,1)}), bf16[32,16,1024]{2,1,0:T(8,128)(2,1)S(1)}, u32[]{:S(2)}, u32[]{:S(2)}) async-start(bf16[32,16,1024]{2,1,0:T(8,128)(2,1)} %shard_map.94), calls=%async_computation.2 | async-start | bytes 2097152 | tf_op jit(solution)/shard_map/all_to_all | solution.py:189
  63.1 1.3 shard_map.86
  64.4 26.7 %all-to-all-done.2 = bf16[32,16,1024]{2,1,0:T(8,128)(2,1)S(1)} async-done(((bf16[32,16,1024]{2,1,0:T(8,128)(2,1)}), bf16[32,16,1024]{2,1,0:T(8,128)(2,1)S(1)}, u32[]{:S(2)}, u32[]{:S(2)}) %all-to-all-start.2) | async-done | bytes 1048608 | tf_op jit(solution)/shard_map/all_to_all | solution.py:189
  91.0 7.6 %all-to-all-start.1 = ((bf16[32,2,16,128]{3,2,1,0:T(8,128)(2,1)}), bf16[32,2,16,128]{3,2,1,0:T(8,128)(2,1)S(1)}, u32[]{:S(2)}, u32[]{:S(2)}) async-start(bf16[32,2,16,128]{3,2,1,0:T(8,128)(2,1)} %shard_map.86), calls=%async_computation.1 | async-start | bytes 524288 | tf_op jit(solution)/shard_map/all_to_all | solution.py:189
  98.6 1.9 %collective-permute-start.12 = (bf16[8,4,16,1024]{3,2,1,0:T(8,128)(2,1)S(1)}, bf16[8,4,16,1024]{3,2,1,0:T(8,128)(2,1)S(1)}, u32[]{:S(2)}, u32[]{:S(2)}) collective-permute-start(bf16[8,4,16,1024]{3,2,1,0:T(8,128)(2,1)S(1)} %bitcast.4), channel_id=1, source_target_pairs={{0,32},{32,0},{1,33},{33,1},{2,34},{34,2},{3,35},{35,3},{4,36},{36... | collective-permute-start | bytes 3145736 | tf_op jit(solution)/shard_map/ppermute | solution.py:193
  100.5 9.6 %all-to-all-done.1.in_ref = bf16[32,2,16,128]{3,2,1,0:T(8,128)(2,1)S(1)} async-done(((bf16[32,2,16,128]{3,2,1,0:T(8,128)(2,1)}), bf16[32,2,16,128]{3,2,1,0:T(8,128)(2,1)S(1)}, u32[]{:S(2)}, u32[]{:S(2)}) %all-to-all-start.1) | async-done | bytes 262176 | tf_op jit(solution)/shard_map/all_to_all | solution.py:189
  110.1 1.9 %collective-permute-start = (bf16[4,16,1024]{2,1,0:T(8,128)(2,1)S(1)}, bf16[4,16,1024]{2,1,0:T(8,128)(2,1)S(1)}, u32[]{:S(2)}, u32[]{:S(2)}) collective-permute-start(bf16[4,16,1024]{2,1,0:T(8,128)(2,1)S(1)} %get-tuple-element.14.mine_ref), channel_id=1, source_target_pairs={{0,32},{32,0},{1,33},{33,1},{2,34},{34,2},{3,35},{35,3},{4,36},{36... | collective-permute-start | bytes 393224 | tf_op jit(solution)/shard_map/ppermute | solution.py:193
  112.1 1.3 collective-permute-done.other_ref
  113.4 0.6 shard_map.88.pair_ref
  113.9 3.9 %collective-permute-start.2 = (bf16[2,4,16,1024]{3,2,1,0:T(8,128)(2,1)S(1)}, bf16[2,4,16,1024]{3,2,1,0:T(8,128)(2,1)S(1)}, u32[]{:S(2)}, u32[]{:S(2)}) collective-permute-start(bf16[2,4,16,1024]{3,2,1,0:T(8,128)(2,1)S(1)} %shard_map.88.pair_ref), channel_id=1, source_target_pairs={{0,384},{32,160},{64,448},{96,224},{128,0},{160,288},{192,64},{224... | collective-permute-start | bytes 786440 | tf_op jit(solution)/shard_map/ppermute | solution.py:198
  117.8 2.0 %collective-permute-start.1 = (bf16[2,4,16,1024]{3,2,1,0:T(8,128)(2,1)S(1)}, bf16[2,4,16,1024]{3,2,1,0:T(8,128)(2,1)S(1)}, u32[]{:S(2)}, u32[]{:S(2)}) collective-permute-start(bf16[2,4,16,1024]{3,2,1,0:T(8,128)(2,1)S(1)} %shard_map.88.pair_ref), channel_id=1, source_target_pairs={{0,448},{32,96},{64,0},{96,160},{128,64},{160,224},{192,128},{224,... | collective-permute-start | bytes 786440 | tf_op jit(solution)/shard_map/ppermute | solution.py:198
  119.9 6.2 %collective-permute-done.2.in_ref.second_ref = bf16[2,4,16,1024]{3,2,1,0:T(8,128)(2,1)S(1)} collective-permute-done((bf16[2,4,16,1024]{3,2,1,0:T(8,128)(2,1)S(1)}, bf16[2,4,16,1024]{3,2,1,0:T(8,128)(2,1)S(1)}, u32[]{:S(2)}, u32[]{:S(2)}) %collective-permute-start.2) | collective-permute-done | bytes 262176 | tf_op jit(solution)/shard_map/ppermute | solution.py:198
  126.0 1.9 %collective-permute-start.3 = (bf16[2,4,16,1024]{3,2,1,0:T(8,128)(2,1)S(1)}, bf16[2,4,16,1024]{3,2,1,0:T(8,128)(2,1)S(1)}, u32[]{:S(2)}, u32[]{:S(2)}) collective-permute-start(bf16[2,4,16,1024]{3,2,1,0:T(8,128)(2,1)S(1)} %collective-permute-done.2.in_ref.second_ref), channel_id=1, source_target_pairs={{0,448},{32,96},{64,0},{96,160},{128,64},{160,224},{192,128},{224,... | collective-permute-start | bytes 786440 | tf_op jit(solution)/shard_map/ppermute | solution.py:198
  127.9 0.6 shard_map.89
  128.5 4.4 %collective-permute-start.4 = (bf16[4,16,1024]{2,1,0:T(8,128)(2,1)S(1)}, bf16[4,16,1024]{2,1,0:T(8,128)(2,1)S(1)}, u32[]{:S(2)}, u32[]{:S(2)}) collective-permute-start(bf16[4,16,1024]{2,1,0:T(8,128)(2,1)S(1)} %shard_map.89), channel_id=1, source_target_pairs={{0,384},{32,160},{64,448},{96,224},{128,0},{160,288},{192,64},{224... | collective-permute-start | bytes 393224 | tf_op jit(solution)/shard_map/ppermute | solution.py:198
  132.9 3.3 %collective-permute-done.4.last_ref = bf16[4,16,1024]{2,1,0:T(8,128)(2,1)S(1)} collective-permute-done((bf16[4,16,1024]{2,1,0:T(8,128)(2,1)S(1)}, bf16[4,16,1024]{2,1,0:T(8,128)(2,1)S(1)}, u32[]{:S(2)}, u32[]{:S(2)}) %collective-permute-start.4) | collective-permute-done | bytes 131104 | tf_op jit(solution)/shard_map/ppermute | solution.py:198
  136.3 0.1 shard_map.90.mine_ref
  136.3 4.1 %collective-permute-start.5 = (bf16[7,4,16,1024]{3,2,1,0:T(8,128)(2,1)S(1)}, bf16[7,4,16,1024]{3,2,1,0:T(8,128)(2,1)}, u32[]{:S(2)}, u32[]{:S(2)}) collective-permute-start(bf16[7,4,16,1024]{3,2,1,0:T(8,128)(2,1)S(1)} %shard_map.90.mine_ref), channel_id=1, source_target_pairs={{0,32},{32,0},{1,33},{33,1},{2,34},{34,2},{3,35},{35,3},{4,36},{36... | collective-permute-start | bytes 2752520 | tf_op jit(solution)/shard_map/ppermute | solution.py:193
  140.5 2.5 %shard_map.95 = (bf16[32,2,16,128]{3,2,1,0:T(8,128)(2,1)}, bf16[64,1024]{1,0:T(8,128)(2,1)S(1)}) custom-call(bf16[8,4,16,1024]{3,2,1,0:T(8,128)(2,1)S(1)} %bitcast.5, bf16[8,4,16,1024]{3,2,1,0:T(8,128)(2,1)S(1)} %collective-permute-done.12.other_ref, bf16[4,16,1024]{2,1,0:T(8,128)(2,1)S(1)} %get-tuple-element.20.left_ref, s32[2]{0:T(128)S(1)} %pad_add_fusion.where_ref), custom_call_target="tpu_custom_call" | custom-call | flops 536870912 | bytes 2228232 | tf_op jit(solution)/shard_map/pallas_call | solution.py:19
  143.0 4.6 %all-to-all-start.4 = ((bf16[32,2,16,128]{3,2,1,0:T(8,128)(2,1)}), bf16[32,2,16,128]{3,2,1,0:T(8,128)(2,1)S(1)}, u32[]{:S(2)}, u32[]{:S(2)}) async-start(bf16[32,2,16,128]{3,2,1,0:T(8,128)(2,1)} %get-tuple-element.22), calls=%async_computation.4 | async-start | bytes 524288 | tf_op jit(solution)/shard_map/all_to_all | solution.py:189
  147.6 0.1 select_reduce_fusion
  147.7 2.6 %shard_map.96 = bf16[4,16,1024]{2,1,0:T(8,128)(2,1)} custom-call(bf16[2,4,16,1024]{3,2,1,0:T(8,128)(2,1)S(1)} %shard_map.88.pair_ref, bf16[7,4,16,1024]{3,2,1,0:T(8,128)(2,1)S(1)} %shard_map.90.mine_ref, bf16[7,4,16,1024]{3,2,1,0:T(8,128)(2,1)} %collective-permute-done.5.other_ref, bf16[64,1024]{1,0:T(8,128)(2,1)S(1)} %get-tuple-element.21.mixed_ref, ...), custom_call_target="tpu_custom_call" | custom-call | flops 134217728 | bytes 2228232 | tf_op jit(solution)/shard_map/pallas_call | solution.py:19
  150.3 9.8 %all-to-all-done.4.in_ref = bf16[32,2,16,128]{3,2,1,0:T(8,128)(2,1)S(1)} async-done(((bf16[32,2,16,128]{3,2,1,0:T(8,128)(2,1)}), bf16[32,2,16,128]{3,2,1,0:T(8,128)(2,1)S(1)}, u32[]{:S(2)}, u32[]{:S(2)}) %all-to-all-start.4) | async-done | bytes 262176 | tf_op jit(solution)/shard_map/all_to_all | solution.py:189
  160.0 3.6 %all-to-all-start.3 = ((bf16[4,16,1024]{2,1,0:T(8,128)(2,1)}), bf16[4,16,1024]{2,1,0:T(8,128)(2,1)S(1)}, u32[]{:S(2)}, u32[]{:S(2)}) async-start(bf16[4,16,1024]{2,1,0:T(8,128)(2,1)} %shard_map.96), calls=%async_computation.3 | async-start | bytes 262144 | tf_op jit(solution)/shard_map/all_to_all | solution.py:189
  163.6 1.5 shard_map.98
  165.2 3.6 %all-to-all-done.3.in_ref = bf16[4,16,1024]{2,1,0:T(8,128)(2,1)S(1)} async-done(((bf16[4,16,1024]{2,1,0:T(8,128)(2,1)}), bf16[4,16,1024]{2,1,0:T(8,128)(2,1)S(1)}, u32[]{:S(2)}, u32[]{:S(2)}) %all-to-all-start.3) | async-done | bytes 131104 | tf_op jit(solution)/shard_map/all_to_all | solution.py:189
  168.8 5.5 %all-to-all-start.5 = ((bf16[32,2,2,16,128]{4,3,2,1,0:T(8,128)(2,1)}), bf16[32,2,2,16,128]{4,3,2,1,0:T(8,128)(2,1)S(1)}, u32[]{:S(2)}, u32[]{:S(2)}) async-start(bf16[32,2,2,16,128]{4,3,2,1,0:T(8,128)(2,1)} %shard_map.98), calls=%async_computation.5 | async-start | bytes 1048576 | tf_op jit(solution)/shard_map/all_to_all | solution.py:189
  174.3 0.7 shard_map.97
  175.0 14.5 %all-to-all-done.5.in_ref = bf16[32,2,2,16,128]{4,3,2,1,0:T(8,128)(2,1)S(1)} async-done(((bf16[32,2,2,16,128]{4,3,2,1,0:T(8,128)(2,1)}), bf16[32,2,2,16,128]{4,3,2,1,0:T(8,128)(2,1)S(1)}, u32[]{:S(2)}, u32[]{:S(2)}) %all-to-all-start.5) | async-done | bytes 524320 | tf_op jit(solution)/shard_map/all_to_all | solution.py:189
  189.5 1.1 shard_map.99
  (21 shorter events, 0.1 us)
Async XLA Ops:
  0.6 15.1 %copy-start = (bf16[1,256,4096]{2,1,0:T(8,128)(2,1)S(1)}, bf16[1,256,4096]{2,1,0:T(8,128)(2,1)}, u32[]{:S(2)}) copy-start(bf16[1,256,4096]{2,1,0:T(8,128)(2,1)} %grads_ref.1) | copy-start | bytes 6291460
  0.6 15.1 %collective-permute-start.6 = (bf16[1,256,4096]{2,1,0:T(8,128)(2,1)}, bf16[1,256,4096]{2,1,0:T(8,128)(2,1)}, u32[]{:S(2)}, u32[]{:S(2)}) collective-permute-start(bf16[1,256,4096]{2,1,0:T(8,128)(2,1)} %grads_ref.1), channel_id=1, source_target_pairs={{0,32},{32,0},{1,33},{33,1},{2,34},{34,2},{3,35},{35,3},{4,36},{36... | collective-permute-start | bytes 6291464 | tf_op jit(solution)/shard_map/ppermute | solution.py:193
  2.7 1.0 copy-start.3
  3.7 0.9 copy-start.4
  5.5 48.8 %all-to-all-start = ((bf16[32,2,2,16,128]{4,3,2,1,0:T(8,128)(2,1)}), bf16[32,2,2,16,128]{4,3,2,1,0:T(8,128)(2,1)S(1)}, u32[]{:S(2)}, u32[]{:S(2)}) async-start(bf16[32,2,2,16,128]{4,3,2,1,0:T(8,128)(2,1)} %shard_map.85), calls=%async_computation | async-start | bytes 1048576 | tf_op jit(solution)/shard_map/all_to_all | solution.py:189
  17.6 19.7 %collective-permute-start.8 = (bf16[2,16,4096]{2,1,0:T(8,128)(2,1)S(1)}, bf16[2,16,4096]{2,1,0:T(8,128)(2,1)S(1)}, u32[]{:S(2)}, u32[]{:S(2)}) collective-permute-start(bf16[2,16,4096]{2,1,0:T(8,128)(2,1)S(1)} %get-tuple-element.18), channel_id=1, source_target_pairs={{0,64},{32,480},{64,128},{96,32},{128,192},{160,96},{192,256},{224... | collective-permute-start | bytes 786440 | tf_op jit(solution)/shard_map/ppermute | solution.py:198
  21.9 15.4 %collective-permute-start.9 = (bf16[16,4096]{1,0:T(8,128)(2,1)S(1)}, bf16[16,4096]{1,0:T(8,128)(2,1)S(1)}, u32[]{:S(2)}, u32[]{:S(2)}) collective-permute-start(bf16[16,4096]{1,0:T(8,128)(2,1)S(1)} %get-tuple-element.19), channel_id=1, source_target_pairs={{0,128},{32,416},{64,192},{96,480},{128,256},{160,32},{192,320},{2... | collective-permute-start | bytes 393224 | tf_op jit(solution)/shard_map/ppermute | solution.py:198
  28.0 11.9 %collective-permute-start.7 = (bf16[2,16,4096]{2,1,0:T(8,128)(2,1)S(1)}, bf16[2,16,4096]{2,1,0:T(8,128)(2,1)S(1)}, u32[]{:S(2)}, u32[]{:S(2)}) collective-permute-start(bf16[2,16,4096]{2,1,0:T(8,128)(2,1)S(1)} %get-tuple-element.16), channel_id=1, source_target_pairs={{0,64},{32,480},{64,128},{96,32},{128,192},{160,96},{192,256},{224... | collective-permute-start | bytes 786440 | tf_op jit(solution)/shard_map/ppermute | solution.py:198
  37.9 10.9 %collective-permute-start.10 = (bf16[2,16,4096]{2,1,0:T(8,128)(2,1)S(1)}, bf16[2,16,4096]{2,1,0:T(8,128)(2,1)S(1)}, u32[]{:S(2)}, u32[]{:S(2)}) collective-permute-start(bf16[2,16,4096]{2,1,0:T(8,128)(2,1)S(1)} %shard_map.92), channel_id=1, source_target_pairs={{0,128},{32,416},{64,192},{96,480},{128,256},{160,32},{192,320},{2... | collective-permute-start | bytes 786440 | tf_op jit(solution)/shard_map/ppermute | solution.py:198
  49.4 13.7 %copy-start.5 = (s32[32]{0:T(128)S(1)}, s32[32]{0:T(128)}, u32[]{:S(2)}) copy-start(s32[32]{0:T(128)} %table_ref.1) | copy-start | bytes 388
  49.4 3.2 %collective-permute-start.11 = (bf16[16,4096]{1,0:T(8,128)(2,1)S(1)}, bf16[16,4096]{1,0:T(8,128)(2,1)S(1)}, u32[]{:S(2)}, u32[]{:S(2)}) collective-permute-start(bf16[16,4096]{1,0:T(8,128)(2,1)S(1)} %shard_map.93), channel_id=1, source_target_pairs={{0,32},{32,0},{1,33},{33,1},{2,34},{34,2},{3,35},{35,3},{4,36},{36... | collective-permute-start | bytes 393224 | tf_op jit(solution)/shard_map/ppermute | solution.py:193
  54.3 36.8 %all-to-all-start.2 = ((bf16[32,16,1024]{2,1,0:T(8,128)(2,1)}), bf16[32,16,1024]{2,1,0:T(8,128)(2,1)S(1)}, u32[]{:S(2)}, u32[]{:S(2)}) async-start(bf16[32,16,1024]{2,1,0:T(8,128)(2,1)} %shard_map.94), calls=%async_computation.2 | async-start | bytes 2097152 | tf_op jit(solution)/shard_map/all_to_all | solution.py:189
  91.0 19.1 %all-to-all-start.1 = ((bf16[32,2,16,128]{3,2,1,0:T(8,128)(2,1)}), bf16[32,2,16,128]{3,2,1,0:T(8,128)(2,1)S(1)}, u32[]{:S(2)}, u32[]{:S(2)}) async-start(bf16[32,2,16,128]{3,2,1,0:T(8,128)(2,1)} %shard_map.86), calls=%async_computation.1 | async-start | bytes 524288 | tf_op jit(solution)/shard_map/all_to_all | solution.py:189
  98.6 41.9 %collective-permute-start.12 = (bf16[8,4,16,1024]{3,2,1,0:T(8,128)(2,1)S(1)}, bf16[8,4,16,1024]{3,2,1,0:T(8,128)(2,1)S(1)}, u32[]{:S(2)}, u32[]{:S(2)}) collective-permute-start(bf16[8,4,16,1024]{3,2,1,0:T(8,128)(2,1)S(1)} %bitcast.4), channel_id=1, source_target_pairs={{0,32},{32,0},{1,33},{33,1},{2,34},{34,2},{3,35},{35,3},{4,36},{36... | collective-permute-start | bytes 3145736 | tf_op jit(solution)/shard_map/ppermute | solution.py:193
  110.1 3.2 %collective-permute-start = (bf16[4,16,1024]{2,1,0:T(8,128)(2,1)S(1)}, bf16[4,16,1024]{2,1,0:T(8,128)(2,1)S(1)}, u32[]{:S(2)}, u32[]{:S(2)}) collective-permute-start(bf16[4,16,1024]{2,1,0:T(8,128)(2,1)S(1)} %get-tuple-element.14.mine_ref), channel_id=1, source_target_pairs={{0,32},{32,0},{1,33},{33,1},{2,34},{34,2},{3,35},{35,3},{4,36},{36... | collective-permute-start | bytes 393224 | tf_op jit(solution)/shard_map/ppermute | solution.py:193
  113.9 12.1 %collective-permute-start.2 = (bf16[2,4,16,1024]{3,2,1,0:T(8,128)(2,1)S(1)}, bf16[2,4,16,1024]{3,2,1,0:T(8,128)(2,1)S(1)}, u32[]{:S(2)}, u32[]{:S(2)}) collective-permute-start(bf16[2,4,16,1024]{3,2,1,0:T(8,128)(2,1)S(1)} %shard_map.88.pair_ref), channel_id=1, source_target_pairs={{0,384},{32,160},{64,448},{96,224},{128,0},{160,288},{192,64},{224... | collective-permute-start | bytes 786440 | tf_op jit(solution)/shard_map/ppermute | solution.py:198
  117.8 15.1 %collective-permute-start.1 = (bf16[2,4,16,1024]{3,2,1,0:T(8,128)(2,1)S(1)}, bf16[2,4,16,1024]{3,2,1,0:T(8,128)(2,1)S(1)}, u32[]{:S(2)}, u32[]{:S(2)}) collective-permute-start(bf16[2,4,16,1024]{3,2,1,0:T(8,128)(2,1)S(1)} %shard_map.88.pair_ref), channel_id=1, source_target_pairs={{0,448},{32,96},{64,0},{96,160},{128,64},{160,224},{192,128},{224,... | collective-permute-start | bytes 786440 | tf_op jit(solution)/shard_map/ppermute | solution.py:198
  126.0 10.2 %collective-permute-start.3 = (bf16[2,4,16,1024]{3,2,1,0:T(8,128)(2,1)S(1)}, bf16[2,4,16,1024]{3,2,1,0:T(8,128)(2,1)S(1)}, u32[]{:S(2)}, u32[]{:S(2)}) collective-permute-start(bf16[2,4,16,1024]{3,2,1,0:T(8,128)(2,1)S(1)} %collective-permute-done.2.in_ref.second_ref), channel_id=1, source_target_pairs={{0,448},{32,96},{64,0},{96,160},{128,64},{160,224},{192,128},{224,... | collective-permute-start | bytes 786440 | tf_op jit(solution)/shard_map/ppermute | solution.py:198
  128.5 7.8 %collective-permute-start.4 = (bf16[4,16,1024]{2,1,0:T(8,128)(2,1)S(1)}, bf16[4,16,1024]{2,1,0:T(8,128)(2,1)S(1)}, u32[]{:S(2)}, u32[]{:S(2)}) collective-permute-start(bf16[4,16,1024]{2,1,0:T(8,128)(2,1)S(1)} %shard_map.89), channel_id=1, source_target_pairs={{0,384},{32,160},{64,448},{96,224},{128,0},{160,288},{192,64},{224... | collective-permute-start | bytes 393224 | tf_op jit(solution)/shard_map/ppermute | solution.py:198
  136.3 11.3 %collective-permute-start.5 = (bf16[7,4,16,1024]{3,2,1,0:T(8,128)(2,1)S(1)}, bf16[7,4,16,1024]{3,2,1,0:T(8,128)(2,1)}, u32[]{:S(2)}, u32[]{:S(2)}) collective-permute-start(bf16[7,4,16,1024]{3,2,1,0:T(8,128)(2,1)S(1)} %shard_map.90.mine_ref), channel_id=1, source_target_pairs={{0,32},{32,0},{1,33},{33,1},{2,34},{34,2},{3,35},{35,3},{4,36},{36... | collective-permute-start | bytes 2752520 | tf_op jit(solution)/shard_map/ppermute | solution.py:193
  143.0 17.0 %all-to-all-start.4 = ((bf16[32,2,16,128]{3,2,1,0:T(8,128)(2,1)}), bf16[32,2,16,128]{3,2,1,0:T(8,128)(2,1)S(1)}, u32[]{:S(2)}, u32[]{:S(2)}) async-start(bf16[32,2,16,128]{3,2,1,0:T(8,128)(2,1)} %get-tuple-element.22), calls=%async_computation.4 | async-start | bytes 524288 | tf_op jit(solution)/shard_map/all_to_all | solution.py:189
  147.7 41.8 %copy-start.1 = (f32[2,4,1,16,1024]{4,3,2,1,0:T(8,128)S(1)}, f32[2,4,1,16,1024]{4,3,2,1,0:T(8,128)}, u32[]{:S(2)}) copy-start(f32[2,4,1,16,1024]{4,3,2,1,0:T(8,128)} %left_ref.3) | copy-start | bytes 1572868
  147.7 41.8 %copy-start.2 = (f32[2,4,1,16,1024]{4,3,2,1,0:T(8,128)S(1)}, f32[2,4,1,16,1024]{4,3,2,1,0:T(8,128)}, u32[]{:S(2)}) copy-start(f32[2,4,1,16,1024]{4,3,2,1,0:T(8,128)} %right_ref.3) | copy-start | bytes 1572868
  160.0 8.8 %all-to-all-start.3 = ((bf16[4,16,1024]{2,1,0:T(8,128)(2,1)}), bf16[4,16,1024]{2,1,0:T(8,128)(2,1)S(1)}, u32[]{:S(2)}, u32[]{:S(2)}) async-start(bf16[4,16,1024]{2,1,0:T(8,128)(2,1)} %shard_map.96), calls=%async_computation.3 | async-start | bytes 262144 | tf_op jit(solution)/shard_map/all_to_all | solution.py:189
  168.8 20.7 %all-to-all-start.5 = ((bf16[32,2,2,16,128]{4,3,2,1,0:T(8,128)(2,1)}), bf16[32,2,2,16,128]{4,3,2,1,0:T(8,128)(2,1)S(1)}, u32[]{:S(2)}, u32[]{:S(2)}) async-start(bf16[32,2,2,16,128]{4,3,2,1,0:T(8,128)(2,1)} %shard_map.98), calls=%async_computation.5 | async-start | bytes 1048576 | tf_op jit(solution)/shard_map/all_to_all | solution.py:189

commit v6 on v3

--- a/solution.py
+++ b/solution.py
@@ -1,3 +1,5 @@
+import functools
+
 import jax
 import jax.numpy as jnp
 from jax import lax
@@ -10,7 +12,6 @@
 F32 = jnp.float32
 BANDS = ("x", "yh", "yl")
 ROWS = ("z", "c")
-DISTANCES = (4, 3, 5, 2, 6, 1, 7)
 VM = pl.BlockSpec(memory_space=pltpu.VMEM)
 SM = pl.BlockSpec(memory_space=pltpu.SMEM)
 
@@ -32,13 +33,20 @@
     return jax.ShapeDtypeStruct(dims, dtype)
 
 
-def spread_roots(left_ref, right_ref, out_ref):
-    for slot in range(2):
-        for sub in range(4):
-            for part in range(8):
-                columns = slice(part * 128, part * 128 + 128)
-                out_ref[sub * 8 + part, slot, 0] = left_ref[slot, sub, 0, :, columns]
-                out_ref[sub * 8 + part, slot, 1] = right_ref[slot, sub, 0, :, columns]
+def spread_roots(left_hbm, right_hbm, out_ref, left_ref, right_ref, sems):
+    copies = (
+        pltpu.make_async_copy(left_hbm, left_ref, sems.at[0]),
+        pltpu.make_async_copy(right_hbm, right_ref, sems.at[1]),
+    )
+    for copy in copies:
+        copy.start()
+    for root, (copy, ref) in enumerate(zip(copies, (left_ref, right_ref))):
+        copy.wait()
+        for slot in range(2):
+            for sub in range(4):
+                for part in range(8):
+                    columns = slice(part * 128, part * 128 + 128)
+                    out_ref[sub * 8 + part, slot, root] = ref[slot, sub, 0, :, columns]
 
 
 def pick_roots(in_ref, table_ref, out_ref):
@@ -54,23 +62,64 @@
             right_ref[sub, :, columns] = in_ref[sub * 8 + part, 1]
 
 
-def add_pair(grads_ref, theirs_ref, where_ref, *out_refs):
-    for k in range(8):
-        strip = lax.rem(where_ref[0] + k, 8) * 2 + where_ref[1]
+def add_pairs(wanted, grads_ref, theirs_hbm, where_ref, *refs):
+    z, core = where_ref[0], where_ref[1]
+    outs, theirs_ref, sems = refs[:-2], refs[-2], refs[-1]
+    copies = []
+    for index, (_, _, k, parity) in enumerate(wanted):
+        strip = lax.rem(z + 8 + k * (1 - 2 * core), 8) * 2 + (core if parity is None else parity)
         rows = pl.ds(pl.multiple_of(strip * 16, 16), 16)
-        out_refs[k][...] = (
-            grads_ref[0, rows, :].astype(F32) + theirs_ref[0, rows, :].astype(F32)
-        ).astype(BF)
-
-
-def add_replicas(*refs):
-    out_ref = refs[-1]
+        copy = pltpu.make_async_copy(theirs_hbm.at[0, rows, :], theirs_ref.at[index], sems.at[index])
+        copy.start()
+        copies.append((copy, rows))
+    for index, (out, place_in, _, _) in enumerate(wanted):
+        copy, rows = copies[index]
+        copy.wait()
+        total = grads_ref[0, rows, :].astype(F32) + theirs_ref[index].astype(F32)
+        if place_in is None:
+            outs[out][...] = total.astype(BF)
+        else:
+            outs[out][place_in] = total.astype(BF)
+
+
+def pair_sums(wanted, outs, grads, theirs, where):
+    return pl.pallas_call(
+        functools.partial(add_pairs, wanted),
+        out_shape=outs,
+        in_specs=[VM, pl.BlockSpec(memory_space=pltpu.HBM), SM],
+        out_specs=(VM,) * len(outs),
+        scratch_shapes=[
+            pltpu.VMEM((len(wanted), 16, 4096), BF),
+            pltpu.SemaphoreType.DMA((len(wanted),)),
+        ],
+        compiler_params=pltpu.CompilerParams(vmem_limit_bytes=32 * 1024 * 1024),
+        cost_estimate=pl.CostEstimate(flops=1000000, bytes_accessed=2097152, transcendentals=0),
+    )(grads, theirs, where)
+
+
+def add_passed(two_ref, near_ref, four_ref, where_ref, out_ref):
+    core = where_ref[1]
+    for parity in range(2):
+        out_ref[parity] = (two_ref[parity].astype(F32) + near_ref[parity].astype(F32)).astype(BF)
+    out_ref[core] = (
+        two_ref[core].astype(F32) + near_ref[core].astype(F32) + four_ref[...].astype(F32)
+    ).astype(BF)
+
+
+def add_other(near_ref, two_ref, where_ref, out_ref):
+    parity = 1 - where_ref[1]
+    out_ref[...] = (near_ref[2 + parity].astype(F32) + two_ref[parity].astype(F32)).astype(BF)
+
+
+def add_replicas(own_ref, near_ref, two_ref, theirs_ref, where_ref, out_ref):
     for column in range(4):
         columns = slice(column * 1024, column * 1024 + 1024)
-        total = refs[0][:, columns].astype(F32)
-        for term in refs[1:-1]:
-            total = total + term[:, columns].astype(F32)
-        total = total.astype(BF)
+        total = (
+            own_ref[:, columns].astype(F32)
+            + near_ref[2 + where_ref[1], :, columns].astype(F32)
+            + two_ref[where_ref[1], :, columns].astype(F32)
+            + theirs_ref[:, columns].astype(F32)
+        ).astype(BF)
         for z in range(8):
             out_ref[z * 4 + column] = total
 
@@ -182,8 +231,8 @@
     return lax.ppermute(value, axis, [(i, (i + distance) % size) for i in range(size)])
 
 
-def around(value):
-    pairs = [(2 * z + c, 2 * ((z - 1 + 2 * c) % 8) + c) for z in range(8) for c in range(2)]
+def around(value, way):
+    pairs = [(2 * z + c, 2 * ((z + way - 2 * way * c) % 8) + c) for z in range(8) for c in range(2)]
     return lax.ppermute(value, ROWS, pairs)
 
 
@@ -195,11 +244,43 @@
     holder = jnp.sum(jnp.where(table[None, :] == slots[:, None], blocks[None, :] + 1, 0), axis=1) - 1
 
     theirs = swap(grads)
-    pairs = call(add_pair, (shape((16, 4096)),) * 8, [grads, theirs, where], scalars=1)
-    terms = [pairs[0]] + [shift(pairs[k], "z", k) for k in DISTANCES]
-    strip = call(add_replicas, shape((32, 16, 1024)), terms)
-
-    pieces = call(spread_roots, shape((32, 2, 2, 16, 128)), [left_root, right_root])
+    strip_shape, both = shape((16, 4096)), shape((2, 16, 4096))
+    four, near = pair_sums(
+        ((0, None, 4, None), (1, 0, 3, 0), (1, 1, 3, 1), (1, 2, 1, 0), (1, 3, 1, 1)),
+        (strip_shape, shape((4, 16, 4096))),
+        grads,
+        theirs,
+        where,
+    )
+    four = around(four, 2)
+    near = around(near, 1)
+    two, own = pair_sums(
+        ((0, 0, 2, 0), (0, 1, 2, 1), (1, None, 0, None)),
+        (both, strip_shape),
+        grads,
+        theirs,
+        where,
+    )
+    two = call(add_passed, both, [two, near, four, where], scalars=1)
+    two = around(two, 2)
+    other = call(add_other, strip_shape, [near, two, where], scalars=1)
+    other = swap(other)
+    strip = call(
+        add_replicas, shape((32, 16, 1024)), [own, near, two, other, where], scalars=1
+    )
+
+    pieces = pl.pallas_call(
+        spread_roots,
+        out_shape=shape((32, 2, 2, 16, 128)),
+        in_specs=[pl.BlockSpec(memory_space=pltpu.HBM)] * 2,
+        out_specs=VM,
+        scratch_shapes=[
+            pltpu.VMEM(left_root.shape, BF),
+            pltpu.VMEM(left_root.shape, BF),
+            pltpu.SemaphoreType.DMA((2,)),
+        ],
+        cost_estimate=pl.CostEstimate(flops=1000000, bytes_accessed=524288, transcendentals=0),
+    )(left_root, right_root)
     pieces = exchange(pieces, BANDS).reshape(64, 2, 16, 128)
     picked = call(pick_roots, shape((32, 2, 16, 128)), [pieces, table], scalars=1)
     picked = exchange(picked, BANDS)
@@ -229,12 +310,12 @@
     pair = call(
         pair_up, shape((2, 4, 16, 1024)), [right_rows, theirs, where], scalars=1
     )
-    rings = [around(pair)]
-    rings.append(around(rings[0]))
-    rings.append(around(rings[1]))
-    half = call(take_parity, shape((4, 16, 1024)), [rings[2], where], scalars=1)
-    rings.append(around(half))
-    right_mine = call(stack_rows, shape((7, 4, 16, 1024)), rings)
+    second = around(pair, -2)
+    first = around(pair, -1)
+    half = call(take_parity, shape((4, 16, 1024)), [second, where], scalars=1)
+    third = around(second, -1)
+    last = around(half, -2)
+    right_mine = call(stack_rows, shape((7, 4, 16, 1024)), [first, second, third, last])
     right_other = swap(right_mine)
     result = call(
         right_product,

time: 187 us -> 189 us (1.011)
  starting transfers between devices: 110 us -> 76.1 us
  waiting for transfers between devices: 58.7 us -> 76.5 us
  blocking collectives: 0 us -> 16.2 us
  Pallas kernels: 13.8 us -> 16.9 us
    ppermute x10 -> x3, starting transfers between devices: 44.9 us -> 10.1 us  [shift(): lax.ppermute(value, axis, [(i, (i + distance) % size) for i in range(size)])]
    all_to_all x0 -> x1, blocking collectives: none -> 16.2 us  [exchange(): return lax.all_to_all(value, axes, split_axis=0, concat_axis=0, tiled=True)]
    ppermute x4 -> x7, waiting for transfers between devices: 11 us -> 25.5 us  [around(): return lax.ppermute(value, ROWS, pairs)]
    all_to_all x5 -> x4, starting transfers between devices: 44 us -> 30.3 us  [exchange(): return lax.all_to_all(value, axes, split_axis=0, concat_axis=0, tiled=True)]
    ppermute x4 -> x7, starting transfers between devices: 13.3 us -> 26 us  [around(): return lax.ppermute(value, ROWS, pairs)]
    ppermute x10 -> x3, waiting for transfers between devices: 11.3 us -> 4.57 us  [shift(): lax.ppermute(value, axis, [(i, (i + distance) % size) for i in range(size)])]
    all_to_all x5 -> x4, waiting for transfers between devices: 32.7 us -> 38.4 us  [exchange(): return lax.all_to_all(value, axes, split_axis=0, concat_axis=0, tiled=True)]
    pallas_call x0 -> x3, Pallas kernels: none -> 4.76 us  [the longest x2 2.87 us: pair_sums(): pl.pallas_call(functools.partial(add_pairs, wanted), out_shape=outs, in_s...]
  transfers between devices with their start and end apart: 23 -> 19, of which waited for: 11 -> 10; matrix products, arithmetic and copies ran while one was open for 0% -> 0% of each run, Pallas kernels for 7% -> 6%
where the time goes in v6:
time: 189 us; the launch traced here: 188 us
  waiting for transfers between devices  76.5 us (40%)
  starting transfers between devices  76.1 us (40%)
  Pallas kernels  16.9 us (9%)
  blocking collectives  16.2 us (9%)
    all_to_all x4, waiting for transfers between devices, exchange(): return lax.all_to_all(value, axes, split_axis=0, concat_axis=0, tiled=True)  38.4 us
    all_to_all x4, starting transfers between devices, exchange(): return lax.all_to_all(value, axes, split_axis=0, concat_axis=0, tiled=True)  30.3 us
    ppermute x7, starting transfers between devices, around(): return lax.ppermute(value, ROWS, pairs)  26 us
    ppermute x7, waiting for transfers between devices, around(): return lax.ppermute(value, ROWS, pairs)  25.5 us
    all_to_all x1, blocking collectives, exchange(): return lax.all_to_all(value, axes, split_axis=0, concat_axis=0, tiled=True)  16.2 us
    pallas_call x13, Pallas kernels, call(): pl.pallas_call(kernel, out_shape=out, in_specs=[VM] * (len(inputs) - scal...  12.1 us
    ppermute x3, starting transfers between devices, shift(): lax.ppermute(value, axis, [(i, (i + distance) % size) for i in range(size)])  10.1 us
    ppermute x5, starting transfers between devices, swap(): return lax.ppermute(value, 'c', [(0, 1), (1, 0)])  9.74 us
  transfers between devices with their start and end apart: 19, of which 10 were waited for; matrix products, arithmetic and copies ran while one was open for 0% of the time, Pallas kernels for 6%

profile of v6, /device:TPU:56, one launch (start us, length us, event | category | flops | bytes accessed | tf_op | source)
XLA Modules:
  0.0 188.4 jit_solution(14246637852138172796)
XLA Ops:
  0.6 1.9 %collective-permute-start.6 = (bf16[1,256,4096]{2,1,0:T(8,128)(2,1)}, bf16[1,256,4096]{2,1,0:T(8,128)(2,1)S(1)}, u32[]{:S(2)}, u32[]{:S(2)}) collective-permute-start(bf16[1,256,4096]{2,1,0:T(8,128)(2,1)} %grads_ref.3), channel_id=1, source_target_pairs={{0,32},{32,0},{1,33},{33,1},{2,34},{34,2},{3,35},{35,3},{4,36},{36... | collective-permute-start | bytes 6291464 | tf_op jit(solution)/shard_map/ppermute | solution.py:226
  2.6 0.1 pad_add_fusion.where_ref.refs_4_
  2.6 4.3 %collective-permute-done.6.theirs_hbm = bf16[1,256,4096]{2,1,0:T(8,128)(2,1)S(1)} collective-permute-done((bf16[1,256,4096]{2,1,0:T(8,128)(2,1)}, bf16[1,256,4096]{2,1,0:T(8,128)(2,1)S(1)}, u32[]{:S(2)}, u32[]{:S(2)}) %collective-permute-start.6) | collective-permute-done | bytes 2097184 | tf_op jit(solution)/shard_map/ppermute | solution.py:226
  6.9 1.6 copy-done
  8.5 1.7 shard_map.92
  10.2 4.3 %collective-permute-start.7 = (bf16[4,16,4096]{2,1,0:T(8,128)(2,1)S(1)}, bf16[4,16,4096]{2,1,0:T(8,128)(2,1)S(1)}, u32[]{:S(2)}, u32[]{:S(2)}) collective-permute-start(bf16[4,16,4096]{2,1,0:T(8,128)(2,1)S(1)} %get-tuple-element.19), channel_id=1, source_target_pairs={{0,64},{32,480},{64,128},{96,32},{128,192},{160,96},{192,256},{224... | collective-permute-start | bytes 1572872 | tf_op jit(solution)/shard_map/ppermute | solution.py:236
  14.4 6.1 %collective-permute-start.8 = (bf16[16,4096]{1,0:T(8,128)(2,1)S(1)}, bf16[16,4096]{1,0:T(8,128)(2,1)S(1)}, u32[]{:S(2)}, u32[]{:S(2)}) collective-permute-start(bf16[16,4096]{1,0:T(8,128)(2,1)S(1)} %get-tuple-element.21), channel_id=1, source_target_pairs={{0,128},{32,416},{64,192},{96,480},{128,256},{160,32},{192,320},{2... | collective-permute-start | bytes 393224 | tf_op jit(solution)/shard_map/ppermute | solution.py:236
  20.5 1.2 shard_map.91
  21.8 9.5 %collective-permute-done.8.four_ref = bf16[16,4096]{1,0:T(8,128)(2,1)S(1)} collective-permute-done((bf16[16,4096]{1,0:T(8,128)(2,1)S(1)}, bf16[16,4096]{1,0:T(8,128)(2,1)S(1)}, u32[]{:S(2)}, u32[]{:S(2)}) %collective-permute-start.8) | collective-permute-done | bytes 131104 | tf_op jit(solution)/shard_map/ppermute | solution.py:236
  31.2 0.7 shard_map.93
  31.9 1.9 %collective-permute-start.9 = (bf16[2,16,4096]{2,1,0:T(8,128)(2,1)S(1)}, bf16[2,16,4096]{2,1,0:T(8,128)(2,1)S(1)}, u32[]{:S(2)}, u32[]{:S(2)}) collective-permute-start(bf16[2,16,4096]{2,1,0:T(8,128)(2,1)S(1)} %shard_map.93), channel_id=1, source_target_pairs={{0,128},{32,416},{64,192},{96,480},{128,256},{160,32},{192,320},{2... | collective-permute-start | bytes 786440 | tf_op jit(solution)/shard_map/ppermute | solution.py:236
  33.8 11.3 %collective-permute-done.9.two_ref = bf16[2,16,4096]{2,1,0:T(8,128)(2,1)S(1)} collective-permute-done((bf16[2,16,4096]{2,1,0:T(8,128)(2,1)S(1)}, bf16[2,16,4096]{2,1,0:T(8,128)(2,1)S(1)}, u32[]{:S(2)}, u32[]{:S(2)}) %collective-permute-start.9) | collective-permute-done | bytes 262176 | tf_op jit(solution)/shard_map/ppermute | solution.py:236
  45.1 0.6 shard_map.94
  45.6 1.9 %collective-permute-start.10 = (bf16[16,4096]{1,0:T(8,128)(2,1)S(1)}, bf16[16,4096]{1,0:T(8,128)(2,1)S(1)}, u32[]{:S(2)}, u32[]{:S(2)}) collective-permute-start(bf16[16,4096]{1,0:T(8,128)(2,1)S(1)} %shard_map.94), channel_id=1, source_target_pairs={{0,32},{32,0},{1,33},{33,1},{2,34},{34,2},{3,35},{35,3},{4,36},{36... | collective-permute-start | bytes 393224 | tf_op jit(solution)/shard_map/ppermute | solution.py:226
  47.6 1.3 collective-permute-done.10.theirs_ref
  48.9 1.6 shard_map.95
  50.5 6.7 %all-to-all-start.2 = ((bf16[32,16,1024]{2,1,0:T(8,128)(2,1)}), bf16[32,16,1024]{2,1,0:T(8,128)(2,1)S(1)}, u32[]{:S(2)}, u32[]{:S(2)}) async-start(bf16[32,16,1024]{2,1,0:T(8,128)(2,1)} %shard_map.95), calls=%async_computation.2 | async-start | bytes 2097152 | tf_op jit(solution)/shard_map/all_to_all | solution.py:222
  57.2 1.9 %shard_map.85 = bf16[32,2,2,16,128]{4,3,2,1,0:T(8,128)(2,1)} custom-call(bf16[2,4,1,16,1024]{4,3,2,1,0:T(8,128)(2,1)} %left_hbm.1, bf16[2,4,1,16,1024]{4,3,2,1,0:T(8,128)(2,1)} %right_hbm.1), custom_call_target="tpu_custom_call" | custom-call | flops 1000000 | bytes 524288 | tf_op jit(solution)/shard_map/pallas_call | solution.py:272
  59.1 26.8 %all-to-all-done.2 = bf16[32,16,1024]{2,1,0:T(8,128)(2,1)S(1)} async-done(((bf16[32,16,1024]{2,1,0:T(8,128)(2,1)}), bf16[32,16,1024]{2,1,0:T(8,128)(2,1)S(1)}, u32[]{:S(2)}, u32[]{:S(2)}) %all-to-all-start.2) | async-done | bytes 1048608 | tf_op jit(solution)/shard_map/all_to_all | solution.py:222
  85.9 7.1 %all-to-all-start = ((bf16[32,2,2,16,128]{4,3,2,1,0:T(8,128)(2,1)}), bf16[32,2,2,16,128]{4,3,2,1,0:T(8,128)(2,1)S(1)}, u32[]{:S(2)}, u32[]{:S(2)}) async-start(bf16[32,2,2,16,128]{4,3,2,1,0:T(8,128)(2,1)} %shard_map.85), calls=%async_computation | async-start | bytes 1048576 | tf_op jit(solution)/shard_map/all_to_all | solution.py:222
  93.1 1.9 %collective-permute-start.11 = (bf16[8,4,16,1024]{3,2,1,0:T(8,128)(2,1)S(1)}, bf16[8,4,16,1024]{3,2,1,0:T(8,128)(2,1)S(1)}, u32[]{:S(2)}, u32[]{:S(2)}) collective-permute-start(bf16[8,4,16,1024]{3,2,1,0:T(8,128)(2,1)S(1)} %bitcast.5), channel_id=1, source_target_pairs={{0,32},{32,0},{1,33},{33,1},{2,34},{34,2},{3,35},{35,3},{4,36},{36... | collective-permute-start | bytes 3145736 | tf_op jit(solution)/shard_map/ppermute | solution.py:226
  95.0 11.6 %all-to-all-done = bf16[32,2,2,16,128]{4,3,2,1,0:T(8,128)(2,1)S(1)} async-done(((bf16[32,2,2,16,128]{4,3,2,1,0:T(8,128)(2,1)}), bf16[32,2,2,16,128]{4,3,2,1,0:T(8,128)(2,1)S(1)}, u32[]{:S(2)}, u32[]{:S(2)}) %all-to-all-start) | async-done | bytes 524320 | tf_op jit(solution)/shard_map/all_to_all | solution.py:222
  106.6 0.6 shard_map.86
  107.2 16.2 %all_to_all.25.in_ref = bf16[32,2,16,128]{3,2,1,0:T(8,128)(2,1)S(1)} all-to-all(bf16[32,2,16,128]{3,2,1,0:T(8,128)(2,1)S(1)} %shard_map.86), channel_id=1, replica_groups=mesh['z'=8,'c'=2,'x'=4,'yh'=2,'yl'=4] {'x','yh','yl'}, dimensions={0} | all-to-all | bytes 524288 | tf_op jit(solution)/shard_map/all_to_all | solution.py:222
  123.4 1.9 %collective-permute-start = (bf16[4,16,1024]{2,1,0:T(8,128)(2,1)S(1)}, bf16[4,16,1024]{2,1,0:T(8,128)(2,1)S(1)}, u32[]{:S(2)}, u32[]{:S(2)}) collective-permute-start(bf16[4,16,1024]{2,1,0:T(8,128)(2,1)S(1)} %get-tuple-element.17.mine_ref), channel_id=1, source_target_pairs={{0,32},{32,0},{1,33},{33,1},{2,34},{34,2},{3,35},{35,3},{4,36},{36... | collective-permute-start | bytes 393224 | tf_op jit(solution)/shard_map/ppermute | solution.py:226
  125.3 2.5 %shard_map.96 = (bf16[32,2,16,128]{3,2,1,0:T(8,128)(2,1)}, bf16[64,1024]{1,0:T(8,128)(2,1)S(1)}) custom-call(bf16[8,4,16,1024]{3,2,1,0:T(8,128)(2,1)S(1)} %bitcast.6, bf16[8,4,16,1024]{3,2,1,0:T(8,128)(2,1)S(1)} %collective-permute-done.11.other_ref, bf16[4,16,1024]{2,1,0:T(8,128)(2,1)S(1)} %get-tuple-element.22.left_ref, s32[3]{0:T(128)S(1)} %pad_add_fusion.where_ref.refs_4_), custom_call_target="tpu_custom_call" | custom-call | flops 536870912 | bytes 2228236 | tf_op jit(solution)/shard_map/pallas_call | solution.py:21
  127.8 6.7 %all-to-all-start.3 = ((bf16[32,2,16,128]{3,2,1,0:T(8,128)(2,1)}), bf16[32,2,16,128]{3,2,1,0:T(8,128)(2,1)S(1)}, u32[]{:S(2)}, u32[]{:S(2)}) async-start(bf16[32,2,16,128]{3,2,1,0:T(8,128)(2,1)} %get-tuple-element.28), calls=%async_computation.3 | async-start | bytes 524288 | tf_op jit(solution)/shard_map/all_to_all | solution.py:222
  134.5 0.6 shard_map.88.pair_ref
  135.1 4.5 %collective-permute-start.2 = (bf16[2,4,16,1024]{3,2,1,0:T(8,128)(2,1)S(1)}, bf16[2,4,16,1024]{3,2,1,0:T(8,128)(2,1)S(1)}, u32[]{:S(2)}, u32[]{:S(2)}) collective-permute-start(bf16[2,4,16,1024]{3,2,1,0:T(8,128)(2,1)S(1)} %shard_map.88.pair_ref), channel_id=1, source_target_pairs={{0,384},{32,160},{64,448},{96,224},{128,0},{160,288},{192,64},{224... | collective-permute-start | bytes 786440 | tf_op jit(solution)/shard_map/ppermute | solution.py:236
  139.6 0.1 select_reduce_fusion
  139.7 2.8 %collective-permute-start.1 = (bf16[2,4,16,1024]{3,2,1,0:T(8,128)(2,1)S(1)}, bf16[2,4,16,1024]{3,2,1,0:T(8,128)(2,1)S(1)}, u32[]{:S(2)}, u32[]{:S(2)}) collective-permute-start(bf16[2,4,16,1024]{3,2,1,0:T(8,128)(2,1)S(1)} %shard_map.88.pair_ref), channel_id=1, source_target_pairs={{0,448},{32,96},{64,0},{96,160},{128,64},{160,224},{192,128},{224,... | collective-permute-start | bytes 786440 | tf_op jit(solution)/shard_map/ppermute | solution.py:236
  142.5 4.8 %collective-permute-done.2.in_ref.second_ref = bf16[2,4,16,1024]{3,2,1,0:T(8,128)(2,1)S(1)} collective-permute-done((bf16[2,4,16,1024]{3,2,1,0:T(8,128)(2,1)S(1)}, bf16[2,4,16,1024]{3,2,1,0:T(8,128)(2,1)S(1)}, u32[]{:S(2)}, u32[]{:S(2)}) %collective-permute-start.2) | collective-permute-done | bytes 262176 | tf_op jit(solution)/shard_map/ppermute | solution.py:236
  147.3 0.6 shard_map.89
  147.8 4.5 %collective-permute-start.4 = (bf16[4,16,1024]{2,1,0:T(8,128)(2,1)S(1)}, bf16[4,16,1024]{2,1,0:T(8,128)(2,1)S(1)}, u32[]{:S(2)}, u32[]{:S(2)}) collective-permute-start(bf16[4,16,1024]{2,1,0:T(8,128)(2,1)S(1)} %shard_map.89), channel_id=1, source_target_pairs={{0,384},{32,160},{64,448},{96,224},{128,0},{160,288},{192,64},{224... | collective-permute-start | bytes 393224 | tf_op jit(solution)/shard_map/ppermute | solution.py:236
  152.4 1.9 %collective-permute-start.3 = (bf16[2,4,16,1024]{3,2,1,0:T(8,128)(2,1)S(1)}, bf16[2,4,16,1024]{3,2,1,0:T(8,128)(2,1)S(1)}, u32[]{:S(2)}, u32[]{:S(2)}) collective-permute-start(bf16[2,4,16,1024]{3,2,1,0:T(8,128)(2,1)S(1)} %collective-permute-done.2.in_ref.second_ref), channel_id=1, source_target_pairs={{0,448},{32,96},{64,0},{96,160},{128,64},{160,224},{192,128},{224,... | collective-permute-start | bytes 786440 | tf_op jit(solution)/shard_map/ppermute | solution.py:236
  154.3 1.5 shard_map.99
  155.8 9.8 %all-to-all-start.4 = ((bf16[32,2,2,16,128]{4,3,2,1,0:T(8,128)(2,1)}), bf16[32,2,2,16,128]{4,3,2,1,0:T(8,128)(2,1)S(1)}, u32[]{:S(2)}, u32[]{:S(2)}) async-start(bf16[32,2,2,16,128]{4,3,2,1,0:T(8,128)(2,1)} %shard_map.99), calls=%async_computation.4 | async-start | bytes 1048576 | tf_op jit(solution)/shard_map/all_to_all | solution.py:222
  165.7 0.1 shard_map.90.mine_ref
  165.8 2.1 %collective-permute-start.5 = (bf16[7,4,16,1024]{3,2,1,0:T(8,128)(2,1)S(1)}, bf16[7,4,16,1024]{3,2,1,0:T(8,128)(2,1)S(1)}, u32[]{:S(2)}, u32[]{:S(2)}) collective-permute-start(bf16[7,4,16,1024]{3,2,1,0:T(8,128)(2,1)S(1)} %shard_map.90.mine_ref), channel_id=1, source_target_pairs={{0,32},{32,0},{1,33},{33,1},{2,34},{34,2},{3,35},{35,3},{4,36},{36... | collective-permute-start | bytes 2752520 | tf_op jit(solution)/shard_map/ppermute | solution.py:226
  167.8 2.4 %collective-permute-done.5.other_ref = bf16[7,4,16,1024]{3,2,1,0:T(8,128)(2,1)S(1)} collective-permute-done((bf16[7,4,16,1024]{3,2,1,0:T(8,128)(2,1)S(1)}, bf16[7,4,16,1024]{3,2,1,0:T(8,128)(2,1)S(1)}, u32[]{:S(2)}, u32[]{:S(2)}) %collective-permute-start.5) | collective-permute-done | bytes 917536 | tf_op jit(solution)/shard_map/ppermute | solution.py:226
  170.3 1.2 shard_map.97
  171.4 5.2 %collective-permute-start.12 = (bf16[16,1024]{1,0:T(8,128)(2,1)S(1)}, bf16[16,1024]{1,0:T(8,128)(2,1)S(1)}, u32[]{:S(2)}, u32[]{:S(2)}) collective-permute-start(bf16[16,1024]{1,0:T(8,128)(2,1)S(1)} %get-tuple-element.25), channel_id=1, source_target_pairs={{0,1},{1,2},{2,3},{3,0},{4,5},{5,6},{6,7},{7,4},{8,9},{9,10},{10,1... | collective-permute-start | bytes 98312 | tf_op jit(solution)/shard_map/ppermute | solution.py:231
  176.6 1.9 %collective-permute-start.13 = (bf16[16,1024]{1,0:T(8,128)(2,1)S(1)}, bf16[16,1024]{1,0:T(8,128)(2,1)S(1)}, u32[]{:S(2)}, u32[]{:S(2)}) collective-permute-start(bf16[16,1024]{1,0:T(8,128)(2,1)S(1)} %get-tuple-element.26), channel_id=1, source_target_pairs={{0,2},{1,3},{2,0},{3,1},{4,6},{5,7},{6,4},{7,5},{8,10},{9,11},{10,... | collective-permute-start | bytes 98312 | tf_op jit(solution)/shard_map/ppermute | solution.py:231
  178.5 3.0 %collective-permute-start.14 = (bf16[16,1024]{1,0:T(8,128)(2,1)S(1)}, bf16[16,1024]{1,0:T(8,128)(2,1)S(1)}, u32[]{:S(2)}, u32[]{:S(2)}) collective-permute-start(bf16[16,1024]{1,0:T(8,128)(2,1)S(1)} %get-tuple-element.27), channel_id=1, source_target_pairs={{0,3},{1,0},{2,1},{3,2},{4,7},{5,4},{6,5},{7,6},{8,11},{9,8},{10,9... | collective-permute-start | bytes 98312 | tf_op jit(solution)/shard_map/ppermute | solution.py:231
  181.6 1.7 collective-permute-done.13.refs_2_
  183.3 2.8 %collective-permute-done.14.refs_3_ = bf16[16,1024]{1,0:T(8,128)(2,1)S(1)} collective-permute-done((bf16[16,1024]{1,0:T(8,128)(2,1)S(1)}, bf16[16,1024]{1,0:T(8,128)(2,1)S(1)}, u32[]{:S(2)}, u32[]{:S(2)}) %collective-permute-start.14) | collective-permute-done | bytes 32800 | tf_op jit(solution)/shard_map/ppermute | solution.py:231
  186.2 1.2 shard_map.98
  187.4 1.1 shard_map.100
  (19 shorter events, 0.1 us)
Async XLA Ops:
  0.6 6.3 %collective-permute-start.6 = (bf16[1,256,4096]{2,1,0:T(8,128)(2,1)}, bf16[1,256,4096]{2,1,0:T(8,128)(2,1)S(1)}, u32[]{:S(2)}, u32[]{:S(2)}) collective-permute-start(bf16[1,256,4096]{2,1,0:T(8,128)(2,1)} %grads_ref.3), channel_id=1, source_target_pairs={{0,32},{32,0},{1,33},{33,1},{2,34},{34,2},{3,35},{35,3},{4,36},{36... | collective-permute-start | bytes 6291464 | tf_op jit(solution)/shard_map/ppermute | solution.py:226
  6.9 1.6 copy-start
  10.2 21.1 %collective-permute-start.7 = (bf16[4,16,4096]{2,1,0:T(8,128)(2,1)S(1)}, bf16[4,16,4096]{2,1,0:T(8,128)(2,1)S(1)}, u32[]{:S(2)}, u32[]{:S(2)}) collective-permute-start(bf16[4,16,4096]{2,1,0:T(8,128)(2,1)S(1)} %get-tuple-element.19), channel_id=1, source_target_pairs={{0,64},{32,480},{64,128},{96,32},{128,192},{160,96},{192,256},{224... | collective-permute-start | bytes 1572872 | tf_op jit(solution)/shard_map/ppermute | solution.py:236
  14.4 16.8 %collective-permute-start.8 = (bf16[16,4096]{1,0:T(8,128)(2,1)S(1)}, bf16[16,4096]{1,0:T(8,128)(2,1)S(1)}, u32[]{:S(2)}, u32[]{:S(2)}) collective-permute-start(bf16[16,4096]{1,0:T(8,128)(2,1)S(1)} %get-tuple-element.21), channel_id=1, source_target_pairs={{0,128},{32,416},{64,192},{96,480},{128,256},{160,32},{192,320},{2... | collective-permute-start | bytes 393224 | tf_op jit(solution)/shard_map/ppermute | solution.py:236
  31.9 13.2 %collective-permute-start.9 = (bf16[2,16,4096]{2,1,0:T(8,128)(2,1)S(1)}, bf16[2,16,4096]{2,1,0:T(8,128)(2,1)S(1)}, u32[]{:S(2)}, u32[]{:S(2)}) collective-permute-start(bf16[2,16,4096]{2,1,0:T(8,128)(2,1)S(1)} %shard_map.93), channel_id=1, source_target_pairs={{0,128},{32,416},{64,192},{96,480},{128,256},{160,32},{192,320},{2... | collective-permute-start | bytes 786440 | tf_op jit(solution)/shard_map/ppermute | solution.py:236
  45.6 3.2 %collective-permute-start.10 = (bf16[16,4096]{1,0:T(8,128)(2,1)S(1)}, bf16[16,4096]{1,0:T(8,128)(2,1)S(1)}, u32[]{:S(2)}, u32[]{:S(2)}) collective-permute-start(bf16[16,4096]{1,0:T(8,128)(2,1)S(1)} %shard_map.94), channel_id=1, source_target_pairs={{0,32},{32,0},{1,33},{33,1},{2,34},{34,2},{3,35},{35,3},{4,36},{36... | collective-permute-start | bytes 393224 | tf_op jit(solution)/shard_map/ppermute | solution.py:226
  50.5 56.1 %copy-start.3 = (s32[32]{0:T(128)S(1)}, s32[32]{0:T(128)}, u32[]{:S(2)}) copy-start(s32[32]{0:T(128)} %table_ref.1) | copy-start | bytes 388
  50.5 35.4 %all-to-all-start.2 = ((bf16[32,16,1024]{2,1,0:T(8,128)(2,1)}), bf16[32,16,1024]{2,1,0:T(8,128)(2,1)S(1)}, u32[]{:S(2)}, u32[]{:S(2)}) async-start(bf16[32,16,1024]{2,1,0:T(8,128)(2,1)} %shard_map.95), calls=%async_computation.2 | async-start | bytes 2097152 | tf_op jit(solution)/shard_map/all_to_all | solution.py:222
  85.9 20.7 %all-to-all-start = ((bf16[32,2,2,16,128]{4,3,2,1,0:T(8,128)(2,1)}), bf16[32,2,2,16,128]{4,3,2,1,0:T(8,128)(2,1)S(1)}, u32[]{:S(2)}, u32[]{:S(2)}) async-start(bf16[32,2,2,16,128]{4,3,2,1,0:T(8,128)(2,1)} %shard_map.85), calls=%async_computation | async-start | bytes 1048576 | tf_op jit(solution)/shard_map/all_to_all | solution.py:222
  93.1 32.2 %collective-permute-start.11 = (bf16[8,4,16,1024]{3,2,1,0:T(8,128)(2,1)S(1)}, bf16[8,4,16,1024]{3,2,1,0:T(8,128)(2,1)S(1)}, u32[]{:S(2)}, u32[]{:S(2)}) collective-permute-start(bf16[8,4,16,1024]{3,2,1,0:T(8,128)(2,1)S(1)} %bitcast.5), channel_id=1, source_target_pairs={{0,32},{32,0},{1,33},{33,1},{2,34},{34,2},{3,35},{35,3},{4,36},{36... | collective-permute-start | bytes 3145736 | tf_op jit(solution)/shard_map/ppermute | solution.py:226
  123.4 11.2 %collective-permute-start = (bf16[4,16,1024]{2,1,0:T(8,128)(2,1)S(1)}, bf16[4,16,1024]{2,1,0:T(8,128)(2,1)S(1)}, u32[]{:S(2)}, u32[]{:S(2)}) collective-permute-start(bf16[4,16,1024]{2,1,0:T(8,128)(2,1)S(1)} %get-tuple-element.17.mine_ref), channel_id=1, source_target_pairs={{0,32},{32,0},{1,33},{33,1},{2,34},{34,2},{3,35},{35,3},{4,36},{36... | collective-permute-start | bytes 393224 | tf_op jit(solution)/shard_map/ppermute | solution.py:226
  127.8 26.5 %all-to-all-start.3 = ((bf16[32,2,16,128]{3,2,1,0:T(8,128)(2,1)}), bf16[32,2,16,128]{3,2,1,0:T(8,128)(2,1)S(1)}, u32[]{:S(2)}, u32[]{:S(2)}) async-start(bf16[32,2,16,128]{3,2,1,0:T(8,128)(2,1)} %get-tuple-element.28), calls=%async_computation.3 | async-start | bytes 524288 | tf_op jit(solution)/shard_map/all_to_all | solution.py:222
  135.1 12.2 %collective-permute-start.2 = (bf16[2,4,16,1024]{3,2,1,0:T(8,128)(2,1)S(1)}, bf16[2,4,16,1024]{3,2,1,0:T(8,128)(2,1)S(1)}, u32[]{:S(2)}, u32[]{:S(2)}) collective-permute-start(bf16[2,4,16,1024]{3,2,1,0:T(8,128)(2,1)S(1)} %shard_map.88.pair_ref), channel_id=1, source_target_pairs={{0,384},{32,160},{64,448},{96,224},{128,0},{160,288},{192,64},{224... | collective-permute-start | bytes 786440 | tf_op jit(solution)/shard_map/ppermute | solution.py:236
  139.7 26.0 %collective-permute-start.1 = (bf16[2,4,16,1024]{3,2,1,0:T(8,128)(2,1)S(1)}, bf16[2,4,16,1024]{3,2,1,0:T(8,128)(2,1)S(1)}, u32[]{:S(2)}, u32[]{:S(2)}) collective-permute-start(bf16[2,4,16,1024]{3,2,1,0:T(8,128)(2,1)S(1)} %shard_map.88.pair_ref), channel_id=1, source_target_pairs={{0,448},{32,96},{64,0},{96,160},{128,64},{160,224},{192,128},{224,... | collective-permute-start | bytes 786440 | tf_op jit(solution)/shard_map/ppermute | solution.py:236
  147.8 17.8 %collective-permute-start.4 = (bf16[4,16,1024]{2,1,0:T(8,128)(2,1)S(1)}, bf16[4,16,1024]{2,1,0:T(8,128)(2,1)S(1)}, u32[]{:S(2)}, u32[]{:S(2)}) collective-permute-start(bf16[4,16,1024]{2,1,0:T(8,128)(2,1)S(1)} %shard_map.89), channel_id=1, source_target_pairs={{0,384},{32,160},{64,448},{96,224},{128,0},{160,288},{192,64},{224... | collective-permute-start | bytes 393224 | tf_op jit(solution)/shard_map/ppermute | solution.py:236
  152.4 13.3 %collective-permute-start.3 = (bf16[2,4,16,1024]{3,2,1,0:T(8,128)(2,1)S(1)}, bf16[2,4,16,1024]{3,2,1,0:T(8,128)(2,1)S(1)}, u32[]{:S(2)}, u32[]{:S(2)}) collective-permute-start(bf16[2,4,16,1024]{3,2,1,0:T(8,128)(2,1)S(1)} %collective-permute-done.2.in_ref.second_ref), channel_id=1, source_target_pairs={{0,448},{32,96},{64,0},{96,160},{128,64},{160,224},{192,128},{224,... | collective-permute-start | bytes 786440 | tf_op jit(solution)/shard_map/ppermute | solution.py:236
  155.8 31.5 %all-to-all-start.4 = ((bf16[32,2,2,16,128]{4,3,2,1,0:T(8,128)(2,1)}), bf16[32,2,2,16,128]{4,3,2,1,0:T(8,128)(2,1)S(1)}, u32[]{:S(2)}, u32[]{:S(2)}) async-start(bf16[32,2,2,16,128]{4,3,2,1,0:T(8,128)(2,1)} %shard_map.99), calls=%async_computation.4 | async-start | bytes 1048576 | tf_op jit(solution)/shard_map/all_to_all | solution.py:222
  165.6 21.7 %copy-start.1 = (f32[2,4,1,16,1024]{4,3,2,1,0:T(8,128)S(1)}, f32[2,4,1,16,1024]{4,3,2,1,0:T(8,128)}, u32[]{:S(2)}) copy-start(f32[2,4,1,16,1024]{4,3,2,1,0:T(8,128)} %left_ref.1) | copy-start | bytes 1572868
  165.7 21.7 %copy-start.2 = (f32[2,4,1,16,1024]{4,3,2,1,0:T(8,128)S(1)}, f32[2,4,1,16,1024]{4,3,2,1,0:T(8,128)}, u32[]{:S(2)}) copy-start(f32[2,4,1,16,1024]{4,3,2,1,0:T(8,128)} %right_ref.1) | copy-start | bytes 1572868
  165.8 4.5 %collective-permute-start.5 = (bf16[7,4,16,1024]{3,2,1,0:T(8,128)(2,1)S(1)}, bf16[7,4,16,1024]{3,2,1,0:T(8,128)(2,1)S(1)}, u32[]{:S(2)}, u32[]{:S(2)}) collective-permute-start(bf16[7,4,16,1024]{3,2,1,0:T(8,128)(2,1)S(1)} %shard_map.90.mine_ref), channel_id=1, source_target_pairs={{0,32},{32,0},{1,33},{33,1},{2,34},{34,2},{3,35},{35,3},{4,36},{36... | collective-permute-start | bytes 2752520 | tf_op jit(solution)/shard_map/ppermute | solution.py:226
  171.4 10.1 %collective-permute-start.12 = (bf16[16,1024]{1,0:T(8,128)(2,1)S(1)}, bf16[16,1024]{1,0:T(8,128)(2,1)S(1)}, u32[]{:S(2)}, u32[]{:S(2)}) collective-permute-start(bf16[16,1024]{1,0:T(8,128)(2,1)S(1)} %get-tuple-element.25), channel_id=1, source_target_pairs={{0,1},{1,2},{2,3},{3,0},{4,5},{5,6},{6,7},{7,4},{8,9},{9,10},{10,1... | collective-permute-start | bytes 98312 | tf_op jit(solution)/shard_map/ppermute | solution.py:231
  176.6 6.7 %collective-permute-start.13 = (bf16[16,1024]{1,0:T(8,128)(2,1)S(1)}, bf16[16,1024]{1,0:T(8,128)(2,1)S(1)}, u32[]{:S(2)}, u32[]{:S(2)}) collective-permute-start(bf16[16,1024]{1,0:T(8,128)(2,1)S(1)} %get-tuple-element.26), channel_id=1, source_target_pairs={{0,2},{1,3},{2,0},{3,1},{4,6},{5,7},{6,4},{7,5},{8,10},{9,11},{10,... | collective-permute-start | bytes 98312 | tf_op jit(solution)/shard_map/ppermute | solution.py:231
  178.5 7.6 %collective-permute-start.14 = (bf16[16,1024]{1,0:T(8,128)(2,1)S(1)}, bf16[16,1024]{1,0:T(8,128)(2,1)S(1)}, u32[]{:S(2)}, u32[]{:S(2)}) collective-permute-start(bf16[16,1024]{1,0:T(8,128)(2,1)S(1)} %get-tuple-element.27), channel_id=1, source_target_pairs={{0,3},{1,0},{2,1},{3,2},{4,7},{5,4},{6,5},{7,6},{8,11},{9,8},{10,9... | collective-permute-start | bytes 98312 | tf_op jit(solution)/shard_map/ppermute | solution.py:231

commit v7 on v6

--- a/solution.py
+++ b/solution.py
@@ -24,7 +24,7 @@
         in_specs=[VM] * (len(inputs) - scalars) + [SM] * scalars,
         out_specs=jax.tree.map(lambda _: VM, out),
         scratch_shapes=scratch,
-        compiler_params=pltpu.CompilerParams(vmem_limit_bytes=32 * 1024 * 1024),
+        compiler_params=pltpu.CompilerParams(vmem_limit_bytes=16 * 1024 * 1024),
         cost_estimate=pl.CostEstimate(flops=flops, bytes_accessed=moved, transcendentals=0),
     )(*inputs)
 
@@ -92,7 +92,7 @@
             pltpu.VMEM((len(wanted), 16, 4096), BF),
             pltpu.SemaphoreType.DMA((len(wanted),)),
         ],
-        compiler_params=pltpu.CompilerParams(vmem_limit_bytes=32 * 1024 * 1024),
+        compiler_params=pltpu.CompilerParams(vmem_limit_bytes=16 * 1024 * 1024),
         cost_estimate=pl.CostEstimate(flops=1000000, bytes_accessed=2097152, transcendentals=0),
     )(grads, theirs, where)
 
@@ -111,17 +111,24 @@
     out_ref[...] = (near_ref[2 + parity].astype(F32) + two_ref[parity].astype(F32)).astype(BF)
 
 
-def add_replicas(own_ref, near_ref, two_ref, theirs_ref, where_ref, out_ref):
+def add_replicas(own_ref, near_ref, two_ref, theirs_ref, where_ref, out_hbm, strip, sems):
+    copies = []
     for column in range(4):
         columns = slice(column * 1024, column * 1024 + 1024)
-        total = (
+        strip[column] = (
             own_ref[:, columns].astype(F32)
             + near_ref[2 + where_ref[1], :, columns].astype(F32)
             + two_ref[where_ref[1], :, columns].astype(F32)
             + theirs_ref[:, columns].astype(F32)
         ).astype(BF)
         for z in range(8):
-            out_ref[z * 4 + column] = total
+            copy = pltpu.make_async_copy(
+                strip.at[column], out_hbm.at[z * 4 + column], sems.at[z * 4 + column]
+            )
+            copy.start()
+            copies.append(copy)
+    for copy in copies:
+        copy.wait()
 
 
 def place(whole, rows, z, parity):
@@ -265,9 +272,15 @@
     two = around(two, 2)
     other = call(add_other, strip_shape, [near, two, where], scalars=1)
     other = swap(other)
-    strip = call(
-        add_replicas, shape((32, 16, 1024)), [own, near, two, other, where], scalars=1
-    )
+    strip = pl.pallas_call(
+        add_replicas,
+        out_shape=shape((32, 16, 1024)),
+        in_specs=[VM] * 4 + [SM],
+        out_specs=pl.BlockSpec(memory_space=pltpu.HBM),
+        scratch_shapes=[pltpu.VMEM((4, 16, 1024), BF), pltpu.SemaphoreType.DMA((32,))],
+        compiler_params=pltpu.CompilerParams(vmem_limit_bytes=16 * 1024 * 1024),
+        cost_estimate=pl.CostEstimate(flops=1000000, bytes_accessed=1048576, transcendentals=0),
+    )(own, near, two, other, where)
 
     pieces = pl.pallas_call(
         spread_roots,
@@ -279,6 +292,7 @@
             pltpu.VMEM(left_root.shape, BF),
             pltpu.SemaphoreType.DMA((2,)),
         ],
+        compiler_params=pltpu.CompilerParams(vmem_limit_bytes=16 * 1024 * 1024),
         cost_estimate=pl.CostEstimate(flops=1000000, bytes_accessed=524288, transcendentals=0),
     )(left_root, right_root)
     pieces = exchange(pieces, BANDS).reshape(64, 2, 16, 128)

time: 189 us -> 189 us (level)
    pallas_call x13 -> x12, Pallas kernels: 12.1 us -> 10.5 us  [call(): pl.pallas_call(kernel, out_shape=out, in_specs=[VM] * (len(inputs) - scal...]
  transfers between devices with their start and end apart: 19 -> 19, of which waited for: 10 -> 10; matrix products, arithmetic and copies ran while one was open for 0% -> 0% of each run, Pallas kernels for 6% -> 5%
where the time goes in v7:
time: 189 us
  waiting for transfers between devices  77.4 us (41%)
  starting transfers between devices  76 us (40%)
  blocking collectives  16.2 us (9%)
  Pallas kernels  16.1 us (9%)
    all_to_all x4, waiting for transfers between devices, exchange(): return lax.all_to_all(value, axes, split_axis=0, concat_axis=0, tiled=True)  39.3 us
    all_to_all x4, starting transfers between devices, exchange(): return lax.all_to_all(value, axes, split_axis=0, concat_axis=0, tiled=True)  30.2 us
    ppermute x7, starting transfers between devices, around(): return lax.ppermute(value, ROWS, pairs)  25.9 us
    ppermute x7, waiting for transfers between devices, around(): return lax.ppermute(value, ROWS, pairs)  25.6 us
    all_to_all x1, blocking collectives, exchange(): return lax.all_to_all(value, axes, split_axis=0, concat_axis=0, tiled=True)  16.2 us
    pallas_call x12, Pallas kernels, call(): pl.pallas_call(kernel, out_shape=out, in_specs=[VM] * (len(inputs) - scal...  10.5 us
    ppermute x3, starting transfers between devices, shift(): lax.ppermute(value, axis, [(i, (i + distance) % size) for i in range(size)])  10.1 us
    ppermute x5, starting transfers between devices, swap(): return lax.ppermute(value, 'c', [(0, 1), (1, 0)])  9.74 us
  transfers between devices with their start and end apart: 19, of which 10 were waited for; matrix products, arithmetic and copies ran while one was open for 0% of the time, Pallas kernels for 5%

profile of v7, /device:TPU:56, one launch (start us, length us, event | category | flops | bytes accessed | tf_op | source)
XLA Modules:
  0.0 188.5 jit_solution(7853532117297458920)
XLA Ops:
  0.6 1.9 %collective-permute-start.6 = (bf16[1,256,4096]{2,1,0:T(8,128)(2,1)}, bf16[1,256,4096]{2,1,0:T(8,128)(2,1)S(1)}, u32[]{:S(2)}, u32[]{:S(2)}) collective-permute-start(bf16[1,256,4096]{2,1,0:T(8,128)(2,1)} %grads_ref.3), channel_id=1, source_target_pairs={{0,32},{32,0},{1,33},{33,1},{2,34},{34,2},{3,35},{35,3},{4,36},{36... | collective-permute-start | bytes 6291464 | tf_op jit(solution)/shard_map/ppermute | solution.py:233
  2.6 0.1 pad_add_fusion.where_ref.refs_4_
  2.6 4.3 %collective-permute-done.6.theirs_hbm = bf16[1,256,4096]{2,1,0:T(8,128)(2,1)S(1)} collective-permute-done((bf16[1,256,4096]{2,1,0:T(8,128)(2,1)}, bf16[1,256,4096]{2,1,0:T(8,128)(2,1)S(1)}, u32[]{:S(2)}, u32[]{:S(2)}) %collective-permute-start.6) | collective-permute-done | bytes 2097184 | tf_op jit(solution)/shard_map/ppermute | solution.py:233
  6.9 1.6 copy-done
  8.5 1.6 shard_map.92
  10.1 4.3 %collective-permute-start.7 = (bf16[4,16,4096]{2,1,0:T(8,128)(2,1)S(1)}, bf16[4,16,4096]{2,1,0:T(8,128)(2,1)S(1)}, u32[]{:S(2)}, u32[]{:S(2)}) collective-permute-start(bf16[4,16,4096]{2,1,0:T(8,128)(2,1)S(1)} %get-tuple-element.19), channel_id=1, source_target_pairs={{0,64},{32,480},{64,128},{96,32},{128,192},{160,96},{192,256},{224... | collective-permute-start | bytes 1572872 | tf_op jit(solution)/shard_map/ppermute | solution.py:243
  14.4 6.1 %collective-permute-start.8 = (bf16[16,4096]{1,0:T(8,128)(2,1)S(1)}, bf16[16,4096]{1,0:T(8,128)(2,1)S(1)}, u32[]{:S(2)}, u32[]{:S(2)}) collective-permute-start(bf16[16,4096]{1,0:T(8,128)(2,1)S(1)} %get-tuple-element.21), channel_id=1, source_target_pairs={{0,128},{32,416},{64,192},{96,480},{128,256},{160,32},{192,320},{2... | collective-permute-start | bytes 393224 | tf_op jit(solution)/shard_map/ppermute | solution.py:243
  20.5 1.2 shard_map.91
  21.7 9.5 %collective-permute-done.8.four_ref = bf16[16,4096]{1,0:T(8,128)(2,1)S(1)} collective-permute-done((bf16[16,4096]{1,0:T(8,128)(2,1)S(1)}, bf16[16,4096]{1,0:T(8,128)(2,1)S(1)}, u32[]{:S(2)}, u32[]{:S(2)}) %collective-permute-start.8) | collective-permute-done | bytes 131104 | tf_op jit(solution)/shard_map/ppermute | solution.py:243
  31.2 0.7 shard_map.93
  31.8 1.9 %collective-permute-start.9 = (bf16[2,16,4096]{2,1,0:T(8,128)(2,1)S(1)}, bf16[2,16,4096]{2,1,0:T(8,128)(2,1)S(1)}, u32[]{:S(2)}, u32[]{:S(2)}) collective-permute-start(bf16[2,16,4096]{2,1,0:T(8,128)(2,1)S(1)} %shard_map.93), channel_id=1, source_target_pairs={{0,128},{32,416},{64,192},{96,480},{128,256},{160,32},{192,320},{2... | collective-permute-start | bytes 786440 | tf_op jit(solution)/shard_map/ppermute | solution.py:243
  33.8 11.3 %collective-permute-done.9.two_ref = bf16[2,16,4096]{2,1,0:T(8,128)(2,1)S(1)} collective-permute-done((bf16[2,16,4096]{2,1,0:T(8,128)(2,1)S(1)}, bf16[2,16,4096]{2,1,0:T(8,128)(2,1)S(1)}, u32[]{:S(2)}, u32[]{:S(2)}) %collective-permute-start.9) | collective-permute-done | bytes 262176 | tf_op jit(solution)/shard_map/ppermute | solution.py:243
  45.0 0.6 shard_map.94
  45.6 1.9 %collective-permute-start.10 = (bf16[16,4096]{1,0:T(8,128)(2,1)S(1)}, bf16[16,4096]{1,0:T(8,128)(2,1)S(1)}, u32[]{:S(2)}, u32[]{:S(2)}) collective-permute-start(bf16[16,4096]{1,0:T(8,128)(2,1)S(1)} %shard_map.94), channel_id=1, source_target_pairs={{0,32},{32,0},{1,33},{33,1},{2,34},{34,2},{3,35},{35,3},{4,36},{36... | collective-permute-start | bytes 393224 | tf_op jit(solution)/shard_map/ppermute | solution.py:233
  47.5 1.3 collective-permute-done.10.theirs_ref
  48.9 1.8 shard_map.95
  50.7 6.6 %all-to-all-start.2 = ((bf16[32,16,1024]{2,1,0:T(8,128)(2,1)}), bf16[32,16,1024]{2,1,0:T(8,128)(2,1)S(1)}, u32[]{:S(2)}, u32[]{:S(2)}) async-start(bf16[32,16,1024]{2,1,0:T(8,128)(2,1)} %shard_map.95), calls=%async_computation.2 | async-start | bytes 2097152 | tf_op jit(solution)/shard_map/all_to_all | solution.py:229
  57.4 0.9 shard_map.85
  58.3 27.7 %all-to-all-done.2 = bf16[32,16,1024]{2,1,0:T(8,128)(2,1)S(1)} async-done(((bf16[32,16,1024]{2,1,0:T(8,128)(2,1)}), bf16[32,16,1024]{2,1,0:T(8,128)(2,1)S(1)}, u32[]{:S(2)}, u32[]{:S(2)}) %all-to-all-start.2) | async-done | bytes 1048608 | tf_op jit(solution)/shard_map/all_to_all | solution.py:229
  86.0 7.1 %all-to-all-start = ((bf16[32,2,2,16,128]{4,3,2,1,0:T(8,128)(2,1)}), bf16[32,2,2,16,128]{4,3,2,1,0:T(8,128)(2,1)S(1)}, u32[]{:S(2)}, u32[]{:S(2)}) async-start(bf16[32,2,2,16,128]{4,3,2,1,0:T(8,128)(2,1)} %shard_map.85), calls=%async_computation | async-start | bytes 1048576 | tf_op jit(solution)/shard_map/all_to_all | solution.py:229
  93.2 1.9 %collective-permute-start.11 = (bf16[8,4,16,1024]{3,2,1,0:T(8,128)(2,1)S(1)}, bf16[8,4,16,1024]{3,2,1,0:T(8,128)(2,1)S(1)}, u32[]{:S(2)}, u32[]{:S(2)}) collective-permute-start(bf16[8,4,16,1024]{3,2,1,0:T(8,128)(2,1)S(1)} %bitcast.5), channel_id=1, source_target_pairs={{0,32},{32,0},{1,33},{33,1},{2,34},{34,2},{3,35},{35,3},{4,36},{36... | collective-permute-start | bytes 3145736 | tf_op jit(solution)/shard_map/ppermute | solution.py:233
  95.1 11.6 %all-to-all-done = bf16[32,2,2,16,128]{4,3,2,1,0:T(8,128)(2,1)S(1)} async-done(((bf16[32,2,2,16,128]{4,3,2,1,0:T(8,128)(2,1)}), bf16[32,2,2,16,128]{4,3,2,1,0:T(8,128)(2,1)S(1)}, u32[]{:S(2)}, u32[]{:S(2)}) %all-to-all-start) | async-done | bytes 524320 | tf_op jit(solution)/shard_map/all_to_all | solution.py:229
  106.7 0.6 shard_map.86
  107.3 16.2 %all_to_all.25.in_ref = bf16[32,2,16,128]{3,2,1,0:T(8,128)(2,1)S(1)} all-to-all(bf16[32,2,16,128]{3,2,1,0:T(8,128)(2,1)S(1)} %shard_map.86), channel_id=1, replica_groups=mesh['z'=8,'c'=2,'x'=4,'yh'=2,'yl'=4] {'x','yh','yl'}, dimensions={0} | all-to-all | bytes 524288 | tf_op jit(solution)/shard_map/all_to_all | solution.py:229
  123.5 1.9 %collective-permute-start = (bf16[4,16,1024]{2,1,0:T(8,128)(2,1)S(1)}, bf16[4,16,1024]{2,1,0:T(8,128)(2,1)S(1)}, u32[]{:S(2)}, u32[]{:S(2)}) collective-permute-start(bf16[4,16,1024]{2,1,0:T(8,128)(2,1)S(1)} %get-tuple-element.17.mine_ref), channel_id=1, source_target_pairs={{0,32},{32,0},{1,33},{33,1},{2,34},{34,2},{3,35},{35,3},{4,36},{36... | collective-permute-start | bytes 393224 | tf_op jit(solution)/shard_map/ppermute | solution.py:233
  125.4 2.5 %shard_map.96 = (bf16[32,2,16,128]{3,2,1,0:T(8,128)(2,1)}, bf16[64,1024]{1,0:T(8,128)(2,1)S(1)}) custom-call(bf16[8,4,16,1024]{3,2,1,0:T(8,128)(2,1)S(1)} %bitcast.6, bf16[8,4,16,1024]{3,2,1,0:T(8,128)(2,1)S(1)} %collective-permute-done.11.other_ref, bf16[4,16,1024]{2,1,0:T(8,128)(2,1)S(1)} %get-tuple-element.22.left_ref, s32[3]{0:T(128)S(1)} %pad_add_fusion.where_ref.refs_4_), custom_call_target="tpu_custom_call" | custom-call | flops 536870912 | bytes 2228236 | tf_op jit(solution)/shard_map/pallas_call | solution.py:21
  127.9 6.7 %all-to-all-start.3 = ((bf16[32,2,16,128]{3,2,1,0:T(8,128)(2,1)}), bf16[32,2,16,128]{3,2,1,0:T(8,128)(2,1)S(1)}, u32[]{:S(2)}, u32[]{:S(2)}) async-start(bf16[32,2,16,128]{3,2,1,0:T(8,128)(2,1)} %get-tuple-element.28), calls=%async_computation.3 | async-start | bytes 524288 | tf_op jit(solution)/shard_map/all_to_all | solution.py:229
  134.6 0.6 shard_map.88.pair_ref
  135.2 4.4 %collective-permute-start.2 = (bf16[2,4,16,1024]{3,2,1,0:T(8,128)(2,1)S(1)}, bf16[2,4,16,1024]{3,2,1,0:T(8,128)(2,1)S(1)}, u32[]{:S(2)}, u32[]{:S(2)}) collective-permute-start(bf16[2,4,16,1024]{3,2,1,0:T(8,128)(2,1)S(1)} %shard_map.88.pair_ref), channel_id=1, source_target_pairs={{0,384},{32,160},{64,448},{96,224},{128,0},{160,288},{192,64},{224... | collective-permute-start | bytes 786440 | tf_op jit(solution)/shard_map/ppermute | solution.py:243
  139.7 0.1 select_reduce_fusion
  139.8 2.8 %collective-permute-start.1 = (bf16[2,4,16,1024]{3,2,1,0:T(8,128)(2,1)S(1)}, bf16[2,4,16,1024]{3,2,1,0:T(8,128)(2,1)S(1)}, u32[]{:S(2)}, u32[]{:S(2)}) collective-permute-start(bf16[2,4,16,1024]{3,2,1,0:T(8,128)(2,1)S(1)} %shard_map.88.pair_ref), channel_id=1, source_target_pairs={{0,448},{32,96},{64,0},{96,160},{128,64},{160,224},{192,128},{224,... | collective-permute-start | bytes 786440 | tf_op jit(solution)/shard_map/ppermute | solution.py:243
  142.6 4.8 %collective-permute-done.2.in_ref.second_ref = bf16[2,4,16,1024]{3,2,1,0:T(8,128)(2,1)S(1)} collective-permute-done((bf16[2,4,16,1024]{3,2,1,0:T(8,128)(2,1)S(1)}, bf16[2,4,16,1024]{3,2,1,0:T(8,128)(2,1)S(1)}, u32[]{:S(2)}, u32[]{:S(2)}) %collective-permute-start.2) | collective-permute-done | bytes 262176 | tf_op jit(solution)/shard_map/ppermute | solution.py:243
  147.4 0.6 shard_map.89
  147.9 4.5 %collective-permute-start.4 = (bf16[4,16,1024]{2,1,0:T(8,128)(2,1)S(1)}, bf16[4,16,1024]{2,1,0:T(8,128)(2,1)S(1)}, u32[]{:S(2)}, u32[]{:S(2)}) collective-permute-start(bf16[4,16,1024]{2,1,0:T(8,128)(2,1)S(1)} %shard_map.89), channel_id=1, source_target_pairs={{0,384},{32,160},{64,448},{96,224},{128,0},{160,288},{192,64},{224... | collective-permute-start | bytes 393224 | tf_op jit(solution)/shard_map/ppermute | solution.py:243
  152.4 1.9 %collective-permute-start.3 = (bf16[2,4,16,1024]{3,2,1,0:T(8,128)(2,1)S(1)}, bf16[2,4,16,1024]{3,2,1,0:T(8,128)(2,1)S(1)}, u32[]{:S(2)}, u32[]{:S(2)}) collective-permute-start(bf16[2,4,16,1024]{3,2,1,0:T(8,128)(2,1)S(1)} %collective-permute-done.2.in_ref.second_ref), channel_id=1, source_target_pairs={{0,448},{32,96},{64,0},{96,160},{128,64},{160,224},{192,128},{224,... | collective-permute-start | bytes 786440 | tf_op jit(solution)/shard_map/ppermute | solution.py:243
  154.4 1.5 shard_map.99
  155.9 9.8 %all-to-all-start.4 = ((bf16[32,2,2,16,128]{4,3,2,1,0:T(8,128)(2,1)}), bf16[32,2,2,16,128]{4,3,2,1,0:T(8,128)(2,1)S(1)}, u32[]{:S(2)}, u32[]{:S(2)}) async-start(bf16[32,2,2,16,128]{4,3,2,1,0:T(8,128)(2,1)} %shard_map.99), calls=%async_computation.4 | async-start | bytes 1048576 | tf_op jit(solution)/shard_map/all_to_all | solution.py:229
  165.8 0.1 shard_map.90.mine_ref
  165.8 2.1 %collective-permute-start.5 = (bf16[7,4,16,1024]{3,2,1,0:T(8,128)(2,1)S(1)}, bf16[7,4,16,1024]{3,2,1,0:T(8,128)(2,1)S(1)}, u32[]{:S(2)}, u32[]{:S(2)}) collective-permute-start(bf16[7,4,16,1024]{3,2,1,0:T(8,128)(2,1)S(1)} %shard_map.90.mine_ref), channel_id=1, source_target_pairs={{0,32},{32,0},{1,33},{33,1},{2,34},{34,2},{3,35},{35,3},{4,36},{36... | collective-permute-start | bytes 2752520 | tf_op jit(solution)/shard_map/ppermute | solution.py:233
  167.9 2.4 %collective-permute-done.5.other_ref = bf16[7,4,16,1024]{3,2,1,0:T(8,128)(2,1)S(1)} collective-permute-done((bf16[7,4,16,1024]{3,2,1,0:T(8,128)(2,1)S(1)}, bf16[7,4,16,1024]{3,2,1,0:T(8,128)(2,1)S(1)}, u32[]{:S(2)}, u32[]{:S(2)}) %collective-permute-start.5) | collective-permute-done | bytes 917536 | tf_op jit(solution)/shard_map/ppermute | solution.py:233
  170.3 1.2 shard_map.97
  171.5 5.2 %collective-permute-start.12 = (bf16[16,1024]{1,0:T(8,128)(2,1)S(1)}, bf16[16,1024]{1,0:T(8,128)(2,1)S(1)}, u32[]{:S(2)}, u32[]{:S(2)}) collective-permute-start(bf16[16,1024]{1,0:T(8,128)(2,1)S(1)} %get-tuple-element.25), channel_id=1, source_target_pairs={{0,1},{1,2},{2,3},{3,0},{4,5},{5,6},{6,7},{7,4},{8,9},{9,10},{10,1... | collective-permute-start | bytes 98312 | tf_op jit(solution)/shard_map/ppermute | solution.py:238
  176.7 1.9 %collective-permute-start.13 = (bf16[16,1024]{1,0:T(8,128)(2,1)S(1)}, bf16[16,1024]{1,0:T(8,128)(2,1)S(1)}, u32[]{:S(2)}, u32[]{:S(2)}) collective-permute-start(bf16[16,1024]{1,0:T(8,128)(2,1)S(1)} %get-tuple-element.26), channel_id=1, source_target_pairs={{0,2},{1,3},{2,0},{3,1},{4,6},{5,7},{6,4},{7,5},{8,10},{9,11},{10,... | collective-permute-start | bytes 98312 | tf_op jit(solution)/shard_map/ppermute | solution.py:238
  178.6 3.0 %collective-permute-start.14 = (bf16[16,1024]{1,0:T(8,128)(2,1)S(1)}, bf16[16,1024]{1,0:T(8,128)(2,1)S(1)}, u32[]{:S(2)}, u32[]{:S(2)}) collective-permute-start(bf16[16,1024]{1,0:T(8,128)(2,1)S(1)} %get-tuple-element.27), channel_id=1, source_target_pairs={{0,3},{1,0},{2,1},{3,2},{4,7},{5,4},{6,5},{7,6},{8,11},{9,8},{10,9... | collective-permute-start | bytes 98312 | tf_op jit(solution)/shard_map/ppermute | solution.py:238
  181.7 1.7 collective-permute-done.13.refs_2_
  183.4 2.8 %collective-permute-done.14.refs_3_ = bf16[16,1024]{1,0:T(8,128)(2,1)S(1)} collective-permute-done((bf16[16,1024]{1,0:T(8,128)(2,1)S(1)}, bf16[16,1024]{1,0:T(8,128)(2,1)S(1)}, u32[]{:S(2)}, u32[]{:S(2)}) %collective-permute-start.14) | collective-permute-done | bytes 32800 | tf_op jit(solution)/shard_map/ppermute | solution.py:238
  186.2 1.2 shard_map.98
  187.5 1.1 shard_map.100
  (23 shorter events, 0.1 us)
Async XLA Ops:
  0.6 6.3 %collective-permute-start.6 = (bf16[1,256,4096]{2,1,0:T(8,128)(2,1)}, bf16[1,256,4096]{2,1,0:T(8,128)(2,1)S(1)}, u32[]{:S(2)}, u32[]{:S(2)}) collective-permute-start(bf16[1,256,4096]{2,1,0:T(8,128)(2,1)} %grads_ref.3), channel_id=1, source_target_pairs={{0,32},{32,0},{1,33},{33,1},{2,34},{34,2},{3,35},{35,3},{4,36},{36... | collective-permute-start | bytes 6291464 | tf_op jit(solution)/shard_map/ppermute | solution.py:233
  6.9 1.6 copy-start
  10.1 21.1 %collective-permute-start.7 = (bf16[4,16,4096]{2,1,0:T(8,128)(2,1)S(1)}, bf16[4,16,4096]{2,1,0:T(8,128)(2,1)S(1)}, u32[]{:S(2)}, u32[]{:S(2)}) collective-permute-start(bf16[4,16,4096]{2,1,0:T(8,128)(2,1)S(1)} %get-tuple-element.19), channel_id=1, source_target_pairs={{0,64},{32,480},{64,128},{96,32},{128,192},{160,96},{192,256},{224... | collective-permute-start | bytes 1572872 | tf_op jit(solution)/shard_map/ppermute | solution.py:243
  14.4 16.8 %collective-permute-start.8 = (bf16[16,4096]{1,0:T(8,128)(2,1)S(1)}, bf16[16,4096]{1,0:T(8,128)(2,1)S(1)}, u32[]{:S(2)}, u32[]{:S(2)}) collective-permute-start(bf16[16,4096]{1,0:T(8,128)(2,1)S(1)} %get-tuple-element.21), channel_id=1, source_target_pairs={{0,128},{32,416},{64,192},{96,480},{128,256},{160,32},{192,320},{2... | collective-permute-start | bytes 393224 | tf_op jit(solution)/shard_map/ppermute | solution.py:243
  31.8 13.2 %collective-permute-start.9 = (bf16[2,16,4096]{2,1,0:T(8,128)(2,1)S(1)}, bf16[2,16,4096]{2,1,0:T(8,128)(2,1)S(1)}, u32[]{:S(2)}, u32[]{:S(2)}) collective-permute-start(bf16[2,16,4096]{2,1,0:T(8,128)(2,1)S(1)} %shard_map.93), channel_id=1, source_target_pairs={{0,128},{32,416},{64,192},{96,480},{128,256},{160,32},{192,320},{2... | collective-permute-start | bytes 786440 | tf_op jit(solution)/shard_map/ppermute | solution.py:243
  45.6 3.2 %collective-permute-start.10 = (bf16[16,4096]{1,0:T(8,128)(2,1)S(1)}, bf16[16,4096]{1,0:T(8,128)(2,1)S(1)}, u32[]{:S(2)}, u32[]{:S(2)}) collective-permute-start(bf16[16,4096]{1,0:T(8,128)(2,1)S(1)} %shard_map.94), channel_id=1, source_target_pairs={{0,32},{32,0},{1,33},{33,1},{2,34},{34,2},{3,35},{35,3},{4,36},{36... | collective-permute-start | bytes 393224 | tf_op jit(solution)/shard_map/ppermute | solution.py:233
  48.8 8.5 %copy-start.3 = (bf16[2,4,1,16,1024]{4,3,2,1,0:T(8,128)(2,1)S(1)}, bf16[2,4,1,16,1024]{4,3,2,1,0:T(8,128)(2,1)}, u32[]{:S(2)}) copy-start(bf16[2,4,1,16,1024]{4,3,2,1,0:T(8,128)(2,1)} %left_hbm.1) | copy-start | bytes 786436
  48.8 8.5 %copy-start.4 = (bf16[2,4,1,16,1024]{4,3,2,1,0:T(8,128)(2,1)S(1)}, bf16[2,4,1,16,1024]{4,3,2,1,0:T(8,128)(2,1)}, u32[]{:S(2)}) copy-start(bf16[2,4,1,16,1024]{4,3,2,1,0:T(8,128)(2,1)} %right_hbm.1) | copy-start | bytes 786436
  50.7 56.0 %copy-start.5 = (s32[32]{0:T(128)S(1)}, s32[32]{0:T(128)}, u32[]{:S(2)}) copy-start(s32[32]{0:T(128)} %table_ref.1) | copy-start | bytes 388
  50.7 35.3 %all-to-all-start.2 = ((bf16[32,16,1024]{2,1,0:T(8,128)(2,1)}), bf16[32,16,1024]{2,1,0:T(8,128)(2,1)S(1)}, u32[]{:S(2)}, u32[]{:S(2)}) async-start(bf16[32,16,1024]{2,1,0:T(8,128)(2,1)} %shard_map.95), calls=%async_computation.2 | async-start | bytes 2097152 | tf_op jit(solution)/shard_map/all_to_all | solution.py:229
  86.0 20.7 %all-to-all-start = ((bf16[32,2,2,16,128]{4,3,2,1,0:T(8,128)(2,1)}), bf16[32,2,2,16,128]{4,3,2,1,0:T(8,128)(2,1)S(1)}, u32[]{:S(2)}, u32[]{:S(2)}) async-start(bf16[32,2,2,16,128]{4,3,2,1,0:T(8,128)(2,1)} %shard_map.85), calls=%async_computation | async-start | bytes 1048576 | tf_op jit(solution)/shard_map/all_to_all | solution.py:229
  93.2 32.2 %collective-permute-start.11 = (bf16[8,4,16,1024]{3,2,1,0:T(8,128)(2,1)S(1)}, bf16[8,4,16,1024]{3,2,1,0:T(8,128)(2,1)S(1)}, u32[]{:S(2)}, u32[]{:S(2)}) collective-permute-start(bf16[8,4,16,1024]{3,2,1,0:T(8,128)(2,1)S(1)} %bitcast.5), channel_id=1, source_target_pairs={{0,32},{32,0},{1,33},{33,1},{2,34},{34,2},{3,35},{35,3},{4,36},{36... | collective-permute-start | bytes 3145736 | tf_op jit(solution)/shard_map/ppermute | solution.py:233
  123.5 11.2 %collective-permute-start = (bf16[4,16,1024]{2,1,0:T(8,128)(2,1)S(1)}, bf16[4,16,1024]{2,1,0:T(8,128)(2,1)S(1)}, u32[]{:S(2)}, u32[]{:S(2)}) collective-permute-start(bf16[4,16,1024]{2,1,0:T(8,128)(2,1)S(1)} %get-tuple-element.17.mine_ref), channel_id=1, source_target_pairs={{0,32},{32,0},{1,33},{33,1},{2,34},{34,2},{3,35},{35,3},{4,36},{36... | collective-permute-start | bytes 393224 | tf_op jit(solution)/shard_map/ppermute | solution.py:233
  127.9 26.5 %all-to-all-start.3 = ((bf16[32,2,16,128]{3,2,1,0:T(8,128)(2,1)}), bf16[32,2,16,128]{3,2,1,0:T(8,128)(2,1)S(1)}, u32[]{:S(2)}, u32[]{:S(2)}) async-start(bf16[32,2,16,128]{3,2,1,0:T(8,128)(2,1)} %get-tuple-element.28), calls=%async_computation.3 | async-start | bytes 524288 | tf_op jit(solution)/shard_map/all_to_all | solution.py:229
  135.2 12.2 %collective-permute-start.2 = (bf16[2,4,16,1024]{3,2,1,0:T(8,128)(2,1)S(1)}, bf16[2,4,16,1024]{3,2,1,0:T(8,128)(2,1)S(1)}, u32[]{:S(2)}, u32[]{:S(2)}) collective-permute-start(bf16[2,4,16,1024]{3,2,1,0:T(8,128)(2,1)S(1)} %shard_map.88.pair_ref), channel_id=1, source_target_pairs={{0,384},{32,160},{64,448},{96,224},{128,0},{160,288},{192,64},{224... | collective-permute-start | bytes 786440 | tf_op jit(solution)/shard_map/ppermute | solution.py:243
  139.8 26.0 %collective-permute-start.1 = (bf16[2,4,16,1024]{3,2,1,0:T(8,128)(2,1)S(1)}, bf16[2,4,16,1024]{3,2,1,0:T(8,128)(2,1)S(1)}, u32[]{:S(2)}, u32[]{:S(2)}) collective-permute-start(bf16[2,4,16,1024]{3,2,1,0:T(8,128)(2,1)S(1)} %shard_map.88.pair_ref), channel_id=1, source_target_pairs={{0,448},{32,96},{64,0},{96,160},{128,64},{160,224},{192,128},{224,... | collective-permute-start | bytes 786440 | tf_op jit(solution)/shard_map/ppermute | solution.py:243
  147.9 17.8 %collective-permute-start.4 = (bf16[4,16,1024]{2,1,0:T(8,128)(2,1)S(1)}, bf16[4,16,1024]{2,1,0:T(8,128)(2,1)S(1)}, u32[]{:S(2)}, u32[]{:S(2)}) collective-permute-start(bf16[4,16,1024]{2,1,0:T(8,128)(2,1)S(1)} %shard_map.89), channel_id=1, source_target_pairs={{0,384},{32,160},{64,448},{96,224},{128,0},{160,288},{192,64},{224... | collective-permute-start | bytes 393224 | tf_op jit(solution)/shard_map/ppermute | solution.py:243
  152.4 13.3 %collective-permute-start.3 = (bf16[2,4,16,1024]{3,2,1,0:T(8,128)(2,1)S(1)}, bf16[2,4,16,1024]{3,2,1,0:T(8,128)(2,1)S(1)}, u32[]{:S(2)}, u32[]{:S(2)}) collective-permute-start(bf16[2,4,16,1024]{3,2,1,0:T(8,128)(2,1)S(1)} %collective-permute-done.2.in_ref.second_ref), channel_id=1, source_target_pairs={{0,448},{32,96},{64,0},{96,160},{128,64},{160,224},{192,128},{224,... | collective-permute-start | bytes 786440 | tf_op jit(solution)/shard_map/ppermute | solution.py:243
  155.9 31.5 %all-to-all-start.4 = ((bf16[32,2,2,16,128]{4,3,2,1,0:T(8,128)(2,1)}), bf16[32,2,2,16,128]{4,3,2,1,0:T(8,128)(2,1)S(1)}, u32[]{:S(2)}, u32[]{:S(2)}) async-start(bf16[32,2,2,16,128]{4,3,2,1,0:T(8,128)(2,1)} %shard_map.99), calls=%async_computation.4 | async-start | bytes 1048576 | tf_op jit(solution)/shard_map/all_to_all | solution.py:229
  165.7 21.7 %copy-start.1 = (f32[2,4,1,16,1024]{4,3,2,1,0:T(8,128)S(1)}, f32[2,4,1,16,1024]{4,3,2,1,0:T(8,128)}, u32[]{:S(2)}) copy-start(f32[2,4,1,16,1024]{4,3,2,1,0:T(8,128)} %left_ref.1) | copy-start | bytes 1572868
  165.7 21.7 %copy-start.2 = (f32[2,4,1,16,1024]{4,3,2,1,0:T(8,128)S(1)}, f32[2,4,1,16,1024]{4,3,2,1,0:T(8,128)}, u32[]{:S(2)}) copy-start(f32[2,4,1,16,1024]{4,3,2,1,0:T(8,128)} %right_ref.1) | copy-start | bytes 1572868
  165.8 4.5 %collective-permute-start.5 = (bf16[7,4,16,1024]{3,2,1,0:T(8,128)(2,1)S(1)}, bf16[7,4,16,1024]{3,2,1,0:T(8,128)(2,1)S(1)}, u32[]{:S(2)}, u32[]{:S(2)}) collective-permute-start(bf16[7,4,16,1024]{3,2,1,0:T(8,128)(2,1)S(1)} %shard_map.90.mine_ref), channel_id=1, source_target_pairs={{0,32},{32,0},{1,33},{33,1},{2,34},{34,2},{3,35},{35,3},{4,36},{36... | collective-permute-start | bytes 2752520 | tf_op jit(solution)/shard_map/ppermute | solution.py:233
  171.5 10.1 %collective-permute-start.12 = (bf16[16,1024]{1,0:T(8,128)(2,1)S(1)}, bf16[16,1024]{1,0:T(8,128)(2,1)S(1)}, u32[]{:S(2)}, u32[]{:S(2)}) collective-permute-start(bf16[16,1024]{1,0:T(8,128)(2,1)S(1)} %get-tuple-element.25), channel_id=1, source_target_pairs={{0,1},{1,2},{2,3},{3,0},{4,5},{5,6},{6,7},{7,4},{8,9},{9,10},{10,1... | collective-permute-start | bytes 98312 | tf_op jit(solution)/shard_map/ppermute | solution.py:238
  176.7 6.7 %collective-permute-start.13 = (bf16[16,1024]{1,0:T(8,128)(2,1)S(1)}, bf16[16,1024]{1,0:T(8,128)(2,1)S(1)}, u32[]{:S(2)}, u32[]{:S(2)}) collective-permute-start(bf16[16,1024]{1,0:T(8,128)(2,1)S(1)} %get-tuple-element.26), channel_id=1, source_target_pairs={{0,2},{1,3},{2,0},{3,1},{4,6},{5,7},{6,4},{7,5},{8,10},{9,11},{10,... | collective-permute-start | bytes 98312 | tf_op jit(solution)/shard_map/ppermute | solution.py:238
  178.6 7.6 %collective-permute-start.14 = (bf16[16,1024]{1,0:T(8,128)(2,1)S(1)}, bf16[16,1024]{1,0:T(8,128)(2,1)S(1)}, u32[]{:S(2)}, u32[]{:S(2)}) collective-permute-start(bf16[16,1024]{1,0:T(8,128)(2,1)S(1)} %get-tuple-element.27), channel_id=1, source_target_pairs={{0,3},{1,0},{2,1},{3,2},{4,7},{5,4},{6,5},{7,6},{8,11},{9,8},{10,9... | collective-permute-start | bytes 98312 | tf_op jit(solution)/shard_map/ppermute | solution.py:238

commit v8 on v6

--- a/solution.py
+++ b/solution.py
@@ -62,20 +62,23 @@
             right_ref[sub, :, columns] = in_ref[sub * 8 + part, 1]
 
 
-def add_pairs(wanted, grads_ref, theirs_hbm, where_ref, *refs):
+def add_pairs(wanted, grads_hbm, theirs_hbm, where_ref, *refs):
     z, core = where_ref[0], where_ref[1]
-    outs, theirs_ref, sems = refs[:-2], refs[-2], refs[-1]
+    outs, grads_ref, theirs_ref, sems = refs[:-3], *refs[-3:]
     copies = []
     for index, (_, _, k, parity) in enumerate(wanted):
         strip = lax.rem(z + 8 + k * (1 - 2 * core), 8) * 2 + (core if parity is None else parity)
         rows = pl.ds(pl.multiple_of(strip * 16, 16), 16)
-        copy = pltpu.make_async_copy(theirs_hbm.at[0, rows, :], theirs_ref.at[index], sems.at[index])
-        copy.start()
-        copies.append((copy, rows))
+        for source, (hbm, ref) in enumerate(((grads_hbm, grads_ref), (theirs_hbm, theirs_ref))):
+            copy = pltpu.make_async_copy(
+                hbm.at[0, rows, :], ref.at[index], sems.at[2 * index + source]
+            )
+            copy.start()
+            copies.append(copy)
     for index, (out, place_in, _, _) in enumerate(wanted):
-        copy, rows = copies[index]
-        copy.wait()
-        total = grads_ref[0, rows, :].astype(F32) + theirs_ref[index].astype(F32)
+        copies[2 * index].wait()
+        copies[2 * index + 1].wait()
+        total = grads_ref[index].astype(F32) + theirs_ref[index].astype(F32)
         if place_in is None:
             outs[out][...] = total.astype(BF)
         else:
@@ -86,40 +89,33 @@
     return pl.pallas_call(
         functools.partial(add_pairs, wanted),
         out_shape=outs,
-        in_specs=[VM, pl.BlockSpec(memory_space=pltpu.HBM), SM],
+        in_specs=[pl.BlockSpec(memory_space=pltpu.HBM)] * 2 + [SM],
         out_specs=(VM,) * len(outs),
         scratch_shapes=[
             pltpu.VMEM((len(wanted), 16, 4096), BF),
-            pltpu.SemaphoreType.DMA((len(wanted),)),
+            pltpu.VMEM((len(wanted), 16, 4096), BF),
+            pltpu.SemaphoreType.DMA((2 * len(wanted),)),
         ],
-        compiler_params=pltpu.CompilerParams(vmem_limit_bytes=32 * 1024 * 1024),
+        compiler_params=pltpu.CompilerParams(vmem_limit_bytes=65273856),
         cost_estimate=pl.CostEstimate(flops=1000000, bytes_accessed=2097152, transcendentals=0),
     )(grads, theirs, where)
 
 
-def add_passed(two_ref, near_ref, four_ref, where_ref, out_ref):
+def add_other(one_ref, two_ref, three_ref, where_ref, out_ref):
+    parity = 1 - where_ref[1]
+    out_ref[...] = (
+        one_ref[parity].astype(F32) + two_ref[parity].astype(F32) + three_ref[parity].astype(F32)
+    ).astype(BF)
+
+
+def add_replicas(own_ref, one_ref, two_ref, three_ref, four_ref, theirs_ref, where_ref, out_ref):
     core = where_ref[1]
-    for parity in range(2):
-        out_ref[parity] = (two_ref[parity].astype(F32) + near_ref[parity].astype(F32)).astype(BF)
-    out_ref[core] = (
-        two_ref[core].astype(F32) + near_ref[core].astype(F32) + four_ref[...].astype(F32)
-    ).astype(BF)
-
-
-def add_other(near_ref, two_ref, where_ref, out_ref):
-    parity = 1 - where_ref[1]
-    out_ref[...] = (near_ref[2 + parity].astype(F32) + two_ref[parity].astype(F32)).astype(BF)
-
-
-def add_replicas(own_ref, near_ref, two_ref, theirs_ref, where_ref, out_ref):
     for column in range(4):
         columns = slice(column * 1024, column * 1024 + 1024)
-        total = (
-            own_ref[:, columns].astype(F32)
-            + near_ref[2 + where_ref[1], :, columns].astype(F32)
-            + two_ref[where_ref[1], :, columns].astype(F32)
-            + theirs_ref[:, columns].astype(F32)
-        ).astype(BF)
+        total = own_ref[:, columns].astype(F32) + theirs_ref[:, columns].astype(F32)
+        for ref in (one_ref, two_ref, three_ref):
+            total = total + ref[core, :, columns].astype(F32)
+        total = (total + four_ref[:, columns].astype(F32)).astype(BF)
         for z in range(8):
             out_ref[z * 4 + column] = total
 
@@ -245,28 +241,31 @@
 
     theirs = swap(grads)
     strip_shape, both = shape((16, 4096)), shape((2, 16, 4096))
-    four, near = pair_sums(
-        ((0, None, 4, None), (1, 0, 3, 0), (1, 1, 3, 1), (1, 2, 1, 0), (1, 3, 1, 1)),
-        (strip_shape, shape((4, 16, 4096))),
-        grads,
-        theirs,
-        where,
-    )
-    four = around(four, 2)
-    near = around(near, 1)
-    two, own = pair_sums(
-        ((0, 0, 2, 0), (0, 1, 2, 1), (1, None, 0, None)),
+    three, four = pair_sums(
+        ((0, 0, 3, 0), (0, 1, 3, 1), (1, None, 4, None)),
         (both, strip_shape),
         grads,
         theirs,
         where,
     )
-    two = call(add_passed, both, [two, near, four, where], scalars=1)
+    three = around(three, 3)
+    four = around(four, 4)
+    two, one, own = pair_sums(
+        ((0, 0, 2, 0), (0, 1, 2, 1), (1, 0, 1, 0), (1, 1, 1, 1), (2, None, 0, None)),
+        (both, both, strip_shape),
+        grads,
+        theirs,
+        where,
+    )
     two = around(two, 2)
-    other = call(add_other, strip_shape, [near, two, where], scalars=1)
+    one = around(one, 1)
+    other = call(add_other, strip_shape, [one, two, three, where], scalars=1)
     other = swap(other)
     strip = call(
-        add_replicas, shape((32, 16, 1024)), [own, near, two, other, where], scalars=1
+        add_replicas,
+        shape((32, 16, 1024)),
+        [own, one, two, three, four, other, where],
+        scalars=1,
     )
 
     pieces = pl.pallas_call(

time: 189 us -> 195 us (1.032)
  starting transfers between devices: 76.1 us -> 91.1 us
  waiting for transfers between devices: 76.5 us -> 65.9 us
  Pallas kernels: 16.9 us -> 19 us
    ppermute x7 -> x8, starting transfers between devices: 26 us -> 34.4 us  [around(): return lax.ppermute(value, ROWS, pairs)]
    ppermute x7 -> x8, waiting for transfers between devices: 25.5 us -> 17.5 us  [around(): return lax.ppermute(value, ROWS, pairs)]
    all_to_all x4, starting transfers between devices: 30.3 us -> 36.9 us  [exchange(): return lax.all_to_all(value, axes, split_axis=0, concat_axis=0, tiled=True)]
    pallas_call x2, Pallas kernels: 2.87 us -> 5.62 us  [pair_sums(): pl.pallas_call(functools.partial(add_pairs, wanted), out_shape=outs, in_s...]
    pallas_call x13 -> x12, Pallas kernels: 12.1 us -> 11.5 us  [call(): pl.pallas_call(kernel, out_shape=out, in_specs=[VM] * (len(inputs) - scal...]
  transfers between devices with their start and end apart: 19 -> 20, of which waited for: 10 -> 10; matrix products, arithmetic and copies ran while one was open for 0% -> 0% of each run, Pallas kernels for 6% -> 7%
where the time goes in v8:
time: 195 us; the launch traced here: 194 us
  starting transfers between devices  91.1 us (47%)
  waiting for transfers between devices  65.9 us (34%)
  Pallas kernels  19 us (10%)
  blocking collectives  16.2 us (8%)
    all_to_all x4, waiting for transfers between devices, exchange(): return lax.all_to_all(value, axes, split_axis=0, concat_axis=0, tiled=True)  37.6 us
    all_to_all x4, starting transfers between devices, exchange(): return lax.all_to_all(value, axes, split_axis=0, concat_axis=0, tiled=True)  36.9 us
    ppermute x8, starting transfers between devices, around(): return lax.ppermute(value, ROWS, pairs)  34.4 us
    ppermute x8, waiting for transfers between devices, around(): return lax.ppermute(value, ROWS, pairs)  17.5 us
    all_to_all x1, blocking collectives, exchange(): return lax.all_to_all(value, axes, split_axis=0, concat_axis=0, tiled=True)  16.2 us
    pallas_call x12, Pallas kernels, call(): pl.pallas_call(kernel, out_shape=out, in_specs=[VM] * (len(inputs) - scal...  11.5 us
    ppermute x3, starting transfers between devices, shift(): lax.ppermute(value, axis, [(i, (i + distance) % size) for i in range(size)])  10.1 us
    ppermute x5, starting transfers between devices, swap(): return lax.ppermute(value, 'c', [(0, 1), (1, 0)])  9.74 us
  transfers between devices with their start and end apart: 20, of which 10 were waited for; matrix products, arithmetic and copies ran while one was open for 0% of the time, Pallas kernels for 7%

profile of v8, /device:TPU:56, one launch (start us, length us, event | category | flops | bytes accessed | tf_op | source)
XLA Modules:
  0.0 193.9 jit_solution(16618628407941725529)
XLA Ops:
  0.6 1.9 collective-permute-start.6
  2.6 0.6 pad_add_fusion.where_ref.refs_4_
  3.2 3.9 %collective-permute-done.6.theirs_hbm = bf16[1,256,4096]{2,1,0:T(8,128)(2,1)} collective-permute-done((bf16[1,256,4096]{2,1,0:T(8,128)(2,1)}, bf16[1,256,4096]{2,1,0:T(8,128)(2,1)}, u32[]{:S(2)}, u32[]{:S(2)}) %collective-permute-start.6) | collective-permute-done | bytes 2097184 | tf_op jit(solution)/shard_map/ppermute | solution.py:222
  7.0 2.9 %shard_map.91 = (bf16[2,16,4096]{2,1,0:T(8,128)(2,1)}, bf16[2,16,4096]{2,1,0:T(8,128)(2,1)}, bf16[16,4096]{1,0:T(8,128)(2,1)}) custom-call(bf16[1,256,4096]{2,1,0:T(8,128)(2,1)} %grads_hbm.3, bf16[1,256,4096]{2,1,0:T(8,128)(2,1)} %collective-permute-done.6.theirs_hbm, s32[3]{0:T(128)} %pad_add_fusion.where_ref.refs_4_), custom_call_target="tpu_custom_call" | custom-call | flops 1000000 | bytes 2097152 | tf_op jit(solution)/shard_map/pallas_call | solution.py:89
  10.0 4.3 %collective-permute-start.7 = (bf16[2,16,4096]{2,1,0:T(8,128)(2,1)}, bf16[2,16,4096]{2,1,0:T(8,128)(2,1)S(1)}, u32[]{:S(2)}, u32[]{:S(2)}) collective-permute-start(bf16[2,16,4096]{2,1,0:T(8,128)(2,1)} %get-tuple-element.20), channel_id=1, source_target_pairs={{0,64},{32,480},{64,128},{96,32},{128,192},{160,96},{192,256},{224... | collective-permute-start | bytes 786440 | tf_op jit(solution)/shard_map/ppermute | solution.py:232
  14.3 0.0 copy-start.2
  14.3 6.2 %collective-permute-start.8 = (bf16[2,16,4096]{2,1,0:T(8,128)(2,1)}, bf16[2,16,4096]{2,1,0:T(8,128)(2,1)S(1)}, u32[]{:S(2)}, u32[]{:S(2)}) collective-permute-start(bf16[2,16,4096]{2,1,0:T(8,128)(2,1)} %get-tuple-element.21), channel_id=1, source_target_pairs={{0,128},{32,416},{64,192},{96,480},{128,256},{160,32},{192,320},{2... | collective-permute-start | bytes 786440 | tf_op jit(solution)/shard_map/ppermute | solution.py:232
  20.5 2.7 %shard_map.92 = (bf16[2,16,4096]{2,1,0:T(8,128)(2,1)}, bf16[16,4096]{1,0:T(8,128)(2,1)}) custom-call(bf16[1,256,4096]{2,1,0:T(8,128)(2,1)} %grads_hbm.3, bf16[1,256,4096]{2,1,0:T(8,128)(2,1)} %collective-permute-done.6.theirs_hbm, s32[3]{0:T(128)} %pad_add_fusion.where_ref.refs_4_), custom_call_target="tpu_custom_call" | custom-call | flops 1000000 | bytes 2097152 | tf_op jit(solution)/shard_map/pallas_call | solution.py:89
  23.2 7.3 %collective-permute-start.9 = (bf16[2,16,4096]{2,1,0:T(8,128)(2,1)}, bf16[2,16,4096]{2,1,0:T(8,128)(2,1)S(1)}, u32[]{:S(2)}, u32[]{:S(2)}) collective-permute-start(bf16[2,16,4096]{2,1,0:T(8,128)(2,1)} %get-tuple-element.22), channel_id=1, source_target_pairs={{0,192},{32,352},{64,256},{96,416},{128,320},{160,480},{192,384},{... | collective-permute-start | bytes 786440 | tf_op jit(solution)/shard_map/ppermute | solution.py:232
  30.5 2.8 %collective-permute-start.10 = (bf16[16,4096]{1,0:T(8,128)(2,1)}, bf16[16,4096]{1,0:T(8,128)(2,1)S(1)}, u32[]{:S(2)}, u32[]{:S(2)}) collective-permute-start(bf16[16,4096]{1,0:T(8,128)(2,1)} %get-tuple-element.23), channel_id=1, source_target_pairs={{0,256},{32,288},{64,320},{96,352},{128,384},{160,416},{192,448},{... | collective-permute-start | bytes 393224 | tf_op jit(solution)/shard_map/ppermute | solution.py:232
  33.4 0.7 collective-permute-done.8.two_ref
  34.1 9.8 %collective-permute-done.9.three_ref = bf16[2,16,4096]{2,1,0:T(8,128)(2,1)S(1)} collective-permute-done((bf16[2,16,4096]{2,1,0:T(8,128)(2,1)}, bf16[2,16,4096]{2,1,0:T(8,128)(2,1)S(1)}, u32[]{:S(2)}, u32[]{:S(2)}) %collective-permute-start.9) | collective-permute-done | bytes 262176 | tf_op jit(solution)/shard_map/ppermute | solution.py:232
  43.9 0.6 shard_map.93
  44.5 1.9 collective-permute-start.11
  46.5 1.8 collective-permute-done.10.four_ref
  48.3 1.6 shard_map.94
  49.9 12.6 %all-to-all-start.2 = ((bf16[32,16,1024]{2,1,0:T(8,128)(2,1)}), bf16[32,16,1024]{2,1,0:T(8,128)(2,1)S(1)}, u32[]{:S(2)}, u32[]{:S(2)}) async-start(bf16[32,16,1024]{2,1,0:T(8,128)(2,1)} %shard_map.94), calls=%async_computation.2 | async-start | bytes 2097152 | tf_op jit(solution)/shard_map/all_to_all | solution.py:218
  62.6 1.9 shard_map.85
  64.5 25.8 %all-to-all-done.2 = bf16[32,16,1024]{2,1,0:T(8,128)(2,1)S(1)} async-done(((bf16[32,16,1024]{2,1,0:T(8,128)(2,1)}), bf16[32,16,1024]{2,1,0:T(8,128)(2,1)S(1)}, u32[]{:S(2)}, u32[]{:S(2)}) %all-to-all-start.2) | async-done | bytes 1048608 | tf_op jit(solution)/shard_map/all_to_all | solution.py:218
  90.3 7.8 %all-to-all-start = ((bf16[32,2,2,16,128]{4,3,2,1,0:T(8,128)(2,1)}), bf16[32,2,2,16,128]{4,3,2,1,0:T(8,128)(2,1)S(1)}, u32[]{:S(2)}, u32[]{:S(2)}) async-start(bf16[32,2,2,16,128]{4,3,2,1,0:T(8,128)(2,1)} %shard_map.85), calls=%async_computation | async-start | bytes 1048576 | tf_op jit(solution)/shard_map/all_to_all | solution.py:218
  98.1 1.9 collective-permute-start.12
  100.0 11.8 %all-to-all-done = bf16[32,2,2,16,128]{4,3,2,1,0:T(8,128)(2,1)S(1)} async-done(((bf16[32,2,2,16,128]{4,3,2,1,0:T(8,128)(2,1)}), bf16[32,2,2,16,128]{4,3,2,1,0:T(8,128)(2,1)S(1)}, u32[]{:S(2)}, u32[]{:S(2)}) %all-to-all-start) | async-done | bytes 524320 | tf_op jit(solution)/shard_map/all_to_all | solution.py:218
  111.8 0.6 shard_map.86
  112.4 16.2 %all_to_all.25.in_ref = bf16[32,2,16,128]{3,2,1,0:T(8,128)(2,1)S(1)} all-to-all(bf16[32,2,16,128]{3,2,1,0:T(8,128)(2,1)S(1)} %shard_map.86), channel_id=1, replica_groups=mesh['z'=8,'c'=2,'x'=4,'yh'=2,'yl'=4] {'x','yh','yl'}, dimensions={0} | all-to-all | bytes 524288 | tf_op jit(solution)/shard_map/all_to_all | solution.py:218
  128.6 1.9 collective-permute-start
  130.6 2.5 %shard_map.95 = (bf16[32,2,16,128]{3,2,1,0:T(8,128)(2,1)}, bf16[64,1024]{1,0:T(8,128)(2,1)S(1)}) custom-call(bf16[8,4,16,1024]{3,2,1,0:T(8,128)(2,1)S(1)} %bitcast.6, bf16[8,4,16,1024]{3,2,1,0:T(8,128)(2,1)S(1)} %collective-permute-done.12.other_ref, bf16[4,16,1024]{2,1,0:T(8,128)(2,1)S(1)} %get-tuple-element.24.left_ref, s32[3]{0:T(128)S(1)} %copy-done.3), custom_call_target="tpu_custom_call" | custom-call | flops 536870912 | bytes 2228236 | tf_op jit(solution)/shard_map/pallas_call | solution.py:21
  133.1 6.6 %all-to-all-start.3 = ((bf16[32,2,16,128]{3,2,1,0:T(8,128)(2,1)}), bf16[32,2,16,128]{3,2,1,0:T(8,128)(2,1)S(1)}, u32[]{:S(2)}, u32[]{:S(2)}) async-start(bf16[32,2,16,128]{3,2,1,0:T(8,128)(2,1)} %get-tuple-element.30), calls=%async_computation.3 | async-start | bytes 524288 | tf_op jit(solution)/shard_map/all_to_all | solution.py:218
  139.7 0.6 shard_map.88.pair_ref
  140.3 4.6 %collective-permute-start.2 = (bf16[2,4,16,1024]{3,2,1,0:T(8,128)(2,1)S(1)}, bf16[2,4,16,1024]{3,2,1,0:T(8,128)(2,1)S(1)}, u32[]{:S(2)}, u32[]{:S(2)}) collective-permute-start(bf16[2,4,16,1024]{3,2,1,0:T(8,128)(2,1)S(1)} %shard_map.88.pair_ref), channel_id=1, source_target_pairs={{0,384},{32,160},{64,448},{96,224},{128,0},{160,288},{192,64},{224... | collective-permute-start | bytes 786440 | tf_op jit(solution)/shard_map/ppermute | solution.py:232
  144.9 0.1 select_reduce_fusion
  145.0 2.3 %collective-permute-start.1 = (bf16[2,4,16,1024]{3,2,1,0:T(8,128)(2,1)S(1)}, bf16[2,4,16,1024]{3,2,1,0:T(8,128)(2,1)S(1)}, u32[]{:S(2)}, u32[]{:S(2)}) collective-permute-start(bf16[2,4,16,1024]{3,2,1,0:T(8,128)(2,1)S(1)} %shard_map.88.pair_ref), channel_id=1, source_target_pairs={{0,448},{32,96},{64,0},{96,160},{128,64},{160,224},{192,128},{224,... | collective-permute-start | bytes 786440 | tf_op jit(solution)/shard_map/ppermute | solution.py:232
  147.4 5.0 %collective-permute-done.2.in_ref.second_ref = bf16[2,4,16,1024]{3,2,1,0:T(8,128)(2,1)S(1)} collective-permute-done((bf16[2,4,16,1024]{3,2,1,0:T(8,128)(2,1)S(1)}, bf16[2,4,16,1024]{3,2,1,0:T(8,128)(2,1)S(1)}, u32[]{:S(2)}, u32[]{:S(2)}) %collective-permute-start.2) | collective-permute-done | bytes 262176 | tf_op jit(solution)/shard_map/ppermute | solution.py:232
  152.4 0.6 shard_map.89
  153.0 4.9 %collective-permute-start.4 = (bf16[4,16,1024]{2,1,0:T(8,128)(2,1)S(1)}, bf16[4,16,1024]{2,1,0:T(8,128)(2,1)S(1)}, u32[]{:S(2)}, u32[]{:S(2)}) collective-permute-start(bf16[4,16,1024]{2,1,0:T(8,128)(2,1)S(1)} %shard_map.89), channel_id=1, source_target_pairs={{0,384},{32,160},{64,448},{96,224},{128,0},{160,288},{192,64},{224... | collective-permute-start | bytes 393224 | tf_op jit(solution)/shard_map/ppermute | solution.py:232
  157.8 1.9 collective-permute-start.3
  159.8 1.5 shard_map.98
  161.3 9.8 %all-to-all-start.4 = ((bf16[32,2,2,16,128]{4,3,2,1,0:T(8,128)(2,1)}), bf16[32,2,2,16,128]{4,3,2,1,0:T(8,128)(2,1)S(1)}, u32[]{:S(2)}, u32[]{:S(2)}) async-start(bf16[32,2,2,16,128]{4,3,2,1,0:T(8,128)(2,1)} %shard_map.98), calls=%async_computation.4 | async-start | bytes 1048576 | tf_op jit(solution)/shard_map/all_to_all | solution.py:218
  171.2 0.1 shard_map.90.mine_ref
  171.2 2.1 %collective-permute-start.5 = (bf16[7,4,16,1024]{3,2,1,0:T(8,128)(2,1)S(1)}, bf16[7,4,16,1024]{3,2,1,0:T(8,128)(2,1)S(1)}, u32[]{:S(2)}, u32[]{:S(2)}) collective-permute-start(bf16[7,4,16,1024]{3,2,1,0:T(8,128)(2,1)S(1)} %shard_map.90.mine_ref), channel_id=1, source_target_pairs={{0,32},{32,0},{1,33},{33,1},{2,34},{34,2},{3,35},{35,3},{4,36},{36... | collective-permute-start | bytes 2752520 | tf_op jit(solution)/shard_map/ppermute | solution.py:222
  173.3 2.4 %collective-permute-done.5.other_ref = bf16[7,4,16,1024]{3,2,1,0:T(8,128)(2,1)S(1)} collective-permute-done((bf16[7,4,16,1024]{3,2,1,0:T(8,128)(2,1)S(1)}, bf16[7,4,16,1024]{3,2,1,0:T(8,128)(2,1)S(1)}, u32[]{:S(2)}, u32[]{:S(2)}) %collective-permute-start.5) | collective-permute-done | bytes 917536 | tf_op jit(solution)/shard_map/ppermute | solution.py:222
  175.7 1.2 shard_map.96
  176.9 5.2 %collective-permute-start.13 = (bf16[16,1024]{1,0:T(8,128)(2,1)S(1)}, bf16[16,1024]{1,0:T(8,128)(2,1)S(1)}, u32[]{:S(2)}, u32[]{:S(2)}) collective-permute-start(bf16[16,1024]{1,0:T(8,128)(2,1)S(1)} %get-tuple-element.27), channel_id=1, source_target_pairs={{0,1},{1,2},{2,3},{3,0},{4,5},{5,6},{6,7},{7,4},{8,9},{9,10},{10,1... | collective-permute-start | bytes 98312 | tf_op jit(solution)/shard_map/ppermute | solution.py:227
  182.1 1.9 collective-permute-start.14
  184.0 3.0 %collective-permute-start.15 = (bf16[16,1024]{1,0:T(8,128)(2,1)S(1)}, bf16[16,1024]{1,0:T(8,128)(2,1)S(1)}, u32[]{:S(2)}, u32[]{:S(2)}) collective-permute-start(bf16[16,1024]{1,0:T(8,128)(2,1)S(1)} %get-tuple-element.29), channel_id=1, source_target_pairs={{0,3},{1,0},{2,1},{3,2},{4,7},{5,4},{6,5},{7,6},{8,11},{9,8},{10,9... | collective-permute-start | bytes 98312 | tf_op jit(solution)/shard_map/ppermute | solution.py:227
  187.1 1.7 collective-permute-done.14.refs_2_
  188.8 2.8 %collective-permute-done.15.refs_3_ = bf16[16,1024]{1,0:T(8,128)(2,1)S(1)} collective-permute-done((bf16[16,1024]{1,0:T(8,128)(2,1)S(1)}, bf16[16,1024]{1,0:T(8,128)(2,1)S(1)}, u32[]{:S(2)}, u32[]{:S(2)}) %collective-permute-start.15) | collective-permute-done | bytes 32800 | tf_op jit(solution)/shard_map/ppermute | solution.py:227
  191.6 1.2 shard_map.97
  192.8 1.1 shard_map.99
  (22 shorter events, 0.1 us)
Async XLA Ops:
  0.6 6.4 %collective-permute-start.6 = (bf16[1,256,4096]{2,1,0:T(8,128)(2,1)}, bf16[1,256,4096]{2,1,0:T(8,128)(2,1)}, u32[]{:S(2)}, u32[]{:S(2)}) collective-permute-start(bf16[1,256,4096]{2,1,0:T(8,128)(2,1)} %grads_hbm.3), channel_id=1, source_target_pairs={{0,32},{32,0},{1,33},{33,1},{2,34},{34,2},{3,35},{35,3},{4,36},{36... | collective-permute-start | bytes 6291464 | tf_op jit(solution)/shard_map/ppermute | solution.py:222
  10.0 23.4 %collective-permute-start.7 = (bf16[2,16,4096]{2,1,0:T(8,128)(2,1)}, bf16[2,16,4096]{2,1,0:T(8,128)(2,1)S(1)}, u32[]{:S(2)}, u32[]{:S(2)}) collective-permute-start(bf16[2,16,4096]{2,1,0:T(8,128)(2,1)} %get-tuple-element.20), channel_id=1, source_target_pairs={{0,64},{32,480},{64,128},{96,32},{128,192},{160,96},{192,256},{224... | collective-permute-start | bytes 786440 | tf_op jit(solution)/shard_map/ppermute | solution.py:232
  14.3 29.7 %copy-start.3 = (s32[3]{0:T(128)S(1)}, s32[3]{0:T(128)}, u32[]{:S(2)}) copy-start(s32[3]{0:T(128)} %pad_add_fusion.where_ref.refs_4_) | copy-start | bytes 40
  14.3 34.0 %copy-start.2 = (bf16[16,4096]{1,0:T(8,128)(2,1)S(1)}, bf16[16,4096]{1,0:T(8,128)(2,1)}, u32[]{:S(2)}) copy-start(bf16[16,4096]{1,0:T(8,128)(2,1)} %get-tuple-element.19.own_ref) | copy-start | bytes 393220
  14.3 19.8 %collective-permute-start.8 = (bf16[2,16,4096]{2,1,0:T(8,128)(2,1)}, bf16[2,16,4096]{2,1,0:T(8,128)(2,1)S(1)}, u32[]{:S(2)}, u32[]{:S(2)}) collective-permute-start(bf16[2,16,4096]{2,1,0:T(8,128)(2,1)} %get-tuple-element.21), channel_id=1, source_target_pairs={{0,128},{32,416},{64,192},{96,480},{128,256},{160,32},{192,320},{2... | collective-permute-start | bytes 786440 | tf_op jit(solution)/shard_map/ppermute | solution.py:232
  23.2 20.7 %collective-permute-start.9 = (bf16[2,16,4096]{2,1,0:T(8,128)(2,1)}, bf16[2,16,4096]{2,1,0:T(8,128)(2,1)S(1)}, u32[]{:S(2)}, u32[]{:S(2)}) collective-permute-start(bf16[2,16,4096]{2,1,0:T(8,128)(2,1)} %get-tuple-element.22), channel_id=1, source_target_pairs={{0,192},{32,352},{64,256},{96,416},{128,320},{160,480},{192,384},{... | collective-permute-start | bytes 786440 | tf_op jit(solution)/shard_map/ppermute | solution.py:232
  30.5 17.8 %collective-permute-start.10 = (bf16[16,4096]{1,0:T(8,128)(2,1)}, bf16[16,4096]{1,0:T(8,128)(2,1)S(1)}, u32[]{:S(2)}, u32[]{:S(2)}) collective-permute-start(bf16[16,4096]{1,0:T(8,128)(2,1)} %get-tuple-element.23), channel_id=1, source_target_pairs={{0,256},{32,288},{64,320},{96,352},{128,384},{160,416},{192,448},{... | collective-permute-start | bytes 393224 | tf_op jit(solution)/shard_map/ppermute | solution.py:232
  44.5 3.8 %collective-permute-start.11 = (bf16[16,4096]{1,0:T(8,128)(2,1)S(1)}, bf16[16,4096]{1,0:T(8,128)(2,1)S(1)}, u32[]{:S(2)}, u32[]{:S(2)}) collective-permute-start(bf16[16,4096]{1,0:T(8,128)(2,1)S(1)} %shard_map.93), channel_id=1, source_target_pairs={{0,32},{32,0},{1,33},{33,1},{2,34},{34,2},{3,35},{35,3},{4,36},{36... | collective-permute-start | bytes 393224 | tf_op jit(solution)/shard_map/ppermute | solution.py:222
  49.9 61.9 %copy-start.4 = (s32[32]{0:T(128)S(1)}, s32[32]{0:T(128)}, u32[]{:S(2)}) copy-start(s32[32]{0:T(128)} %table_ref.1) | copy-start | bytes 388
  49.9 40.3 %all-to-all-start.2 = ((bf16[32,16,1024]{2,1,0:T(8,128)(2,1)}), bf16[32,16,1024]{2,1,0:T(8,128)(2,1)S(1)}, u32[]{:S(2)}, u32[]{:S(2)}) async-start(bf16[32,16,1024]{2,1,0:T(8,128)(2,1)} %shard_map.94), calls=%async_computation.2 | async-start | bytes 2097152 | tf_op jit(solution)/shard_map/all_to_all | solution.py:218
  90.3 21.5 %all-to-all-start = ((bf16[32,2,2,16,128]{4,3,2,1,0:T(8,128)(2,1)}), bf16[32,2,2,16,128]{4,3,2,1,0:T(8,128)(2,1)S(1)}, u32[]{:S(2)}, u32[]{:S(2)}) async-start(bf16[32,2,2,16,128]{4,3,2,1,0:T(8,128)(2,1)} %shard_map.85), calls=%async_computation | async-start | bytes 1048576 | tf_op jit(solution)/shard_map/all_to_all | solution.py:218
  98.1 32.5 %collective-permute-start.12 = (bf16[8,4,16,1024]{3,2,1,0:T(8,128)(2,1)S(1)}, bf16[8,4,16,1024]{3,2,1,0:T(8,128)(2,1)S(1)}, u32[]{:S(2)}, u32[]{:S(2)}) collective-permute-start(bf16[8,4,16,1024]{3,2,1,0:T(8,128)(2,1)S(1)} %bitcast.5), channel_id=1, source_target_pairs={{0,32},{32,0},{1,33},{33,1},{2,34},{34,2},{3,35},{35,3},{4,36},{36... | collective-permute-start | bytes 3145736 | tf_op jit(solution)/shard_map/ppermute | solution.py:222
  128.6 11.1 %collective-permute-start = (bf16[4,16,1024]{2,1,0:T(8,128)(2,1)S(1)}, bf16[4,16,1024]{2,1,0:T(8,128)(2,1)S(1)}, u32[]{:S(2)}, u32[]{:S(2)}) collective-permute-start(bf16[4,16,1024]{2,1,0:T(8,128)(2,1)S(1)} %get-tuple-element.18.mine_ref), channel_id=1, source_target_pairs={{0,32},{32,0},{1,33},{33,1},{2,34},{34,2},{3,35},{35,3},{4,36},{36... | collective-permute-start | bytes 393224 | tf_op jit(solution)/shard_map/ppermute | solution.py:222
  133.1 26.7 %all-to-all-start.3 = ((bf16[32,2,16,128]{3,2,1,0:T(8,128)(2,1)}), bf16[32,2,16,128]{3,2,1,0:T(8,128)(2,1)S(1)}, u32[]{:S(2)}, u32[]{:S(2)}) async-start(bf16[32,2,16,128]{3,2,1,0:T(8,128)(2,1)} %get-tuple-element.30), calls=%async_computation.3 | async-start | bytes 524288 | tf_op jit(solution)/shard_map/all_to_all | solution.py:218
  140.3 12.1 %collective-permute-start.2 = (bf16[2,4,16,1024]{3,2,1,0:T(8,128)(2,1)S(1)}, bf16[2,4,16,1024]{3,2,1,0:T(8,128)(2,1)S(1)}, u32[]{:S(2)}, u32[]{:S(2)}) collective-permute-start(bf16[2,4,16,1024]{3,2,1,0:T(8,128)(2,1)S(1)} %shard_map.88.pair_ref), channel_id=1, source_target_pairs={{0,384},{32,160},{64,448},{96,224},{128,0},{160,288},{192,64},{224... | collective-permute-start | bytes 786440 | tf_op jit(solution)/shard_map/ppermute | solution.py:232
  145.0 26.1 %collective-permute-start.1 = (bf16[2,4,16,1024]{3,2,1,0:T(8,128)(2,1)S(1)}, bf16[2,4,16,1024]{3,2,1,0:T(8,128)(2,1)S(1)}, u32[]{:S(2)}, u32[]{:S(2)}) collective-permute-start(bf16[2,4,16,1024]{3,2,1,0:T(8,128)(2,1)S(1)} %shard_map.88.pair_ref), channel_id=1, source_target_pairs={{0,448},{32,96},{64,0},{96,160},{128,64},{160,224},{192,128},{224,... | collective-permute-start | bytes 786440 | tf_op jit(solution)/shard_map/ppermute | solution.py:232
  153.0 18.2 %collective-permute-start.4 = (bf16[4,16,1024]{2,1,0:T(8,128)(2,1)S(1)}, bf16[4,16,1024]{2,1,0:T(8,128)(2,1)S(1)}, u32[]{:S(2)}, u32[]{:S(2)}) collective-permute-start(bf16[4,16,1024]{2,1,0:T(8,128)(2,1)S(1)} %shard_map.89), channel_id=1, source_target_pairs={{0,384},{32,160},{64,448},{96,224},{128,0},{160,288},{192,64},{224... | collective-permute-start | bytes 393224 | tf_op jit(solution)/shard_map/ppermute | solution.py:232
  157.8 13.3 %collective-permute-start.3 = (bf16[2,4,16,1024]{3,2,1,0:T(8,128)(2,1)S(1)}, bf16[2,4,16,1024]{3,2,1,0:T(8,128)(2,1)S(1)}, u32[]{:S(2)}, u32[]{:S(2)}) collective-permute-start(bf16[2,4,16,1024]{3,2,1,0:T(8,128)(2,1)S(1)} %collective-permute-done.2.in_ref.second_ref), channel_id=1, source_target_pairs={{0,448},{32,96},{64,0},{96,160},{128,64},{160,224},{192,128},{224,... | collective-permute-start | bytes 786440 | tf_op jit(solution)/shard_map/ppermute | solution.py:232
  161.3 31.5 %all-to-all-start.4 = ((bf16[32,2,2,16,128]{4,3,2,1,0:T(8,128)(2,1)}), bf16[32,2,2,16,128]{4,3,2,1,0:T(8,128)(2,1)S(1)}, u32[]{:S(2)}, u32[]{:S(2)}) async-start(bf16[32,2,2,16,128]{4,3,2,1,0:T(8,128)(2,1)} %shard_map.98), calls=%async_computation.4 | async-start | bytes 1048576 | tf_op jit(solution)/shard_map/all_to_all | solution.py:218
  171.1 21.7 %copy-start = (f32[2,4,1,16,1024]{4,3,2,1,0:T(8,128)S(1)}, f32[2,4,1,16,1024]{4,3,2,1,0:T(8,128)}, u32[]{:S(2)}) copy-start(f32[2,4,1,16,1024]{4,3,2,1,0:T(8,128)} %left_ref.1) | copy-start | bytes 1572868
  171.1 21.7 %copy-start.1 = (f32[2,4,1,16,1024]{4,3,2,1,0:T(8,128)S(1)}, f32[2,4,1,16,1024]{4,3,2,1,0:T(8,128)}, u32[]{:S(2)}) copy-start(f32[2,4,1,16,1024]{4,3,2,1,0:T(8,128)} %right_ref.1) | copy-start | bytes 1572868
  171.2 4.5 %collective-permute-start.5 = (bf16[7,4,16,1024]{3,2,1,0:T(8,128)(2,1)S(1)}, bf16[7,4,16,1024]{3,2,1,0:T(8,128)(2,1)S(1)}, u32[]{:S(2)}, u32[]{:S(2)}) collective-permute-start(bf16[7,4,16,1024]{3,2,1,0:T(8,128)(2,1)S(1)} %shard_map.90.mine_ref), channel_id=1, source_target_pairs={{0,32},{32,0},{1,33},{33,1},{2,34},{34,2},{3,35},{35,3},{4,36},{36... | collective-permute-start | bytes 2752520 | tf_op jit(solution)/shard_map/ppermute | solution.py:222
  176.9 10.1 %collective-permute-start.13 = (bf16[16,1024]{1,0:T(8,128)(2,1)S(1)}, bf16[16,1024]{1,0:T(8,128)(2,1)S(1)}, u32[]{:S(2)}, u32[]{:S(2)}) collective-permute-start(bf16[16,1024]{1,0:T(8,128)(2,1)S(1)} %get-tuple-element.27), channel_id=1, source_target_pairs={{0,1},{1,2},{2,3},{3,0},{4,5},{5,6},{6,7},{7,4},{8,9},{9,10},{10,1... | collective-permute-start | bytes 98312 | tf_op jit(solution)/shard_map/ppermute | solution.py:227
  182.1 6.7 %collective-permute-start.14 = (bf16[16,1024]{1,0:T(8,128)(2,1)S(1)}, bf16[16,1024]{1,0:T(8,128)(2,1)S(1)}, u32[]{:S(2)}, u32[]{:S(2)}) collective-permute-start(bf16[16,1024]{1,0:T(8,128)(2,1)S(1)} %get-tuple-element.28), channel_id=1, source_target_pairs={{0,2},{1,3},{2,0},{3,1},{4,6},{5,7},{6,4},{7,5},{8,10},{9,11},{10,... | collective-permute-start | bytes 98312 | tf_op jit(solution)/shard_map/ppermute | solution.py:227
  184.0 7.6 %collective-permute-start.15 = (bf16[16,1024]{1,0:T(8,128)(2,1)S(1)}, bf16[16,1024]{1,0:T(8,128)(2,1)S(1)}, u32[]{:S(2)}, u32[]{:S(2)}) collective-permute-start(bf16[16,1024]{1,0:T(8,128)(2,1)S(1)} %get-tuple-element.29), channel_id=1, source_target_pairs={{0,3},{1,0},{2,1},{3,2},{4,7},{5,4},{6,5},{7,6},{8,11},{9,8},{10,9... | collective-permute-start | bytes 98312 | tf_op jit(solution)/shard_map/ppermute | solution.py:227

commit v9 on v8

--- a/solution.py
+++ b/solution.py
@@ -62,23 +62,20 @@
             right_ref[sub, :, columns] = in_ref[sub * 8 + part, 1]
 
 
-def add_pairs(wanted, grads_hbm, theirs_hbm, where_ref, *refs):
+def add_pairs(wanted, grads_ref, theirs_hbm, where_ref, *refs):
     z, core = where_ref[0], where_ref[1]
-    outs, grads_ref, theirs_ref, sems = refs[:-3], *refs[-3:]
+    outs, theirs_ref, sems = refs[:-2], refs[-2], refs[-1]
     copies = []
     for index, (_, _, k, parity) in enumerate(wanted):
         strip = lax.rem(z + 8 + k * (1 - 2 * core), 8) * 2 + (core if parity is None else parity)
         rows = pl.ds(pl.multiple_of(strip * 16, 16), 16)
-        for source, (hbm, ref) in enumerate(((grads_hbm, grads_ref), (theirs_hbm, theirs_ref))):
-            copy = pltpu.make_async_copy(
-                hbm.at[0, rows, :], ref.at[index], sems.at[2 * index + source]
-            )
-            copy.start()
-            copies.append(copy)
+        copy = pltpu.make_async_copy(theirs_hbm.at[0, rows, :], theirs_ref.at[index], sems.at[index])
+        copy.start()
+        copies.append((copy, rows))
     for index, (out, place_in, _, _) in enumerate(wanted):
-        copies[2 * index].wait()
-        copies[2 * index + 1].wait()
-        total = grads_ref[index].astype(F32) + theirs_ref[index].astype(F32)
+        copy, rows = copies[index]
+        copy.wait()
+        total = grads_ref[0, rows, :].astype(F32) + theirs_ref[index].astype(F32)
         if place_in is None:
             outs[out][...] = total.astype(BF)
         else:
@@ -89,14 +86,13 @@
     return pl.pallas_call(
         functools.partial(add_pairs, wanted),
         out_shape=outs,
-        in_specs=[pl.BlockSpec(memory_space=pltpu.HBM)] * 2 + [SM],
+        in_specs=[VM, pl.BlockSpec(memory_space=pltpu.HBM), SM],
         out_specs=(VM,) * len(outs),
         scratch_shapes=[
             pltpu.VMEM((len(wanted), 16, 4096), BF),
-            pltpu.VMEM((len(wanted), 16, 4096), BF),
-            pltpu.SemaphoreType.DMA((2 * len(wanted),)),
+            pltpu.SemaphoreType.DMA((len(wanted),)),
         ],
-        compiler_params=pltpu.CompilerParams(vmem_limit_bytes=65273856),
+        compiler_params=pltpu.CompilerParams(vmem_limit_bytes=32 * 1024 * 1024),
         cost_estimate=pl.CostEstimate(flops=1000000, bytes_accessed=2097152, transcendentals=0),
     )(grads, theirs, where)
 
@@ -179,15 +175,18 @@
     out_ref[1 - where_ref[1]] = other_ref[...]
 
 
-def take_parity(in_ref, where_ref, out_ref):
-    out_ref[...] = in_ref[where_ref[1]]
-
-
-def stack_rows(first_ref, second_ref, third_ref, last_ref, out_ref):
-    for hop, ref in enumerate((first_ref, second_ref, third_ref)):
-        out_ref[2 * hop] = ref[0]
-        out_ref[2 * hop + 1] = ref[1]
-    out_ref[6] = last_ref[...]
+def pick_relay(first_ref, third_ref, where_ref, out_ref):
+    out_ref[0] = first_ref[0]
+    out_ref[1] = first_ref[1]
+    out_ref[2] = third_ref[where_ref[1]]
+
+
+def stack_rows(first_ref, relayed_ref, third_ref, out_ref):
+    for parity in range(2):
+        out_ref[parity] = first_ref[parity]
+        out_ref[2 + parity] = relayed_ref[parity]
+        out_ref[4 + parity] = third_ref[parity]
+    out_ref[6] = relayed_ref[2]
 
 
 def right_product(pair_ref, mine_ref, other_ref, mixed_ref, where_ref, *refs):
@@ -309,12 +308,11 @@
     pair = call(
         pair_up, shape((2, 4, 16, 1024)), [right_rows, theirs, where], scalars=1
     )
-    second = around(pair, -2)
+    third = around(pair, -3)
     first = around(pair, -1)
-    half = call(take_parity, shape((4, 16, 1024)), [second, where], scalars=1)
-    third = around(second, -1)
-    last = around(half, -2)
-    right_mine = call(stack_rows, shape((7, 4, 16, 1024)), [first, second, third, last])
+    relay = call(pick_relay, shape((3, 4, 16, 1024)), [first, third, where], scalars=1)
+    relay = around(relay, -1)
+    right_mine = call(stack_rows, shape((7, 4, 16, 1024)), [first, relay, third])
     right_other = swap(right_mine)
     result = call(
         right_product,

time: 195 us -> 186 us (0.954)
  starting transfers between devices: 91.1 us -> 84.5 us
  Pallas kernels: 19 us -> 16.2 us
    ppermute x8 -> x7, waiting for transfers between devices: 17.5 us -> 11.7 us  [around(): return lax.ppermute(value, ROWS, pairs)]
    all_to_all x4, starting transfers between devices: 36.9 us -> 32.3 us  [exchange(): return lax.all_to_all(value, axes, split_axis=0, concat_axis=0, tiled=True)]
    all_to_all x4, waiting for transfers between devices: 37.6 us -> 41 us  [exchange(): return lax.all_to_all(value, axes, split_axis=0, concat_axis=0, tiled=True)]
    pallas_call x2, Pallas kernels: 5.62 us -> 2.81 us  [pair_sums(): pl.pallas_call(functools.partial(add_pairs, wanted), out_shape=outs, in_s...]
    ppermute x8 -> x7, starting transfers between devices: 34.4 us -> 32.3 us  [around(): return lax.ppermute(value, ROWS, pairs)]
    ppermute x5, waiting for transfers between devices: 6.31 us -> 8.26 us  [swap(): return lax.ppermute(value, 'c', [(0, 1), (1, 0)])]
  transfers between devices with their start and end apart: 20 -> 19, of which waited for: 10 -> 12; matrix products, arithmetic and copies ran while one was open for 0% -> 0% of each run, Pallas kernels for 7% -> 6%
where the time goes in v9:
time: 186 us; the launch traced here: 185 us
  starting transfers between devices  84.5 us (45%)
  waiting for transfers between devices  65.4 us (35%)
  Pallas kernels  16.2 us (9%)
  blocking collectives  16.2 us (9%)
    all_to_all x4, waiting for transfers between devices, exchange(): return lax.all_to_all(value, axes, split_axis=0, concat_axis=0, tiled=True)  41 us
    all_to_all x4, starting transfers between devices, exchange(): return lax.all_to_all(value, axes, split_axis=0, concat_axis=0, tiled=True)  32.3 us
    ppermute x7, starting transfers between devices, around(): return lax.ppermute(value, ROWS, pairs)  32.3 us
    all_to_all x1, blocking collectives, exchange(): return lax.all_to_all(value, axes, split_axis=0, concat_axis=0, tiled=True)  16.2 us
    ppermute x7, waiting for transfers between devices, around(): return lax.ppermute(value, ROWS, pairs)  11.7 us
    pallas_call x12, Pallas kernels, call(): pl.pallas_call(kernel, out_shape=out, in_specs=[VM] * (len(inputs) - scal...  11.5 us
    ppermute x3, starting transfers between devices, shift(): lax.ppermute(value, axis, [(i, (i + distance) % size) for i in range(size)])  10.1 us
    ppermute x5, starting transfers between devices, swap(): return lax.ppermute(value, 'c', [(0, 1), (1, 0)])  9.74 us
  transfers between devices with their start and end apart: 19, of which 12 were waited for; matrix products, arithmetic and copies ran while one was open for 0% of the time, Pallas kernels for 6%

profile of v9, /device:TPU:56, one launch (start us, length us, event | category | flops | bytes accessed | tf_op | source)
XLA Modules:
  0.0 185.1 jit_solution(8311062023685369758)
XLA Ops:
  0.6 1.9 %collective-permute-start.5 = (bf16[1,256,4096]{2,1,0:T(8,128)(2,1)}, bf16[1,256,4096]{2,1,0:T(8,128)(2,1)S(1)}, u32[]{:S(2)}, u32[]{:S(2)}) collective-permute-start(bf16[1,256,4096]{2,1,0:T(8,128)(2,1)} %grads_ref.3), channel_id=1, source_target_pairs={{0,32},{32,0},{1,33},{33,1},{2,34},{34,2},{3,35},{35,3},{4,36},{36... | collective-permute-start | bytes 6291464 | tf_op jit(solution)/shard_map/ppermute | solution.py:221
  2.6 0.1 pad_add_fusion.where_ref.refs_4_
  2.6 4.3 %collective-permute-done.5.theirs_hbm = bf16[1,256,4096]{2,1,0:T(8,128)(2,1)S(1)} collective-permute-done((bf16[1,256,4096]{2,1,0:T(8,128)(2,1)}, bf16[1,256,4096]{2,1,0:T(8,128)(2,1)S(1)}, u32[]{:S(2)}, u32[]{:S(2)}) %collective-permute-start.5) | collective-permute-done | bytes 2097184 | tf_op jit(solution)/shard_map/ppermute | solution.py:221
  6.9 1.6 copy-done
  8.5 1.6 shard_map.91
  10.1 4.3 %collective-permute-start.6 = (bf16[2,16,4096]{2,1,0:T(8,128)(2,1)S(1)}, bf16[2,16,4096]{2,1,0:T(8,128)(2,1)S(1)}, u32[]{:S(2)}, u32[]{:S(2)}) collective-permute-start(bf16[2,16,4096]{2,1,0:T(8,128)(2,1)S(1)} %get-tuple-element.20), channel_id=1, source_target_pairs={{0,64},{32,480},{64,128},{96,32},{128,192},{160,96},{192,256},{224... | collective-permute-start | bytes 786440 | tf_op jit(solution)/shard_map/ppermute | solution.py:231
  14.4 6.1 %collective-permute-start.7 = (bf16[2,16,4096]{2,1,0:T(8,128)(2,1)S(1)}, bf16[2,16,4096]{2,1,0:T(8,128)(2,1)S(1)}, u32[]{:S(2)}, u32[]{:S(2)}) collective-permute-start(bf16[2,16,4096]{2,1,0:T(8,128)(2,1)S(1)} %get-tuple-element.21), channel_id=1, source_target_pairs={{0,128},{32,416},{64,192},{96,480},{128,256},{160,32},{192,320},{2... | collective-permute-start | bytes 786440 | tf_op jit(solution)/shard_map/ppermute | solution.py:231
  20.5 1.2 shard_map.92
  21.7 7.3 %collective-permute-start.8 = (bf16[2,16,4096]{2,1,0:T(8,128)(2,1)S(1)}, bf16[2,16,4096]{2,1,0:T(8,128)(2,1)S(1)}, u32[]{:S(2)}, u32[]{:S(2)}) collective-permute-start(bf16[2,16,4096]{2,1,0:T(8,128)(2,1)S(1)} %get-tuple-element.22), channel_id=1, source_target_pairs={{0,192},{32,352},{64,256},{96,416},{128,320},{160,480},{192,384},{... | collective-permute-start | bytes 786440 | tf_op jit(solution)/shard_map/ppermute | solution.py:231
  29.0 2.8 %collective-permute-start.9 = (bf16[16,4096]{1,0:T(8,128)(2,1)S(1)}, bf16[16,4096]{1,0:T(8,128)(2,1)S(1)}, u32[]{:S(2)}, u32[]{:S(2)}) collective-permute-start(bf16[16,4096]{1,0:T(8,128)(2,1)S(1)} %get-tuple-element.23), channel_id=1, source_target_pairs={{0,256},{32,288},{64,320},{96,352},{128,384},{160,416},{192,448},{... | collective-permute-start | bytes 393224 | tf_op jit(solution)/shard_map/ppermute | solution.py:231
  31.9 2.3 %collective-permute-done.7.two_ref = bf16[2,16,4096]{2,1,0:T(8,128)(2,1)S(1)} collective-permute-done((bf16[2,16,4096]{2,1,0:T(8,128)(2,1)S(1)}, bf16[2,16,4096]{2,1,0:T(8,128)(2,1)S(1)}, u32[]{:S(2)}, u32[]{:S(2)}) %collective-permute-start.7) | collective-permute-done | bytes 262176 | tf_op jit(solution)/shard_map/ppermute | solution.py:231
  34.1 8.3 %collective-permute-done.8.three_ref = bf16[2,16,4096]{2,1,0:T(8,128)(2,1)S(1)} collective-permute-done((bf16[2,16,4096]{2,1,0:T(8,128)(2,1)S(1)}, bf16[2,16,4096]{2,1,0:T(8,128)(2,1)S(1)}, u32[]{:S(2)}, u32[]{:S(2)}) %collective-permute-start.8) | collective-permute-done | bytes 262176 | tf_op jit(solution)/shard_map/ppermute | solution.py:231
  42.5 0.6 shard_map.93
  43.1 1.9 %collective-permute-start.10 = (bf16[16,4096]{1,0:T(8,128)(2,1)S(1)}, bf16[16,4096]{1,0:T(8,128)(2,1)S(1)}, u32[]{:S(2)}, u32[]{:S(2)}) collective-permute-start(bf16[16,4096]{1,0:T(8,128)(2,1)S(1)} %shard_map.93), channel_id=1, source_target_pairs={{0,32},{32,0},{1,33},{33,1},{2,34},{34,2},{3,35},{35,3},{4,36},{36... | collective-permute-start | bytes 393224 | tf_op jit(solution)/shard_map/ppermute | solution.py:221
  45.0 1.1 collective-permute-done.9.four_ref
  46.1 0.3 collective-permute-done.10.theirs_ref
  46.3 1.6 shard_map.94
  47.9 10.5 %all-to-all-start.2 = ((bf16[32,16,1024]{2,1,0:T(8,128)(2,1)}), bf16[32,16,1024]{2,1,0:T(8,128)(2,1)S(1)}, u32[]{:S(2)}, u32[]{:S(2)}) async-start(bf16[32,16,1024]{2,1,0:T(8,128)(2,1)} %shard_map.94), calls=%async_computation.2 | async-start | bytes 2097152 | tf_op jit(solution)/shard_map/all_to_all | solution.py:217
  58.4 1.9 %shard_map.85 = bf16[32,2,2,16,128]{4,3,2,1,0:T(8,128)(2,1)} custom-call(bf16[2,4,1,16,1024]{4,3,2,1,0:T(8,128)(2,1)} %left_hbm.1, bf16[2,4,1,16,1024]{4,3,2,1,0:T(8,128)(2,1)} %right_hbm.1), custom_call_target="tpu_custom_call" | custom-call | flops 1000000 | bytes 524288 | tf_op jit(solution)/shard_map/pallas_call | solution.py:270
  60.3 25.8 %all-to-all-done.2 = bf16[32,16,1024]{2,1,0:T(8,128)(2,1)S(1)} async-done(((bf16[32,16,1024]{2,1,0:T(8,128)(2,1)}), bf16[32,16,1024]{2,1,0:T(8,128)(2,1)S(1)}, u32[]{:S(2)}, u32[]{:S(2)}) %all-to-all-start.2) | async-done | bytes 1048608 | tf_op jit(solution)/shard_map/all_to_all | solution.py:217
  86.1 7.8 %all-to-all-start = ((bf16[32,2,2,16,128]{4,3,2,1,0:T(8,128)(2,1)}), bf16[32,2,2,16,128]{4,3,2,1,0:T(8,128)(2,1)S(1)}, u32[]{:S(2)}, u32[]{:S(2)}) async-start(bf16[32,2,2,16,128]{4,3,2,1,0:T(8,128)(2,1)} %shard_map.85), calls=%async_computation | async-start | bytes 1048576 | tf_op jit(solution)/shard_map/all_to_all | solution.py:217
  93.9 1.9 %collective-permute-start.11 = (bf16[8,4,16,1024]{3,2,1,0:T(8,128)(2,1)S(1)}, bf16[8,4,16,1024]{3,2,1,0:T(8,128)(2,1)S(1)}, u32[]{:S(2)}, u32[]{:S(2)}) collective-permute-start(bf16[8,4,16,1024]{3,2,1,0:T(8,128)(2,1)S(1)} %bitcast.5), channel_id=1, source_target_pairs={{0,32},{32,0},{1,33},{33,1},{2,34},{34,2},{3,35},{35,3},{4,36},{36... | collective-permute-start | bytes 3145736 | tf_op jit(solution)/shard_map/ppermute | solution.py:221
  95.9 11.8 %all-to-all-done = bf16[32,2,2,16,128]{4,3,2,1,0:T(8,128)(2,1)S(1)} async-done(((bf16[32,2,2,16,128]{4,3,2,1,0:T(8,128)(2,1)}), bf16[32,2,2,16,128]{4,3,2,1,0:T(8,128)(2,1)S(1)}, u32[]{:S(2)}, u32[]{:S(2)}) %all-to-all-start) | async-done | bytes 524320 | tf_op jit(solution)/shard_map/all_to_all | solution.py:217
  107.6 0.6 shard_map.86
  108.2 16.2 %all_to_all.25.in_ref = bf16[32,2,16,128]{3,2,1,0:T(8,128)(2,1)S(1)} all-to-all(bf16[32,2,16,128]{3,2,1,0:T(8,128)(2,1)S(1)} %shard_map.86), channel_id=1, replica_groups=mesh['z'=8,'c'=2,'x'=4,'yh'=2,'yl'=4] {'x','yh','yl'}, dimensions={0} | all-to-all | bytes 524288 | tf_op jit(solution)/shard_map/all_to_all | solution.py:217
  124.5 1.9 %collective-permute-start = (bf16[4,16,1024]{2,1,0:T(8,128)(2,1)S(1)}, bf16[4,16,1024]{2,1,0:T(8,128)(2,1)S(1)}, u32[]{:S(2)}, u32[]{:S(2)}) collective-permute-start(bf16[4,16,1024]{2,1,0:T(8,128)(2,1)S(1)} %get-tuple-element.18.mine_ref), channel_id=1, source_target_pairs={{0,32},{32,0},{1,33},{33,1},{2,34},{34,2},{3,35},{35,3},{4,36},{36... | collective-permute-start | bytes 393224 | tf_op jit(solution)/shard_map/ppermute | solution.py:221
  126.4 1.3 collective-permute-done.other_ref
  127.7 0.6 shard_map.88.pair_ref
  128.3 2.5 %collective-permute-start.1 = (bf16[2,4,16,1024]{3,2,1,0:T(8,128)(2,1)S(1)}, bf16[2,4,16,1024]{3,2,1,0:T(8,128)(2,1)S(1)}, u32[]{:S(2)}, u32[]{:S(2)}) collective-permute-start(bf16[2,4,16,1024]{3,2,1,0:T(8,128)(2,1)S(1)} %shard_map.88.pair_ref), channel_id=1, source_target_pairs={{0,448},{32,96},{64,0},{96,160},{128,64},{160,224},{192,128},{224,... | collective-permute-start | bytes 786440 | tf_op jit(solution)/shard_map/ppermute | solution.py:231
  130.8 3.9 %collective-permute-start.2 = (bf16[2,4,16,1024]{3,2,1,0:T(8,128)(2,1)S(1)}, bf16[2,4,16,1024]{3,2,1,0:T(8,128)(2,1)S(1)}, u32[]{:S(2)}, u32[]{:S(2)}) collective-permute-start(bf16[2,4,16,1024]{3,2,1,0:T(8,128)(2,1)S(1)} %shard_map.88.pair_ref), channel_id=1, source_target_pairs={{0,320},{32,224},{64,384},{96,288},{128,448},{160,352},{192,0},{22... | collective-permute-start | bytes 786440 | tf_op jit(solution)/shard_map/ppermute | solution.py:231
  134.7 2.5 %shard_map.95 = (bf16[32,2,16,128]{3,2,1,0:T(8,128)(2,1)}, bf16[64,1024]{1,0:T(8,128)(2,1)S(1)}) custom-call(bf16[8,4,16,1024]{3,2,1,0:T(8,128)(2,1)S(1)} %bitcast.6, bf16[8,4,16,1024]{3,2,1,0:T(8,128)(2,1)S(1)} %collective-permute-done.11.other_ref, bf16[4,16,1024]{2,1,0:T(8,128)(2,1)S(1)} %get-tuple-element.24.left_ref, s32[3]{0:T(128)S(1)} %pad_add_fusion.where_ref.refs_4_), custom_call_target="tpu_custom_call" | custom-call | flops 536870912 | bytes 2228236 | tf_op jit(solution)/shard_map/pallas_call | solution.py:21
  137.2 6.7 %all-to-all-start.3 = ((bf16[32,2,16,128]{3,2,1,0:T(8,128)(2,1)}), bf16[32,2,16,128]{3,2,1,0:T(8,128)(2,1)S(1)}, u32[]{:S(2)}, u32[]{:S(2)}) async-start(bf16[32,2,16,128]{3,2,1,0:T(8,128)(2,1)} %get-tuple-element.30), calls=%async_computation.3 | async-start | bytes 524288 | tf_op jit(solution)/shard_map/all_to_all | solution.py:217
  143.9 0.6 shard_map.89
  144.5 5.4 %collective-permute-start.3 = (bf16[3,4,16,1024]{3,2,1,0:T(8,128)(2,1)S(1)}, bf16[3,4,16,1024]{3,2,1,0:T(8,128)(2,1)S(1)}, u32[]{:S(2)}, u32[]{:S(2)}) collective-permute-start(bf16[3,4,16,1024]{3,2,1,0:T(8,128)(2,1)S(1)} %shard_map.89), channel_id=1, source_target_pairs={{0,448},{32,96},{64,0},{96,160},{128,64},{160,224},{192,128},{224,... | collective-permute-start | bytes 1179656 | tf_op jit(solution)/shard_map/ppermute | solution.py:231
  150.0 0.1 select_reduce_fusion
  150.1 3.4 %all-to-all-done.3.in_ref = bf16[32,2,16,128]{3,2,1,0:T(8,128)(2,1)S(1)} async-done(((bf16[32,2,16,128]{3,2,1,0:T(8,128)(2,1)}), bf16[32,2,16,128]{3,2,1,0:T(8,128)(2,1)S(1)}, u32[]{:S(2)}, u32[]{:S(2)}) %all-to-all-start.3) | async-done | bytes 262176 | tf_op jit(solution)/shard_map/all_to_all | solution.py:217
  153.5 1.5 shard_map.98
  155.0 7.4 %all-to-all-start.4 = ((bf16[32,2,2,16,128]{4,3,2,1,0:T(8,128)(2,1)}), bf16[32,2,2,16,128]{4,3,2,1,0:T(8,128)(2,1)S(1)}, u32[]{:S(2)}, u32[]{:S(2)}) async-start(bf16[32,2,2,16,128]{4,3,2,1,0:T(8,128)(2,1)} %shard_map.98), calls=%async_computation.4 | async-start | bytes 1048576 | tf_op jit(solution)/shard_map/all_to_all | solution.py:217
  162.5 2.1 %collective-permute-start.4 = (bf16[7,4,16,1024]{3,2,1,0:T(8,128)(2,1)S(1)}, bf16[7,4,16,1024]{3,2,1,0:T(8,128)(2,1)S(1)}, u32[]{:S(2)}, u32[]{:S(2)}) collective-permute-start(bf16[7,4,16,1024]{3,2,1,0:T(8,128)(2,1)S(1)} %shard_map.90.mine_ref), channel_id=1, source_target_pairs={{0,32},{32,0},{1,33},{33,1},{2,34},{34,2},{3,35},{35,3},{4,36},{36... | collective-permute-start | bytes 2752520 | tf_op jit(solution)/shard_map/ppermute | solution.py:221
  164.5 2.4 %collective-permute-done.4.other_ref = bf16[7,4,16,1024]{3,2,1,0:T(8,128)(2,1)S(1)} collective-permute-done((bf16[7,4,16,1024]{3,2,1,0:T(8,128)(2,1)S(1)}, bf16[7,4,16,1024]{3,2,1,0:T(8,128)(2,1)S(1)}, u32[]{:S(2)}, u32[]{:S(2)}) %collective-permute-start.4) | collective-permute-done | bytes 917536 | tf_op jit(solution)/shard_map/ppermute | solution.py:221
  167.0 1.2 shard_map.96
  168.1 5.2 %collective-permute-start.12 = (bf16[16,1024]{1,0:T(8,128)(2,1)S(1)}, bf16[16,1024]{1,0:T(8,128)(2,1)S(1)}, u32[]{:S(2)}, u32[]{:S(2)}) collective-permute-start(bf16[16,1024]{1,0:T(8,128)(2,1)S(1)} %get-tuple-element.27), channel_id=1, source_target_pairs={{0,1},{1,2},{2,3},{3,0},{4,5},{5,6},{6,7},{7,4},{8,9},{9,10},{10,1... | collective-permute-start | bytes 98312 | tf_op jit(solution)/shard_map/ppermute | solution.py:226
  173.3 1.9 %collective-permute-start.13 = (bf16[16,1024]{1,0:T(8,128)(2,1)S(1)}, bf16[16,1024]{1,0:T(8,128)(2,1)S(1)}, u32[]{:S(2)}, u32[]{:S(2)}) collective-permute-start(bf16[16,1024]{1,0:T(8,128)(2,1)S(1)} %get-tuple-element.28), channel_id=1, source_target_pairs={{0,2},{1,3},{2,0},{3,1},{4,6},{5,7},{6,4},{7,5},{8,10},{9,11},{10,... | collective-permute-start | bytes 98312 | tf_op jit(solution)/shard_map/ppermute | solution.py:226
  175.2 3.0 %collective-permute-start.14 = (bf16[16,1024]{1,0:T(8,128)(2,1)S(1)}, bf16[16,1024]{1,0:T(8,128)(2,1)S(1)}, u32[]{:S(2)}, u32[]{:S(2)}) collective-permute-start(bf16[16,1024]{1,0:T(8,128)(2,1)S(1)} %get-tuple-element.29), channel_id=1, source_target_pairs={{0,3},{1,0},{2,1},{3,2},{4,7},{5,4},{6,5},{7,6},{8,11},{9,8},{10,9... | collective-permute-start | bytes 98312 | tf_op jit(solution)/shard_map/ppermute | solution.py:226
  178.3 1.7 collective-permute-done.13.refs_2_
  180.0 2.8 %collective-permute-done.14.refs_3_ = bf16[16,1024]{1,0:T(8,128)(2,1)S(1)} collective-permute-done((bf16[16,1024]{1,0:T(8,128)(2,1)S(1)}, bf16[16,1024]{1,0:T(8,128)(2,1)S(1)}, u32[]{:S(2)}, u32[]{:S(2)}) %collective-permute-start.14) | collective-permute-done | bytes 32800 | tf_op jit(solution)/shard_map/ppermute | solution.py:226
  182.8 1.2 shard_map.97
  184.1 1.1 shard_map.99
  (18 shorter events, 0.2 us)
Async XLA Ops:
  0.6 6.3 %collective-permute-start.5 = (bf16[1,256,4096]{2,1,0:T(8,128)(2,1)}, bf16[1,256,4096]{2,1,0:T(8,128)(2,1)S(1)}, u32[]{:S(2)}, u32[]{:S(2)}) collective-permute-start(bf16[1,256,4096]{2,1,0:T(8,128)(2,1)} %grads_ref.3), channel_id=1, source_target_pairs={{0,32},{32,0},{1,33},{33,1},{2,34},{34,2},{3,35},{35,3},{4,36},{36... | collective-permute-start | bytes 6291464 | tf_op jit(solution)/shard_map/ppermute | solution.py:221
  6.9 1.6 copy-start
  10.1 21.7 %collective-permute-start.6 = (bf16[2,16,4096]{2,1,0:T(8,128)(2,1)S(1)}, bf16[2,16,4096]{2,1,0:T(8,128)(2,1)S(1)}, u32[]{:S(2)}, u32[]{:S(2)}) collective-permute-start(bf16[2,16,4096]{2,1,0:T(8,128)(2,1)S(1)} %get-tuple-element.20), channel_id=1, source_target_pairs={{0,64},{32,480},{64,128},{96,32},{128,192},{160,96},{192,256},{224... | collective-permute-start | bytes 786440 | tf_op jit(solution)/shard_map/ppermute | solution.py:231
  14.4 19.7 %collective-permute-start.7 = (bf16[2,16,4096]{2,1,0:T(8,128)(2,1)S(1)}, bf16[2,16,4096]{2,1,0:T(8,128)(2,1)S(1)}, u32[]{:S(2)}, u32[]{:S(2)}) collective-permute-start(bf16[2,16,4096]{2,1,0:T(8,128)(2,1)S(1)} %get-tuple-element.21), channel_id=1, source_target_pairs={{0,128},{32,416},{64,192},{96,480},{128,256},{160,32},{192,320},{2... | collective-permute-start | bytes 786440 | tf_op jit(solution)/shard_map/ppermute | solution.py:231
  21.7 20.8 %collective-permute-start.8 = (bf16[2,16,4096]{2,1,0:T(8,128)(2,1)S(1)}, bf16[2,16,4096]{2,1,0:T(8,128)(2,1)S(1)}, u32[]{:S(2)}, u32[]{:S(2)}) collective-permute-start(bf16[2,16,4096]{2,1,0:T(8,128)(2,1)S(1)} %get-tuple-element.22), channel_id=1, source_target_pairs={{0,192},{32,352},{64,256},{96,416},{128,320},{160,480},{192,384},{... | collective-permute-start | bytes 786440 | tf_op jit(solution)/shard_map/ppermute | solution.py:231
  29.0 17.0 %collective-permute-start.9 = (bf16[16,4096]{1,0:T(8,128)(2,1)S(1)}, bf16[16,4096]{1,0:T(8,128)(2,1)S(1)}, u32[]{:S(2)}, u32[]{:S(2)}) collective-permute-start(bf16[16,4096]{1,0:T(8,128)(2,1)S(1)} %get-tuple-element.23), channel_id=1, source_target_pairs={{0,256},{32,288},{64,320},{96,352},{128,384},{160,416},{192,448},{... | collective-permute-start | bytes 393224 | tf_op jit(solution)/shard_map/ppermute | solution.py:231
  43.1 3.2 %collective-permute-start.10 = (bf16[16,4096]{1,0:T(8,128)(2,1)S(1)}, bf16[16,4096]{1,0:T(8,128)(2,1)S(1)}, u32[]{:S(2)}, u32[]{:S(2)}) collective-permute-start(bf16[16,4096]{1,0:T(8,128)(2,1)S(1)} %shard_map.93), channel_id=1, source_target_pairs={{0,32},{32,0},{1,33},{33,1},{2,34},{34,2},{3,35},{35,3},{4,36},{36... | collective-permute-start | bytes 393224 | tf_op jit(solution)/shard_map/ppermute | solution.py:221
  47.9 59.7 %copy-start.3 = (s32[32]{0:T(128)S(1)}, s32[32]{0:T(128)}, u32[]{:S(2)}) copy-start(s32[32]{0:T(128)} %table_ref.1) | copy-start | bytes 388
  47.9 38.1 %all-to-all-start.2 = ((bf16[32,16,1024]{2,1,0:T(8,128)(2,1)}), bf16[32,16,1024]{2,1,0:T(8,128)(2,1)S(1)}, u32[]{:S(2)}, u32[]{:S(2)}) async-start(bf16[32,16,1024]{2,1,0:T(8,128)(2,1)} %shard_map.94), calls=%async_computation.2 | async-start | bytes 2097152 | tf_op jit(solution)/shard_map/all_to_all | solution.py:217
  86.1 21.5 %all-to-all-start = ((bf16[32,2,2,16,128]{4,3,2,1,0:T(8,128)(2,1)}), bf16[32,2,2,16,128]{4,3,2,1,0:T(8,128)(2,1)S(1)}, u32[]{:S(2)}, u32[]{:S(2)}) async-start(bf16[32,2,2,16,128]{4,3,2,1,0:T(8,128)(2,1)} %shard_map.85), calls=%async_computation | async-start | bytes 1048576 | tf_op jit(solution)/shard_map/all_to_all | solution.py:217
  93.9 40.8 %collective-permute-start.11 = (bf16[8,4,16,1024]{3,2,1,0:T(8,128)(2,1)S(1)}, bf16[8,4,16,1024]{3,2,1,0:T(8,128)(2,1)S(1)}, u32[]{:S(2)}, u32[]{:S(2)}) collective-permute-start(bf16[8,4,16,1024]{3,2,1,0:T(8,128)(2,1)S(1)} %bitcast.5), channel_id=1, source_target_pairs={{0,32},{32,0},{1,33},{33,1},{2,34},{34,2},{3,35},{35,3},{4,36},{36... | collective-permute-start | bytes 3145736 | tf_op jit(solution)/shard_map/ppermute | solution.py:221
  124.5 3.2 %collective-permute-start = (bf16[4,16,1024]{2,1,0:T(8,128)(2,1)S(1)}, bf16[4,16,1024]{2,1,0:T(8,128)(2,1)S(1)}, u32[]{:S(2)}, u32[]{:S(2)}) collective-permute-start(bf16[4,16,1024]{2,1,0:T(8,128)(2,1)S(1)} %get-tuple-element.18.mine_ref), channel_id=1, source_target_pairs={{0,32},{32,0},{1,33},{33,1},{2,34},{34,2},{3,35},{35,3},{4,36},{36... | collective-permute-start | bytes 393224 | tf_op jit(solution)/shard_map/ppermute | solution.py:221
  128.3 15.6 %collective-permute-start.1 = (bf16[2,4,16,1024]{3,2,1,0:T(8,128)(2,1)S(1)}, bf16[2,4,16,1024]{3,2,1,0:T(8,128)(2,1)S(1)}, u32[]{:S(2)}, u32[]{:S(2)}) collective-permute-start(bf16[2,4,16,1024]{3,2,1,0:T(8,128)(2,1)S(1)} %shard_map.88.pair_ref), channel_id=1, source_target_pairs={{0,448},{32,96},{64,0},{96,160},{128,64},{160,224},{192,128},{224,... | collective-permute-start | bytes 786440 | tf_op jit(solution)/shard_map/ppermute | solution.py:231
  130.8 13.2 %collective-permute-start.2 = (bf16[2,4,16,1024]{3,2,1,0:T(8,128)(2,1)S(1)}, bf16[2,4,16,1024]{3,2,1,0:T(8,128)(2,1)S(1)}, u32[]{:S(2)}, u32[]{:S(2)}) collective-permute-start(bf16[2,4,16,1024]{3,2,1,0:T(8,128)(2,1)S(1)} %shard_map.88.pair_ref), channel_id=1, source_target_pairs={{0,320},{32,224},{64,384},{96,288},{128,448},{160,352},{192,0},{22... | collective-permute-start | bytes 786440 | tf_op jit(solution)/shard_map/ppermute | solution.py:231
  137.2 16.2 %all-to-all-start.3 = ((bf16[32,2,16,128]{3,2,1,0:T(8,128)(2,1)}), bf16[32,2,16,128]{3,2,1,0:T(8,128)(2,1)S(1)}, u32[]{:S(2)}, u32[]{:S(2)}) async-start(bf16[32,2,16,128]{3,2,1,0:T(8,128)(2,1)} %get-tuple-element.30), calls=%async_computation.3 | async-start | bytes 524288 | tf_op jit(solution)/shard_map/all_to_all | solution.py:217
  144.5 17.9 %collective-permute-start.3 = (bf16[3,4,16,1024]{3,2,1,0:T(8,128)(2,1)S(1)}, bf16[3,4,16,1024]{3,2,1,0:T(8,128)(2,1)S(1)}, u32[]{:S(2)}, u32[]{:S(2)}) collective-permute-start(bf16[3,4,16,1024]{3,2,1,0:T(8,128)(2,1)S(1)} %shard_map.89), channel_id=1, source_target_pairs={{0,448},{32,96},{64,0},{96,160},{128,64},{160,224},{192,128},{224,... | collective-permute-start | bytes 1179656 | tf_op jit(solution)/shard_map/ppermute | solution.py:231
  155.0 29.1 %all-to-all-start.4 = ((bf16[32,2,2,16,128]{4,3,2,1,0:T(8,128)(2,1)}), bf16[32,2,2,16,128]{4,3,2,1,0:T(8,128)(2,1)S(1)}, u32[]{:S(2)}, u32[]{:S(2)}) async-start(bf16[32,2,2,16,128]{4,3,2,1,0:T(8,128)(2,1)} %shard_map.98), calls=%async_computation.4 | async-start | bytes 1048576 | tf_op jit(solution)/shard_map/all_to_all | solution.py:217
  162.4 21.7 %copy-start.1 = (f32[2,4,1,16,1024]{4,3,2,1,0:T(8,128)S(1)}, f32[2,4,1,16,1024]{4,3,2,1,0:T(8,128)}, u32[]{:S(2)}) copy-start(f32[2,4,1,16,1024]{4,3,2,1,0:T(8,128)} %left_ref.1) | copy-start | bytes 1572868
  162.4 21.7 %copy-start.2 = (f32[2,4,1,16,1024]{4,3,2,1,0:T(8,128)S(1)}, f32[2,4,1,16,1024]{4,3,2,1,0:T(8,128)}, u32[]{:S(2)}) copy-start(f32[2,4,1,16,1024]{4,3,2,1,0:T(8,128)} %right_ref.1) | copy-start | bytes 1572868
  162.5 4.5 %collective-permute-start.4 = (bf16[7,4,16,1024]{3,2,1,0:T(8,128)(2,1)S(1)}, bf16[7,4,16,1024]{3,2,1,0:T(8,128)(2,1)S(1)}, u32[]{:S(2)}, u32[]{:S(2)}) collective-permute-start(bf16[7,4,16,1024]{3,2,1,0:T(8,128)(2,1)S(1)} %shard_map.90.mine_ref), channel_id=1, source_target_pairs={{0,32},{32,0},{1,33},{33,1},{2,34},{34,2},{3,35},{35,3},{4,36},{36... | collective-permute-start | bytes 2752520 | tf_op jit(solution)/shard_map/ppermute | solution.py:221
  168.1 10.1 %collective-permute-start.12 = (bf16[16,1024]{1,0:T(8,128)(2,1)S(1)}, bf16[16,1024]{1,0:T(8,128)(2,1)S(1)}, u32[]{:S(2)}, u32[]{:S(2)}) collective-permute-start(bf16[16,1024]{1,0:T(8,128)(2,1)S(1)} %get-tuple-element.27), channel_id=1, source_target_pairs={{0,1},{1,2},{2,3},{3,0},{4,5},{5,6},{6,7},{7,4},{8,9},{9,10},{10,1... | collective-permute-start | bytes 98312 | tf_op jit(solution)/shard_map/ppermute | solution.py:226
  173.3 6.7 %collective-permute-start.13 = (bf16[16,1024]{1,0:T(8,128)(2,1)S(1)}, bf16[16,1024]{1,0:T(8,128)(2,1)S(1)}, u32[]{:S(2)}, u32[]{:S(2)}) collective-permute-start(bf16[16,1024]{1,0:T(8,128)(2,1)S(1)} %get-tuple-element.28), channel_id=1, source_target_pairs={{0,2},{1,3},{2,0},{3,1},{4,6},{5,7},{6,4},{7,5},{8,10},{9,11},{10,... | collective-permute-start | bytes 98312 | tf_op jit(solution)/shard_map/ppermute | solution.py:226
  175.2 7.6 %collective-permute-start.14 = (bf16[16,1024]{1,0:T(8,128)(2,1)S(1)}, bf16[16,1024]{1,0:T(8,128)(2,1)S(1)}, u32[]{:S(2)}, u32[]{:S(2)}) collective-permute-start(bf16[16,1024]{1,0:T(8,128)(2,1)S(1)} %get-tuple-element.29), channel_id=1, source_target_pairs={{0,3},{1,0},{2,1},{3,2},{4,7},{5,4},{6,5},{7,6},{8,11},{9,8},{10,9... | collective-permute-start | bytes 98312 | tf_op jit(solution)/shard_map/ppermute | solution.py:226

commit v10 on v9

--- a/solution.py
+++ b/solution.py
@@ -175,18 +175,15 @@
     out_ref[1 - where_ref[1]] = other_ref[...]
 
 
-def pick_relay(first_ref, third_ref, where_ref, out_ref):
-    out_ref[0] = first_ref[0]
-    out_ref[1] = first_ref[1]
-    out_ref[2] = third_ref[where_ref[1]]
-
-
-def stack_rows(first_ref, relayed_ref, third_ref, out_ref):
-    for parity in range(2):
-        out_ref[parity] = first_ref[parity]
-        out_ref[2 + parity] = relayed_ref[parity]
-        out_ref[4 + parity] = third_ref[parity]
-    out_ref[6] = relayed_ref[2]
+def take_parity(in_ref, where_ref, out_ref):
+    out_ref[...] = in_ref[where_ref[1]]
+
+
+def stack_rows(first_ref, second_ref, third_ref, last_ref, out_ref):
+    for hop, ref in enumerate((first_ref, second_ref, third_ref)):
+        out_ref[2 * hop] = ref[0]
+        out_ref[2 * hop + 1] = ref[1]
+    out_ref[6] = last_ref[...]
 
 
 def right_product(pair_ref, mine_ref, other_ref, mixed_ref, where_ref, *refs):
@@ -308,11 +305,12 @@
     pair = call(
         pair_up, shape((2, 4, 16, 1024)), [right_rows, theirs, where], scalars=1
     )
-    third = around(pair, -3)
+    second = around(pair, -2)
     first = around(pair, -1)
-    relay = call(pick_relay, shape((3, 4, 16, 1024)), [first, third, where], scalars=1)
-    relay = around(relay, -1)
-    right_mine = call(stack_rows, shape((7, 4, 16, 1024)), [first, relay, third])
+    half = call(take_parity, shape((4, 16, 1024)), [second, where], scalars=1)
+    third = around(second, -1)
+    last = around(half, -2)
+    right_mine = call(stack_rows, shape((7, 4, 16, 1024)), [first, second, third, last])
     right_other = swap(right_mine)
     result = call(
         right_product,

time: 186 us -> 191 us (1.027)
  starting transfers between devices: 84.5 us -> 88.7 us
    ppermute x7 -> x8, waiting for transfers between devices: 11.7 us -> 16.7 us  [around(): return lax.ppermute(value, ROWS, pairs)]
    all_to_all x4, waiting for transfers between devices: 41 us -> 37.6 us  [exchange(): return lax.all_to_all(value, axes, split_axis=0, concat_axis=0, tiled=True)]
    all_to_all x4, starting transfers between devices: 32.3 us -> 34.7 us  [exchange(): return lax.all_to_all(value, axes, split_axis=0, concat_axis=0, tiled=True)]
    ppermute x7 -> x8, starting transfers between devices: 32.3 us -> 34.2 us  [around(): return lax.ppermute(value, ROWS, pairs)]
  transfers between devices with their start and end apart: 19 -> 20, of which waited for: 12 -> 11; matrix products, arithmetic and copies ran while one was open for 0% -> 0% of each run, Pallas kernels for 6% -> 6%
where the time goes in v10:
time: 191 us; the launch traced here: 190 us
  starting transfers between devices  88.7 us (46%)
  waiting for transfers between devices  65.7 us (34%)
  Pallas kernels  16.3 us (9%)
  blocking collectives  16.2 us (8%)
    all_to_all x4, waiting for transfers between devices, exchange(): return lax.all_to_all(value, axes, split_axis=0, concat_axis=0, tiled=True)  37.6 us
    all_to_all x4, starting transfers between devices, exchange(): return lax.all_to_all(value, axes, split_axis=0, concat_axis=0, tiled=True)  34.7 us
    ppermute x8, starting transfers between devices, around(): return lax.ppermute(value, ROWS, pairs)  34.2 us
    ppermute x8, waiting for transfers between devices, around(): return lax.ppermute(value, ROWS, pairs)  16.7 us
    all_to_all x1, blocking collectives, exchange(): return lax.all_to_all(value, axes, split_axis=0, concat_axis=0, tiled=True)  16.2 us
    pallas_call x12, Pallas kernels, call(): pl.pallas_call(kernel, out_shape=out, in_specs=[VM] * (len(inputs) - scal...  11.5 us
    ppermute x3, starting transfers between devices, shift(): lax.ppermute(value, axis, [(i, (i + distance) % size) for i in range(size)])  10.1 us
    ppermute x5, starting transfers between devices, swap(): return lax.ppermute(value, 'c', [(0, 1), (1, 0)])  9.74 us
  transfers between devices with their start and end apart: 20, of which 11 were waited for; matrix products, arithmetic and copies ran while one was open for 0% of the time, Pallas kernels for 6%

profile of v10, /device:TPU:56, one launch (start us, length us, event | category | flops | bytes accessed | tf_op | source)
XLA Modules:
  0.0 189.7 jit_solution(2399405608382615099)
XLA Ops:
  0.6 1.9 %collective-permute-start.6 = (bf16[1,256,4096]{2,1,0:T(8,128)(2,1)}, bf16[1,256,4096]{2,1,0:T(8,128)(2,1)S(1)}, u32[]{:S(2)}, u32[]{:S(2)}) collective-permute-start(bf16[1,256,4096]{2,1,0:T(8,128)(2,1)} %grads_ref.3), channel_id=1, source_target_pairs={{0,32},{32,0},{1,33},{33,1},{2,34},{34,2},{3,35},{35,3},{4,36},{36... | collective-permute-start | bytes 6291464 | tf_op jit(solution)/shard_map/ppermute | solution.py:218
  2.6 0.1 pad_add_fusion.where_ref.refs_4_
  2.6 4.3 %collective-permute-done.6.theirs_hbm = bf16[1,256,4096]{2,1,0:T(8,128)(2,1)S(1)} collective-permute-done((bf16[1,256,4096]{2,1,0:T(8,128)(2,1)}, bf16[1,256,4096]{2,1,0:T(8,128)(2,1)S(1)}, u32[]{:S(2)}, u32[]{:S(2)}) %collective-permute-start.6) | collective-permute-done | bytes 2097184 | tf_op jit(solution)/shard_map/ppermute | solution.py:218
  6.9 1.6 copy-done
  8.5 1.7 shard_map.91
  10.2 4.3 %collective-permute-start.7 = (bf16[2,16,4096]{2,1,0:T(8,128)(2,1)S(1)}, bf16[2,16,4096]{2,1,0:T(8,128)(2,1)S(1)}, u32[]{:S(2)}, u32[]{:S(2)}) collective-permute-start(bf16[2,16,4096]{2,1,0:T(8,128)(2,1)S(1)} %get-tuple-element.20), channel_id=1, source_target_pairs={{0,64},{32,480},{64,128},{96,32},{128,192},{160,96},{192,256},{224... | collective-permute-start | bytes 786440 | tf_op jit(solution)/shard_map/ppermute | solution.py:228
  14.4 6.1 %collective-permute-start.8 = (bf16[2,16,4096]{2,1,0:T(8,128)(2,1)S(1)}, bf16[2,16,4096]{2,1,0:T(8,128)(2,1)S(1)}, u32[]{:S(2)}, u32[]{:S(2)}) collective-permute-start(bf16[2,16,4096]{2,1,0:T(8,128)(2,1)S(1)} %get-tuple-element.21), channel_id=1, source_target_pairs={{0,128},{32,416},{64,192},{96,480},{128,256},{160,32},{192,320},{2... | collective-permute-start | bytes 786440 | tf_op jit(solution)/shard_map/ppermute | solution.py:228
  20.5 1.2 shard_map.92
  21.8 7.3 %collective-permute-start.9 = (bf16[2,16,4096]{2,1,0:T(8,128)(2,1)S(1)}, bf16[2,16,4096]{2,1,0:T(8,128)(2,1)S(1)}, u32[]{:S(2)}, u32[]{:S(2)}) collective-permute-start(bf16[2,16,4096]{2,1,0:T(8,128)(2,1)S(1)} %get-tuple-element.22), channel_id=1, source_target_pairs={{0,192},{32,352},{64,256},{96,416},{128,320},{160,480},{192,384},{... | collective-permute-start | bytes 786440 | tf_op jit(solution)/shard_map/ppermute | solution.py:228
  29.1 2.8 %collective-permute-start.10 = (bf16[16,4096]{1,0:T(8,128)(2,1)S(1)}, bf16[16,4096]{1,0:T(8,128)(2,1)S(1)}, u32[]{:S(2)}, u32[]{:S(2)}) collective-permute-start(bf16[16,4096]{1,0:T(8,128)(2,1)S(1)} %get-tuple-element.23), channel_id=1, source_target_pairs={{0,256},{32,288},{64,320},{96,352},{128,384},{160,416},{192,448},{... | collective-permute-start | bytes 393224 | tf_op jit(solution)/shard_map/ppermute | solution.py:228
  31.9 2.2 %collective-permute-done.8.two_ref = bf16[2,16,4096]{2,1,0:T(8,128)(2,1)S(1)} collective-permute-done((bf16[2,16,4096]{2,1,0:T(8,128)(2,1)S(1)}, bf16[2,16,4096]{2,1,0:T(8,128)(2,1)S(1)}, u32[]{:S(2)}, u32[]{:S(2)}) %collective-permute-start.8) | collective-permute-done | bytes 262176 | tf_op jit(solution)/shard_map/ppermute | solution.py:228
  34.2 8.3 %collective-permute-done.9.three_ref = bf16[2,16,4096]{2,1,0:T(8,128)(2,1)S(1)} collective-permute-done((bf16[2,16,4096]{2,1,0:T(8,128)(2,1)S(1)}, bf16[2,16,4096]{2,1,0:T(8,128)(2,1)S(1)}, u32[]{:S(2)}, u32[]{:S(2)}) %collective-permute-start.9) | collective-permute-done | bytes 262176 | tf_op jit(solution)/shard_map/ppermute | solution.py:228
  42.5 0.6 shard_map.93
  43.1 1.9 %collective-permute-start.11 = (bf16[16,4096]{1,0:T(8,128)(2,1)S(1)}, bf16[16,4096]{1,0:T(8,128)(2,1)S(1)}, u32[]{:S(2)}, u32[]{:S(2)}) collective-permute-start(bf16[16,4096]{1,0:T(8,128)(2,1)S(1)} %shard_map.93), channel_id=1, source_target_pairs={{0,32},{32,0},{1,33},{33,1},{2,34},{34,2},{3,35},{35,3},{4,36},{36... | collective-permute-start | bytes 393224 | tf_op jit(solution)/shard_map/ppermute | solution.py:218
  45.0 1.1 collective-permute-done.10.four_ref
  46.1 0.2 collective-permute-done.11.theirs_ref
  46.3 1.6 shard_map.94
  47.9 10.4 %all-to-all-start.2 = ((bf16[32,16,1024]{2,1,0:T(8,128)(2,1)}), bf16[32,16,1024]{2,1,0:T(8,128)(2,1)S(1)}, u32[]{:S(2)}, u32[]{:S(2)}) async-start(bf16[32,16,1024]{2,1,0:T(8,128)(2,1)} %shard_map.94), calls=%async_computation.2 | async-start | bytes 2097152 | tf_op jit(solution)/shard_map/all_to_all | solution.py:214
  58.4 1.9 shard_map.85
  60.3 25.8 %all-to-all-done.2 = bf16[32,16,1024]{2,1,0:T(8,128)(2,1)S(1)} async-done(((bf16[32,16,1024]{2,1,0:T(8,128)(2,1)}), bf16[32,16,1024]{2,1,0:T(8,128)(2,1)S(1)}, u32[]{:S(2)}, u32[]{:S(2)}) %all-to-all-start.2) | async-done | bytes 1048608 | tf_op jit(solution)/shard_map/all_to_all | solution.py:214
  86.1 7.8 %all-to-all-start = ((bf16[32,2,2,16,128]{4,3,2,1,0:T(8,128)(2,1)}), bf16[32,2,2,16,128]{4,3,2,1,0:T(8,128)(2,1)S(1)}, u32[]{:S(2)}, u32[]{:S(2)}) async-start(bf16[32,2,2,16,128]{4,3,2,1,0:T(8,128)(2,1)} %shard_map.85), calls=%async_computation | async-start | bytes 1048576 | tf_op jit(solution)/shard_map/all_to_all | solution.py:214
  93.9 1.9 %collective-permute-start.12 = (bf16[8,4,16,1024]{3,2,1,0:T(8,128)(2,1)S(1)}, bf16[8,4,16,1024]{3,2,1,0:T(8,128)(2,1)S(1)}, u32[]{:S(2)}, u32[]{:S(2)}) collective-permute-start(bf16[8,4,16,1024]{3,2,1,0:T(8,128)(2,1)S(1)} %bitcast.5), channel_id=1, source_target_pairs={{0,32},{32,0},{1,33},{33,1},{2,34},{34,2},{3,35},{35,3},{4,36},{36... | collective-permute-start | bytes 3145736 | tf_op jit(solution)/shard_map/ppermute | solution.py:218
  95.8 11.8 %all-to-all-done = bf16[32,2,2,16,128]{4,3,2,1,0:T(8,128)(2,1)S(1)} async-done(((bf16[32,2,2,16,128]{4,3,2,1,0:T(8,128)(2,1)}), bf16[32,2,2,16,128]{4,3,2,1,0:T(8,128)(2,1)S(1)}, u32[]{:S(2)}, u32[]{:S(2)}) %all-to-all-start) | async-done | bytes 524320 | tf_op jit(solution)/shard_map/all_to_all | solution.py:214
  107.6 0.6 shard_map.86
  108.2 16.2 %all_to_all.25.in_ref = bf16[32,2,16,128]{3,2,1,0:T(8,128)(2,1)S(1)} all-to-all(bf16[32,2,16,128]{3,2,1,0:T(8,128)(2,1)S(1)} %shard_map.86), channel_id=1, replica_groups=mesh['z'=8,'c'=2,'x'=4,'yh'=2,'yl'=4] {'x','yh','yl'}, dimensions={0} | all-to-all | bytes 524288 | tf_op jit(solution)/shard_map/all_to_all | solution.py:214
  124.5 1.9 %collective-permute-start = (bf16[4,16,1024]{2,1,0:T(8,128)(2,1)S(1)}, bf16[4,16,1024]{2,1,0:T(8,128)(2,1)S(1)}, u32[]{:S(2)}, u32[]{:S(2)}) collective-permute-start(bf16[4,16,1024]{2,1,0:T(8,128)(2,1)S(1)} %get-tuple-element.18.mine_ref), channel_id=1, source_target_pairs={{0,32},{32,0},{1,33},{33,1},{2,34},{34,2},{3,35},{35,3},{4,36},{36... | collective-permute-start | bytes 393224 | tf_op jit(solution)/shard_map/ppermute | solution.py:218
  126.4 2.5 %shard_map.95 = (bf16[32,2,16,128]{3,2,1,0:T(8,128)(2,1)}, bf16[64,1024]{1,0:T(8,128)(2,1)S(1)}) custom-call(bf16[8,4,16,1024]{3,2,1,0:T(8,128)(2,1)S(1)} %bitcast.6, bf16[8,4,16,1024]{3,2,1,0:T(8,128)(2,1)S(1)} %collective-permute-done.12.other_ref, bf16[4,16,1024]{2,1,0:T(8,128)(2,1)S(1)} %get-tuple-element.24.left_ref, s32[3]{0:T(128)S(1)} %pad_add_fusion.where_ref.refs_4_), custom_call_target="tpu_custom_call" | custom-call | flops 536870912 | bytes 2228236 | tf_op jit(solution)/shard_map/pallas_call | solution.py:21
  128.9 6.6 %all-to-all-start.3 = ((bf16[32,2,16,128]{3,2,1,0:T(8,128)(2,1)}), bf16[32,2,16,128]{3,2,1,0:T(8,128)(2,1)S(1)}, u32[]{:S(2)}, u32[]{:S(2)}) async-start(bf16[32,2,16,128]{3,2,1,0:T(8,128)(2,1)} %get-tuple-element.30), calls=%async_computation.3 | async-start | bytes 524288 | tf_op jit(solution)/shard_map/all_to_all | solution.py:214
  135.5 0.6 shard_map.88.pair_ref
  136.1 4.6 %collective-permute-start.2 = (bf16[2,4,16,1024]{3,2,1,0:T(8,128)(2,1)S(1)}, bf16[2,4,16,1024]{3,2,1,0:T(8,128)(2,1)S(1)}, u32[]{:S(2)}, u32[]{:S(2)}) collective-permute-start(bf16[2,4,16,1024]{3,2,1,0:T(8,128)(2,1)S(1)} %shard_map.88.pair_ref), channel_id=1, source_target_pairs={{0,384},{32,160},{64,448},{96,224},{128,0},{160,288},{192,64},{224... | collective-permute-start | bytes 786440 | tf_op jit(solution)/shard_map/ppermute | solution.py:228
  140.7 0.1 select_reduce_fusion
  140.8 2.3 %collective-permute-start.1 = (bf16[2,4,16,1024]{3,2,1,0:T(8,128)(2,1)S(1)}, bf16[2,4,16,1024]{3,2,1,0:T(8,128)(2,1)S(1)}, u32[]{:S(2)}, u32[]{:S(2)}) collective-permute-start(bf16[2,4,16,1024]{3,2,1,0:T(8,128)(2,1)S(1)} %shard_map.88.pair_ref), channel_id=1, source_target_pairs={{0,448},{32,96},{64,0},{96,160},{128,64},{160,224},{192,128},{224,... | collective-permute-start | bytes 786440 | tf_op jit(solution)/shard_map/ppermute | solution.py:228
  143.2 5.0 %collective-permute-done.2.in_ref.second_ref = bf16[2,4,16,1024]{3,2,1,0:T(8,128)(2,1)S(1)} collective-permute-done((bf16[2,4,16,1024]{3,2,1,0:T(8,128)(2,1)S(1)}, bf16[2,4,16,1024]{3,2,1,0:T(8,128)(2,1)S(1)}, u32[]{:S(2)}, u32[]{:S(2)}) %collective-permute-start.2) | collective-permute-done | bytes 262176 | tf_op jit(solution)/shard_map/ppermute | solution.py:228
  148.2 0.6 shard_map.89
  148.8 4.9 %collective-permute-start.4 = (bf16[4,16,1024]{2,1,0:T(8,128)(2,1)S(1)}, bf16[4,16,1024]{2,1,0:T(8,128)(2,1)S(1)}, u32[]{:S(2)}, u32[]{:S(2)}) collective-permute-start(bf16[4,16,1024]{2,1,0:T(8,128)(2,1)S(1)} %shard_map.89), channel_id=1, source_target_pairs={{0,384},{32,160},{64,448},{96,224},{128,0},{160,288},{192,64},{224... | collective-permute-start | bytes 393224 | tf_op jit(solution)/shard_map/ppermute | solution.py:228
  153.6 1.9 %collective-permute-start.3 = (bf16[2,4,16,1024]{3,2,1,0:T(8,128)(2,1)S(1)}, bf16[2,4,16,1024]{3,2,1,0:T(8,128)(2,1)S(1)}, u32[]{:S(2)}, u32[]{:S(2)}) collective-permute-start(bf16[2,4,16,1024]{3,2,1,0:T(8,128)(2,1)S(1)} %collective-permute-done.2.in_ref.second_ref), channel_id=1, source_target_pairs={{0,448},{32,96},{64,0},{96,160},{128,64},{160,224},{192,128},{224,... | collective-permute-start | bytes 786440 | tf_op jit(solution)/shard_map/ppermute | solution.py:228
  155.6 1.5 shard_map.98
  157.1 9.8 %all-to-all-start.4 = ((bf16[32,2,2,16,128]{4,3,2,1,0:T(8,128)(2,1)}), bf16[32,2,2,16,128]{4,3,2,1,0:T(8,128)(2,1)S(1)}, u32[]{:S(2)}, u32[]{:S(2)}) async-start(bf16[32,2,2,16,128]{4,3,2,1,0:T(8,128)(2,1)} %shard_map.98), calls=%async_computation.4 | async-start | bytes 1048576 | tf_op jit(solution)/shard_map/all_to_all | solution.py:214
  167.0 2.1 %collective-permute-start.5 = (bf16[7,4,16,1024]{3,2,1,0:T(8,128)(2,1)S(1)}, bf16[7,4,16,1024]{3,2,1,0:T(8,128)(2,1)S(1)}, u32[]{:S(2)}, u32[]{:S(2)}) collective-permute-start(bf16[7,4,16,1024]{3,2,1,0:T(8,128)(2,1)S(1)} %shard_map.90.mine_ref), channel_id=1, source_target_pairs={{0,32},{32,0},{1,33},{33,1},{2,34},{34,2},{3,35},{35,3},{4,36},{36... | collective-permute-start | bytes 2752520 | tf_op jit(solution)/shard_map/ppermute | solution.py:218
  169.1 2.4 %collective-permute-done.5.other_ref = bf16[7,4,16,1024]{3,2,1,0:T(8,128)(2,1)S(1)} collective-permute-done((bf16[7,4,16,1024]{3,2,1,0:T(8,128)(2,1)S(1)}, bf16[7,4,16,1024]{3,2,1,0:T(8,128)(2,1)S(1)}, u32[]{:S(2)}, u32[]{:S(2)}) %collective-permute-start.5) | collective-permute-done | bytes 917536 | tf_op jit(solution)/shard_map/ppermute | solution.py:218
  171.5 1.2 shard_map.96
  172.7 5.2 %collective-permute-start.13 = (bf16[16,1024]{1,0:T(8,128)(2,1)S(1)}, bf16[16,1024]{1,0:T(8,128)(2,1)S(1)}, u32[]{:S(2)}, u32[]{:S(2)}) collective-permute-start(bf16[16,1024]{1,0:T(8,128)(2,1)S(1)} %get-tuple-element.27), channel_id=1, source_target_pairs={{0,1},{1,2},{2,3},{3,0},{4,5},{5,6},{6,7},{7,4},{8,9},{9,10},{10,1... | collective-permute-start | bytes 98312 | tf_op jit(solution)/shard_map/ppermute | solution.py:223
  177.9 1.9 %collective-permute-start.14 = (bf16[16,1024]{1,0:T(8,128)(2,1)S(1)}, bf16[16,1024]{1,0:T(8,128)(2,1)S(1)}, u32[]{:S(2)}, u32[]{:S(2)}) collective-permute-start(bf16[16,1024]{1,0:T(8,128)(2,1)S(1)} %get-tuple-element.28), channel_id=1, source_target_pairs={{0,2},{1,3},{2,0},{3,1},{4,6},{5,7},{6,4},{7,5},{8,10},{9,11},{10,... | collective-permute-start | bytes 98312 | tf_op jit(solution)/shard_map/ppermute | solution.py:223
  179.8 3.0 %collective-permute-start.15 = (bf16[16,1024]{1,0:T(8,128)(2,1)S(1)}, bf16[16,1024]{1,0:T(8,128)(2,1)S(1)}, u32[]{:S(2)}, u32[]{:S(2)}) collective-permute-start(bf16[16,1024]{1,0:T(8,128)(2,1)S(1)} %get-tuple-element.29), channel_id=1, source_target_pairs={{0,3},{1,0},{2,1},{3,2},{4,7},{5,4},{6,5},{7,6},{8,11},{9,8},{10,9... | collective-permute-start | bytes 98312 | tf_op jit(solution)/shard_map/ppermute | solution.py:223
  182.9 1.7 collective-permute-done.14.refs_2_
  184.6 2.8 %collective-permute-done.15.refs_3_ = bf16[16,1024]{1,0:T(8,128)(2,1)S(1)} collective-permute-done((bf16[16,1024]{1,0:T(8,128)(2,1)S(1)}, bf16[16,1024]{1,0:T(8,128)(2,1)S(1)}, u32[]{:S(2)}, u32[]{:S(2)}) %collective-permute-start.15) | collective-permute-done | bytes 32800 | tf_op jit(solution)/shard_map/ppermute | solution.py:223
  187.4 1.2 shard_map.97
  188.7 1.1 shard_map.99
  (20 shorter events, 0.2 us)
Async XLA Ops:
  0.6 6.3 %collective-permute-start.6 = (bf16[1,256,4096]{2,1,0:T(8,128)(2,1)}, bf16[1,256,4096]{2,1,0:T(8,128)(2,1)S(1)}, u32[]{:S(2)}, u32[]{:S(2)}) collective-permute-start(bf16[1,256,4096]{2,1,0:T(8,128)(2,1)} %grads_ref.3), channel_id=1, source_target_pairs={{0,32},{32,0},{1,33},{33,1},{2,34},{34,2},{3,35},{35,3},{4,36},{36... | collective-permute-start | bytes 6291464 | tf_op jit(solution)/shard_map/ppermute | solution.py:218
  6.9 1.6 copy-start
  10.2 21.8 %collective-permute-start.7 = (bf16[2,16,4096]{2,1,0:T(8,128)(2,1)S(1)}, bf16[2,16,4096]{2,1,0:T(8,128)(2,1)S(1)}, u32[]{:S(2)}, u32[]{:S(2)}) collective-permute-start(bf16[2,16,4096]{2,1,0:T(8,128)(2,1)S(1)} %get-tuple-element.20), channel_id=1, source_target_pairs={{0,64},{32,480},{64,128},{96,32},{128,192},{160,96},{192,256},{224... | collective-permute-start | bytes 786440 | tf_op jit(solution)/shard_map/ppermute | solution.py:228
  14.4 19.7 %collective-permute-start.8 = (bf16[2,16,4096]{2,1,0:T(8,128)(2,1)S(1)}, bf16[2,16,4096]{2,1,0:T(8,128)(2,1)S(1)}, u32[]{:S(2)}, u32[]{:S(2)}) collective-permute-start(bf16[2,16,4096]{2,1,0:T(8,128)(2,1)S(1)} %get-tuple-element.21), channel_id=1, source_target_pairs={{0,128},{32,416},{64,192},{96,480},{128,256},{160,32},{192,320},{2... | collective-permute-start | bytes 786440 | tf_op jit(solution)/shard_map/ppermute | solution.py:228
  21.8 20.7 %collective-permute-start.9 = (bf16[2,16,4096]{2,1,0:T(8,128)(2,1)S(1)}, bf16[2,16,4096]{2,1,0:T(8,128)(2,1)S(1)}, u32[]{:S(2)}, u32[]{:S(2)}) collective-permute-start(bf16[2,16,4096]{2,1,0:T(8,128)(2,1)S(1)} %get-tuple-element.22), channel_id=1, source_target_pairs={{0,192},{32,352},{64,256},{96,416},{128,320},{160,480},{192,384},{... | collective-permute-start | bytes 786440 | tf_op jit(solution)/shard_map/ppermute | solution.py:228
  29.1 17.0 %collective-permute-start.10 = (bf16[16,4096]{1,0:T(8,128)(2,1)S(1)}, bf16[16,4096]{1,0:T(8,128)(2,1)S(1)}, u32[]{:S(2)}, u32[]{:S(2)}) collective-permute-start(bf16[16,4096]{1,0:T(8,128)(2,1)S(1)} %get-tuple-element.23), channel_id=1, source_target_pairs={{0,256},{32,288},{64,320},{96,352},{128,384},{160,416},{192,448},{... | collective-permute-start | bytes 393224 | tf_op jit(solution)/shard_map/ppermute | solution.py:228
  43.1 3.2 %collective-permute-start.11 = (bf16[16,4096]{1,0:T(8,128)(2,1)S(1)}, bf16[16,4096]{1,0:T(8,128)(2,1)S(1)}, u32[]{:S(2)}, u32[]{:S(2)}) collective-permute-start(bf16[16,4096]{1,0:T(8,128)(2,1)S(1)} %shard_map.93), channel_id=1, source_target_pairs={{0,32},{32,0},{1,33},{33,1},{2,34},{34,2},{3,35},{35,3},{4,36},{36... | collective-permute-start | bytes 393224 | tf_op jit(solution)/shard_map/ppermute | solution.py:218
  47.9 59.7 %copy-start.3 = (s32[32]{0:T(128)S(1)}, s32[32]{0:T(128)}, u32[]{:S(2)}) copy-start(s32[32]{0:T(128)} %table_ref.1) | copy-start | bytes 388
  47.9 38.1 %all-to-all-start.2 = ((bf16[32,16,1024]{2,1,0:T(8,128)(2,1)}), bf16[32,16,1024]{2,1,0:T(8,128)(2,1)S(1)}, u32[]{:S(2)}, u32[]{:S(2)}) async-start(bf16[32,16,1024]{2,1,0:T(8,128)(2,1)} %shard_map.94), calls=%async_computation.2 | async-start | bytes 2097152 | tf_op jit(solution)/shard_map/all_to_all | solution.py:214
  86.1 21.5 %all-to-all-start = ((bf16[32,2,2,16,128]{4,3,2,1,0:T(8,128)(2,1)}), bf16[32,2,2,16,128]{4,3,2,1,0:T(8,128)(2,1)S(1)}, u32[]{:S(2)}, u32[]{:S(2)}) async-start(bf16[32,2,2,16,128]{4,3,2,1,0:T(8,128)(2,1)} %shard_map.85), calls=%async_computation | async-start | bytes 1048576 | tf_op jit(solution)/shard_map/all_to_all | solution.py:214
  93.9 32.5 %collective-permute-start.12 = (bf16[8,4,16,1024]{3,2,1,0:T(8,128)(2,1)S(1)}, bf16[8,4,16,1024]{3,2,1,0:T(8,128)(2,1)S(1)}, u32[]{:S(2)}, u32[]{:S(2)}) collective-permute-start(bf16[8,4,16,1024]{3,2,1,0:T(8,128)(2,1)S(1)} %bitcast.5), channel_id=1, source_target_pairs={{0,32},{32,0},{1,33},{33,1},{2,34},{34,2},{3,35},{35,3},{4,36},{36... | collective-permute-start | bytes 3145736 | tf_op jit(solution)/shard_map/ppermute | solution.py:218
  124.5 11.1 %collective-permute-start = (bf16[4,16,1024]{2,1,0:T(8,128)(2,1)S(1)}, bf16[4,16,1024]{2,1,0:T(8,128)(2,1)S(1)}, u32[]{:S(2)}, u32[]{:S(2)}) collective-permute-start(bf16[4,16,1024]{2,1,0:T(8,128)(2,1)S(1)} %get-tuple-element.18.mine_ref), channel_id=1, source_target_pairs={{0,32},{32,0},{1,33},{33,1},{2,34},{34,2},{3,35},{35,3},{4,36},{36... | collective-permute-start | bytes 393224 | tf_op jit(solution)/shard_map/ppermute | solution.py:218
  128.9 26.7 %all-to-all-start.3 = ((bf16[32,2,16,128]{3,2,1,0:T(8,128)(2,1)}), bf16[32,2,16,128]{3,2,1,0:T(8,128)(2,1)S(1)}, u32[]{:S(2)}, u32[]{:S(2)}) async-start(bf16[32,2,16,128]{3,2,1,0:T(8,128)(2,1)} %get-tuple-element.30), calls=%async_computation.3 | async-start | bytes 524288 | tf_op jit(solution)/shard_map/all_to_all | solution.py:214
  136.1 12.1 %collective-permute-start.2 = (bf16[2,4,16,1024]{3,2,1,0:T(8,128)(2,1)S(1)}, bf16[2,4,16,1024]{3,2,1,0:T(8,128)(2,1)S(1)}, u32[]{:S(2)}, u32[]{:S(2)}) collective-permute-start(bf16[2,4,16,1024]{3,2,1,0:T(8,128)(2,1)S(1)} %shard_map.88.pair_ref), channel_id=1, source_target_pairs={{0,384},{32,160},{64,448},{96,224},{128,0},{160,288},{192,64},{224... | collective-permute-start | bytes 786440 | tf_op jit(solution)/shard_map/ppermute | solution.py:228
  140.8 26.1 %collective-permute-start.1 = (bf16[2,4,16,1024]{3,2,1,0:T(8,128)(2,1)S(1)}, bf16[2,4,16,1024]{3,2,1,0:T(8,128)(2,1)S(1)}, u32[]{:S(2)}, u32[]{:S(2)}) collective-permute-start(bf16[2,4,16,1024]{3,2,1,0:T(8,128)(2,1)S(1)} %shard_map.88.pair_ref), channel_id=1, source_target_pairs={{0,448},{32,96},{64,0},{96,160},{128,64},{160,224},{192,128},{224,... | collective-permute-start | bytes 786440 | tf_op jit(solution)/shard_map/ppermute | solution.py:228
  148.8 18.2 %collective-permute-start.4 = (bf16[4,16,1024]{2,1,0:T(8,128)(2,1)S(1)}, bf16[4,16,1024]{2,1,0:T(8,128)(2,1)S(1)}, u32[]{:S(2)}, u32[]{:S(2)}) collective-permute-start(bf16[4,16,1024]{2,1,0:T(8,128)(2,1)S(1)} %shard_map.89), channel_id=1, source_target_pairs={{0,384},{32,160},{64,448},{96,224},{128,0},{160,288},{192,64},{224... | collective-permute-start | bytes 393224 | tf_op jit(solution)/shard_map/ppermute | solution.py:228
  153.6 13.3 %collective-permute-start.3 = (bf16[2,4,16,1024]{3,2,1,0:T(8,128)(2,1)S(1)}, bf16[2,4,16,1024]{3,2,1,0:T(8,128)(2,1)S(1)}, u32[]{:S(2)}, u32[]{:S(2)}) collective-permute-start(bf16[2,4,16,1024]{3,2,1,0:T(8,128)(2,1)S(1)} %collective-permute-done.2.in_ref.second_ref), channel_id=1, source_target_pairs={{0,448},{32,96},{64,0},{96,160},{128,64},{160,224},{192,128},{224,... | collective-permute-start | bytes 786440 | tf_op jit(solution)/shard_map/ppermute | solution.py:228
  157.1 31.5 %all-to-all-start.4 = ((bf16[32,2,2,16,128]{4,3,2,1,0:T(8,128)(2,1)}), bf16[32,2,2,16,128]{4,3,2,1,0:T(8,128)(2,1)S(1)}, u32[]{:S(2)}, u32[]{:S(2)}) async-start(bf16[32,2,2,16,128]{4,3,2,1,0:T(8,128)(2,1)} %shard_map.98), calls=%async_computation.4 | async-start | bytes 1048576 | tf_op jit(solution)/shard_map/all_to_all | solution.py:214
  166.9 21.7 %copy-start.1 = (f32[2,4,1,16,1024]{4,3,2,1,0:T(8,128)S(1)}, f32[2,4,1,16,1024]{4,3,2,1,0:T(8,128)}, u32[]{:S(2)}) copy-start(f32[2,4,1,16,1024]{4,3,2,1,0:T(8,128)} %left_ref.1) | copy-start | bytes 1572868
  166.9 21.7 %copy-start.2 = (f32[2,4,1,16,1024]{4,3,2,1,0:T(8,128)S(1)}, f32[2,4,1,16,1024]{4,3,2,1,0:T(8,128)}, u32[]{:S(2)}) copy-start(f32[2,4,1,16,1024]{4,3,2,1,0:T(8,128)} %right_ref.1) | copy-start | bytes 1572868
  167.0 4.5 %collective-permute-start.5 = (bf16[7,4,16,1024]{3,2,1,0:T(8,128)(2,1)S(1)}, bf16[7,4,16,1024]{3,2,1,0:T(8,128)(2,1)S(1)}, u32[]{:S(2)}, u32[]{:S(2)}) collective-permute-start(bf16[7,4,16,1024]{3,2,1,0:T(8,128)(2,1)S(1)} %shard_map.90.mine_ref), channel_id=1, source_target_pairs={{0,32},{32,0},{1,33},{33,1},{2,34},{34,2},{3,35},{35,3},{4,36},{36... | collective-permute-start | bytes 2752520 | tf_op jit(solution)/shard_map/ppermute | solution.py:218
  172.7 10.1 %collective-permute-start.13 = (bf16[16,1024]{1,0:T(8,128)(2,1)S(1)}, bf16[16,1024]{1,0:T(8,128)(2,1)S(1)}, u32[]{:S(2)}, u32[]{:S(2)}) collective-permute-start(bf16[16,1024]{1,0:T(8,128)(2,1)S(1)} %get-tuple-element.27), channel_id=1, source_target_pairs={{0,1},{1,2},{2,3},{3,0},{4,5},{5,6},{6,7},{7,4},{8,9},{9,10},{10,1... | collective-permute-start | bytes 98312 | tf_op jit(solution)/shard_map/ppermute | solution.py:223
  177.9 6.7 %collective-permute-start.14 = (bf16[16,1024]{1,0:T(8,128)(2,1)S(1)}, bf16[16,1024]{1,0:T(8,128)(2,1)S(1)}, u32[]{:S(2)}, u32[]{:S(2)}) collective-permute-start(bf16[16,1024]{1,0:T(8,128)(2,1)S(1)} %get-tuple-element.28), channel_id=1, source_target_pairs={{0,2},{1,3},{2,0},{3,1},{4,6},{5,7},{6,4},{7,5},{8,10},{9,11},{10,... | collective-permute-start | bytes 98312 | tf_op jit(solution)/shard_map/ppermute | solution.py:223
  179.8 7.6 %collective-permute-start.15 = (bf16[16,1024]{1,0:T(8,128)(2,1)S(1)}, bf16[16,1024]{1,0:T(8,128)(2,1)S(1)}, u32[]{:S(2)}, u32[]{:S(2)}) collective-permute-start(bf16[16,1024]{1,0:T(8,128)(2,1)S(1)} %get-tuple-element.29), channel_id=1, source_target_pairs={{0,3},{1,0},{2,1},{3,2},{4,7},{5,4},{6,5},{7,6},{8,11},{9,8},{10,9... | collective-permute-start | bytes 98312 | tf_op jit(solution)/shard_map/ppermute | solution.py:223
